TPU v7x, 32 devices: a whole 2x2x4 slice. The times are simulated.
32 devices in a mesh: wide: 16 (over z, x, core), narrow: 2 (over y).
Axes of the slice: x: 2, y: 2, z: 4, core: 2. Of those that a mesh axis runs over, the one named last changes fastest.
Arguments:
- layer_in: bfloat16 [16384, 768], P(('wide', 'narrow')), may hold values from -6 to 6
- doc_ids: int32 [32, 512], P('wide'), may hold values from 0 to 3, never falling along the last dimension, each value on 1 to 256 neighbouring positions
- query_weight: bfloat16 [768, 768], P(('wide', 'narrow')), may hold values from -0.21875 to 0.21875
- query_bias: bfloat16 [768], P(('wide', 'narrow')), may hold values from -2 to 2
- key_weight: bfloat16 [768, 768], P(('wide', 'narrow')), may hold values from -0.21875 to 0.21875
- key_bias: bfloat16 [768], P(('wide', 'narrow')), may hold values from -2 to 2
- value_weight: bfloat16 [768, 768], P(('wide', 'narrow')), may hold values from -0.21875 to 0.21875
- value_bias: bfloat16 [768], P(('wide', 'narrow')), may hold values from -2 to 2
- output_weight: bfloat16 [768, 768], P(('wide', 'narrow')), may hold values from -0.875 to 0.875
- output_bias: bfloat16 [768], P(('wide', 'narrow')), may hold values from -2 to 2
- attn_gain: bfloat16 [768], P(('wide', 'narrow')), may hold values from 0.25 to 1.75
- attn_shift: bfloat16 [768], P(('wide', 'narrow')), may hold values from -2 to 2
- inner_weight: bfloat16 [768, 3072], P('wide', 'narrow'), may hold values from -0.21875 to 0.21875
- inner_bias: bfloat16 [3072], P(('narrow', 'wide')), may hold values from -2 to 2
- outer_weight: bfloat16 [3072, 768], P('narrow', 'wide'), may hold values from -0.109375 to 0.109375
- outer_bias: bfloat16 [768], P(('wide', 'narrow')), may hold values from -2 to 2
- ffn_gain: bfloat16 [768], P(('wide', 'narrow')), may hold values from 0.25 to 1.75
- ffn_shift: bfloat16 [768], P(('wide', 'narrow')), may hold values from -2 to 2
- cotangent: bfloat16 [16384, 768], P(('wide', 'narrow')), may hold values from -6 to 6
Outputs:
- layer_out: float32 [16384, 768], P(('wide', 'narrow'))
- input_grad: float32 [16384, 768], P(('wide', 'narrow'))
- query_wgrad: float32 [768, 768], P(('wide', 'narrow'))
- query_bgrad: float32 [768], P(('wide', 'narrow'))
- key_wgrad: float32 [768, 768], P(('wide', 'narrow'))
- key_bgrad: float32 [768], P(('wide', 'narrow'))
- value_wgrad: float32 [768, 768], P(('wide', 'narrow'))
- value_bgrad: float32 [768], P(('wide', 'narrow'))
- output_wgrad: float32 [768, 768], P(('wide', 'narrow'))
- output_bgrad: float32 [768], P(('wide', 'narrow'))
- attn_ggrad: float32 [768], P(('wide', 'narrow'))
- attn_sgrad: float32 [768], P(('wide', 'narrow'))
- inner_wgrad: float32 [768, 3072], P('wide', 'narrow')
- inner_bgrad: float32 [3072], P(('narrow', 'wide'))
- outer_wgrad: float32 [3072, 768], P('narrow', 'wide')
- outer_bgrad: float32 [768], P(('wide', 'narrow'))
- ffn_ggrad: float32 [768], P(('wide', 'narrow'))
- ffn_sgrad: float32 [768], P(('wide', 'narrow'))
Inputs may be any that keep to these rules, and one draw needn't show every extreme that they name: `doc_ids`: within each pack the ids never fall, so each document is one run of 1 to 256 tokens.
All inputs are finite; a program needn't handle non-finite values.
Results may differ from a plain program's by a relative error of at most 0.018.
Values may be sent and summed in bfloat16 or wider, within the bound.
A program may use at most 192 MiB of HBM per device.

v0:
```python
import jax
import jax.numpy as jnp
from jax import lax
from jax.sharding import PartitionSpec as P

D = 768
HEADS = 12
HEAD_DIM = 64

ALL = ("wide", "narrow")
layer_eps = 1e-12
masked_score = -1e30


def swapped(shard, axis, bit):
    return lax.ppermute(shard, axis, [(i, i ^ 1 << bit) for i in range(lax.axis_size(axis))])


def part_orders(total, narrow_n, parts):
    bits = total.bit_length() - 1
    core_bit = narrow_n.bit_length() - 1
    narrow_bits = list(range(core_bit))
    wide_bits = [b for b in reversed(range(core_bit + 1, bits))]
    orders = []
    for p in range(parts):
        k = p % max(1, len(wide_bits))
        orders.append(narrow_bits + wide_bits[k:] + wide_bits[:k] + [core_bit])
    return orders


def is_pow2(n):
    return n & (n - 1) == 0


def column_splits(cols, parts):
    tiles = -(-cols // 128)
    parts = max(1, min(parts, tiles))
    edges = [min(cols, (tiles * i // parts) * 128) for i in range(parts)] + [cols]
    return [(a, b) for a, b in zip(edges[:-1], edges[1:]) if b > a]


def doubling_gather(shard, order, total):
    me = lax.axis_index(ALL)
    cur = shard
    for b in order:
        other = lax.ppermute(cur, ALL, [(i, i ^ (1 << b)) for i in range(total)])
        bit = (me >> b) & 1
        pick = (jnp.arange(2) == bit).reshape((2,) + (1,) * cur.ndim)
        cur = jnp.where(pick, cur[None], other[None])
    k = len(order)
    perm = [k - 1 - order.index(b) for b in reversed(range(k))]
    cur = cur.transpose(perm + list(range(k, cur.ndim)))
    return cur.reshape((total,) + shard.shape)


def gather_all(shard, parts=3):
    total = lax.axis_size("wide") * lax.axis_size("narrow")
    narrow_n = lax.axis_size("narrow")
    if not (is_pow2(total) and is_pow2(narrow_n)):
        return lax.all_gather(shard, ALL, axis=0, tiled=False)
    splits = column_splits(shard.shape[-1], parts)
    orders = part_orders(total, narrow_n, len(splits))
    pieces = [
        doubling_gather(shard[..., a:b], order, total) for (a, b), order in zip(splits, orders)
    ]
    return jnp.concatenate(pieces, axis=-1)


def halving_scatter(parts_in, order, total):
    me = lax.axis_index(ALL)
    nbits = total.bit_length() - 1
    cur = parts_in.reshape((2,) * nbits + parts_in.shape[1:])
    axes = list(reversed(range(nbits)))
    for b in order:
        a = axes.index(b)
        bit = (me >> b) & 1
        mine = lax.dynamic_index_in_dim(cur, bit, axis=a, keepdims=False)
        theirs = lax.dynamic_index_in_dim(cur, 1 - bit, axis=a, keepdims=False)
        got = lax.ppermute(
            theirs.astype(jnp.bfloat16), ALL, [(i, i ^ (1 << b)) for i in range(total)]
        )
        cur = mine + got.astype(jnp.float32)
        axes.pop(a)
    return cur


def scatter_sum_all(parts_in, parts=3):
    total = lax.axis_size("wide") * lax.axis_size("narrow")
    narrow_n = lax.axis_size("narrow")
    if not (is_pow2(total) and is_pow2(narrow_n)):
        return lax.psum_scatter(
            parts_in.astype(jnp.bfloat16), ALL, scatter_dimension=0, tiled=False
        ).astype(jnp.float32)
    splits = column_splits(parts_in.shape[-1], parts)
    orders = part_orders(total, narrow_n, len(splits))
    pieces = [
        halving_scatter(parts_in[..., a:b], list(reversed(order)), total)
        for (a, b), order in zip(splits, orders)
    ]
    return jnp.concatenate(pieces, axis=-1)


def narrow_gather(rows):
    n = lax.axis_size("narrow")
    if n != 2:
        return lax.all_gather(rows, "narrow", axis=0, tiled=True)
    other = swapped(rows, "narrow", 0)
    first = lax.axis_index("narrow") == 0
    return jnp.where(first, jnp.concatenate([rows, other]), jnp.concatenate([other, rows]))


def narrow_scatter_sum(part):
    n = lax.axis_size("narrow")
    if n != 2:
        return lax.psum_scatter(
            part.astype(jnp.bfloat16), "narrow", scatter_dimension=0, tiled=True
        ).astype(jnp.float32)
    rows = part.shape[0] // 2
    me = lax.axis_index("narrow")
    mine = lax.dynamic_slice_in_dim(part, me * rows, rows, 0)
    theirs = lax.dynamic_slice_in_dim(part, (1 - me) * rows, rows, 0)
    return mine + swapped(theirs.astype(jnp.bfloat16), "narrow", 0).astype(jnp.float32)


def layer_norm(values, gain_vec, shift_vec):
    center = values - jnp.mean(values, axis=-1, keepdims=True)
    spread = jnp.mean(center * center, axis=-1, keepdims=True)
    return center * lax.rsqrt(spread + layer_eps) * gain_vec + shift_vec


def gelu_exact(values):
    return jax.nn.gelu(values, approximate=False)


def rotary_tables(doc_row):
    places = jnp.arange(doc_row.shape[0], dtype=jnp.int32)
    before = jnp.sum((doc_row[None, :] < doc_row[:, None]).astype(jnp.int32), axis=1)
    position = (places - before).astype(jnp.float32)
    frequency = 10000.0 ** (-2.0 * jnp.arange(HEAD_DIM // 2, dtype=jnp.float32) / HEAD_DIM)
    angles = position[:, None] * frequency[None, :]
    return (jnp.cos(angles), jnp.sin(angles))


def rotate(values, cosine, sine_tab):
    half_dim = values.shape[-1] // 2
    first_half = values[..., :half_dim]
    second = values[..., half_dim:]
    return jnp.concatenate(
        [first_half * cosine - second * sine_tab, second * cosine + first_half * sine_tab], axis=-1
    )


def unrotate(values, cosine, sine_tab):
    half_dim = values.shape[-1] // 2
    first_half = values[..., :half_dim]
    second = values[..., half_dim:]
    return jnp.concatenate(
        [first_half * cosine + second * sine_tab, second * cosine - first_half * sine_tab], axis=-1
    )


def contract_rows(left_op, right_op):
    return lax.dot_general(
        left_op, right_op, (((0,), (0,)), ((), ())), preferred_element_type=jnp.float32
    )


def contract_cols(left_op, right_op):
    return lax.dot_general(
        left_op, right_op, (((1,), (1,)), ((), ())), preferred_element_type=jnp.float32
    )


def score_block(query_rot, key_rot, query_docs, key_docs):
    scores = jnp.einsum(
        "pqhd,pkhd->phqk", query_rot, key_rot, preferred_element_type=jnp.float32
    ) * HEAD_DIM ** (-0.5)
    same_doc = query_docs[:, :, None] == key_docs[:, None, :]
    return jnp.where(same_doc[:, None], scores, masked_score)


def attend(query_rot, key_rot, value_low, query_docs, key_docs):
    scores = score_block(query_rot, key_rot, query_docs, key_docs)
    row_peak = jnp.max(scores, axis=-1, keepdims=True)
    exponent = jnp.exp(scores - row_peak)
    totals = jnp.sum(exponent, axis=-1, keepdims=True)
    probability = (exponent / totals).astype(jnp.bfloat16)
    mixed_out = jnp.einsum(
        "phqk,pkhd->pqhd", probability, value_low, preferred_element_type=jnp.float32
    )
    return (mixed_out, row_peak + jnp.log(totals))


def attend_back(query_rot, key_rot, value_low, query_docs, key_docs, logsum, grad_mixed):
    probability = jnp.exp(score_block(query_rot, key_rot, query_docs, key_docs) - logsum)
    grad_values = jnp.einsum(
        "phqk,pqhd->pkhd",
        probability.astype(jnp.bfloat16),
        grad_mixed,
        preferred_element_type=jnp.float32,
    )
    grad_probs = jnp.einsum(
        "pqhd,pkhd->phqk", grad_mixed, value_low, preferred_element_type=jnp.float32
    )
    inner_sum = jnp.sum(probability * grad_probs, axis=-1, keepdims=True)
    grad_scores = (probability * (grad_probs - inner_sum)).astype(jnp.bfloat16)
    grad_query = jnp.einsum(
        "phqk,pkhd->pqhd", grad_scores, key_rot, preferred_element_type=jnp.float32
    ) * HEAD_DIM ** (-0.5)
    grad_keys = jnp.einsum(
        "phqk,pqhd->pkhd", grad_scores, query_rot, preferred_element_type=jnp.float32
    ) * HEAD_DIM ** (-0.5)
    return (grad_query, grad_keys, grad_values)


def ffn_forward(rows, inner_cols, inner_offset, outer_cols):
    inner_pre = jnp.dot(rows, inner_cols, preferred_element_type=jnp.float32) + inner_offset
    act_value, gelu_pull = jax.vjp(gelu_exact, inner_pre)
    act_low = act_value.astype(jnp.bfloat16)
    return act_low, gelu_pull, contract_cols(act_low, outer_cols)


def ffn_backward(grads, gelu_pull, inner_cols, outer_cols):
    grad_act = jnp.dot(grads, outer_cols, preferred_element_type=jnp.float32)
    grad_inner = gelu_pull(grad_act)[0].astype(jnp.bfloat16)
    return grad_inner, contract_cols(grad_inner, inner_cols)


def local(
    layer_in,
    doc_ids,
    query_weight,
    query_bias,
    key_weight,
    key_bias,
    value_weight,
    value_bias,
    output_weight,
    output_bias,
    attn_gain,
    attn_shift,
    inner_weight,
    inner_bias,
    outer_weight,
    outer_bias,
    ffn_gain,
    ffn_shift,
    cotangent,
):
    wide_n = lax.axis_size("wide")
    narrow_n = lax.axis_size("narrow")
    total = wide_n * narrow_n
    share = query_weight.shape[0]
    small_list = (
        query_bias,
        key_bias,
        value_bias,
        output_bias,
        attn_gain,
        attn_shift,
        outer_bias,
        ffn_gain,
        ffn_shift,
    )
    small = jnp.stack(small_list, axis=1)
    small = jnp.pad(small, ((0, 0), (0, 128 - len(small_list))))
    shard = jnp.concatenate([query_weight, key_weight, value_weight, output_weight, small], axis=1)
    full = gather_all(shard).reshape(total * share, shard.shape[1])
    qkv_full = full[:, : 3 * D]
    output_full = full[:, 3 * D : 4 * D]
    vecs = full[:, 4 * D :].astype(jnp.float32)
    (
        query_offset,
        key_offset,
        value_offset,
        output_offset,
        attn_scale,
        attn_offset,
        outer_offset,
        ffn_scale,
        ffn_offset,
    ) = [vecs[:, i] for i in range(len(small_list))]
    qkv_offset = jnp.concatenate([query_offset, key_offset, value_offset])

    ffn_rows, ffn_cols = inner_weight.shape
    bias_n = inner_bias.shape[0]
    bias_k = -(-bias_n // ffn_rows)
    bias_rows = jnp.pad(inner_bias, (0, ffn_rows * bias_k - bias_n)).reshape(ffn_rows, bias_k)
    ffn_shard = jnp.concatenate([inner_weight, outer_weight.T, bias_rows], axis=1)
    ffn_shard, full = lax.optimization_barrier((ffn_shard, full))
    ffn_all = lax.all_gather(ffn_shard, "wide", axis=0, tiled=True)
    inner_cols = ffn_all[:, :ffn_cols]
    outer_cols = ffn_all[:, ffn_cols : 2 * ffn_cols]
    inner_offset = ffn_all[:, 2 * ffn_cols :].reshape(wide_n, ffn_rows * bias_k)[:, :bias_n]
    inner_offset = inner_offset.reshape(-1).astype(jnp.float32)

    rows_dev = layer_in.shape[0]
    half_len = doc_ids.shape[1] // 2
    pack_count = rows_dev // half_len
    narrow_place = lax.axis_index("narrow")
    half_bit = narrow_place % 2
    pair_slot = narrow_place // 2
    pack_docs = lax.dynamic_slice_in_dim(doc_ids, pair_slot * pack_count, pack_count, 0)
    cosine, sine_tab = jax.vmap(rotary_tables)(pack_docs)
    cosine = cosine[:, :, None, :]
    sine_tab = sine_tab[:, :, None, :]
    own_start = half_bit * half_len
    far_start = (1 - half_bit) * half_len
    own_cos = lax.dynamic_slice_in_dim(cosine, own_start, half_len, 1)
    own_sin = lax.dynamic_slice_in_dim(sine_tab, own_start, half_len, 1)
    own_docs = lax.dynamic_slice_in_dim(pack_docs, own_start, half_len, 1)
    far_docs = lax.dynamic_slice_in_dim(pack_docs, far_start, half_len, 1)
    key_docs = jnp.concatenate([own_docs, far_docs], axis=1)

    def heads_of(values):
        return values.reshape(pack_count, half_len, HEADS, HEAD_DIM)

    qkv = jnp.dot(layer_in, qkv_full, preferred_element_type=jnp.float32) + qkv_offset
    query_rot = rotate(heads_of(qkv[:, :D]), own_cos, own_sin).astype(jnp.bfloat16)
    key_rot = rotate(heads_of(qkv[:, D : 2 * D]), own_cos, own_sin).astype(jnp.bfloat16)
    value_low = heads_of(qkv[:, 2 * D :]).astype(jnp.bfloat16)
    far_keys, far_values = swapped((key_rot, value_low), "narrow", 0)
    all_keys = jnp.concatenate([key_rot, far_keys], axis=1)
    all_values = jnp.concatenate([value_low, far_values], axis=1)
    mixed_out, logsum = attend(query_rot, all_keys, all_values, own_docs, key_docs)
    mixed_low = mixed_out.reshape(rows_dev, D).astype(jnp.bfloat16)
    attn_out = jnp.dot(mixed_low, output_full, preferred_element_type=jnp.float32) + output_offset
    res_one = layer_in.astype(jnp.float32) + attn_out
    norm_one, norm_pull = jax.vjp(layer_norm, res_one, attn_scale, attn_offset)
    norm_low = norm_one.astype(jnp.bfloat16)

    if narrow_n == 2:
        far_rows = swapped(norm_low, "narrow", 0)
        own_act, own_pull, own_part = ffn_forward(norm_low, inner_cols, inner_offset, outer_cols)
        far_act, far_pull, far_part = ffn_forward(far_rows, inner_cols, inner_offset, outer_cols)
        outer_sum = own_part + swapped(far_part.astype(jnp.bfloat16), "narrow", 0).astype(
            jnp.float32
        )
    else:
        group_rows = lax.all_gather(norm_low, "narrow", axis=0, tiled=True)
        all_act, all_pull, all_part = ffn_forward(group_rows, inner_cols, inner_offset, outer_cols)
        outer_sum = narrow_scatter_sum(all_part)
    outer_out = outer_sum + outer_offset
    res_two = norm_one + outer_out
    layer_out, ffn_pull = jax.vjp(layer_norm, res_two, ffn_scale, ffn_offset)
    grad_two, ffn_gsum, ffn_ssum = ffn_pull(cotangent.astype(jnp.float32))
    grad_outer = grad_two.astype(jnp.bfloat16)
    outer_bsum = jnp.sum(grad_outer.astype(jnp.float32), axis=0)
    if narrow_n == 2:
        far_grads = swapped(grad_outer, "narrow", 0)
        own_inner, own_back = ffn_backward(grad_outer, own_pull, inner_cols, outer_cols)
        far_inner, far_back = ffn_backward(far_grads, far_pull, inner_cols, outer_cols)
        grad_part = own_back + swapped(far_back.astype(jnp.bfloat16), "narrow", 0).astype(
            jnp.float32
        )
        outer_wsum_t = contract_rows(grad_outer, own_act) + contract_rows(far_grads, far_act)
        inner_wsum = contract_rows(norm_low, own_inner) + contract_rows(far_rows, far_inner)
        inner_bsum = jnp.sum(own_inner.astype(jnp.float32), axis=0) + jnp.sum(
            far_inner.astype(jnp.float32), axis=0
        )
    else:
        group_grads = lax.all_gather(grad_outer, "narrow", axis=0, tiled=True)
        all_inner, all_back = ffn_backward(group_grads, all_pull, inner_cols, outer_cols)
        grad_part = narrow_scatter_sum(all_back)
        outer_wsum_t = contract_rows(group_grads, all_act)
        inner_wsum = contract_rows(group_rows, all_inner)
        inner_bsum = jnp.sum(all_inner.astype(jnp.float32), axis=0)
    bsum_rows = jnp.pad(
        inner_bsum.reshape(wide_n, bias_n), ((0, 0), (0, ffn_rows * bias_k - bias_n))
    ).reshape(wide_n * ffn_rows, bias_k)
    ffn_sums = jnp.concatenate([inner_wsum, outer_wsum_t, bsum_rows], axis=1).astype(jnp.bfloat16)
    ffn_mine = lax.psum_scatter(ffn_sums, "wide", scatter_dimension=0, tiled=True)
    ffn_mine = ffn_mine.astype(jnp.float32)
    inner_wgrad = ffn_mine[:, :ffn_cols]
    outer_wgrad = ffn_mine[:, ffn_cols : 2 * ffn_cols].T
    inner_bgrad = ffn_mine[:, 2 * ffn_cols :].reshape(-1)[:bias_n]

    grad_norm = grad_two + grad_part
    grad_one, attn_gsum, attn_ssum = norm_pull(grad_norm)
    grad_attn = grad_one.astype(jnp.bfloat16)
    output_bsum = jnp.sum(grad_attn.astype(jnp.float32), axis=0)
    output_wsum = contract_rows(mixed_low, grad_attn)
    early_small = jnp.stack(
        [output_bsum, attn_gsum, attn_ssum, outer_bsum, ffn_gsum, ffn_ssum], axis=1
    )
    early = jnp.concatenate(
        [output_wsum.reshape(total, share, D), early_small.reshape(total, share, -1)], axis=2
    )

    grad_mixed = heads_of(contract_cols(grad_attn, output_full).astype(jnp.bfloat16))
    grad_qrot, grad_kall, grad_vall = attend_back(
        query_rot, all_keys, all_values, own_docs, key_docs, logsum, grad_mixed
    )
    back_keys, back_values = swapped(
        (
            grad_kall[:, half_len:].astype(jnp.bfloat16),
            grad_vall[:, half_len:].astype(jnp.bfloat16),
        ),
        "narrow",
        0,
    )
    grad_krot = grad_kall[:, :half_len] + back_keys.astype(jnp.float32)
    grad_values = (grad_vall[:, :half_len] + back_values.astype(jnp.float32)).astype(jnp.bfloat16)
    grad_query = unrotate(grad_qrot, own_cos, own_sin).astype(jnp.bfloat16)
    grad_keys = unrotate(grad_krot, own_cos, own_sin).astype(jnp.bfloat16)
    grad_qkv = jnp.concatenate(
        [
            grad_query.reshape(rows_dev, D),
            grad_keys.reshape(rows_dev, D),
            grad_values.reshape(rows_dev, D),
        ],
        axis=1,
    )
    qkv_wsum = contract_rows(layer_in, grad_qkv)
    qkv_bsum = jnp.sum(grad_qkv.astype(jnp.float32), axis=0).reshape(3, D)
    input_grad = grad_one + contract_cols(grad_qkv, qkv_full)
    late = jnp.concatenate(
        [
            qkv_wsum.reshape(total, share, 3 * D),
            qkv_bsum.T.reshape(total, share, 3),
            early,
        ],
        axis=2,
    )
    late_mine = scatter_sum_all(late)
    early_mine = late_mine[:, 3 * D + 3 :]
    query_wgrad = late_mine[:, :D]
    key_wgrad = late_mine[:, D : 2 * D]
    value_wgrad = late_mine[:, 2 * D : 3 * D]
    query_bgrad = late_mine[:, 3 * D]
    key_bgrad = late_mine[:, 3 * D + 1]
    value_bgrad = late_mine[:, 3 * D + 2]
    output_wgrad = early_mine[:, :D]
    output_bgrad = early_mine[:, D]
    attn_ggrad = early_mine[:, D + 1]
    attn_sgrad = early_mine[:, D + 2]
    outer_bgrad = early_mine[:, D + 3]
    ffn_ggrad = early_mine[:, D + 4]
    ffn_sgrad = early_mine[:, D + 5]
    return (
        layer_out,
        input_grad,
        query_wgrad,
        query_bgrad,
        key_wgrad,
        key_bgrad,
        value_wgrad,
        value_bgrad,
        output_wgrad,
        output_bgrad,
        attn_ggrad,
        attn_sgrad,
        inner_wgrad,
        inner_bgrad,
        outer_wgrad,
        outer_bgrad,
        ffn_ggrad,
        ffn_sgrad,
    )


def solution(mesh):
    return jax.shard_map(
        local,
        mesh=mesh,
        in_specs=(
            P(("wide", "narrow"), None),
            P("wide", None),
            P(("wide", "narrow"), None),
            P(("wide", "narrow")),
            P(("wide", "narrow"), None),
            P(("wide", "narrow")),
            P(("wide", "narrow"), None),
            P(("wide", "narrow")),
            P(("wide", "narrow"), None),
            P(("wide", "narrow")),
            P(("wide", "narrow")),
            P(("wide", "narrow")),
            P("wide", "narrow"),
            P(("narrow", "wide")),
            P("narrow", "wide"),
            P(("wide", "narrow")),
            P(("wide", "narrow")),
            P(("wide", "narrow")),
            P(("wide", "narrow"), None),
        ),
        out_specs=(
            P(("wide", "narrow"), None),
            P(("wide", "narrow"), None),
            P(("wide", "narrow"), None),
            P(("wide", "narrow")),
            P(("wide", "narrow"), None),
            P(("wide", "narrow")),
            P(("wide", "narrow"), None),
            P(("wide", "narrow")),
            P(("wide", "narrow"), None),
            P(("wide", "narrow")),
            P(("wide", "narrow")),
            P(("wide", "narrow")),
            P("wide", "narrow"),
            P(("narrow", "wide")),
            P("narrow", "wide"),
            P(("wide", "narrow")),
            P(("wide", "narrow")),
            P(("wide", "narrow")),
        ),
        check_vma=False,
    )
```

profile of v0, /device:TPU:0, one launch (start us, length us, event | category | flops | bytes accessed | tf_op | source)
XLA Modules:
  0.0 426.6 jit_solution(14010367139882392598)
XLA Ops:
  38.0 13.0 %collective-permute-done.12 = bf16[2,2,24,1152]{3,2,1,0:T(8,128)(2,1)S(1)} collective-permute-done((bf16[2,2,24,1152]{3,2,1,0:T(8,128)(2,1)S(1)}, bf16[2,2,24,1152]{3,2,1,0:T(8,128)(2,1)S(1)}, u32[]{:S(2)}, u32[]{:S(2)}) %collective-permute-start.12) | collective-permute-done | bytes 221216 | tf_op jit(solution)/shard_map/ppermute | solution.py:46
  51.4 5.2 %collective-permute-done.8 = bf16[2,2,2,24,1024]{4,3,2,0,1:T(8,128)(2,1)S(1)} collective-permute-done((bf16[2,2,2,24,1024]{4,3,2,0,1:T(8,128)(2,1)S(1)}, bf16[2,2,2,24,1024]{4,3,2,0,1:T(8,128)(2,1)S(1)}, u32[]{:S(2)}, u32[]{:S(2)}) %collective-permute-start.8) | collective-permute-done | bytes 393248 | tf_op jit(solution)/shard_map/ppermute | solution.py:46
  57.3 8.7 %collective-permute-done.13 = bf16[2,2,2,24,1152]{4,3,2,1,0:T(8,128)(2,1)S(1)} collective-permute-done((bf16[2,2,2,24,1152]{4,3,2,1,0:T(8,128)(2,1)S(1)}, bf16[2,2,2,24,1152]{4,3,2,1,0:T(8,128)(2,1)S(1)}, u32[]{:S(2)}, u32[]{:S(2)}) %collective-permute-start.13) | collective-permute-done | bytes 442400 | tf_op jit(solution)/shard_map/ppermute | solution.py:46
  75.9 4.6 %fusion.6 = f32[512,2304]{0,1:T(8,128)S(1)} fusion(bf16[512,768]{1,0:T(8,128)(2,1)S(1)} %copy-done.45, bf16[768,3200]{1,0:T(8,128)(2,1)} %pad_maximum_fusion, f32[2304]{0:T(1024)S(1)} %pad_maximum_fusion.17), kind=kOutput, calls=%fused_computation.14 | convolution fusion | flops 1813118976 | bytes 9053184 | tf_op jit(solution)/shard_map/dot_general | solution.py:318
  99.9 15.4 %collective-permute-done.15 = bf16[2,256,12,64]{1,3,2,0:T(8,128)(2,1)} collective-permute-done((bf16[2,256,12,64]{1,3,2,0:T(8,128)(2,1)}, bf16[2,256,12,64]{1,3,2,0:T(8,128)(2,1)}, u32[]{:S(2)}, u32[]{:S(2)}) %collective-permute-start.15) | collective-permute-done | bytes 786464 | tf_op jit(solution)/shard_map/ppermute | solution.py:16
  117.4 13.9 %collective-permute-done.16 = bf16[2,256,12,64]{1,3,2,0:T(8,128)(2,1)} collective-permute-done((bf16[2,256,12,64]{1,3,2,0:T(8,128)(2,1)}, bf16[2,256,12,64]{1,3,2,0:T(8,128)(2,1)}, u32[]{:S(2)}, u32[]{:S(2)}) %collective-permute-start.16) | collective-permute-done | bytes 786464 | tf_op jit(solution)/shard_map/ppermute | solution.py:16
  139.7 4.7 %fusion.60 = bf16[2,256,12,64]{1,3,2,0:T(8,128)(2,1)S(1)} fusion(bf16[2,512,12,64]{1,3,2,0:T(8,128)(2,1)S(1)} %copy-done.17, f32[2,12,256]{2,1,0:T(8,128)S(1)} %fusion, f32[2,12,256]{2,1,0:T(8,128)S(1)} %get-tuple-element.95, f32[2,12,256,512]{3,2,1,0:T(8,128)S(1)} %get-tuple-element.96, pred[2,256,512]{2,1,0:T(8,128)(4,1)S(1)} %broadcast_compare_fusion), kind=kOutput, calls=%fused_computation.121 | convolution fusion | flops 418775040 | bytes 15253504 | tf_op jit(solution)/shard_map/phqk,pkhd->pqhd/dot_general | solution.py:188
  152.1 15.0 %collective-permute-done.17 = bf16[512,768]{1,0:T(8,128)(2,1)} collective-permute-done((bf16[512,768]{1,0:T(8,128)(2,1)}, bf16[512,768]{1,0:T(8,128)(2,1)}, u32[]{:S(2)}, u32[]{:S(2)}) %collective-permute-start.17) | collective-permute-done | bytes 786464 | tf_op jit(solution)/shard_map/ppermute | solution.py:16
  167.1 23.8 %multiply_convert_fusion.1 = (bf16[512,1536]{1,0:T(8,128)(2,1)S(1)}, f32[512,1536]{1,0:T(8,128)}, f32[512,1536]{1,0:T(8,128)}) fusion(f32[1536]{0:T(1024)S(1)} %reshape.357, bf16[512,768]{1,0:T(8,128)(2,1)} %collective-permute-done.17, bf16[768,3074]{1,0:T(8,128)(2,1)} %all-gather.2.cloned.1.call-done), kind=kOutput, calls=%fused_computation.30 | convolution fusion | flops 1259864064 | bytes 11016192 | tf_op jit(solution)/shard_map/dot_general | solution.py:217
  192.9 11.0 %multiply_convert_fusion.2 = (bf16[512,1536]{1,0:T(8,128)(2,1)S(1)}, f32[512,1536]{1,0:T(8,128)}, f32[512,1536]{1,0:T(8,128)}) fusion(f32[1536]{0:T(1024)S(1)} %reshape.357, bf16[512,768]{1,0:T(8,128)(2,1)} %fusion.61, bf16[768,3074]{1,0:T(8,128)(2,1)S(1)} %copy-done.42), kind=kOutput, calls=%fused_computation.43 | convolution fusion | flops 1259864064 | bytes 11018240 | tf_op jit(solution)/shard_map/dot_general | solution.py:217
  203.9 6.4 %collective-permute-done.18 = bf16[512,768]{1,0:T(8,128)(2,1)S(1)} collective-permute-done((bf16[512,768]{1,0:T(8,128)(2,1)S(1)}, bf16[512,768]{1,0:T(8,128)(2,1)S(1)}, u32[]{:S(2)}, u32[]{:S(2)}) %collective-permute-start.18) | collective-permute-done | bytes 786464 | tf_op jit(solution)/shard_map/ppermute | solution.py:16
  220.8 6.1 %convert_reduce_fusion.2 = (f32[1536]{0:T(1024)S(1)}, bf16[512,1536]{1,0:T(8,128)(2,1)S(1)}) fusion(f32[512,1536]{1,0:T(8,128)} %get-tuple-element.53, f32[512,1536]{1,0:T(8,128)} %get-tuple-element.100, bf16[512,768]{1,0:T(8,128)(2,1)} %get-tuple-element.45, bf16[768,3074]{1,0:T(8,128)(2,1)} %all-gather.2.cloned.1.call-done), kind=kOutput, calls=%fused_computation.26 | convolution fusion | flops 1220540928 | bytes 11016192 | tf_op jit(solution)/shard_map/dot_general | solution.py:224
  253.2 5.4 %pad_maximum_fusion.1 = bf16[768,3074]{1,0:T(8,128)(2,1)} fusion(bf16[768,2]{1,0:T(8,128)(2,1)S(1)} %add.344, bf16[768,1536]{1,0:T(8,128)(2,1)} %add_convert_fusion, bf16[768,1536]{1,0:T(8,128)(2,1)} %add_convert_fusion.1), kind=kLoop, calls=%fused_computation.12 | loop fusion | flops 14164992 | bytes 9443328 | tf_op jit(solution)/shard_map/concatenate | solution.py:371
  259.3 5.3 %multiply_reduce_fusion.1 = (f32[768]{0:T(1024)}, f32[512]{0:T(512)S(1)}, f32[768]{0:T(1024)}, f32[512,768]{1,0:T(8,128)S(1)}) fusion(f32[512,768]{1,0:T(8,128)S(1)} %get-tuple-element.98, f32[512]{0:T(512)S(1)} %fusion.89, f32[512]{0:T(512)S(1)} %broadcast_multiply_fusion.2, f32[768]{0:T(1024)S(1)} %get-tuple-element.30, ...), kind=kOutput, calls=%fused_computation.88 | convolution fusion | flops 1212676096 | bytes 9454592 | tf_op jit(solution)/shard_map/dot_general | solution.py:169
  270.9 8.4 %fusion.23 = f32[2,512,12,64]{1,3,2,0:T(8,128)S(1)} fusion(f32[2,12,256]{2,1,0:T(8,128)S(1)} %copy-done.38, f32[2,12,256,512]{3,2,1,0:T(8,128)} %copy-done, pred[2,256,512]{2,1,0:T(8,128)(4,1)S(1)} %copy-done.10, bf16[2,256,12,64]{1,0,3,2:T(2,128)(2,1)S(1)} %reshape.348), kind=kOutput, calls=%fused_computation.67 | convolution fusion | flops 415236096 | bytes 16801792 | tf_op jit(solution)/shard_map/phqk,pqhd->pkhd/dot_general | solution.py:196
  279.4 11.1 %multiply_reduce_fusion = (f32[2,12,256]{2,1,0:T(8,128)S(1)}, f32[2,12,256,512]{3,2,1,0:T(8,128)}) fusion(f32[2,12,256]{2,1,0:T(8,128)S(1)} %copy-done.38, f32[2,12,256,512]{3,2,1,0:T(8,128)} %copy-done, pred[2,256,512]{2,1,0:T(8,128)(4,1)S(1)} %copy-done.10, bf16[2,512,12,64]{1,3,2,0:T(8,128)(2,1)S(1)} %copy-done.18, bf16[2,256,12,64]{1,0,3,2:T(2,128)(2,1)S(1)} %reshape.348), kind=kOutput, calls=%fused_computation.1 | convolution fusion | flops 418375680 | bytes 27836416 | tf_op jit(solution)/shard_map/pqhd,pkhd->phqk/dot_general | solution.py:202
  293.1 7.1 %multiply_convert_fusion = bf16[2,12,256,512]{3,2,1,0:T(8,128)(2,1)S(1)} fusion(f32[2,12,256,512]{3,2,1,0:T(8,128)} %get-tuple-element.105, f32[2,12,256]{2,1,0:T(8,128)S(1)} %get-tuple-element.104, f32[2,12,256]{2,1,0:T(8,128)S(1)} %copy-done.38, f32[2,12,256,512]{3,2,1,0:T(8,128)S(1)} %bitcast.173, pred[2,256,512]{2,1,0:T(8,128)(4,1)S(1)} %copy-done.10), kind=kLoop, calls=%fused_computation | loop fusion | flops 18874368 | bytes 31768576 | tf_op jit(solution)/shard_map/convert_element_type | solution.py:206
  311.1 5.2 %multiply_bitcast_fusion.1 = f32[2,256,12,64]{1,3,2,0:T(8,128)S(1)} fusion(bf16[2,12,256,512]{3,2,1,0:T(8,128)(2,1)} %copy-done.1, bf16[2,256,12,64]{1,3,2,0:T(8,128)(2,1)} %collective-permute-done.16, bf16[2,256,12,32]{1,3,2,0:T(8,128)(2,1)S(1)} %copy-done.14, bf16[2,256,12,32]{1,3,2,0:T(8,128)(2,1)S(1)} %copy-done.16), kind=kOutput, calls=%fused_computation.91 | convolution fusion | flops 407764992 | bytes 9437184 | tf_op jit(solution)/shard_map/phqk,pkhd->pqhd/dot_general | solution.py:207
  318.8 6.1 %collective-permute-done.21 = bf16[2,256,12,64]{1,3,2,0:T(8,128)(2,1)} collective-permute-done((bf16[2,256,12,64]{1,3,2,0:T(8,128)(2,1)}, bf16[2,256,12,64]{1,3,2,0:T(8,128)(2,1)}, u32[]{:S(2)}, u32[]{:S(2)}) %collective-permute-start.21) | collective-permute-done | bytes 786464 | tf_op jit(solution)/shard_map/ppermute | solution.py:16
  341.4 12.6 %concatenate.78 = f32[32,24,3081]{2,1,0:T(8,128)} concatenate(f32[32,24,2304]{2,1,0:T(8,128)} %bitcast.175, f32[32,24,3]{2,1,0:T(8,128)} %bitcast.193, f32[32,24,768]{2,1,0:T(8,128)} %fusion.69, f32[32,24,1]{2,1,0:T(8,128)} %stack.65, f32[32,24,1]{2,1,0:T(8,128)} %stack.66, f32[32,24,1]{2,1,0:T(8,128)} %stack.67, f32[32,24,1]{2,1,0:T(8,128)S(1)} %copy-done.33, ...), dimensions={2} | concatenate | bytes 18929664 | tf_op jit(solution)/shard_map/concatenate | solution.py:417
  357.2 5.4 %add_add_fusion.5 = f32[512,768]{1,0:T(8,128)} fusion(f32[512,768]{1,0:T(8,128)S(1)} %copy-done.7, bf16[512,2304]{0,1:T(8,128)(2,1)S(1)} %copy-done.12, bf16[768,3200]{1,0:T(8,128)(2,1)} %pad_maximum_fusion, f32[512]{0:T(512)S(1)} %negate_multiply_fusion.2), kind=kOutput, calls=%fused_computation.114 | convolution fusion | flops 1812725760 | bytes 9046016 | tf_op jit(solution)/shard_map/dot_general | solution.py:169
  370.6 4.6 %collective-permute-done.24 = bf16[2,2,2,24,1024]{4,3,2,1,0:T(8,128)(2,1)S(1)} collective-permute-done((bf16[2,2,2,24,1024]{4,3,2,1,0:T(8,128)(2,1)S(1)}, bf16[2,2,2,24,1024]{4,3,2,1,0:T(8,128)(2,1)S(1)}, u32[]{:S(2)}, u32[]{:S(2)}) %collective-permute-start.24) | collective-permute-done | bytes 393248 | tf_op jit(solution)/shard_map/ppermute | solution.py:79
  375.4 11.8 %collective-permute-done.34 = bf16[2,2,2,24,1024]{4,3,2,0,1:T(8,128)(2,1)S(1)} collective-permute-done((bf16[2,2,2,24,1024]{4,3,2,0,1:T(8,128)(2,1)S(1)}, bf16[2,2,2,24,1024]{4,3,2,0,1:T(8,128)(2,1)S(1)}, u32[]{:S(2)}, u32[]{:S(2)}) %collective-permute-start.34) | collective-permute-done | bytes 393248 | tf_op jit(solution)/shard_map/ppermute | solution.py:79
  396.5 7.5 %collective-permute-done.30 = bf16[2,2,24,1033]{3,2,1,0:T(8,128)(2,1)S(1)} collective-permute-done((bf16[2,2,24,1033]{3,2,1,0:T(8,128)(2,1)S(1)}, bf16[2,2,24,1033]{3,2,1,0:T(8,128)(2,1)S(1)}, u32[]{:S(2)}, u32[]{:S(2)}) %collective-permute-start.30) | collective-permute-done | bytes 198368 | tf_op jit(solution)/shard_map/ppermute | solution.py:79
  (336 shorter events, 192.4 us)
Async XLA Ops:
  7.2 142.0 %all-gather.2.cloned.1.call-start = ((), (), s32[]{:S(2)}) async-start(), calls=%async_computation.1 | async-start | bytes 5222400 | tf_op jit(solution)/shard_map/all_gather | solution.py:291
  8.1 11.6 %collective-permute-start = (bf16[24,1024]{1,0:T(8,128)(2,1)S(1)}, bf16[24,1024]{1,0:T(8,128)(2,1)S(1)}, u32[]{:S(2)}, u32[]{:S(2)}) collective-permute-start(bf16[24,1024]{1,0:T(8,128)(2,1)S(1)} %get-tuple-element.85), channel_id=1, source_target_pairs={{0,1},{1,0},{2,3},{3,2},{4,5},{5,4},{6,7},{7,6},{8,9},{9,8},{10,11... | collective-permute-start | bytes 147464 | tf_op jit(solution)/shard_map/ppermute | solution.py:46
  29.9 21.1 %collective-permute-start.12 = (bf16[2,2,24,1152]{3,2,1,0:T(8,128)(2,1)S(1)}, bf16[2,2,24,1152]{3,2,1,0:T(8,128)(2,1)S(1)}, u32[]{:S(2)}, u32[]{:S(2)}) collective-permute-start(bf16[2,2,24,1152]{3,2,1,0:T(8,128)(2,1)S(1)} %broadcast_select_fusion.11), channel_id=1, source_target_pairs={{0,16},{1,17},{2,18},{3,19},{4,20},{5,21},{6,22},{7,23},{8,24},{9,... | collective-permute-start | bytes 663560 | tf_op jit(solution)/shard_map/ppermute | solution.py:46
  32.0 24.6 %collective-permute-start.8 = (bf16[2,2,2,24,1024]{4,3,2,0,1:T(8,128)(2,1)S(1)}, bf16[2,2,2,24,1024]{4,3,2,0,1:T(8,128)(2,1)S(1)}, u32[]{:S(2)}, u32[]{:S(2)}) collective-permute-start(bf16[2,2,2,24,1024]{4,3,2,0,1:T(8,128)(2,1)S(1)} %broadcast_select_fusion.7), channel_id=1, source_target_pairs={{0,16},{1,17},{2,18},{3,19},{4,20},{5,21},{6,22},{7,23},{8,24},{9,... | collective-permute-start | bytes 1179656 | tf_op jit(solution)/shard_map/ppermute | solution.py:46
  36.4 29.9 %collective-permute-start.3 = (bf16[2,2,2,24,1024]{4,3,2,0,1:T(8,128)(2,1)S(1)}, bf16[2,2,2,24,1024]{4,3,2,0,1:T(8,128)(2,1)S(1)}, u32[]{:S(2)}, u32[]{:S(2)}) collective-permute-start(bf16[2,2,2,24,1024]{4,3,2,0,1:T(8,128)(2,1)S(1)} %broadcast_select_fusion.9), channel_id=1, source_target_pairs={{0,4},{1,5},{2,6},{3,7},{4,0},{5,1},{6,2},{7,3},{8,12},{9,13},{10,... | collective-permute-start | bytes 1179656 | tf_op jit(solution)/shard_map/ppermute | solution.py:46
  51.2 14.8 %collective-permute-start.13 = (bf16[2,2,2,24,1152]{4,3,2,1,0:T(8,128)(2,1)S(1)}, bf16[2,2,2,24,1152]{4,3,2,1,0:T(8,128)(2,1)S(1)}, u32[]{:S(2)}, u32[]{:S(2)}) collective-permute-start(bf16[2,2,2,24,1152]{4,3,2,1,0:T(8,128)(2,1)S(1)} %broadcast_select_fusion.6), channel_id=1, source_target_pairs={{0,8},{1,9},{2,10},{3,11},{4,12},{5,13},{6,14},{7,15},{8,0},{9,1},... | collective-permute-start | bytes 1327112 | tf_op jit(solution)/shard_map/ppermute | solution.py:46
  73.7 341.1 %reduce-scatter.2.cloned.1.call-start = ((), (), s32[]{:S(2)}) async-start(), calls=%async_computation.2 | async-start | bytes 5222400 | tf_op jit(solution)/shard_map/reduce_scatter | solution.py:372
  94.6 20.7 %collective-permute-start.15 = (bf16[2,256,12,64]{1,3,2,0:T(8,128)(2,1)}, bf16[2,256,12,64]{1,3,2,0:T(8,128)(2,1)}, u32[]{:S(2)}, u32[]{:S(2)}) collective-permute-start(bf16[2,256,12,64]{1,3,2,0:T(8,128)(2,1)} %get-tuple-element.73), channel_id=1, source_target_pairs={{0,1},{1,0},{2,3},{3,2},{4,5},{5,4},{6,7},{7,6},{8,9},{9,8},{10,11... | collective-permute-start | bytes 2359304 | tf_op jit(solution)/shard_map/ppermute | solution.py:16
  98.1 33.2 %collective-permute-start.16 = (bf16[2,256,12,64]{1,3,2,0:T(8,128)(2,1)}, bf16[2,256,12,64]{1,3,2,0:T(8,128)(2,1)}, u32[]{:S(2)}, u32[]{:S(2)}) collective-permute-start(bf16[2,256,12,64]{1,3,2,0:T(8,128)(2,1)} %pad_maximum_fusion.4), channel_id=1, source_target_pairs={{0,1},{1,0},{2,3},{3,2},{4,5},{5,4},{6,7},{7,6},{8,9},{9,8},{10,11... | collective-permute-start | bytes 2359304 | tf_op jit(solution)/shard_map/ppermute | solution.py:16
  148.1 19.1 %collective-permute-start.17 = (bf16[512,768]{1,0:T(8,128)(2,1)}, bf16[512,768]{1,0:T(8,128)(2,1)}, u32[]{:S(2)}, u32[]{:S(2)}) collective-permute-start(bf16[512,768]{1,0:T(8,128)(2,1)} %fusion.61), channel_id=1, source_target_pairs={{0,1},{1,0},{2,3},{3,2},{4,5},{5,4},{6,7},{7,6},{8,9},{9,8},{10,11... | collective-permute-start | bytes 2359304 | tf_op jit(solution)/shard_map/ppermute | solution.py:16
  192.4 17.9 %collective-permute-start.18 = (bf16[512,768]{1,0:T(8,128)(2,1)S(1)}, bf16[512,768]{1,0:T(8,128)(2,1)S(1)}, u32[]{:S(2)}, u32[]{:S(2)}) collective-permute-start(bf16[512,768]{1,0:T(8,128)(2,1)S(1)} %fusion.54), channel_id=1, source_target_pairs={{0,1},{1,0},{2,3},{3,2},{4,5},{5,4},{6,7},{7,6},{8,9},{9,8},{10,11... | collective-permute-start | bytes 2359304 | tf_op jit(solution)/shard_map/ppermute | solution.py:16
  217.2 17.3 %collective-permute-start.19 = (bf16[512,768]{1,0:T(8,128)(2,1)}, bf16[512,768]{1,0:T(8,128)(2,1)}, u32[]{:S(2)}, u32[]{:S(2)}) collective-permute-start(bf16[512,768]{1,0:T(8,128)(2,1)} %get-tuple-element.45), channel_id=1, source_target_pairs={{0,1},{1,0},{2,3},{3,2},{4,5},{5,4},{6,7},{7,6},{8,9},{9,8},{10,11... | collective-permute-start | bytes 2359304 | tf_op jit(solution)/shard_map/ppermute | solution.py:16
  242.6 16.5 %collective-permute-start.20 = (bf16[512,768]{1,0:T(8,128)(2,1)}, bf16[512,768]{1,0:T(8,128)(2,1)}, u32[]{:S(2)}, u32[]{:S(2)}) collective-permute-start(bf16[512,768]{1,0:T(8,128)(2,1)} %fusion.51), channel_id=1, source_target_pairs={{0,1},{1,0},{2,3},{3,2},{4,5},{5,4},{6,7},{7,6},{8,9},{9,8},{10,11... | collective-permute-start | bytes 2359304 | tf_op jit(solution)/shard_map/ppermute | solution.py:16
  291.5 24.9 %collective-permute-start.22 = (bf16[2,256,12,64]{1,3,2,0:T(8,128)(2,1)}, bf16[2,256,12,64]{1,3,2,0:T(8,128)(2,1)}, u32[]{:S(2)}, u32[]{:S(2)}) collective-permute-start(bf16[2,256,12,64]{1,3,2,0:T(8,128)(2,1)} %slice.347), channel_id=1, source_target_pairs={{0,1},{1,0},{2,3},{3,2},{4,5},{5,4},{6,7},{7,6},{8,9},{9,8},{10,11... | collective-permute-start | bytes 2359304 | tf_op jit(solution)/shard_map/ppermute | solution.py:16
  303.9 21.0 %collective-permute-start.21 = (bf16[2,256,12,64]{1,3,2,0:T(8,128)(2,1)}, bf16[2,256,12,64]{1,3,2,0:T(8,128)(2,1)}, u32[]{:S(2)}, u32[]{:S(2)}) collective-permute-start(bf16[2,256,12,64]{1,3,2,0:T(8,128)(2,1)} %slice.348), channel_id=1, source_target_pairs={{0,1},{1,0},{2,3},{3,2},{4,5},{5,4},{6,7},{7,6},{8,9},{9,8},{10,11... | collective-permute-start | bytes 2359304 | tf_op jit(solution)/shard_map/ppermute | solution.py:16
  337.6 25.0 %collective-permute-start.23 = (bf16[2,2,2,2,24,1024]{5,4,3,2,1,0:T(8,128)(2,1)}, bf16[2,2,2,2,24,1024]{5,4,3,2,1,0:T(8,128)(2,1)}, u32[]{:S(2)}, u32[]{:S(2)}) collective-permute-start(bf16[2,2,2,2,24,1024]{5,4,3,2,1,0:T(8,128)(2,1)} %fusion.67), channel_id=1, source_target_pairs={{0,2},{1,3},{2,0},{3,1},{4,6},{5,7},{6,4},{7,5},{8,10},{9,11},{10,... | collective-permute-start | bytes 2359304 | tf_op jit(solution)/shard_map/ppermute | solution.py:79
  338.6 27.0 %collective-permute-start.33 = (bf16[2,2,2,2,24,1024]{5,4,3,1,2,0:T(8,128)(2,1)}, bf16[2,2,2,2,24,1024]{5,4,3,1,2,0:T(8,128)(2,1)}, u32[]{:S(2)}, u32[]{:S(2)}) collective-permute-start(bf16[2,2,2,2,24,1024]{5,4,3,1,2,0:T(8,128)(2,1)} %fusion.68), channel_id=1, source_target_pairs={{0,2},{1,3},{2,0},{3,1},{4,6},{5,7},{6,4},{7,5},{8,10},{9,11},{10,... | collective-permute-start | bytes 2359304 | tf_op jit(solution)/shard_map/ppermute | solution.py:79
  356.5 11.5 %collective-permute-start.28 = (bf16[2,2,2,2,24,1033]{5,4,3,2,1,0:T(8,128)(2,1)S(1)}, bf16[2,2,2,2,24,1033]{5,4,3,2,1,0:T(8,128)(2,1)S(1)}, u32[]{:S(2)}, u32[]{:S(2)}) collective-permute-start(bf16[2,2,2,2,24,1033]{5,4,3,2,1,0:T(8,128)(2,1)S(1)} %fusion.66), channel_id=1, source_target_pairs={{0,2},{1,3},{2,0},{3,1},{4,6},{5,7},{6,4},{7,5},{8,10},{9,11},{10,... | collective-permute-start | bytes 2380040 | tf_op jit(solution)/shard_map/ppermute | solution.py:79
  364.1 11.1 %collective-permute-start.24 = (bf16[2,2,2,24,1024]{4,3,2,1,0:T(8,128)(2,1)S(1)}, bf16[2,2,2,24,1024]{4,3,2,1,0:T(8,128)(2,1)S(1)}, u32[]{:S(2)}, u32[]{:S(2)}) collective-permute-start(bf16[2,2,2,24,1024]{4,3,2,1,0:T(8,128)(2,1)S(1)} %fusion.76), channel_id=1, source_target_pairs={{0,4},{1,5},{2,6},{3,7},{4,0},{5,1},{6,2},{7,3},{8,12},{9,13},{10,... | collective-permute-start | bytes 1179656 | tf_op jit(solution)/shard_map/ppermute | solution.py:79
  367.1 20.1 %collective-permute-start.34 = (bf16[2,2,2,24,1024]{4,3,2,0,1:T(8,128)(2,1)S(1)}, bf16[2,2,2,24,1024]{4,3,2,0,1:T(8,128)(2,1)S(1)}, u32[]{:S(2)}, u32[]{:S(2)}) collective-permute-start(bf16[2,2,2,24,1024]{4,3,2,0,1:T(8,128)(2,1)S(1)} %fusion.77), channel_id=1, source_target_pairs={{0,16},{1,17},{2,18},{3,19},{4,20},{5,21},{6,22},{7,23},{8,24},{9,... | collective-permute-start | bytes 1179656 | tf_op jit(solution)/shard_map/ppermute | solution.py:79
  368.2 21.7 %collective-permute-start.29 = (bf16[2,2,2,24,1033]{4,3,2,1,0:T(8,128)(2,1)S(1)}, bf16[2,2,2,24,1033]{4,3,2,1,0:T(8,128)(2,1)S(1)}, u32[]{:S(2)}, u32[]{:S(2)}) collective-permute-start(bf16[2,2,2,24,1033]{4,3,2,1,0:T(8,128)(2,1)S(1)} %fusion.75), channel_id=1, source_target_pairs={{0,8},{1,9},{2,10},{3,11},{4,12},{5,13},{6,14},{7,15},{8,0},{9,1},... | collective-permute-start | bytes 1190024 | tf_op jit(solution)/shard_map/ppermute | solution.py:79
  375.3 18.8 %collective-permute-start.25 = (bf16[2,2,24,1024]{3,2,1,0:T(8,128)(2,1)S(1)}, bf16[2,2,24,1024]{3,2,1,0:T(8,128)(2,1)S(1)}, u32[]{:S(2)}, u32[]{:S(2)}) collective-permute-start(bf16[2,2,24,1024]{3,2,1,0:T(8,128)(2,1)S(1)} %fusion.79), channel_id=1, source_target_pairs={{0,8},{1,9},{2,10},{3,11},{4,12},{5,13},{6,14},{7,15},{8,0},{9,1},... | collective-permute-start | bytes 589832 | tf_op jit(solution)/shard_map/ppermute | solution.py:79
  390.1 14.0 %collective-permute-start.30 = (bf16[2,2,24,1033]{3,2,1,0:T(8,128)(2,1)S(1)}, bf16[2,2,24,1033]{3,2,1,0:T(8,128)(2,1)S(1)}, u32[]{:S(2)}, u32[]{:S(2)}) collective-permute-start(bf16[2,2,24,1033]{3,2,1,0:T(8,128)(2,1)S(1)} %fusion.78), channel_id=1, source_target_pairs={{0,16},{1,17},{2,18},{3,19},{4,20},{5,21},{6,22},{7,23},{8,24},{9,... | collective-permute-start | bytes 595016 | tf_op jit(solution)/shard_map/ppermute | solution.py:79
  394.4 12.1 %collective-permute-start.36 = (bf16[2,24,1024]{2,1,0:T(8,128)(2,1)S(1)}, bf16[2,24,1024]{2,1,0:T(8,128)(2,1)S(1)}, u32[]{:S(2)}, u32[]{:S(2)}) collective-permute-start(bf16[2,24,1024]{2,1,0:T(8,128)(2,1)S(1)} %fusion.84), channel_id=1, source_target_pairs={{0,8},{1,9},{2,10},{3,11},{4,12},{5,13},{6,14},{7,15},{8,0},{9,1},... | collective-permute-start | bytes 294920 | tf_op jit(solution)/shard_map/ppermute | solution.py:79
  (69 other events, 612.6 us)
Sparse Core Ops, SparseCore 0:
  73.8 53.3 all-gather.1
  258.7 75.8 reduce-scatter.1
where the time goes:
time: 429 us; the launch traced here: 427 us
  waiting for transfers between devices  129 us (30%)
  matrix products  124 us (29%)
  local copies, waits for them, and re-layouts  74.5 us (17%)
  other arithmetic  46.8 us (11%)
  starting transfers between devices  36.7 us (9%)
  between operations  15.6 us (4%)
    ppermute x8, waiting for transfers between devices, swapped(): lax.ppermute(shard, axis, [(i, i ^ 1 << bit) for i in range(lax.axis_size...  59.2 us
    ppermute x15, waiting for transfers between devices, doubling_gather(): other = lax.ppermute(cur, ALL, [(i, i ^ 1 << b) for i in range(total)])  34.9 us
    dot_general x2, matrix products, ffn_forward(): jnp.dot(rows, inner_cols, preferred_element_type=jnp.float32) + inner_offset  34.8 us
    ppermute x15, waiting for transfers between devices, halving_scatter(): lax.ppermute(theirs.astype(jnp.bfloat16), ALL, [(i, i ^ 1 << b) for i in...  34.6 us
    dot_general x6, matrix products, contract_rows(): lax.dot_general(left_op, right_op, (((0,), (0,)), ((), ())), preferred_el...  20 us
    dot_general x6, matrix products, contract_cols(): lax.dot_general(left_op, right_op, (((1,), (1,)), ((), ())), preferred_el...  19.5 us
    ppermute x15, starting transfers between devices, doubling_gather(): other = lax.ppermute(cur, ALL, [(i, i ^ 1 << b) for i in range(total)])  18.1 us
    concatenate x1, local copies, waits for them, and re-layouts, local(): jnp.concatenate([qkv_wsum.reshape(total, share, 3 * D), qkv_bsum.T.reshap...  12.6 us
  transfers between devices with their start and end apart: 40, of which 24 were waited for; matrix products, arithmetic and copies ran while one was open for 44% of the time, Pallas kernels for 0%

commit v1 on v0

--- a/solution.py
+++ b/solution.py
@@ -301,31 +301,41 @@
     half_bit = narrow_place % 2
     pair_slot = narrow_place // 2
     pack_docs = lax.dynamic_slice_in_dim(doc_ids, pair_slot * pack_count, pack_count, 0)
-    cosine, sine_tab = jax.vmap(rotary_tables)(pack_docs)
+    my_docs = lax.dynamic_slice_in_dim(pack_docs, half_bit, 1, 0)
+    cosine, sine_tab = jax.vmap(rotary_tables)(my_docs)
     cosine = cosine[:, :, None, :]
     sine_tab = sine_tab[:, :, None, :]
-    own_start = half_bit * half_len
-    far_start = (1 - half_bit) * half_len
-    own_cos = lax.dynamic_slice_in_dim(cosine, own_start, half_len, 1)
-    own_sin = lax.dynamic_slice_in_dim(sine_tab, own_start, half_len, 1)
-    own_docs = lax.dynamic_slice_in_dim(pack_docs, own_start, half_len, 1)
-    far_docs = lax.dynamic_slice_in_dim(pack_docs, far_start, half_len, 1)
-    key_docs = jnp.concatenate([own_docs, far_docs], axis=1)
+
+    def to_pack(rows):
+        keep = lax.dynamic_slice_in_dim(rows, half_bit * half_len, half_len, 0)
+        give = lax.dynamic_slice_in_dim(rows, (1 - half_bit) * half_len, half_len, 0)
+        got = swapped(give, "narrow", 0)
+        return jnp.where(
+            half_bit == 0, jnp.concatenate([keep, got]), jnp.concatenate([got, keep])
+        )
+
+    def from_pack(rows):
+        keep = lax.dynamic_slice_in_dim(rows, half_bit * half_len, half_len, 0)
+        give = lax.dynamic_slice_in_dim(rows, (1 - half_bit) * half_len, half_len, 0)
+        got = swapped(give, "narrow", 0)
+        return jnp.where(
+            half_bit == 0, jnp.concatenate([keep, got]), jnp.concatenate([got, keep])
+        )
+
+    pack_in = to_pack(layer_in)
+    pack_cot = to_pack(cotangent)
 
     def heads_of(values):
-        return values.reshape(pack_count, half_len, HEADS, HEAD_DIM)
-
-    qkv = jnp.dot(layer_in, qkv_full, preferred_element_type=jnp.float32) + qkv_offset
-    query_rot = rotate(heads_of(qkv[:, :D]), own_cos, own_sin).astype(jnp.bfloat16)
-    key_rot = rotate(heads_of(qkv[:, D : 2 * D]), own_cos, own_sin).astype(jnp.bfloat16)
+        return values.reshape(1, rows_dev, HEADS, HEAD_DIM)
+
+    qkv = jnp.dot(pack_in, qkv_full, preferred_element_type=jnp.float32) + qkv_offset
+    query_rot = rotate(heads_of(qkv[:, :D]), cosine, sine_tab).astype(jnp.bfloat16)
+    key_rot = rotate(heads_of(qkv[:, D : 2 * D]), cosine, sine_tab).astype(jnp.bfloat16)
     value_low = heads_of(qkv[:, 2 * D :]).astype(jnp.bfloat16)
-    far_keys, far_values = swapped((key_rot, value_low), "narrow", 0)
-    all_keys = jnp.concatenate([key_rot, far_keys], axis=1)
-    all_values = jnp.concatenate([value_low, far_values], axis=1)
-    mixed_out, logsum = attend(query_rot, all_keys, all_values, own_docs, key_docs)
+    mixed_out, logsum = attend(query_rot, key_rot, value_low, my_docs, my_docs)
     mixed_low = mixed_out.reshape(rows_dev, D).astype(jnp.bfloat16)
     attn_out = jnp.dot(mixed_low, output_full, preferred_element_type=jnp.float32) + output_offset
-    res_one = layer_in.astype(jnp.float32) + attn_out
+    res_one = pack_in.astype(jnp.float32) + attn_out
     norm_one, norm_pull = jax.vjp(layer_norm, res_one, attn_scale, attn_offset)
     norm_low = norm_one.astype(jnp.bfloat16)
 
@@ -342,8 +352,9 @@
         outer_sum = narrow_scatter_sum(all_part)
     outer_out = outer_sum + outer_offset
     res_two = norm_one + outer_out
-    layer_out, ffn_pull = jax.vjp(layer_norm, res_two, ffn_scale, ffn_offset)
-    grad_two, ffn_gsum, ffn_ssum = ffn_pull(cotangent.astype(jnp.float32))
+    pack_out, ffn_pull = jax.vjp(layer_norm, res_two, ffn_scale, ffn_offset)
+    layer_out = from_pack(pack_out)
+    grad_two, ffn_gsum, ffn_ssum = ffn_pull(pack_cot.astype(jnp.float32))
     grad_outer = grad_two.astype(jnp.bfloat16)
     outer_bsum = jnp.sum(grad_outer.astype(jnp.float32), axis=0)
     if narrow_n == 2:
@@ -388,21 +399,12 @@
     )
 
     grad_mixed = heads_of(contract_cols(grad_attn, output_full).astype(jnp.bfloat16))
-    grad_qrot, grad_kall, grad_vall = attend_back(
-        query_rot, all_keys, all_values, own_docs, key_docs, logsum, grad_mixed
-    )
-    back_keys, back_values = swapped(
-        (
-            grad_kall[:, half_len:].astype(jnp.bfloat16),
-            grad_vall[:, half_len:].astype(jnp.bfloat16),
-        ),
-        "narrow",
-        0,
-    )
-    grad_krot = grad_kall[:, :half_len] + back_keys.astype(jnp.float32)
-    grad_values = (grad_vall[:, :half_len] + back_values.astype(jnp.float32)).astype(jnp.bfloat16)
-    grad_query = unrotate(grad_qrot, own_cos, own_sin).astype(jnp.bfloat16)
-    grad_keys = unrotate(grad_krot, own_cos, own_sin).astype(jnp.bfloat16)
+    grad_qrot, grad_krot, grad_values = attend_back(
+        query_rot, key_rot, value_low, my_docs, my_docs, logsum, grad_mixed
+    )
+    grad_values = grad_values.astype(jnp.bfloat16)
+    grad_query = unrotate(grad_qrot, cosine, sine_tab).astype(jnp.bfloat16)
+    grad_keys = unrotate(grad_krot, cosine, sine_tab).astype(jnp.bfloat16)
     grad_qkv = jnp.concatenate(
         [
             grad_query.reshape(rows_dev, D),
@@ -411,9 +413,9 @@
         ],
         axis=1,
     )
-    qkv_wsum = contract_rows(layer_in, grad_qkv)
+    qkv_wsum = contract_rows(pack_in, grad_qkv)
     qkv_bsum = jnp.sum(grad_qkv.astype(jnp.float32), axis=0).reshape(3, D)
-    input_grad = grad_one + contract_cols(grad_qkv, qkv_full)
+    input_grad = from_pack(grad_one + contract_cols(grad_qkv, qkv_full))
     late = jnp.concatenate(
         [
             qkv_wsum.reshape(total, share, 3 * D),

time: 429 us -> 378 us (0.88)
  matrix products: 124 us -> 94.3 us
  waiting for transfers between devices: 129 us -> 104 us
  local copies, waits for them, and re-layouts: 74.5 us -> 67.3 us
  starting transfers between devices: 36.7 us -> 41 us
    ppermute x8, waiting for transfers between devices: 59.2 us -> 33 us  [swapped(): lax.ppermute(shard, axis, [(i, i ^ 1 << bit) for i in range(lax.axis_size...]
    dot_general x2, matrix products: 34.8 us -> 22.3 us  [ffn_forward(): jnp.dot(rows, inner_cols, preferred_element_type=jnp.float32) + inner_offset]
    all_gather x1, waiting for transfers between devices: 0.01 us -> 8.8 us  [local(): ffn_all = lax.all_gather(ffn_shard, 'wide', axis=0, tiled=True)]
    convert_element_type x4 -> x0, local copies, waits for them, and re-layouts: 7.16 us -> none  [the longest x2 5.53 us: local(): value_low = heads_of(qkv[:, 2 * D:]).astype(jnp.bfloat16)]
    ppermute x15, waiting for transfers between devices: 34.6 us -> 27.7 us  [halving_scatter(): lax.ppermute(theirs.astype(jnp.bfloat16), ALL, [(i, i ^ 1 << b) for i in...]
    reshape x3 -> x0, local copies, waits for them, and re-layouts: 5.74 us -> none  [heads_of(): return values.reshape(pack_count, half_len, HEADS, HEAD_DIM)]
    dot_general x1, matrix products: 8.42 us -> 3.34 us  [attend_back(): jnp.einsum('phqk,pqhd->pkhd', probability.astype(jnp.bfloat16), grad_mixe...]
    select_n x0 -> x2, other arithmetic: none -> 4.6 us  [from_pack(): jnp.where(half_bit == 0, jnp.concatenate([keep, got]), jnp.concatenate([g...]
  transfers between devices with their start and end apart: 40 -> 40, of which waited for: 24 -> 24; matrix products, arithmetic and copies ran while one was open for 44% -> 50% of each run, Pallas kernels for 0% -> 0%
where the time goes in v1:
time: 378 us; the launch traced here: 373 us
  waiting for transfers between devices  104 us (28%)
  matrix products  94.3 us (25%)
  local copies, waits for them, and re-layouts  67.3 us (18%)
  other arithmetic  50.2 us (13%)
  starting transfers between devices  41 us (11%)
  between operations  15.7 us (4%)
    ppermute x15, waiting for transfers between devices, doubling_gather(): other = lax.ppermute(cur, ALL, [(i, i ^ 1 << b) for i in range(total)])  34.9 us
    ppermute x8, waiting for transfers between devices, swapped(): lax.ppermute(shard, axis, [(i, i ^ 1 << bit) for i in range(lax.axis_size...  33 us
    ppermute x15, waiting for transfers between devices, halving_scatter(): lax.ppermute(theirs.astype(jnp.bfloat16), ALL, [(i, i ^ 1 << b) for i in...  27.7 us
    dot_general x2, matrix products, ffn_forward(): jnp.dot(rows, inner_cols, preferred_element_type=jnp.float32) + inner_offset  22.3 us
    dot_general x6, matrix products, contract_rows(): lax.dot_general(left_op, right_op, (((0,), (0,)), ((), ())), preferred_el...  18.4 us
    ppermute x15, starting transfers between devices, doubling_gather(): other = lax.ppermute(cur, ALL, [(i, i ^ 1 << b) for i in range(total)])  18.1 us
    dot_general x6, matrix products, contract_cols(): lax.dot_general(left_op, right_op, (((1,), (1,)), ((), ())), preferred_el...  15.9 us
    ppermute x15, starting transfers between devices, halving_scatter(): lax.ppermute(theirs.astype(jnp.bfloat16), ALL, [(i, i ^ 1 << b) for i in...  15 us
  transfers between devices with their start and end apart: 40, of which 24 were waited for; matrix products, arithmetic and copies ran while one was open for 50% of the time, Pallas kernels for 0%

profile of v1, /device:TPU:0, one launch (start us, length us, event | category | flops | bytes accessed | tf_op | source)
XLA Modules:
  0.0 373.0 jit_solution(18327908206969575659)
XLA Ops:
  36.9 13.0 %collective-permute-done.13 = bf16[2,2,24,1152]{3,2,1,0:T(8,128)(2,1)S(1)} collective-permute-done((bf16[2,2,24,1152]{3,2,1,0:T(8,128)(2,1)S(1)}, bf16[2,2,24,1152]{3,2,1,0:T(8,128)(2,1)S(1)}, u32[]{:S(2)}, u32[]{:S(2)}) %collective-permute-start.13) | collective-permute-done | bytes 221216 | tf_op jit(solution)/shard_map/ppermute | solution.py:46
  50.2 5.2 %collective-permute-done.9 = bf16[2,2,2,24,1024]{4,3,2,0,1:T(8,128)(2,1)S(1)} collective-permute-done((bf16[2,2,2,24,1024]{4,3,2,0,1:T(8,128)(2,1)S(1)}, bf16[2,2,2,24,1024]{4,3,2,0,1:T(8,128)(2,1)S(1)}, u32[]{:S(2)}, u32[]{:S(2)}) %collective-permute-start.9) | collective-permute-done | bytes 393248 | tf_op jit(solution)/shard_map/ppermute | solution.py:46
  56.1 8.7 %collective-permute-done.14 = bf16[2,2,2,24,1152]{4,3,2,1,0:T(8,128)(2,1)S(1)} collective-permute-done((bf16[2,2,2,24,1152]{4,3,2,1,0:T(8,128)(2,1)S(1)}, bf16[2,2,2,24,1152]{4,3,2,1,0:T(8,128)(2,1)S(1)}, u32[]{:S(2)}, u32[]{:S(2)}) %collective-permute-start.14) | collective-permute-done | bytes 442400 | tf_op jit(solution)/shard_map/ppermute | solution.py:46
  76.7 7.2 %collective-permute-done = bf16[256,768]{1,0:T(8,128)(2,1)S(1)} collective-permute-done((bf16[256,768]{1,0:T(8,128)(2,1)S(1)}, bf16[256,768]{1,0:T(8,128)(2,1)S(1)}, u32[]{:S(2)}, u32[]{:S(2)}) %collective-permute-start) | collective-permute-done | bytes 393248 | tf_op jit(solution)/shard_map/ppermute | solution.py:16
  84.0 4.2 %convolution_add_fusion = f32[512,2304]{1,0:T(8,128)S(1)} fusion(bf16[768,3200]{1,0:T(8,128)(2,1)} %pad_maximum_fusion, f32[2304]{0:T(1024)S(1)} %pad_maximum_fusion.17, bf16[256,768]{1,0:T(8,128)(2,1)S(1)} %collective-permute-done, bf16[256,768]{1,0:T(8,128)(2,1)S(1)} %get-tuple-element.75, pred[]{:T(512)S(6)} %eq.134), kind=kOutput, calls=%fused_computation.13 | convolution fusion | flops 1816657920 | bytes 9053185 | tf_op jit(solution)/shard_map/dot_general | solution.py:331
  107.2 3.7 %fusion.55 = bf16[12,64,512]{2,1,0:T(8,128)(2,1)S(1)} fusion(bf16[512,12,64]{0,2,1:T(8,128)(2,1)S(1)} %bitcast.175, f32[12,512]{1,0:T(8,128)S(1)} %fusion, f32[12,512]{1,0:T(8,128)S(1)} %get-tuple-element.95, f32[12,512,512]{1,2,0:T(8,128)S(1)} %get-tuple-element.96, pred[512,512]{0,1:T(8,128)(4,1)S(1)} %copy-done.11), kind=kOutput, calls=%fused_computation.115 | convolution fusion | flops 418775040 | bytes 14467072 | tf_op jit(solution)/shard_map/phqk,pkhd->pqhd/dot_general | solution.py:188
  117.1 8.8 %all-gather.2.cloned.1.call-done = bf16[768,3074]{1,0:T(8,128)(2,1)} async-done(((bf16[48,3074]{1,0:T(8,128)(2,1)}), bf16[768,3074]{1,0:T(8,128)(2,1)}) %all-gather.2.cloned.1.call-update) | async-done | bytes 4721680 | tf_op jit(solution)/shard_map/all_gather | solution.py:291
  128.8 5.4 %collective-permute-done.16 = bf16[512,768]{1,0:T(8,128)(2,1)} collective-permute-done((bf16[512,768]{1,0:T(8,128)(2,1)}, bf16[512,768]{1,0:T(8,128)(2,1)}, u32[]{:S(2)}, u32[]{:S(2)}) %collective-permute-start.16) | collective-permute-done | bytes 786464 | tf_op jit(solution)/shard_map/ppermute | solution.py:16
  134.2 11.0 %multiply_convert_fusion.1 = (bf16[512,1536]{1,0:T(8,128)(2,1)S(1)}, f32[512,1536]{1,0:T(8,128)}, f32[512,1536]{1,0:T(8,128)}) fusion(f32[1536]{0:T(1024)S(1)} %reshape.630, bf16[512,768]{1,0:T(8,128)(2,1)} %collective-permute-done.16, bf16[768,3074]{1,0:T(8,128)(2,1)} %all-gather.2.cloned.1.call-done), kind=kOutput, calls=%fused_computation.28 | convolution fusion | flops 1259864064 | bytes 11016192 | tf_op jit(solution)/shard_map/dot_general | solution.py:217
  147.0 11.3 %multiply_convert_fusion.2 = (bf16[512,1536]{1,0:T(8,128)(2,1)S(1)}, f32[512,1536]{1,0:T(8,128)}, f32[512,1536]{1,0:T(8,128)}) fusion(f32[1536]{0:T(1024)S(1)} %reshape.630, bf16[512,768]{1,0:T(8,128)(2,1)} %fusion.58, bf16[768,3074]{1,0:T(8,128)(2,1)S(1)} %copy-done.55), kind=kOutput, calls=%fused_computation.41 | convolution fusion | flops 1259864064 | bytes 11018240 | tf_op jit(solution)/shard_map/dot_general | solution.py:217
  158.3 4.4 %collective-permute-done.17 = bf16[512,768]{1,0:T(8,128)(2,1)S(1)} collective-permute-done((bf16[512,768]{1,0:T(8,128)(2,1)S(1)}, bf16[512,768]{1,0:T(8,128)(2,1)S(1)}, u32[]{:S(2)}, u32[]{:S(2)}) %collective-permute-start.17) | collective-permute-done | bytes 786464 | tf_op jit(solution)/shard_map/ppermute | solution.py:16
  180.0 5.3 %convert_reduce_fusion.2 = (f32[1536]{0:T(1024)S(1)}, bf16[512,1536]{1,0:T(8,128)(2,1)S(1)}) fusion(f32[512,1536]{1,0:T(8,128)S(1)} %copy-done.61, f32[512,1536]{1,0:T(8,128)} %get-tuple-element.100, bf16[512,768]{1,0:T(8,128)(2,1)} %get-tuple-element.45, bf16[768,3074]{1,0:T(8,128)(2,1)} %all-gather.2.cloned.1.call-done), kind=kOutput, calls=%fused_computation.25 | convolution fusion | flops 1220540928 | bytes 11016192 | tf_op jit(solution)/shard_map/dot_general | solution.py:224
  192.8 3.8 %convert_reduce_fusion.1 = (f32[1536]{0:T(1024)S(1)}, bf16[512,1536]{1,0:T(8,128)(2,1)S(1)}) fusion(f32[512,1536]{1,0:T(8,128)S(1)} %copy-done.59, f32[512,1536]{1,0:T(8,128)S(1)} %copy-done.60, bf16[512,768]{1,0:T(8,128)(2,1)} %collective-permute-done.20, bf16[768,3074]{1,0:T(8,128)(2,1)S(1)} %bitcast.200), kind=kOutput, calls=%fused_computation.24 | convolution fusion | flops 1220540928 | bytes 11016192 | tf_op jit(solution)/shard_map/dot_general | solution.py:224
  199.8 4.1 %add_convert_fusion.1 = bf16[768,1536]{1,0:T(8,128)(2,1)} fusion(f32[768,1536]{1,0:T(8,128)S(1)} %fusion.106, bf16[512,768]{1,0:T(8,128)(2,1)} %collective-permute-done.16, bf16[512,1536]{1,0:T(8,128)(2,1)S(1)} %get-tuple-element.109), kind=kOutput, calls=%fused_computation.17 | convolution fusion | flops 1210318848 | bytes 9437184 | tf_op jit(solution)/shard_map/dot_general | solution.py:163
  204.0 4.0 %add_convert_fusion = bf16[768,1536]{1,0:T(8,128)(2,1)} fusion(f32[768,1536]{1,0:T(8,128)S(1)} %fusion.107, bf16[512,768]{1,0:T(8,128)(2,1)} %collective-permute-done.20, bf16[512,1536]{1,0:T(8,128)(2,1)S(1)} %copy-done.27), kind=kOutput, calls=%fused_computation.16 | convolution fusion | flops 1210318848 | bytes 9437184 | tf_op jit(solution)/shard_map/dot_general | solution.py:163
  209.7 5.4 %pad_maximum_fusion.1 = bf16[768,3074]{1,0:T(8,128)(2,1)} fusion(bf16[768,2]{1,0:T(8,128)(2,1)S(1)} %add.340, bf16[768,1536]{1,0:T(8,128)(2,1)} %add_convert_fusion, bf16[768,1536]{1,0:T(8,128)(2,1)} %add_convert_fusion.1), kind=kLoop, calls=%fused_computation.12 | loop fusion | flops 14164992 | bytes 9443328 | tf_op jit(solution)/shard_map/concatenate | solution.py:382
  221.2 4.7 %multiply_reduce_fusion.1 = (f32[768]{0:T(1024)}, f32[512]{0:T(512)S(1)}, f32[768]{0:T(1024)}, f32[512,768]{1,0:T(8,128)S(1)}) fusion(f32[512,768]{1,0:T(8,128)S(1)} %get-tuple-element.98, f32[512]{0:T(512)S(1)} %fusion.87, f32[512]{0:T(512)S(1)} %broadcast_multiply_fusion.1, f32[768]{0:T(1024)S(1)} %get-tuple-element.30, ...), kind=kOutput, calls=%fused_computation.81 | convolution fusion | flops 1212676096 | bytes 9454592 | tf_op jit(solution)/shard_map/dot_general | solution.py:169
  232.0 11.3 %multiply_reduce_fusion = (f32[12,512]{1,0:T(8,128)S(1)}, f32[12,512,512]{1,2,0:T(8,128)}) fusion(f32[12,512]{1,0:T(8,128)S(1)} %copy-done.50, f32[12,512,512]{1,2,0:T(8,128)} %copy-done.2, pred[512,512]{0,1:T(8,128)(4,1)S(1)} %copy-done.12, bf16[512,12,64]{0,2,1:T(8,128)(2,1)S(1)} %bitcast.177, bf16[512,12,64]{0,2,1:T(8,128)(2,1)S(1)} %bitcast.176), kind=kOutput, calls=%fused_computation.1 | convolution fusion | flops 418375680 | bytes 27049984 | tf_op jit(solution)/shard_map/pqhd,pkhd->phqk/dot_general | solution.py:202
  244.9 6.8 %multiply_convert_fusion = bf16[12,512,512]{1,2,0:T(8,128)(2,1)S(1)} fusion(f32[12,512,512]{1,2,0:T(8,128)} %get-tuple-element.105, f32[12,512]{1,0:T(8,128)S(1)} %get-tuple-element.104, f32[12,512]{1,0:T(8,128)S(1)} %copy-done.50, f32[12,512,512]{1,2,0:T(8,128)S(1)} %bitcast.164, pred[512,512]{0,1:T(8,128)(4,1)S(1)} %copy-done.12), kind=kLoop, calls=%fused_computation | loop fusion | flops 18874368 | bytes 31768576 | tf_op jit(solution)/shard_map/convert_element_type | solution.py:206
  278.5 12.7 %concatenate.122 = f32[32,24,3081]{2,1,0:T(8,128)} concatenate(f32[32,24,2304]{2,1,0:T(8,128)} %bitcast.166, f32[32,24,3]{2,1,0:T(8,128)} %bitcast.187, f32[32,24,768]{2,1,0:T(8,128)} %fusion.66, f32[32,24,1]{2,1,0:T(8,128)} %stack.65, f32[32,24,1]{2,1,0:T(8,128)} %stack.66, f32[32,24,1]{2,1,0:T(8,128)} %stack.67, f32[32,24,1]{2,1,0:T(8,128)S(1)} %copy-done.36, ...), dimensions={2} | concatenate | bytes 18929664 | tf_op jit(solution)/shard_map/concatenate | solution.py:419
  294.3 4.1 %add_add_fusion.5 = f32[512,768]{1,0:T(8,128)S(1)} fusion(f32[512,768]{1,0:T(8,128)S(1)} %copy-done.9, bf16[768,3200]{1,0:T(8,128)(2,1)} %pad_maximum_fusion, f32[512]{0:T(512)S(1)} %copy-done.54, bf16[512,768]{0,1:T(8,128)(2,1)S(1)} %bitcast.191, bf16[512,768]{0,1:T(8,128)(2,1)S(1)} %bitcast.184, bf16[512,768]{0,1:T(8,128)(2,1)S(1)} %bitcast.181), kind=kOutput, calls=%fused_computation.108 | convolution fusion | flops 1819803648 | bytes 9046016 | tf_op jit(solution)/shard_map/dot_general | solution.py:169
  307.0 11.7 %collective-permute-done.22 = f32[256,768]{1,0:T(8,128)S(1)} collective-permute-done((f32[256,768]{1,0:T(8,128)S(1)}, f32[256,768]{1,0:T(8,128)S(1)}, u32[]{:S(2)}, u32[]{:S(2)}) %collective-permute-start.22) | collective-permute-done | bytes 786464 | tf_op jit(solution)/shard_map/ppermute | solution.py:16
  326.2 8.8 %collective-permute-done.29 = bf16[2,2,2,24,1033]{4,3,2,1,0:T(8,128)(2,1)S(1)} collective-permute-done((bf16[2,2,2,24,1033]{4,3,2,1,0:T(8,128)(2,1)S(1)}, bf16[2,2,2,24,1033]{4,3,2,1,0:T(8,128)(2,1)S(1)}, u32[]{:S(2)}, u32[]{:S(2)}) %collective-permute-start.29) | collective-permute-done | bytes 396704 | tf_op jit(solution)/shard_map/ppermute | solution.py:79
  342.8 7.6 %collective-permute-done.30 = bf16[2,2,24,1033]{3,2,1,0:T(8,128)(2,1)S(1)} collective-permute-done((bf16[2,2,24,1033]{3,2,1,0:T(8,128)(2,1)S(1)}, bf16[2,2,24,1033]{3,2,1,0:T(8,128)(2,1)S(1)}, u32[]{:S(2)}, u32[]{:S(2)}) %collective-permute-start.30) | collective-permute-done | bytes 198368 | tf_op jit(solution)/shard_map/ppermute | solution.py:79
  (348 shorter events, 184.2 us)
Async XLA Ops:
  7.2 118.7 %all-gather.2.cloned.1.call-start = ((), (), s32[]{:S(2)}) async-start(), calls=%async_computation.1 | async-start | bytes 5222400 | tf_op jit(solution)/shard_map/all_gather | solution.py:291
  28.7 21.1 %collective-permute-start.13 = (bf16[2,2,24,1152]{3,2,1,0:T(8,128)(2,1)S(1)}, bf16[2,2,24,1152]{3,2,1,0:T(8,128)(2,1)S(1)}, u32[]{:S(2)}, u32[]{:S(2)}) collective-permute-start(bf16[2,2,24,1152]{3,2,1,0:T(8,128)(2,1)S(1)} %broadcast_select_fusion.11), channel_id=1, source_target_pairs={{0,16},{1,17},{2,18},{3,19},{4,20},{5,21},{6,22},{7,23},{8,24},{9,... | collective-permute-start | bytes 663560 | tf_op jit(solution)/shard_map/ppermute | solution.py:46
  30.9 24.6 %collective-permute-start.9 = (bf16[2,2,2,24,1024]{4,3,2,0,1:T(8,128)(2,1)S(1)}, bf16[2,2,2,24,1024]{4,3,2,0,1:T(8,128)(2,1)S(1)}, u32[]{:S(2)}, u32[]{:S(2)}) collective-permute-start(bf16[2,2,2,24,1024]{4,3,2,0,1:T(8,128)(2,1)S(1)} %broadcast_select_fusion.7), channel_id=1, source_target_pairs={{0,16},{1,17},{2,18},{3,19},{4,20},{5,21},{6,22},{7,23},{8,24},{9,... | collective-permute-start | bytes 1179656 | tf_op jit(solution)/shard_map/ppermute | solution.py:46
  35.2 29.9 %collective-permute-start.4 = (bf16[2,2,2,24,1024]{4,3,2,0,1:T(8,128)(2,1)S(1)}, bf16[2,2,2,24,1024]{4,3,2,0,1:T(8,128)(2,1)S(1)}, u32[]{:S(2)}, u32[]{:S(2)}) collective-permute-start(bf16[2,2,2,24,1024]{4,3,2,0,1:T(8,128)(2,1)S(1)} %broadcast_select_fusion.9), channel_id=1, source_target_pairs={{0,4},{1,5},{2,6},{3,7},{4,0},{5,1},{6,2},{7,3},{8,12},{9,13},{10,... | collective-permute-start | bytes 1179656 | tf_op jit(solution)/shard_map/ppermute | solution.py:46
  50.0 14.8 %collective-permute-start.14 = (bf16[2,2,2,24,1152]{4,3,2,1,0:T(8,128)(2,1)S(1)}, bf16[2,2,2,24,1152]{4,3,2,1,0:T(8,128)(2,1)S(1)}, u32[]{:S(2)}, u32[]{:S(2)}) collective-permute-start(bf16[2,2,2,24,1152]{4,3,2,1,0:T(8,128)(2,1)S(1)} %broadcast_select_fusion.6), channel_id=1, source_target_pairs={{0,8},{1,9},{2,10},{3,11},{4,12},{5,13},{6,14},{7,15},{8,0},{9,1},... | collective-permute-start | bytes 1327112 | tf_op jit(solution)/shard_map/ppermute | solution.py:46
  72.4 288.7 %reduce-scatter.2.cloned.1.call-start = ((), (), s32[]{:S(2)}) async-start(), calls=%async_computation.2 | async-start | bytes 5222400 | tf_op jit(solution)/shard_map/reduce_scatter | solution.py:383
  113.5 20.7 %collective-permute-start.16 = (bf16[512,768]{1,0:T(8,128)(2,1)}, bf16[512,768]{1,0:T(8,128)(2,1)}, u32[]{:S(2)}, u32[]{:S(2)}) collective-permute-start(bf16[512,768]{1,0:T(8,128)(2,1)} %fusion.58), channel_id=1, source_target_pairs={{0,1},{1,0},{2,3},{3,2},{4,5},{5,4},{6,7},{7,6},{8,9},{9,8},{10,11... | collective-permute-start | bytes 2359304 | tf_op jit(solution)/shard_map/ppermute | solution.py:16
  114.7 50.1 %collective-permute-start.19 = (bf16[256,768]{1,0:T(8,128)(2,1)}, bf16[256,768]{1,0:T(8,128)(2,1)}, u32[]{:S(2)}, u32[]{:S(2)}) collective-permute-start(bf16[256,768]{1,0:T(8,128)(2,1)} %get-tuple-element.73), channel_id=1, source_target_pairs={{0,1},{1,0},{2,3},{3,2},{4,5},{5,4},{6,7},{7,6},{8,9},{9,8},{10,11... | collective-permute-start | bytes 1179656 | tf_op jit(solution)/shard_map/ppermute | solution.py:16
  146.7 16.0 %collective-permute-start.17 = (bf16[512,768]{1,0:T(8,128)(2,1)S(1)}, bf16[512,768]{1,0:T(8,128)(2,1)S(1)}, u32[]{:S(2)}, u32[]{:S(2)}) collective-permute-start(bf16[512,768]{1,0:T(8,128)(2,1)S(1)} %fusion.49), channel_id=1, source_target_pairs={{0,1},{1,0},{2,3},{3,2},{4,5},{5,4},{6,7},{7,6},{8,9},{9,8},{10,11... | collective-permute-start | bytes 2359304 | tf_op jit(solution)/shard_map/ppermute | solution.py:16
  172.1 20.7 %collective-permute-start.20 = (bf16[512,768]{1,0:T(8,128)(2,1)}, bf16[512,768]{1,0:T(8,128)(2,1)}, u32[]{:S(2)}, u32[]{:S(2)}) collective-permute-start(bf16[512,768]{1,0:T(8,128)(2,1)} %get-tuple-element.45), channel_id=1, source_target_pairs={{0,1},{1,0},{2,3},{3,2},{4,5},{5,4},{6,7},{7,6},{8,9},{9,8},{10,11... | collective-permute-start | bytes 2359304 | tf_op jit(solution)/shard_map/ppermute | solution.py:16
  178.9 36.2 %collective-permute-start.18 = (f32[256,768]{1,0:T(8,128)}, f32[256,768]{1,0:T(8,128)}, u32[]{:S(2)}, u32[]{:S(2)}) collective-permute-start(f32[256,768]{1,0:T(8,128)} %get-tuple-element.72), channel_id=1, source_target_pairs={{0,1},{1,0},{2,3},{3,2},{4,5},{5,4},{6,7},{7,6},{8,9},{9,8},{10,11... | collective-permute-start | bytes 2359304 | tf_op jit(solution)/shard_map/ppermute | solution.py:16
  198.9 22.3 %collective-permute-start.21 = (bf16[512,768]{1,0:T(8,128)(2,1)}, bf16[512,768]{1,0:T(8,128)(2,1)}, u32[]{:S(2)}, u32[]{:S(2)}) collective-permute-start(bf16[512,768]{1,0:T(8,128)(2,1)} %fusion.46), channel_id=1, source_target_pairs={{0,1},{1,0},{2,3},{3,2},{4,5},{5,4},{6,7},{7,6},{8,9},{9,8},{10,11... | collective-permute-start | bytes 2359304 | tf_op jit(solution)/shard_map/ppermute | solution.py:16
  267.9 32.6 %collective-permute-start.23 = (bf16[2,2,2,2,24,1024]{5,4,3,2,1,0:T(8,128)(2,1)}, bf16[2,2,2,2,24,1024]{5,4,3,2,1,0:T(8,128)(2,1)}, u32[]{:S(2)}, u32[]{:S(2)}) collective-permute-start(bf16[2,2,2,2,24,1024]{5,4,3,2,1,0:T(8,128)(2,1)} %fusion.64), channel_id=1, source_target_pairs={{0,2},{1,3},{2,0},{3,1},{4,6},{5,7},{6,4},{7,5},{8,10},{9,11},{10,... | collective-permute-start | bytes 2359304 | tf_op jit(solution)/shard_map/ppermute | solution.py:79
  268.9 34.9 %collective-permute-start.33 = (bf16[2,2,2,2,24,1024]{5,4,3,1,2,0:T(8,128)(2,1)}, bf16[2,2,2,2,24,1024]{5,4,3,1,2,0:T(8,128)(2,1)}, u32[]{:S(2)}, u32[]{:S(2)}) collective-permute-start(bf16[2,2,2,2,24,1024]{5,4,3,1,2,0:T(8,128)(2,1)} %fusion.65), channel_id=1, source_target_pairs={{0,2},{1,3},{2,0},{3,1},{4,6},{5,7},{6,4},{7,5},{8,10},{9,11},{10,... | collective-permute-start | bytes 2359304 | tf_op jit(solution)/shard_map/ppermute | solution.py:79
  298.5 21.5 %collective-permute-start.28 = (bf16[2,2,2,2,24,1033]{5,4,3,2,1,0:T(8,128)(2,1)S(1)}, bf16[2,2,2,2,24,1033]{5,4,3,2,1,0:T(8,128)(2,1)S(1)}, u32[]{:S(2)}, u32[]{:S(2)}) collective-permute-start(bf16[2,2,2,2,24,1033]{5,4,3,2,1,0:T(8,128)(2,1)S(1)} %fusion.63), channel_id=1, source_target_pairs={{0,2},{1,3},{2,0},{3,1},{4,6},{5,7},{6,4},{7,5},{8,10},{9,11},{10,... | collective-permute-start | bytes 2380040 | tf_op jit(solution)/shard_map/ppermute | solution.py:79
  298.7 20.0 %collective-permute-start.22 = (f32[256,768]{1,0:T(8,128)S(1)}, f32[256,768]{1,0:T(8,128)S(1)}, u32[]{:S(2)}, u32[]{:S(2)}) collective-permute-start(f32[256,768]{1,0:T(8,128)S(1)} %get-tuple-element.70), channel_id=1, source_target_pairs={{0,1},{1,0},{2,3},{3,2},{4,5},{5,4},{6,7},{7,6},{8,9},{9,8},{10,11... | collective-permute-start | bytes 2359304 | tf_op jit(solution)/shard_map/ppermute | solution.py:16
  302.0 20.0 %collective-permute-start.24 = (bf16[2,2,2,24,1024]{4,3,2,1,0:T(8,128)(2,1)S(1)}, bf16[2,2,2,24,1024]{4,3,2,1,0:T(8,128)(2,1)S(1)}, u32[]{:S(2)}, u32[]{:S(2)}) collective-permute-start(bf16[2,2,2,24,1024]{4,3,2,1,0:T(8,128)(2,1)S(1)} %fusion.74), channel_id=1, source_target_pairs={{0,4},{1,5},{2,6},{3,7},{4,0},{5,1},{6,2},{7,3},{8,12},{9,13},{10,... | collective-permute-start | bytes 1179656 | tf_op jit(solution)/shard_map/ppermute | solution.py:79
  305.2 20.2 %collective-permute-start.34 = (bf16[2,2,2,24,1024]{4,3,2,0,1:T(8,128)(2,1)S(1)}, bf16[2,2,2,24,1024]{4,3,2,0,1:T(8,128)(2,1)S(1)}, u32[]{:S(2)}, u32[]{:S(2)}) collective-permute-start(bf16[2,2,2,24,1024]{4,3,2,0,1:T(8,128)(2,1)S(1)} %fusion.75), channel_id=1, source_target_pairs={{0,16},{1,17},{2,18},{3,19},{4,20},{5,21},{6,22},{7,23},{8,24},{9,... | collective-permute-start | bytes 1179656 | tf_op jit(solution)/shard_map/ppermute | solution.py:79
  320.2 14.7 %collective-permute-start.29 = (bf16[2,2,2,24,1033]{4,3,2,1,0:T(8,128)(2,1)S(1)}, bf16[2,2,2,24,1033]{4,3,2,1,0:T(8,128)(2,1)S(1)}, u32[]{:S(2)}, u32[]{:S(2)}) collective-permute-start(bf16[2,2,2,24,1033]{4,3,2,1,0:T(8,128)(2,1)S(1)} %fusion.69), channel_id=1, source_target_pairs={{0,8},{1,9},{2,10},{3,11},{4,12},{5,13},{6,14},{7,15},{8,0},{9,1},... | collective-permute-start | bytes 1190024 | tf_op jit(solution)/shard_map/ppermute | solution.py:79
  322.1 17.2 %collective-permute-start.25 = (bf16[2,2,24,1024]{3,2,1,0:T(8,128)(2,1)S(1)}, bf16[2,2,24,1024]{3,2,1,0:T(8,128)(2,1)S(1)}, u32[]{:S(2)}, u32[]{:S(2)}) collective-permute-start(bf16[2,2,24,1024]{3,2,1,0:T(8,128)(2,1)S(1)} %fusion.77), channel_id=1, source_target_pairs={{0,8},{1,9},{2,10},{3,11},{4,12},{5,13},{6,14},{7,15},{8,0},{9,1},... | collective-permute-start | bytes 589832 | tf_op jit(solution)/shard_map/ppermute | solution.py:79
  325.7 14.5 %collective-permute-start.35 = (bf16[2,2,24,1024]{3,2,1,0:T(8,128)(2,1)S(1)}, bf16[2,2,24,1024]{3,2,1,0:T(8,128)(2,1)S(1)}, u32[]{:S(2)}, u32[]{:S(2)}) collective-permute-start(bf16[2,2,24,1024]{3,2,1,0:T(8,128)(2,1)S(1)} %fusion.78), channel_id=1, source_target_pairs={{0,4},{1,5},{2,6},{3,7},{4,0},{5,1},{6,2},{7,3},{8,12},{9,13},{10,... | collective-permute-start | bytes 589832 | tf_op jit(solution)/shard_map/ppermute | solution.py:79
  335.1 15.3 %collective-permute-start.30 = (bf16[2,2,24,1033]{3,2,1,0:T(8,128)(2,1)S(1)}, bf16[2,2,24,1033]{3,2,1,0:T(8,128)(2,1)S(1)}, u32[]{:S(2)}, u32[]{:S(2)}) collective-permute-start(bf16[2,2,24,1033]{3,2,1,0:T(8,128)(2,1)S(1)} %fusion.76), channel_id=1, source_target_pairs={{0,16},{1,17},{2,18},{3,19},{4,20},{5,21},{6,22},{7,23},{8,24},{9,... | collective-permute-start | bytes 595016 | tf_op jit(solution)/shard_map/ppermute | solution.py:79
  339.4 12.9 %collective-permute-start.26 = (bf16[2,24,1024]{2,1,0:T(8,128)(2,1)S(1)}, bf16[2,24,1024]{2,1,0:T(8,128)(2,1)S(1)}, u32[]{:S(2)}, u32[]{:S(2)}) collective-permute-start(bf16[2,24,1024]{2,1,0:T(8,128)(2,1)S(1)} %fusion.81), channel_id=1, source_target_pairs={{0,16},{1,17},{2,18},{3,19},{4,20},{5,21},{6,22},{7,23},{8,24},{9,... | collective-permute-start | bytes 294920 | tf_op jit(solution)/shard_map/ppermute | solution.py:79
  340.2 13.1 %collective-permute-start.36 = (bf16[2,24,1024]{2,1,0:T(8,128)(2,1)S(1)}, bf16[2,24,1024]{2,1,0:T(8,128)(2,1)S(1)}, u32[]{:S(2)}, u32[]{:S(2)}) collective-permute-start(bf16[2,24,1024]{2,1,0:T(8,128)(2,1)S(1)} %fusion.82), channel_id=1, source_target_pairs={{0,8},{1,9},{2,10},{3,11},{4,12},{5,13},{6,14},{7,15},{8,0},{9,1},... | collective-permute-start | bytes 294920 | tf_op jit(solution)/shard_map/ppermute | solution.py:79
  (83 other events, 526.6 us)
Sparse Core Ops, SparseCore 0:
  72.5 53.2 all-gather.1
  215.2 75.8 reduce-scatter.1

commit v2 on v1

--- a/solution.py
+++ b/solution.py
@@ -79,7 +79,7 @@
         got = lax.ppermute(
             theirs.astype(jnp.bfloat16), ALL, [(i, i ^ (1 << b)) for i in range(total)]
         )
-        cur = mine + got.astype(jnp.float32)
+        cur = mine.astype(jnp.float32) + got.astype(jnp.float32)
         axes.pop(a)
     return cur
 
@@ -286,12 +286,13 @@
     bias_n = inner_bias.shape[0]
     bias_k = -(-bias_n // ffn_rows)
     bias_rows = jnp.pad(inner_bias, (0, ffn_rows * bias_k - bias_n)).reshape(ffn_rows, bias_k)
-    ffn_shard = jnp.concatenate([inner_weight, outer_weight.T, bias_rows], axis=1)
-    ffn_shard, full = lax.optimization_barrier((ffn_shard, full))
-    ffn_all = lax.all_gather(ffn_shard, "wide", axis=0, tiled=True)
-    inner_cols = ffn_all[:, :ffn_cols]
-    outer_cols = ffn_all[:, ffn_cols : 2 * ffn_cols]
-    inner_offset = ffn_all[:, 2 * ffn_cols :].reshape(wide_n, ffn_rows * bias_k)[:, :bias_n]
+    inner_shard = jnp.concatenate([inner_weight, bias_rows], axis=1)
+    inner_shard, full = lax.optimization_barrier((inner_shard, full))
+    inner_all = lax.all_gather(inner_shard, "wide", axis=0, tiled=True)
+    outer_shard, inner_all = lax.optimization_barrier((outer_weight.T, inner_all))
+    outer_cols = lax.all_gather(outer_shard, "wide", axis=0, tiled=True)
+    inner_cols = inner_all[:, :ffn_cols]
+    inner_offset = inner_all[:, ffn_cols:].reshape(wide_n, ffn_rows * bias_k)[:, :bias_n]
     inner_offset = inner_offset.reshape(-1).astype(jnp.float32)
 
     rows_dev = layer_in.shape[0]
@@ -418,9 +419,9 @@
     input_grad = from_pack(grad_one + contract_cols(grad_qkv, qkv_full))
     late = jnp.concatenate(
         [
-            qkv_wsum.reshape(total, share, 3 * D),
-            qkv_bsum.T.reshape(total, share, 3),
-            early,
+            qkv_wsum.reshape(total, share, 3 * D).astype(jnp.bfloat16),
+            qkv_bsum.T.reshape(total, share, 3).astype(jnp.bfloat16),
+            early.astype(jnp.bfloat16),
         ],
         axis=2,
     )

time: 378 us -> 388 us (1.026)
  waiting for transfers between devices: 104 us -> 121 us
  local copies, waits for them, and re-layouts: 67.3 us -> 55.5 us
    ppermute x8, waiting for transfers between devices: 33 us -> 50.3 us  [swapped(): lax.ppermute(shard, axis, [(i, i ^ 1 << bit) for i in range(lax.axis_size...]
    all_gather x1 -> x2, waiting for transfers between devices: 8.8 us -> 2.02 us  [the longest x1 1.87 us: local(): outer_cols = lax.all_gather(outer_shard, 'wide', axis=0, tiled=True)]
    dot_general x1, matrix products: 3.34 us -> 9.59 us  [attend_back(): jnp.einsum('phqk,pqhd->pkhd', probability.astype(jnp.bfloat16), grad_mixe...]
    unnamed x135 -> x151, local copies, waits for them, and re-layouts: 12.7 us -> 8.09 us
    ppermute x15, waiting for transfers between devices: 27.7 us -> 32.3 us  [halving_scatter(): lax.ppermute(theirs.astype(jnp.bfloat16), ALL, [(i, i ^ 1 << b) for i in...]
    concatenate x1, local copies, waits for them, and re-layouts: 12.7 us -> 8.68 us  [local(): jnp.concatenate([qkv_wsum.reshape(total, share, 3 * D).astype(jnp.bfloat1...]
  transfers between devices with their start and end apart: 40 -> 41, of which waited for: 24 -> 23; matrix products, arithmetic and copies ran while one was open for 50% -> 45% of each run, Pallas kernels for 0% -> 0%
where the time goes in v2:
time: 388 us; the launch traced here: 383 us
  waiting for transfers between devices  121 us (31%)
  matrix products  98.1 us (25%)
  local copies, waits for them, and re-layouts  55.5 us (14%)
  other arithmetic  52.3 us (13%)
  starting transfers between devices  40.3 us (10%)
  between operations  15.6 us (4%)
    ppermute x8, waiting for transfers between devices, swapped(): lax.ppermute(shard, axis, [(i, i ^ 1 << bit) for i in range(lax.axis_size...  50.3 us
    ppermute x15, waiting for transfers between devices, doubling_gather(): other = lax.ppermute(cur, ALL, [(i, i ^ 1 << b) for i in range(total)])  36.3 us
    ppermute x15, waiting for transfers between devices, halving_scatter(): lax.ppermute(theirs.astype(jnp.bfloat16), ALL, [(i, i ^ 1 << b) for i in...  32.3 us
    dot_general x2, matrix products, ffn_forward(): jnp.dot(rows, inner_cols, preferred_element_type=jnp.float32) + inner_offset  21.2 us
    ppermute x15, starting transfers between devices, doubling_gather(): other = lax.ppermute(cur, ALL, [(i, i ^ 1 << b) for i in range(total)])  18.2 us
    dot_general x6, matrix products, contract_rows(): lax.dot_general(left_op, right_op, (((0,), (0,)), ((), ())), preferred_el...  15.8 us
    dot_general x6, matrix products, contract_cols(): lax.dot_general(left_op, right_op, (((1,), (1,)), ((), ())), preferred_el...  15.8 us
    ppermute x15, starting transfers between devices, halving_scatter(): lax.ppermute(theirs.astype(jnp.bfloat16), ALL, [(i, i ^ 1 << b) for i in...  11.7 us
  transfers between devices with their start and end apart: 41, of which 23 were waited for; matrix products, arithmetic and copies ran while one was open for 45% of the time, Pallas kernels for 0%

profile of v2, /device:TPU:0, one launch (start us, length us, event | category | flops | bytes accessed | tf_op | source)
XLA Modules:
  0.0 382.8 jit_solution(12767645792215815915)
XLA Ops:
  35.9 13.8 %collective-permute-done.13 = bf16[2,2,24,1152]{3,2,1,0:T(8,128)(2,1)S(1)} collective-permute-done((bf16[2,2,24,1152]{3,2,1,0:T(8,128)(2,1)S(1)}, bf16[2,2,24,1152]{3,2,1,0:T(8,128)(2,1)S(1)}, u32[]{:S(2)}, u32[]{:S(2)}) %collective-permute-start.13) | collective-permute-done | bytes 221216 | tf_op jit(solution)/shard_map/ppermute | solution.py:46
  50.3 16.0 %collective-permute-done.14 = bf16[2,2,2,24,1152]{4,3,2,1,0:T(8,128)(2,1)S(1)} collective-permute-done((bf16[2,2,2,24,1152]{4,3,2,1,0:T(8,128)(2,1)S(1)}, bf16[2,2,2,24,1152]{4,3,2,1,0:T(8,128)(2,1)S(1)}, u32[]{:S(2)}, u32[]{:S(2)}) %collective-permute-start.14) | collective-permute-done | bytes 442400 | tf_op jit(solution)/shard_map/ppermute | solution.py:46
  81.7 5.9 %collective-permute-done = bf16[256,768]{1,0:T(8,128)(2,1)} collective-permute-done((bf16[256,768]{1,0:T(8,128)(2,1)}, bf16[256,768]{1,0:T(8,128)(2,1)}, u32[]{:S(2)}, u32[]{:S(2)}) %collective-permute-start) | collective-permute-done | bytes 393248 | tf_op jit(solution)/shard_map/ppermute | solution.py:16
  87.5 4.3 %convolution_add_fusion = f32[512,2304]{1,0:T(8,128)S(1)} fusion(bf16[768,3200]{1,0:T(8,128)(2,1)} %pad_maximum_fusion, f32[2304]{0:T(1024)S(1)} %pad_maximum_fusion.17, bf16[256,768]{1,0:T(8,128)(2,1)} %collective-permute-done, bf16[256,768]{1,0:T(8,128)(2,1)S(1)} %copy-done.47, pred[]{:T(512)S(6)} %eq.134), kind=kOutput, calls=%fused_computation.14 | convolution fusion | flops 1816657920 | bytes 9053185 | tf_op jit(solution)/shard_map/dot_general | solution.py:332
  106.3 4.5 %copy-done.2 = f32[12,512,512]{1,2,0:T(8,128)} copy-done((f32[12,512,512]{1,2,0:T(8,128)}, f32[12,512,512]{1,2,0:T(8,128)S(1)}, u32[]{:S(2)}) %copy-start.2) | copy-done | bytes 12582936
  114.0 6.7 %fusion.40 = bf16[12,64,512]{2,1,0:T(8,128)(2,1)S(1)} fusion(bf16[512,12,64]{0,2,1:T(8,128)(2,1)S(1)} %bitcast.186, f32[12,512]{1,0:T(8,128)S(1)} %fusion, f32[12,512]{1,0:T(8,128)S(1)} %get-tuple-element.106, f32[12,512,512]{1,2,0:T(8,128)} %copy-done.2, pred[512,512]{0,1:T(8,128)(4,1)S(1)} %copy-done.12), kind=kOutput, calls=%fused_computation.102 | convolution fusion | flops 418775040 | bytes 14467072 | tf_op jit(solution)/shard_map/phqk,pkhd->pqhd/dot_general | solution.py:188
  129.7 14.1 %collective-permute-done.16 = bf16[512,768]{1,0:T(8,128)(2,1)} collective-permute-done((bf16[512,768]{1,0:T(8,128)(2,1)S(1)}, bf16[512,768]{1,0:T(8,128)(2,1)}, u32[]{:S(2)}, u32[]{:S(2)}) %collective-permute-start.16) | collective-permute-done | bytes 786464 | tf_op jit(solution)/shard_map/ppermute | solution.py:16
  143.8 11.2 %multiply_convert_fusion.1 = (bf16[512,1536]{1,0:T(8,128)(2,1)}, f32[512,1536]{1,0:T(8,128)}, f32[512,1536]{1,0:T(8,128)}) fusion(f32[1536]{0:T(1024)S(1)} %reshape.633, bf16[512,768]{1,0:T(8,128)(2,1)} %collective-permute-done.16, bf16[768,1538]{1,0:T(8,128)(2,1)} %all-gather.3.cloned.1.call-done), kind=kOutput, calls=%fused_computation.28 | convolution fusion | flops 1259864064 | bytes 11016192 | tf_op jit(solution)/shard_map/dot_general | solution.py:217
  162.1 10.0 %multiply_convert_fusion.2 = (bf16[512,1536]{1,0:T(8,128)(2,1)S(1)}, f32[512,1536]{1,0:T(8,128)}, f32[512,1536]{1,0:T(8,128)}) fusion(f32[1536]{0:T(1024)S(1)} %reshape.633, bf16[512,768]{1,0:T(8,128)(2,1)S(1)} %fusion.43, bf16[768,1538]{1,0:T(8,128)(2,1)S(1)} %copy-done.61), kind=kOutput, calls=%fused_computation.41 | convolution fusion | flops 1259864064 | bytes 11018240 | tf_op jit(solution)/shard_map/dot_general | solution.py:217
  172.1 8.2 %collective-permute-done.17 = bf16[512,768]{1,0:T(8,128)(2,1)S(1)} collective-permute-done((bf16[512,768]{1,0:T(8,128)(2,1)S(1)}, bf16[512,768]{1,0:T(8,128)(2,1)S(1)}, u32[]{:S(2)}, u32[]{:S(2)}) %collective-permute-start.17) | collective-permute-done | bytes 786464 | tf_op jit(solution)/shard_map/ppermute | solution.py:16
  196.8 5.2 %convert_reduce_fusion.1 = (f32[1536]{0:T(1024)S(1)}, bf16[512,1536]{1,0:T(8,128)(2,1)S(1)}) fusion(f32[512,1536]{1,0:T(8,128)} %get-tuple-element.64, f32[512,1536]{1,0:T(8,128)} %get-tuple-element.110, bf16[512,768]{1,0:T(8,128)(2,1)S(1)} %copy-done.19, bf16[768,1536]{1,0:T(8,128)(2,1)S(1)} %copy-done.65), kind=kOutput, calls=%fused_computation.25 | convolution fusion | flops 1220540928 | bytes 11016192 | tf_op jit(solution)/shard_map/dot_general | solution.py:224
  205.1 9.0 %collective-permute-done.20 = bf16[512,768]{1,0:T(8,128)(2,1)S(1)} collective-permute-done((bf16[512,768]{1,0:T(8,128)(2,1)}, bf16[512,768]{1,0:T(8,128)(2,1)S(1)}, u32[]{:S(2)}, u32[]{:S(2)}) %collective-permute-start.20) | collective-permute-done | bytes 786464 | tf_op jit(solution)/shard_map/ppermute | solution.py:16
  220.2 4.2 %add_convert_fusion.1 = bf16[768,1536]{1,0:T(8,128)(2,1)} fusion(f32[768,1536]{1,0:T(8,128)S(1)} %fusion.88, bf16[512,768]{1,0:T(8,128)(2,1)} %collective-permute-done.16, bf16[512,1536]{1,0:T(8,128)(2,1)S(1)} %get-tuple-element.48), kind=kOutput, calls=%fused_computation.18 | convolution fusion | flops 1210318848 | bytes 9437184 | tf_op jit(solution)/shard_map/dot_general | solution.py:163
  227.7 5.4 %pad_maximum_fusion.1 = bf16[768,3074]{1,0:T(8,128)(2,1)} fusion(bf16[768,2]{1,0:T(8,128)(2,1)S(1)} %add.340, bf16[768,1536]{1,0:T(8,128)(2,1)} %add_convert_fusion, bf16[768,1536]{1,0:T(8,128)(2,1)} %add_convert_fusion.1), kind=kLoop, calls=%fused_computation.13 | loop fusion | flops 14164992 | bytes 9443328 | tf_op jit(solution)/shard_map/concatenate | solution.py:383
  236.5 9.9 %collective-permute-done.21 = bf16[512,768]{1,0:T(8,128)(2,1)} collective-permute-done((bf16[512,768]{1,0:T(8,128)(2,1)}, bf16[512,768]{1,0:T(8,128)(2,1)}, u32[]{:S(2)}, u32[]{:S(2)}) %collective-permute-start.21) | collective-permute-done | bytes 786464 | tf_op jit(solution)/shard_map/ppermute | solution.py:16
  254.3 9.6 %fusion.37 = bf16[12,64,512]{2,1,0:T(8,128)(2,1)} fusion(bf16[512,12,64]{0,2,1:T(8,128)(2,1)} %bitcast.188, f32[12,512]{1,0:T(8,128)S(1)} %copy-done.49, f32[12,512,512]{1,2,0:T(8,128)} %copy-done.2, pred[512,512]{0,1:T(8,128)(4,1)S(1)} %copy-done.13), kind=kOutput, calls=%fused_computation.100 | convolution fusion | flops 415629312 | bytes 14442496 | tf_op jit(solution)/shard_map/phqk,pqhd->pkhd/dot_general | solution.py:196
  263.9 9.6 %multiply_reduce_fusion = (f32[12,512]{1,0:T(8,128)S(1)}, f32[12,512,512]{1,2,0:T(8,128)}) fusion(f32[12,512]{1,0:T(8,128)S(1)} %copy-done.49, f32[12,512,512]{1,2,0:T(8,128)} %copy-done.2, pred[512,512]{0,1:T(8,128)(4,1)S(1)} %copy-done.13, bf16[512,12,64]{0,2,1:T(8,128)(2,1)S(1)} %bitcast.189, bf16[512,12,64]{0,2,1:T(8,128)(2,1)S(1)} %bitcast.187), kind=kOutput, calls=%fused_computation.1 | convolution fusion | flops 418375680 | bytes 27049984 | tf_op jit(solution)/shard_map/pqhd,pkhd->phqk/dot_general | solution.py:202
  273.5 7.2 %multiply_convert_fusion = bf16[12,512,512]{1,2,0:T(8,128)(2,1)S(1)} fusion(f32[12,512,512]{1,2,0:T(8,128)} %get-tuple-element.114, f32[12,512]{1,0:T(8,128)S(1)} %get-tuple-element.113, f32[12,512]{1,0:T(8,128)S(1)} %copy-done.49, f32[12,512,512]{1,2,0:T(8,128)S(1)} %bitcast.174, pred[512,512]{0,1:T(8,128)(4,1)S(1)} %copy-done.13), kind=kLoop, calls=%fused_computation | loop fusion | flops 18874368 | bytes 31768576 | tf_op jit(solution)/shard_map/convert_element_type | solution.py:206
  293.1 4.1 %convolution_convert_fusion = bf16[768,2304]{1,0:T(8,128)(2,1)S(1)} fusion(bf16[512,768]{0,1:T(8,128)(2,1)} %bitcast.199, bf16[512,768]{0,1:T(8,128)(2,1)} %bitcast.195, bf16[512,768]{0,1:T(8,128)(2,1)} %bitcast.192, bf16[256,768]{1,0:T(8,128)(2,1)} %collective-permute-done, bf16[256,768]{1,0:T(8,128)(2,1)} %get-tuple-element.86, pred[]{:T(512)S(6)} %eq.134), kind=kOutput, calls=%fused_computation.11 | convolution fusion | flops 1824325632 | bytes 6684673 | tf_op jit(solution)/shard_map/dot_general | solution.py:163
  305.3 8.7 %concatenate.125 = bf16[32,24,3081]{2,1,0:T(8,128)(2,1)} concatenate(bf16[32,24,2304]{2,1,0:T(8,128)(2,1)S(1)} %bitcast.176, bf16[32,24,3]{2,1,0:T(8,128)(2,1)} %bitcast.203, bf16[32,24,768]{2,1,0:T(8,128)(2,1)} %convolution_convert_fusion.1, bf16[32,24,1]{2,1,0:T(8,128)(2,1)} %stack.65, bf16[32,24,1]{2,1,0:T(8,128)(2,1)} %stack.66, bf16[32,24,1]{2,1,0:T(8,128)(2,1)} %stack.67, ...), dimensions={2} | concatenate | bytes 9464832 | tf_op jit(solution)/shard_map/concatenate | solution.py:420
  329.7 10.3 %collective-permute-done.34 = bf16[2,2,2,24,1024]{4,3,2,0,1:T(8,128)(2,1)S(1)} collective-permute-done((bf16[2,2,2,24,1024]{4,3,2,0,1:T(8,128)(2,1)S(1)}, bf16[2,2,2,24,1024]{4,3,2,0,1:T(8,128)(2,1)S(1)}, u32[]{:S(2)}, u32[]{:S(2)}) %collective-permute-start.34) | collective-permute-done | bytes 393248 | tf_op jit(solution)/shard_map/ppermute | solution.py:79
  341.9 6.3 %collective-permute-done.29 = bf16[2,2,2,24,1033]{4,3,2,1,0:T(8,128)(2,1)S(1)} collective-permute-done((bf16[2,2,2,24,1033]{4,3,2,1,0:T(8,128)(2,1)S(1)}, bf16[2,2,2,24,1033]{4,3,2,1,0:T(8,128)(2,1)S(1)}, u32[]{:S(2)}, u32[]{:S(2)}) %collective-permute-start.29) | collective-permute-done | bytes 396704 | tf_op jit(solution)/shard_map/ppermute | solution.py:79
  348.3 4.4 %collective-permute-done.25 = bf16[2,2,24,1024]{3,2,1,0:T(8,128)(2,1)S(1)} collective-permute-done((bf16[2,2,24,1024]{3,2,1,0:T(8,128)(2,1)S(1)}, bf16[2,2,24,1024]{3,2,1,0:T(8,128)(2,1)S(1)}, u32[]{:S(2)}, u32[]{:S(2)}) %collective-permute-start.25) | collective-permute-done | bytes 196640 | tf_op jit(solution)/shard_map/ppermute | solution.py:79
  355.1 5.2 %collective-permute-done.30 = bf16[2,2,24,1033]{3,2,1,0:T(8,128)(2,1)S(1)} collective-permute-done((bf16[2,2,24,1033]{3,2,1,0:T(8,128)(2,1)S(1)}, bf16[2,2,24,1033]{3,2,1,0:T(8,128)(2,1)S(1)}, u32[]{:S(2)}, u32[]{:S(2)}) %collective-permute-start.30) | collective-permute-done | bytes 198368 | tf_op jit(solution)/shard_map/ppermute | solution.py:79
  (369 shorter events, 173.5 us)
Async XLA Ops:
  7.2 106.3 %all-gather.3.cloned.1.call-start = ((), (), s32[]{:S(2)}) async-start(), calls=%async_computation.1 | async-start | bytes 2715648 | tf_op jit(solution)/shard_map/all_gather | solution.py:291
  9.6 13.0 %collective-permute-start.11 = (bf16[24,1152]{1,0:T(8,128)(2,1)S(1)}, bf16[24,1152]{1,0:T(8,128)(2,1)S(1)}, u32[]{:S(2)}, u32[]{:S(2)}) collective-permute-start(bf16[24,1152]{1,0:T(8,128)(2,1)S(1)} %fusion.62), channel_id=1, source_target_pairs={{0,1},{1,0},{2,3},{3,2},{4,5},{5,4},{6,7},{7,6},{8,9},{9,8},{10,11... | collective-permute-start | bytes 165896 | tf_op jit(solution)/shard_map/ppermute | solution.py:46
  29.2 20.5 %collective-permute-start.13 = (bf16[2,2,24,1152]{3,2,1,0:T(8,128)(2,1)S(1)}, bf16[2,2,24,1152]{3,2,1,0:T(8,128)(2,1)S(1)}, u32[]{:S(2)}, u32[]{:S(2)}) collective-permute-start(bf16[2,2,24,1152]{3,2,1,0:T(8,128)(2,1)S(1)} %broadcast_select_fusion.11), channel_id=1, source_target_pairs={{0,16},{1,17},{2,18},{3,19},{4,20},{5,21},{6,22},{7,23},{8,24},{9,... | collective-permute-start | bytes 663560 | tf_op jit(solution)/shard_map/ppermute | solution.py:46
  31.9 34.6 %collective-permute-start.9 = (bf16[2,2,2,24,1024]{4,3,2,0,1:T(8,128)(2,1)S(1)}, bf16[2,2,2,24,1024]{4,3,2,0,1:T(8,128)(2,1)S(1)}, u32[]{:S(2)}, u32[]{:S(2)}) collective-permute-start(bf16[2,2,2,24,1024]{4,3,2,0,1:T(8,128)(2,1)S(1)} %broadcast_select_fusion.7), channel_id=1, source_target_pairs={{0,16},{1,17},{2,18},{3,19},{4,20},{5,21},{6,22},{7,23},{8,24},{9,... | collective-permute-start | bytes 1179656 | tf_op jit(solution)/shard_map/ppermute | solution.py:46
  34.7 15.4 %collective-permute-start.4 = (bf16[2,2,2,24,1024]{4,3,2,0,1:T(8,128)(2,1)S(1)}, bf16[2,2,2,24,1024]{4,3,2,0,1:T(8,128)(2,1)S(1)}, u32[]{:S(2)}, u32[]{:S(2)}) collective-permute-start(bf16[2,2,2,24,1024]{4,3,2,0,1:T(8,128)(2,1)S(1)} %broadcast_select_fusion.9), channel_id=1, source_target_pairs={{0,4},{1,5},{2,6},{3,7},{4,0},{5,1},{6,2},{7,3},{8,12},{9,13},{10,... | collective-permute-start | bytes 1179656 | tf_op jit(solution)/shard_map/ppermute | solution.py:46
  49.8 16.4 %collective-permute-start.14 = (bf16[2,2,2,24,1152]{4,3,2,1,0:T(8,128)(2,1)S(1)}, bf16[2,2,2,24,1152]{4,3,2,1,0:T(8,128)(2,1)S(1)}, u32[]{:S(2)}, u32[]{:S(2)}) collective-permute-start(bf16[2,2,2,24,1152]{4,3,2,1,0:T(8,128)(2,1)S(1)} %broadcast_select_fusion.6), channel_id=1, source_target_pairs={{0,8},{1,9},{2,10},{3,11},{4,12},{5,13},{6,14},{7,15},{8,0},{9,1},... | collective-permute-start | bytes 1327112 | tf_op jit(solution)/shard_map/ppermute | solution.py:46
  50.2 17.8 %collective-permute-start.5 = (bf16[2,2,2,2,24,1024]{5,4,3,0,1,2:T(8,128)(2,1)S(1)}, bf16[2,2,2,2,24,1024]{5,4,3,0,1,2:T(8,128)(2,1)S(1)}, u32[]{:S(2)}, u32[]{:S(2)}) collective-permute-start(bf16[2,2,2,2,24,1024]{5,4,3,0,1,2:T(8,128)(2,1)S(1)} %broadcast_select_fusion.4), channel_id=1, source_target_pairs={{0,2},{1,3},{2,0},{3,1},{4,6},{5,7},{6,4},{7,5},{8,10},{9,11},{10,... | collective-permute-start | bytes 2359304 | tf_op jit(solution)/shard_map/ppermute | solution.py:46
  74.0 82.8 %all-gather.5.cloned.1.call-start = ((), (), s32[]{:S(2)}) async-start(), calls=%async_computation.2 | async-start | bytes 2506752 | tf_op jit(solution)/shard_map/all_gather | solution.py:293
  75.2 12.3 %collective-permute-start = (bf16[256,768]{1,0:T(8,128)(2,1)}, bf16[256,768]{1,0:T(8,128)(2,1)}, u32[]{:S(2)}, u32[]{:S(2)}) collective-permute-start(bf16[256,768]{1,0:T(8,128)(2,1)} %get-tuple-element.87), channel_id=1, source_target_pairs={{0,1},{1,0},{2,3},{3,2},{4,5},{5,4},{6,7},{7,6},{8,9},{9,8},{10,11... | collective-permute-start | bytes 1179656 | tf_op jit(solution)/shard_map/ppermute | solution.py:16
  76.2 49.3 %collective-permute-start.19 = (bf16[256,768]{1,0:T(8,128)(2,1)}, bf16[256,768]{1,0:T(8,128)(2,1)}, u32[]{:S(2)}, u32[]{:S(2)}) collective-permute-start(bf16[256,768]{1,0:T(8,128)(2,1)} %get-tuple-element.84), channel_id=1, source_target_pairs={{0,1},{1,0},{2,3},{3,2},{4,5},{5,4},{6,7},{7,6},{8,9},{9,8},{10,11... | collective-permute-start | bytes 1179656 | tf_op jit(solution)/shard_map/ppermute | solution.py:16
  113.5 257.5 %reduce-scatter.2.cloned.1.call-start = ((), (), s32[]{:S(2)}) async-start(), calls=%async_computation.3 | async-start | bytes 5222400 | tf_op jit(solution)/shard_map/reduce_scatter | solution.py:384
  123.9 19.8 %collective-permute-start.16 = (bf16[512,768]{1,0:T(8,128)(2,1)S(1)}, bf16[512,768]{1,0:T(8,128)(2,1)}, u32[]{:S(2)}, u32[]{:S(2)}) collective-permute-start(bf16[512,768]{1,0:T(8,128)(2,1)S(1)} %fusion.43), channel_id=1, source_target_pairs={{0,1},{1,0},{2,3},{3,2},{4,5},{5,4},{6,7},{7,6},{8,9},{9,8},{10,11... | collective-permute-start | bytes 2359304 | tf_op jit(solution)/shard_map/ppermute | solution.py:16
  160.6 19.7 %collective-permute-start.17 = (bf16[512,768]{1,0:T(8,128)(2,1)S(1)}, bf16[512,768]{1,0:T(8,128)(2,1)S(1)}, u32[]{:S(2)}, u32[]{:S(2)}) collective-permute-start(bf16[512,768]{1,0:T(8,128)(2,1)S(1)} %convolution_convert_fusion.3), channel_id=1, source_target_pairs={{0,1},{1,0},{2,3},{3,2},{4,5},{5,4},{6,7},{7,6},{8,9},{9,8},{10,11... | collective-permute-start | bytes 2359304 | tf_op jit(solution)/shard_map/ppermute | solution.py:16
  193.5 20.6 %collective-permute-start.20 = (bf16[512,768]{1,0:T(8,128)(2,1)}, bf16[512,768]{1,0:T(8,128)(2,1)S(1)}, u32[]{:S(2)}, u32[]{:S(2)}) collective-permute-start(bf16[512,768]{1,0:T(8,128)(2,1)} %get-tuple-element.52), channel_id=1, source_target_pairs={{0,1},{1,0},{2,3},{3,2},{4,5},{5,4},{6,7},{7,6},{8,9},{9,8},{10,11... | collective-permute-start | bytes 2359304 | tf_op jit(solution)/shard_map/ppermute | solution.py:16
  196.2 36.9 %collective-permute-start.18 = (f32[256,768]{1,0:T(8,128)}, f32[256,768]{1,0:T(8,128)}, u32[]{:S(2)}, u32[]{:S(2)}) collective-permute-start(f32[256,768]{1,0:T(8,128)} %get-tuple-element.83), channel_id=1, source_target_pairs={{0,1},{1,0},{2,3},{3,2},{4,5},{5,4},{6,7},{7,6},{8,9},{9,8},{10,11... | collective-permute-start | bytes 2359304 | tf_op jit(solution)/shard_map/ppermute | solution.py:16
  218.7 27.6 %collective-permute-start.21 = (bf16[512,768]{1,0:T(8,128)(2,1)}, bf16[512,768]{1,0:T(8,128)(2,1)}, u32[]{:S(2)}, u32[]{:S(2)}) collective-permute-start(bf16[512,768]{1,0:T(8,128)(2,1)} %fusion.34), channel_id=1, source_target_pairs={{0,1},{1,0},{2,3},{3,2},{4,5},{5,4},{6,7},{7,6},{8,9},{9,8},{10,11... | collective-permute-start | bytes 2359304 | tf_op jit(solution)/shard_map/ppermute | solution.py:16
  298.6 17.3 %collective-permute-start.23 = (bf16[2,2,2,2,24,1024]{5,4,3,2,1,0:T(8,128)(2,1)}, bf16[2,2,2,2,24,1024]{5,4,3,2,1,0:T(8,128)(2,1)}, u32[]{:S(2)}, u32[]{:S(2)}) collective-permute-start(bf16[2,2,2,2,24,1024]{5,4,3,2,1,0:T(8,128)(2,1)} %dynamic-slice_bitcast_fusion.1), channel_id=1, source_target_pairs={{0,2},{1,3},{2,0},{3,1},{4,6},{5,7},{6,4},{7,5},{8,10},{9,11},{10,... | collective-permute-start | bytes 2359304 | tf_op jit(solution)/shard_map/ppermute | solution.py:79
  300.6 17.2 %collective-permute-start.33 = (bf16[2,2,2,2,24,1024]{5,4,3,1,2,0:T(8,128)(2,1)}, bf16[2,2,2,2,24,1024]{5,4,3,1,2,0:T(8,128)(2,1)}, u32[]{:S(2)}, u32[]{:S(2)}) collective-permute-start(bf16[2,2,2,2,24,1024]{5,4,3,1,2,0:T(8,128)(2,1)} %bitcast.172), channel_id=1, source_target_pairs={{0,2},{1,3},{2,0},{3,1},{4,6},{5,7},{6,4},{7,5},{8,10},{9,11},{10,... | collective-permute-start | bytes 2359304 | tf_op jit(solution)/shard_map/ppermute | solution.py:79
  304.2 19.8 %collective-permute-start.22 = (f32[256,768]{1,0:T(8,128)}, f32[256,768]{1,0:T(8,128)}, u32[]{:S(2)}, u32[]{:S(2)}) collective-permute-start(f32[256,768]{1,0:T(8,128)} %get-tuple-element.81), channel_id=1, source_target_pairs={{0,1},{1,0},{2,3},{3,2},{4,5},{5,4},{6,7},{7,6},{8,9},{9,8},{10,11... | collective-permute-start | bytes 2359304 | tf_op jit(solution)/shard_map/ppermute | solution.py:16
  319.3 20.8 %collective-permute-start.34 = (bf16[2,2,2,24,1024]{4,3,2,0,1:T(8,128)(2,1)S(1)}, bf16[2,2,2,24,1024]{4,3,2,0,1:T(8,128)(2,1)S(1)}, u32[]{:S(2)}, u32[]{:S(2)}) collective-permute-start(bf16[2,2,2,24,1024]{4,3,2,0,1:T(8,128)(2,1)S(1)} %fusion.54), channel_id=1, source_target_pairs={{0,16},{1,17},{2,18},{3,19},{4,20},{5,21},{6,22},{7,23},{8,24},{9,... | collective-permute-start | bytes 1179656 | tf_op jit(solution)/shard_map/ppermute | solution.py:79
  326.9 21.2 %collective-permute-start.29 = (bf16[2,2,2,24,1033]{4,3,2,1,0:T(8,128)(2,1)S(1)}, bf16[2,2,2,24,1033]{4,3,2,1,0:T(8,128)(2,1)S(1)}, u32[]{:S(2)}, u32[]{:S(2)}) collective-permute-start(bf16[2,2,2,24,1033]{4,3,2,1,0:T(8,128)(2,1)S(1)} %fusion.48), channel_id=1, source_target_pairs={{0,8},{1,9},{2,10},{3,11},{4,12},{5,13},{6,14},{7,15},{8,0},{9,1},... | collective-permute-start | bytes 1190024 | tf_op jit(solution)/shard_map/ppermute | solution.py:79
  329.1 23.7 %collective-permute-start.25 = (bf16[2,2,24,1024]{3,2,1,0:T(8,128)(2,1)S(1)}, bf16[2,2,24,1024]{3,2,1,0:T(8,128)(2,1)S(1)}, u32[]{:S(2)}, u32[]{:S(2)}) collective-permute-start(bf16[2,2,24,1024]{3,2,1,0:T(8,128)(2,1)S(1)} %fusion.56), channel_id=1, source_target_pairs={{0,8},{1,9},{2,10},{3,11},{4,12},{5,13},{6,14},{7,15},{8,0},{9,1},... | collective-permute-start | bytes 589832 | tf_op jit(solution)/shard_map/ppermute | solution.py:79
  340.2 12.8 %collective-permute-start.35 = (bf16[2,2,24,1024]{3,2,1,0:T(8,128)(2,1)S(1)}, bf16[2,2,24,1024]{3,2,1,0:T(8,128)(2,1)S(1)}, u32[]{:S(2)}, u32[]{:S(2)}) collective-permute-start(bf16[2,2,24,1024]{3,2,1,0:T(8,128)(2,1)S(1)} %fusion.57), channel_id=1, source_target_pairs={{0,4},{1,5},{2,6},{3,7},{4,0},{5,1},{6,2},{7,3},{8,12},{9,13},{10,... | collective-permute-start | bytes 589832 | tf_op jit(solution)/shard_map/ppermute | solution.py:79
  348.3 12.0 %collective-permute-start.30 = (bf16[2,2,24,1033]{3,2,1,0:T(8,128)(2,1)S(1)}, bf16[2,2,24,1033]{3,2,1,0:T(8,128)(2,1)S(1)}, u32[]{:S(2)}, u32[]{:S(2)}) collective-permute-start(bf16[2,2,24,1033]{3,2,1,0:T(8,128)(2,1)S(1)} %fusion.55), channel_id=1, source_target_pairs={{0,16},{1,17},{2,18},{3,19},{4,20},{5,21},{6,22},{7,23},{8,24},{9,... | collective-permute-start | bytes 595016 | tf_op jit(solution)/shard_map/ppermute | solution.py:79
  (92 other events, 791.3 us)
Sparse Core Ops, SparseCore 0:
  74.1 39.3 all-gather.2
  115.8 40.9 all-gather.4
  233.3 73.6 reduce-scatter.1

commit v3 on v1

--- a/solution.py
+++ b/solution.py
@@ -79,7 +79,7 @@
         got = lax.ppermute(
             theirs.astype(jnp.bfloat16), ALL, [(i, i ^ (1 << b)) for i in range(total)]
         )
-        cur = mine + got.astype(jnp.float32)
+        cur = mine.astype(jnp.float32) + got.astype(jnp.float32)
         axes.pop(a)
     return cur
 
@@ -413,14 +413,23 @@
         ],
         axis=1,
     )
+    pack_grad = grad_one + contract_cols(grad_qkv, qkv_full)
+    keep_grad = lax.dynamic_slice_in_dim(pack_grad, half_bit * half_len, half_len, 0)
+    give_grad = lax.dynamic_slice_in_dim(pack_grad, (1 - half_bit) * half_len, half_len, 0)
+    give_grad, grad_qkv, pack_in = lax.optimization_barrier((give_grad, grad_qkv, pack_in))
+    got_grad = swapped(give_grad, "narrow", 0)
+    input_grad = jnp.where(
+        half_bit == 0,
+        jnp.concatenate([keep_grad, got_grad]),
+        jnp.concatenate([got_grad, keep_grad]),
+    )
     qkv_wsum = contract_rows(pack_in, grad_qkv)
     qkv_bsum = jnp.sum(grad_qkv.astype(jnp.float32), axis=0).reshape(3, D)
-    input_grad = from_pack(grad_one + contract_cols(grad_qkv, qkv_full))
     late = jnp.concatenate(
         [
-            qkv_wsum.reshape(total, share, 3 * D),
-            qkv_bsum.T.reshape(total, share, 3),
-            early,
+            qkv_wsum.reshape(total, share, 3 * D).astype(jnp.bfloat16),
+            qkv_bsum.T.reshape(total, share, 3).astype(jnp.bfloat16),
+            early.astype(jnp.bfloat16),
         ],
         axis=2,
     )

time: 378 us -> 372 us (0.984)
  waiting for transfers between devices: 104 us -> 121 us
  local copies, waits for them, and re-layouts: 67.3 us -> 55 us
  starting transfers between devices: 41 us -> 33.4 us
  matrix products: 94.3 us -> 86.8 us
  other arithmetic: 50.2 us -> 54.4 us
    ppermute x8, waiting for transfers between devices: 33 us -> 44.1 us  [swapped(): lax.ppermute(shard, axis, [(i, i ^ 1 << bit) for i in range(lax.axis_size...]
    ppermute x15, starting transfers between devices: 15 us -> 7.17 us  [halving_scatter(): lax.ppermute(theirs.astype(jnp.bfloat16), ALL, [(i, i ^ 1 << b) for i in...]
    ppermute x15, waiting for transfers between devices: 27.7 us -> 35.4 us  [halving_scatter(): lax.ppermute(theirs.astype(jnp.bfloat16), ALL, [(i, i ^ 1 << b) for i in...]
    unnamed x135 -> x149, local copies, waits for them, and re-layouts: 12.7 us -> 5.9 us
    dot_general x1, matrix products: 3.34 us -> 8.97 us  [attend_back(): jnp.einsum('phqk,pqhd->pkhd', probability.astype(jnp.bfloat16), grad_mixe...]
    dot_general x6, matrix products: 18.4 us -> 13.7 us  [contract_rows(): lax.dot_general(left_op, right_op, (((0,), (0,)), ((), ())), preferred_el...]
    concatenate x1, local copies, waits for them, and re-layouts: 12.7 us -> 8.66 us  [local(): jnp.concatenate([qkv_wsum.reshape(total, share, 3 * D).astype(jnp.bfloat1...]
  transfers between devices with their start and end apart: 40 -> 40, of which waited for: 24 -> 22; matrix products, arithmetic and copies ran while one was open for 50% -> 43% of each run, Pallas kernels for 0% -> 0%
where the time goes in v3:
time: 372 us; the launch traced here: 367 us
  waiting for transfers between devices  121 us (33%)
  matrix products  86.8 us (23%)
  local copies, waits for them, and re-layouts  55 us (15%)
  other arithmetic  54.4 us (15%)
  starting transfers between devices  33.4 us (9%)
  between operations  15.8 us (4%)
    ppermute x8, waiting for transfers between devices, swapped(): lax.ppermute(shard, axis, [(i, i ^ 1 << bit) for i in range(lax.axis_size...  44.1 us
    ppermute x15, waiting for transfers between devices, doubling_gather(): other = lax.ppermute(cur, ALL, [(i, i ^ 1 << b) for i in range(total)])  36.3 us
    ppermute x15, waiting for transfers between devices, halving_scatter(): lax.ppermute(theirs.astype(jnp.bfloat16), ALL, [(i, i ^ 1 << b) for i in...  35.4 us
    dot_general x2, matrix products, ffn_forward(): jnp.dot(rows, inner_cols, preferred_element_type=jnp.float32) + inner_offset  21.1 us
    ppermute x15, starting transfers between devices, doubling_gather(): other = lax.ppermute(cur, ALL, [(i, i ^ 1 << b) for i in range(total)])  18.2 us
    dot_general x6, matrix products, contract_rows(): lax.dot_general(left_op, right_op, (((0,), (0,)), ((), ())), preferred_el...  13.7 us
    dot_general x6, matrix products, contract_cols(): lax.dot_general(left_op, right_op, (((1,), (1,)), ((), ())), preferred_el...  13 us
    dot_general x1, matrix products, attend_back(): jnp.einsum('pqhd,pkhd->phqk', grad_mixed, value_low, preferred_element_ty...  9.57 us
  transfers between devices with their start and end apart: 40, of which 22 were waited for; matrix products, arithmetic and copies ran while one was open for 43% of the time, Pallas kernels for 0%

profile of v3, /device:TPU:0, one launch (start us, length us, event | category | flops | bytes accessed | tf_op | source)
XLA Modules:
  0.0 366.9 jit_solution(9940169012467160997)
XLA Ops:
  36.0 13.8 %collective-permute-done.13 = bf16[2,2,24,1152]{3,2,1,0:T(8,128)(2,1)S(1)} collective-permute-done((bf16[2,2,24,1152]{3,2,1,0:T(8,128)(2,1)S(1)}, bf16[2,2,24,1152]{3,2,1,0:T(8,128)(2,1)S(1)}, u32[]{:S(2)}, u32[]{:S(2)}) %collective-permute-start.13) | collective-permute-done | bytes 221216 | tf_op jit(solution)/shard_map/ppermute | solution.py:46
  50.4 16.0 %collective-permute-done.14 = bf16[2,2,2,24,1152]{4,3,2,1,0:T(8,128)(2,1)S(1)} collective-permute-done((bf16[2,2,2,24,1152]{4,3,2,1,0:T(8,128)(2,1)S(1)}, bf16[2,2,2,24,1152]{4,3,2,1,0:T(8,128)(2,1)S(1)}, u32[]{:S(2)}, u32[]{:S(2)}) %collective-permute-start.14) | collective-permute-done | bytes 442400 | tf_op jit(solution)/shard_map/ppermute | solution.py:46
  80.8 6.5 %collective-permute-done = bf16[256,768]{1,0:T(8,128)(2,1)S(1)} collective-permute-done((bf16[256,768]{1,0:T(8,128)(2,1)}, bf16[256,768]{1,0:T(8,128)(2,1)S(1)}, u32[]{:S(2)}, u32[]{:S(2)}) %collective-permute-start) | collective-permute-done | bytes 393248 | tf_op jit(solution)/shard_map/ppermute | solution.py:16
  110.6 3.7 %fusion.55 = bf16[12,64,512]{2,1,0:T(8,128)(2,1)S(1)} fusion(bf16[512,12,64]{0,2,1:T(8,128)(2,1)S(1)} %bitcast.185, f32[12,512]{1,0:T(8,128)S(1)} %fusion, f32[12,512]{1,0:T(8,128)S(1)} %get-tuple-element.102, f32[12,512,512]{1,2,0:T(8,128)S(1)} %get-tuple-element.103, pred[512,512]{0,1:T(8,128)(4,1)S(1)} %copy-done.14), kind=kOutput, calls=%fused_computation.110 | convolution fusion | flops 418775040 | bytes 14467072 | tf_op jit(solution)/shard_map/phqk,pkhd->pqhd/dot_general | solution.py:188
  119.4 5.5 %all-gather.2.cloned.1.call-done = bf16[768,3074]{1,0:T(8,128)(2,1)} async-done(((bf16[48,3074]{1,0:T(8,128)(2,1)}), bf16[768,3074]{1,0:T(8,128)(2,1)}) %all-gather.2.cloned.1.call-update) | async-done | bytes 4721680 | tf_op jit(solution)/shard_map/all_gather | solution.py:291
  126.0 8.1 %collective-permute-done.16 = bf16[512,768]{1,0:T(8,128)(2,1)} collective-permute-done((bf16[512,768]{1,0:T(8,128)(2,1)S(1)}, bf16[512,768]{1,0:T(8,128)(2,1)}, u32[]{:S(2)}, u32[]{:S(2)}) %collective-permute-start.16) | collective-permute-done | bytes 786464 | tf_op jit(solution)/shard_map/ppermute | solution.py:16
  134.1 11.0 %multiply_convert_fusion.1 = (bf16[512,1536]{1,0:T(8,128)(2,1)S(1)}, f32[512,1536]{1,0:T(8,128)}, f32[512,1536]{1,0:T(8,128)}) fusion(f32[1536]{0:T(1024)S(1)} %reshape.633, bf16[512,768]{1,0:T(8,128)(2,1)} %collective-permute-done.16, bf16[768,3074]{1,0:T(8,128)(2,1)} %all-gather.2.cloned.1.call-done), kind=kOutput, calls=%fused_computation.28 | convolution fusion | flops 1259864064 | bytes 11016192 | tf_op jit(solution)/shard_map/dot_general | solution.py:217
  147.3 10.2 %multiply_convert_fusion.2 = (bf16[512,1536]{1,0:T(8,128)(2,1)S(1)}, f32[512,1536]{1,0:T(8,128)}, f32[512,1536]{1,0:T(8,128)}) fusion(f32[1536]{0:T(1024)S(1)} %reshape.633, bf16[512,768]{1,0:T(8,128)(2,1)S(1)} %fusion.58, bf16[768,3074]{1,0:T(8,128)(2,1)S(1)} %copy-done.61), kind=kOutput, calls=%fused_computation.41 | convolution fusion | flops 1259864064 | bytes 11018240 | tf_op jit(solution)/shard_map/dot_general | solution.py:217
  157.5 6.2 %collective-permute-done.17 = bf16[512,768]{1,0:T(8,128)(2,1)S(1)} collective-permute-done((bf16[512,768]{1,0:T(8,128)(2,1)S(1)}, bf16[512,768]{1,0:T(8,128)(2,1)S(1)}, u32[]{:S(2)}, u32[]{:S(2)}) %collective-permute-start.17) | collective-permute-done | bytes 786464 | tf_op jit(solution)/shard_map/ppermute | solution.py:16
  180.1 5.9 %convert_reduce_fusion.1 = (f32[1536]{0:T(1024)S(1)}, bf16[512,1536]{1,0:T(8,128)(2,1)S(1)}) fusion(f32[512,1536]{1,0:T(8,128)} %get-tuple-element.58, f32[512,1536]{1,0:T(8,128)} %get-tuple-element.107, bf16[512,768]{1,0:T(8,128)(2,1)S(1)} %copy-done.21, bf16[768,3074]{1,0:T(8,128)(2,1)} %all-gather.2.cloned.1.call-done), kind=kOutput, calls=%fused_computation.25 | convolution fusion | flops 1220540928 | bytes 11016192 | tf_op jit(solution)/shard_map/dot_general | solution.py:224
  189.2 8.3 %collective-permute-done.20 = bf16[512,768]{1,0:T(8,128)(2,1)S(1)} collective-permute-done((bf16[512,768]{1,0:T(8,128)(2,1)}, bf16[512,768]{1,0:T(8,128)(2,1)S(1)}, u32[]{:S(2)}, u32[]{:S(2)}) %collective-permute-start.20) | collective-permute-done | bytes 786464 | tf_op jit(solution)/shard_map/ppermute | solution.py:16
  203.8 4.1 %add_convert_fusion.1 = bf16[768,1536]{1,0:T(8,128)(2,1)} fusion(f32[768,1536]{1,0:T(8,128)S(1)} %fusion.104, bf16[512,768]{1,0:T(8,128)(2,1)} %collective-permute-done.16, bf16[512,1536]{1,0:T(8,128)(2,1)S(1)} %get-tuple-element.116), kind=kOutput, calls=%fused_computation.18 | convolution fusion | flops 1210318848 | bytes 9437184 | tf_op jit(solution)/shard_map/dot_general | solution.py:163
  211.3 5.4 %pad_maximum_fusion.1 = bf16[768,3074]{1,0:T(8,128)(2,1)} fusion(bf16[768,2]{1,0:T(8,128)(2,1)S(1)} %add.340, bf16[768,1536]{1,0:T(8,128)(2,1)} %add_convert_fusion, bf16[768,1536]{1,0:T(8,128)(2,1)} %add_convert_fusion.1), kind=kLoop, calls=%fused_computation.13 | loop fusion | flops 14164992 | bytes 9443328 | tf_op jit(solution)/shard_map/concatenate | solution.py:382
  216.7 10.7 %collective-permute-done.21 = bf16[512,768]{1,0:T(8,128)(2,1)} collective-permute-done((bf16[512,768]{1,0:T(8,128)(2,1)}, bf16[512,768]{1,0:T(8,128)(2,1)}, u32[]{:S(2)}, u32[]{:S(2)}) %collective-permute-start.21) | collective-permute-done | bytes 786464 | tf_op jit(solution)/shard_map/ppermute | solution.py:16
  227.4 4.6 %multiply_reduce_fusion.1 = (bf16[768]{0:T(1024)(128)(2,1)S(1)}, f32[512]{0:T(512)S(1)}, bf16[768]{0:T(1024)(128)(2,1)S(1)}, f32[512,768]{1,0:T(8,128)S(1)}) fusion(f32[512,768]{1,0:T(8,128)S(1)} %get-tuple-element.105, f32[512]{0:T(512)S(1)} %copy-done.55, f32[512]{0:T(512)S(1)} %broadcast_multiply_fusion.1, f32[768]{0:T(1024)S(1)} %get-tuple-element.35, ...), kind=kOutput, calls=%fused_computation.77 | convolution fusion | flops 1212676096 | bytes 9451520 | tf_op jit(solution)/shard_map/dot_general | solution.py:169
  235.8 9.0 %fusion.52 = bf16[12,64,512]{2,1,0:T(8,128)(2,1)} fusion(bf16[512,12,64]{0,2,1:T(8,128)(2,1)} %bitcast.187, f32[12,512]{1,0:T(8,128)S(1)} %copy-done.49, f32[12,512,512]{1,2,0:T(8,128)} %copy-done.2, pred[512,512]{0,1:T(8,128)(4,1)S(1)} %copy-done.15), kind=kOutput, calls=%fused_computation.109 | convolution fusion | flops 415629312 | bytes 14442496 | tf_op jit(solution)/shard_map/phqk,pqhd->pkhd/dot_general | solution.py:196
  244.8 9.6 %multiply_reduce_fusion = (f32[12,512]{1,0:T(8,128)S(1)}, f32[12,512,512]{1,2,0:T(8,128)}) fusion(f32[12,512]{1,0:T(8,128)S(1)} %copy-done.49, f32[12,512,512]{1,2,0:T(8,128)} %copy-done.2, pred[512,512]{0,1:T(8,128)(4,1)S(1)} %copy-done.15, bf16[512,12,64]{0,2,1:T(8,128)(2,1)S(1)} %bitcast.188, bf16[512,12,64]{0,2,1:T(8,128)(2,1)S(1)} %bitcast.186), kind=kOutput, calls=%fused_computation.1 | convolution fusion | flops 418375680 | bytes 27049984 | tf_op jit(solution)/shard_map/pqhd,pkhd->phqk/dot_general | solution.py:202
  254.4 7.1 %multiply_convert_fusion = bf16[12,512,512]{1,2,0:T(8,128)(2,1)S(1)} fusion(f32[12,512,512]{1,2,0:T(8,128)} %get-tuple-element.112, f32[12,512]{1,0:T(8,128)S(1)} %get-tuple-element.111, f32[12,512]{1,0:T(8,128)S(1)} %copy-done.49, f32[12,512,512]{1,2,0:T(8,128)S(1)} %bitcast.173, pred[512,512]{0,1:T(8,128)(4,1)S(1)} %copy-done.15), kind=kLoop, calls=%fused_computation | loop fusion | flops 18874368 | bytes 31768576 | tf_op jit(solution)/shard_map/convert_element_type | solution.py:206
  289.6 8.7 %concatenate.125 = bf16[32,24,3081]{2,1,0:T(8,128)(2,1)} concatenate(bf16[32,24,2304]{2,1,0:T(8,128)(2,1)S(1)} %bitcast.175, bf16[32,24,3]{2,1,0:T(8,128)(2,1)} %bitcast.199, bf16[32,24,768]{2,1,0:T(8,128)(2,1)} %convolution_convert_fusion.1, bf16[32,24,1]{2,1,0:T(8,128)(2,1)} %stack.65, bf16[32,24,1]{2,1,0:T(8,128)(2,1)} %stack.66, bf16[32,24,1]{2,1,0:T(8,128)(2,1)} %stack.67, ...), dimensions={2} | concatenate | bytes 9464832 | tf_op jit(solution)/shard_map/concatenate | solution.py:428
  303.4 4.3 %collective-permute-done.22 = f32[256,768]{1,0:T(8,128)} collective-permute-done((f32[256,768]{1,0:T(8,128)}, f32[256,768]{1,0:T(8,128)}, u32[]{:S(2)}, u32[]{:S(2)}) %collective-permute-start.22) | collective-permute-done | bytes 786464 | tf_op jit(solution)/shard_map/ppermute | solution.py:16
  313.4 9.4 %collective-permute-done.34 = bf16[2,2,2,24,1024]{4,3,2,0,1:T(8,128)(2,1)S(1)} collective-permute-done((bf16[2,2,2,24,1024]{4,3,2,0,1:T(8,128)(2,1)S(1)}, bf16[2,2,2,24,1024]{4,3,2,0,1:T(8,128)(2,1)S(1)}, u32[]{:S(2)}, u32[]{:S(2)}) %collective-permute-start.34) | collective-permute-done | bytes 393248 | tf_op jit(solution)/shard_map/ppermute | solution.py:79
  324.7 7.2 %collective-permute-done.29 = bf16[2,2,2,24,1033]{4,3,2,1,0:T(8,128)(2,1)S(1)} collective-permute-done((bf16[2,2,2,24,1033]{4,3,2,1,0:T(8,128)(2,1)S(1)}, bf16[2,2,2,24,1033]{4,3,2,1,0:T(8,128)(2,1)S(1)}, u32[]{:S(2)}, u32[]{:S(2)}) %collective-permute-start.29) | collective-permute-done | bytes 396704 | tf_op jit(solution)/shard_map/ppermute | solution.py:79
  332.1 4.4 %collective-permute-done.25 = bf16[2,2,24,1024]{3,2,1,0:T(8,128)(2,1)S(1)} collective-permute-done((bf16[2,2,24,1024]{3,2,1,0:T(8,128)(2,1)S(1)}, bf16[2,2,24,1024]{3,2,1,0:T(8,128)(2,1)S(1)}, u32[]{:S(2)}, u32[]{:S(2)}) %collective-permute-start.25) | collective-permute-done | bytes 196640 | tf_op jit(solution)/shard_map/ppermute | solution.py:79
  336.8 7.4 %collective-permute-done.30 = bf16[2,2,24,1033]{3,2,1,0:T(8,128)(2,1)S(1)} collective-permute-done((bf16[2,2,24,1033]{3,2,1,0:T(8,128)(2,1)S(1)}, bf16[2,2,24,1033]{3,2,1,0:T(8,128)(2,1)S(1)}, u32[]{:S(2)}, u32[]{:S(2)}) %collective-permute-start.30) | collective-permute-done | bytes 198368 | tf_op jit(solution)/shard_map/ppermute | solution.py:79
  (367 shorter events, 164.1 us)
Async XLA Ops:
  7.2 117.6 %all-gather.2.cloned.1.call-start = ((), (), s32[]{:S(2)}) async-start(), calls=%async_computation.1 | async-start | bytes 5222400 | tf_op jit(solution)/shard_map/all_gather | solution.py:291
  9.6 13.2 %collective-permute-start.11 = (bf16[24,1152]{1,0:T(8,128)(2,1)S(1)}, bf16[24,1152]{1,0:T(8,128)(2,1)S(1)}, u32[]{:S(2)}, u32[]{:S(2)}) collective-permute-start(bf16[24,1152]{1,0:T(8,128)(2,1)S(1)} %fusion.79), channel_id=1, source_target_pairs={{0,1},{1,0},{2,3},{3,2},{4,5},{5,4},{6,7},{7,6},{8,9},{9,8},{10,11... | collective-permute-start | bytes 165896 | tf_op jit(solution)/shard_map/ppermute | solution.py:46
  29.3 20.5 %collective-permute-start.13 = (bf16[2,2,24,1152]{3,2,1,0:T(8,128)(2,1)S(1)}, bf16[2,2,24,1152]{3,2,1,0:T(8,128)(2,1)S(1)}, u32[]{:S(2)}, u32[]{:S(2)}) collective-permute-start(bf16[2,2,24,1152]{3,2,1,0:T(8,128)(2,1)S(1)} %broadcast_select_fusion.11), channel_id=1, source_target_pairs={{0,16},{1,17},{2,18},{3,19},{4,20},{5,21},{6,22},{7,23},{8,24},{9,... | collective-permute-start | bytes 663560 | tf_op jit(solution)/shard_map/ppermute | solution.py:46
  32.0 34.6 %collective-permute-start.9 = (bf16[2,2,2,24,1024]{4,3,2,0,1:T(8,128)(2,1)S(1)}, bf16[2,2,2,24,1024]{4,3,2,0,1:T(8,128)(2,1)S(1)}, u32[]{:S(2)}, u32[]{:S(2)}) collective-permute-start(bf16[2,2,2,24,1024]{4,3,2,0,1:T(8,128)(2,1)S(1)} %broadcast_select_fusion.7), channel_id=1, source_target_pairs={{0,16},{1,17},{2,18},{3,19},{4,20},{5,21},{6,22},{7,23},{8,24},{9,... | collective-permute-start | bytes 1179656 | tf_op jit(solution)/shard_map/ppermute | solution.py:46
  34.8 15.4 %collective-permute-start.4 = (bf16[2,2,2,24,1024]{4,3,2,0,1:T(8,128)(2,1)S(1)}, bf16[2,2,2,24,1024]{4,3,2,0,1:T(8,128)(2,1)S(1)}, u32[]{:S(2)}, u32[]{:S(2)}) collective-permute-start(bf16[2,2,2,24,1024]{4,3,2,0,1:T(8,128)(2,1)S(1)} %broadcast_select_fusion.9), channel_id=1, source_target_pairs={{0,4},{1,5},{2,6},{3,7},{4,0},{5,1},{6,2},{7,3},{8,12},{9,13},{10,... | collective-permute-start | bytes 1179656 | tf_op jit(solution)/shard_map/ppermute | solution.py:46
  50.0 16.4 %collective-permute-start.14 = (bf16[2,2,2,24,1152]{4,3,2,1,0:T(8,128)(2,1)S(1)}, bf16[2,2,2,24,1152]{4,3,2,1,0:T(8,128)(2,1)S(1)}, u32[]{:S(2)}, u32[]{:S(2)}) collective-permute-start(bf16[2,2,2,24,1152]{4,3,2,1,0:T(8,128)(2,1)S(1)} %broadcast_select_fusion.6), channel_id=1, source_target_pairs={{0,8},{1,9},{2,10},{3,11},{4,12},{5,13},{6,14},{7,15},{8,0},{9,1},... | collective-permute-start | bytes 1327112 | tf_op jit(solution)/shard_map/ppermute | solution.py:46
  50.3 17.8 %collective-permute-start.5 = (bf16[2,2,2,2,24,1024]{5,4,3,0,1,2:T(8,128)(2,1)S(1)}, bf16[2,2,2,2,24,1024]{5,4,3,0,1,2:T(8,128)(2,1)S(1)}, u32[]{:S(2)}, u32[]{:S(2)}) collective-permute-start(bf16[2,2,2,2,24,1024]{5,4,3,0,1,2:T(8,128)(2,1)S(1)} %broadcast_select_fusion.4), channel_id=1, source_target_pairs={{0,2},{1,3},{2,0},{3,1},{4,6},{5,7},{6,4},{7,5},{8,10},{9,11},{10,... | collective-permute-start | bytes 2359304 | tf_op jit(solution)/shard_map/ppermute | solution.py:46
  74.1 280.9 %reduce-scatter.2.cloned.1.call-start = ((), (), s32[]{:S(2)}) async-start(), calls=%async_computation.2 | async-start | bytes 5222400 | tf_op jit(solution)/shard_map/reduce_scatter | solution.py:383
  75.1 12.2 %collective-permute-start = (bf16[256,768]{1,0:T(8,128)(2,1)}, bf16[256,768]{1,0:T(8,128)(2,1)S(1)}, u32[]{:S(2)}, u32[]{:S(2)}) collective-permute-start(bf16[256,768]{1,0:T(8,128)(2,1)} %get-tuple-element.83), channel_id=1, source_target_pairs={{0,1},{1,0},{2,3},{3,2},{4,5},{5,4},{6,7},{7,6},{8,9},{9,8},{10,11... | collective-permute-start | bytes 1179656 | tf_op jit(solution)/shard_map/ppermute | solution.py:16
  77.2 39.0 %collective-permute-start.19 = (bf16[256,768]{1,0:T(8,128)(2,1)}, bf16[256,768]{1,0:T(8,128)(2,1)}, u32[]{:S(2)}, u32[]{:S(2)}) collective-permute-start(bf16[256,768]{1,0:T(8,128)(2,1)} %get-tuple-element.80), channel_id=1, source_target_pairs={{0,1},{1,0},{2,3},{3,2},{4,5},{5,4},{6,7},{7,6},{8,9},{9,8},{10,11... | collective-permute-start | bytes 1179656 | tf_op jit(solution)/shard_map/ppermute | solution.py:16
  116.1 18.1 %collective-permute-start.16 = (bf16[512,768]{1,0:T(8,128)(2,1)S(1)}, bf16[512,768]{1,0:T(8,128)(2,1)}, u32[]{:S(2)}, u32[]{:S(2)}) collective-permute-start(bf16[512,768]{1,0:T(8,128)(2,1)S(1)} %fusion.58), channel_id=1, source_target_pairs={{0,1},{1,0},{2,3},{3,2},{4,5},{5,4},{6,7},{7,6},{8,9},{9,8},{10,11... | collective-permute-start | bytes 2359304 | tf_op jit(solution)/shard_map/ppermute | solution.py:16
  146.6 17.1 %collective-permute-start.17 = (bf16[512,768]{1,0:T(8,128)(2,1)S(1)}, bf16[512,768]{1,0:T(8,128)(2,1)S(1)}, u32[]{:S(2)}, u32[]{:S(2)}) collective-permute-start(bf16[512,768]{1,0:T(8,128)(2,1)S(1)} %fusion.49), channel_id=1, source_target_pairs={{0,1},{1,0},{2,3},{3,2},{4,5},{5,4},{6,7},{7,6},{8,9},{9,8},{10,11... | collective-permute-start | bytes 2359304 | tf_op jit(solution)/shard_map/ppermute | solution.py:16
  176.9 20.6 %collective-permute-start.20 = (bf16[512,768]{1,0:T(8,128)(2,1)}, bf16[512,768]{1,0:T(8,128)(2,1)S(1)}, u32[]{:S(2)}, u32[]{:S(2)}) collective-permute-start(bf16[512,768]{1,0:T(8,128)(2,1)} %get-tuple-element.50), channel_id=1, source_target_pairs={{0,1},{1,0},{2,3},{3,2},{4,5},{5,4},{6,7},{7,6},{8,9},{9,8},{10,11... | collective-permute-start | bytes 2359304 | tf_op jit(solution)/shard_map/ppermute | solution.py:16
  179.5 94.1 %collective-permute-start.18 = (f32[256,768]{1,0:T(8,128)}, f32[256,768]{1,0:T(8,128)}, u32[]{:S(2)}, u32[]{:S(2)}) collective-permute-start(f32[256,768]{1,0:T(8,128)} %get-tuple-element.79), channel_id=1, source_target_pairs={{0,1},{1,0},{2,3},{3,2},{4,5},{5,4},{6,7},{7,6},{8,9},{9,8},{10,11... | collective-permute-start | bytes 2359304 | tf_op jit(solution)/shard_map/ppermute | solution.py:16
  202.5 24.9 %collective-permute-start.21 = (bf16[512,768]{1,0:T(8,128)(2,1)}, bf16[512,768]{1,0:T(8,128)(2,1)}, u32[]{:S(2)}, u32[]{:S(2)}) collective-permute-start(bf16[512,768]{1,0:T(8,128)(2,1)} %fusion.46), channel_id=1, source_target_pairs={{0,1},{1,0},{2,3},{3,2},{4,5},{5,4},{6,7},{7,6},{8,9},{9,8},{10,11... | collective-permute-start | bytes 2359304 | tf_op jit(solution)/shard_map/ppermute | solution.py:16
  273.6 26.6 %collective-permute-start.23 = (bf16[2,2,2,2,24,1024]{5,4,3,2,1,0:T(8,128)(2,1)}, bf16[2,2,2,2,24,1024]{5,4,3,2,1,0:T(8,128)(2,1)}, u32[]{:S(2)}, u32[]{:S(2)}) collective-permute-start(bf16[2,2,2,2,24,1024]{5,4,3,2,1,0:T(8,128)(2,1)} %dynamic-slice_bitcast_fusion.1), channel_id=1, source_target_pairs={{0,2},{1,3},{2,0},{3,1},{4,6},{5,7},{6,4},{7,5},{8,10},{9,11},{10,... | collective-permute-start | bytes 2359304 | tf_op jit(solution)/shard_map/ppermute | solution.py:79
  278.3 23.5 %collective-permute-start.33 = (bf16[2,2,2,2,24,1024]{5,4,3,1,2,0:T(8,128)(2,1)}, bf16[2,2,2,2,24,1024]{5,4,3,1,2,0:T(8,128)(2,1)}, u32[]{:S(2)}, u32[]{:S(2)}) collective-permute-start(bf16[2,2,2,2,24,1024]{5,4,3,1,2,0:T(8,128)(2,1)} %bitcast.171), channel_id=1, source_target_pairs={{0,2},{1,3},{2,0},{3,1},{4,6},{5,7},{6,4},{7,5},{8,10},{9,11},{10,... | collective-permute-start | bytes 2359304 | tf_op jit(solution)/shard_map/ppermute | solution.py:79
  287.9 19.8 %collective-permute-start.22 = (f32[256,768]{1,0:T(8,128)}, f32[256,768]{1,0:T(8,128)}, u32[]{:S(2)}, u32[]{:S(2)}) collective-permute-start(f32[256,768]{1,0:T(8,128)} %get-tuple-element.23), channel_id=1, source_target_pairs={{0,1},{1,0},{2,3},{3,2},{4,5},{5,4},{6,7},{7,6},{8,9},{9,8},{10,11... | collective-permute-start | bytes 2359304 | tf_op jit(solution)/shard_map/ppermute | solution.py:16
  301.7 11.5 %collective-permute-start.24 = (bf16[2,2,2,24,1024]{4,3,2,1,0:T(8,128)(2,1)S(1)}, bf16[2,2,2,24,1024]{4,3,2,1,0:T(8,128)(2,1)S(1)}, u32[]{:S(2)}, u32[]{:S(2)}) collective-permute-start(bf16[2,2,2,24,1024]{4,3,2,1,0:T(8,128)(2,1)S(1)} %fusion.70), channel_id=1, source_target_pairs={{0,4},{1,5},{2,6},{3,7},{4,0},{5,1},{6,2},{7,3},{8,12},{9,13},{10,... | collective-permute-start | bytes 1179656 | tf_op jit(solution)/shard_map/ppermute | solution.py:79
  303.3 19.5 %collective-permute-start.34 = (bf16[2,2,2,24,1024]{4,3,2,0,1:T(8,128)(2,1)S(1)}, bf16[2,2,2,24,1024]{4,3,2,0,1:T(8,128)(2,1)S(1)}, u32[]{:S(2)}, u32[]{:S(2)}) collective-permute-start(bf16[2,2,2,24,1024]{4,3,2,0,1:T(8,128)(2,1)S(1)} %fusion.71), channel_id=1, source_target_pairs={{0,16},{1,17},{2,18},{3,19},{4,20},{5,21},{6,22},{7,23},{8,24},{9,... | collective-permute-start | bytes 1179656 | tf_op jit(solution)/shard_map/ppermute | solution.py:79
  310.7 21.2 %collective-permute-start.29 = (bf16[2,2,2,24,1033]{4,3,2,1,0:T(8,128)(2,1)S(1)}, bf16[2,2,2,24,1033]{4,3,2,1,0:T(8,128)(2,1)S(1)}, u32[]{:S(2)}, u32[]{:S(2)}) collective-permute-start(bf16[2,2,2,24,1033]{4,3,2,1,0:T(8,128)(2,1)S(1)} %fusion.65), channel_id=1, source_target_pairs={{0,8},{1,9},{2,10},{3,11},{4,12},{5,13},{6,14},{7,15},{8,0},{9,1},... | collective-permute-start | bytes 1190024 | tf_op jit(solution)/shard_map/ppermute | solution.py:79
  313.3 23.2 %collective-permute-start.25 = (bf16[2,2,24,1024]{3,2,1,0:T(8,128)(2,1)S(1)}, bf16[2,2,24,1024]{3,2,1,0:T(8,128)(2,1)S(1)}, u32[]{:S(2)}, u32[]{:S(2)}) collective-permute-start(bf16[2,2,24,1024]{3,2,1,0:T(8,128)(2,1)S(1)} %fusion.73), channel_id=1, source_target_pairs={{0,8},{1,9},{2,10},{3,11},{4,12},{5,13},{6,14},{7,15},{8,0},{9,1},... | collective-permute-start | bytes 589832 | tf_op jit(solution)/shard_map/ppermute | solution.py:79
  323.0 13.7 %collective-permute-start.35 = (bf16[2,2,24,1024]{3,2,1,0:T(8,128)(2,1)S(1)}, bf16[2,2,24,1024]{3,2,1,0:T(8,128)(2,1)S(1)}, u32[]{:S(2)}, u32[]{:S(2)}) collective-permute-start(bf16[2,2,24,1024]{3,2,1,0:T(8,128)(2,1)S(1)} %fusion.74), channel_id=1, source_target_pairs={{0,4},{1,5},{2,6},{3,7},{4,0},{5,1},{6,2},{7,3},{8,12},{9,13},{10,... | collective-permute-start | bytes 589832 | tf_op jit(solution)/shard_map/ppermute | solution.py:79
  332.1 12.2 %collective-permute-start.30 = (bf16[2,2,24,1033]{3,2,1,0:T(8,128)(2,1)S(1)}, bf16[2,2,24,1033]{3,2,1,0:T(8,128)(2,1)S(1)}, u32[]{:S(2)}, u32[]{:S(2)}) collective-permute-start(bf16[2,2,24,1033]{3,2,1,0:T(8,128)(2,1)S(1)} %fusion.72), channel_id=1, source_target_pairs={{0,16},{1,17},{2,18},{3,19},{4,20},{5,21},{6,22},{7,23},{8,24},{9,... | collective-permute-start | bytes 595016 | tf_op jit(solution)/shard_map/ppermute | solution.py:79
  (90 other events, 729.3 us)
Sparse Core Ops, SparseCore 0:
  74.2 50.5 all-gather.1
  216.8 72.9 reduce-scatter.1

commit v4 on v3

--- a/solution.py
+++ b/solution.py
@@ -353,7 +353,6 @@
     outer_out = outer_sum + outer_offset
     res_two = norm_one + outer_out
     pack_out, ffn_pull = jax.vjp(layer_norm, res_two, ffn_scale, ffn_offset)
-    layer_out = from_pack(pack_out)
     grad_two, ffn_gsum, ffn_ssum = ffn_pull(pack_cot.astype(jnp.float32))
     grad_outer = grad_two.astype(jnp.bfloat16)
     outer_bsum = jnp.sum(grad_outer.astype(jnp.float32), axis=0)
@@ -386,6 +385,8 @@
     outer_wgrad = ffn_mine[:, ffn_cols : 2 * ffn_cols].T
     inner_bgrad = ffn_mine[:, 2 * ffn_cols :].reshape(-1)[:bias_n]
 
+    pack_out, grad_part = lax.optimization_barrier((pack_out, grad_part))
+    layer_out = from_pack(pack_out)
     grad_norm = grad_two + grad_part
     grad_one, attn_gsum, attn_ssum = norm_pull(grad_norm)
     grad_attn = grad_one.astype(jnp.bfloat16)

time: 372 us -> 370 us (level)
  waiting for transfers between devices: 121 us -> 109 us
  matrix products: 86.8 us -> 92.3 us
    ppermute x15, waiting for transfers between devices: 35.4 us -> 25.5 us  [halving_scatter(): lax.ppermute(theirs.astype(jnp.bfloat16), ALL, [(i, i ^ 1 << b) for i in...]
  transfers between devices with their start and end apart: 40 -> 40, of which waited for: 22 -> 21; matrix products, arithmetic and copies ran while one was open for 43% -> 43% of each run, Pallas kernels for 0% -> 0%
where the time goes in v4:
time: 370 us; the launch traced here: 365 us
  waiting for transfers between devices  109 us (29%)
  matrix products  92.3 us (25%)
  other arithmetic  55.9 us (15%)
  local copies, waits for them, and re-layouts  55.6 us (15%)
  starting transfers between devices  36 us (10%)
  between operations  15.7 us (4%)
    ppermute x8, waiting for transfers between devices, swapped(): lax.ppermute(shard, axis, [(i, i ^ 1 << bit) for i in range(lax.axis_size...  42.4 us
    ppermute x15, waiting for transfers between devices, doubling_gather(): other = lax.ppermute(cur, ALL, [(i, i ^ 1 << b) for i in range(total)])  36.3 us
    ppermute x15, waiting for transfers between devices, halving_scatter(): lax.ppermute(theirs.astype(jnp.bfloat16), ALL, [(i, i ^ 1 << b) for i in...  25.5 us
    dot_general x2, matrix products, ffn_forward(): jnp.dot(rows, inner_cols, preferred_element_type=jnp.float32) + inner_offset  21 us
    ppermute x15, starting transfers between devices, doubling_gather(): other = lax.ppermute(cur, ALL, [(i, i ^ 1 << b) for i in range(total)])  18.2 us
    dot_general x6, matrix products, contract_rows(): lax.dot_general(left_op, right_op, (((0,), (0,)), ((), ())), preferred_el...  15.3 us
    dot_general x6, matrix products, contract_cols(): lax.dot_general(left_op, right_op, (((1,), (1,)), ((), ())), preferred_el...  14 us
    dot_general x1, matrix products, attend_back(): jnp.einsum('pqhd,pkhd->phqk', grad_mixed, value_low, preferred_element_ty...  10 us
  transfers between devices with their start and end apart: 40, of which 21 were waited for; matrix products, arithmetic and copies ran while one was open for 43% of the time, Pallas kernels for 0%

profile of v4, /device:TPU:0, one launch (start us, length us, event | category | flops | bytes accessed | tf_op | source)
XLA Modules:
  0.0 365.0 jit_solution(16459898749583696382)
XLA Ops:
  36.0 13.8 %collective-permute-done.13 = bf16[2,2,24,1152]{3,2,1,0:T(8,128)(2,1)S(1)} collective-permute-done((bf16[2,2,24,1152]{3,2,1,0:T(8,128)(2,1)S(1)}, bf16[2,2,24,1152]{3,2,1,0:T(8,128)(2,1)S(1)}, u32[]{:S(2)}, u32[]{:S(2)}) %collective-permute-start.13) | collective-permute-done | bytes 221216 | tf_op jit(solution)/shard_map/ppermute | solution.py:46
  50.4 16.0 %collective-permute-done.14 = bf16[2,2,2,24,1152]{4,3,2,1,0:T(8,128)(2,1)S(1)} collective-permute-done((bf16[2,2,2,24,1152]{4,3,2,1,0:T(8,128)(2,1)S(1)}, bf16[2,2,2,24,1152]{4,3,2,1,0:T(8,128)(2,1)S(1)}, u32[]{:S(2)}, u32[]{:S(2)}) %collective-permute-start.14) | collective-permute-done | bytes 442400 | tf_op jit(solution)/shard_map/ppermute | solution.py:46
  80.9 6.6 %collective-permute-done = bf16[256,768]{1,0:T(8,128)(2,1)S(1)} collective-permute-done((bf16[256,768]{1,0:T(8,128)(2,1)}, bf16[256,768]{1,0:T(8,128)(2,1)S(1)}, u32[]{:S(2)}, u32[]{:S(2)}) %collective-permute-start) | collective-permute-done | bytes 393248 | tf_op jit(solution)/shard_map/ppermute | solution.py:16
  110.7 4.0 %fusion.57 = bf16[12,64,512]{2,1,0:T(8,128)(2,1)S(1)} fusion(bf16[512,12,64]{0,2,1:T(8,128)(2,1)S(1)} %bitcast.185, f32[12,512]{1,0:T(8,128)S(1)} %fusion, f32[12,512]{1,0:T(8,128)S(1)} %get-tuple-element.107, f32[12,512,512]{1,2,0:T(8,128)S(1)} %get-tuple-element.108, pred[512,512]{0,1:T(8,128)(4,1)S(1)} %copy-done.13), kind=kOutput, calls=%fused_computation.111 | convolution fusion | flops 418775040 | bytes 14467072 | tf_op jit(solution)/shard_map/phqk,pkhd->pqhd/dot_general | solution.py:188
  119.8 5.2 %all-gather.2.cloned.1.call-done = bf16[768,3074]{1,0:T(8,128)(2,1)} async-done(((bf16[48,3074]{1,0:T(8,128)(2,1)}), bf16[768,3074]{1,0:T(8,128)(2,1)}) %all-gather.2.cloned.1.call-update) | async-done | bytes 4721680 | tf_op jit(solution)/shard_map/all_gather | solution.py:291
  126.1 8.4 %collective-permute-done.16 = bf16[512,768]{1,0:T(8,128)(2,1)} collective-permute-done((bf16[512,768]{1,0:T(8,128)(2,1)S(1)}, bf16[512,768]{1,0:T(8,128)(2,1)}, u32[]{:S(2)}, u32[]{:S(2)}) %collective-permute-start.16) | collective-permute-done | bytes 786464 | tf_op jit(solution)/shard_map/ppermute | solution.py:16
  134.5 10.9 %multiply_convert_fusion.1 = (bf16[512,1536]{1,0:T(8,128)(2,1)S(1)}, f32[512,1536]{1,0:T(8,128)}, f32[512,1536]{1,0:T(8,128)}) fusion(f32[1536]{0:T(1024)S(1)} %reshape.633, bf16[512,768]{1,0:T(8,128)(2,1)} %collective-permute-done.16, bf16[768,3074]{1,0:T(8,128)(2,1)} %all-gather.2.cloned.1.call-done), kind=kOutput, calls=%fused_computation.28 | convolution fusion | flops 1259864064 | bytes 11016192 | tf_op jit(solution)/shard_map/dot_general | solution.py:217
  147.6 10.1 %multiply_convert_fusion.2 = (bf16[512,1536]{1,0:T(8,128)(2,1)S(1)}, f32[512,1536]{1,0:T(8,128)}, f32[512,1536]{1,0:T(8,128)}) fusion(f32[1536]{0:T(1024)S(1)} %reshape.633, bf16[512,768]{1,0:T(8,128)(2,1)S(1)} %fusion.58, bf16[768,3074]{1,0:T(8,128)(2,1)S(1)} %copy-done.60), kind=kOutput, calls=%fused_computation.41 | convolution fusion | flops 1259864064 | bytes 11018240 | tf_op jit(solution)/shard_map/dot_general | solution.py:217
  157.7 6.3 %collective-permute-done.17 = bf16[512,768]{1,0:T(8,128)(2,1)S(1)} collective-permute-done((bf16[512,768]{1,0:T(8,128)(2,1)S(1)}, bf16[512,768]{1,0:T(8,128)(2,1)S(1)}, u32[]{:S(2)}, u32[]{:S(2)}) %collective-permute-start.17) | collective-permute-done | bytes 786464 | tf_op jit(solution)/shard_map/ppermute | solution.py:16
  170.4 3.5 fusion.96
  177.4 6.1 %convert_reduce_fusion.1 = (f32[1536]{0:T(1024)S(1)}, bf16[512,1536]{1,0:T(8,128)(2,1)S(1)}) fusion(f32[512,1536]{1,0:T(8,128)} %get-tuple-element.63, f32[512,1536]{1,0:T(8,128)} %get-tuple-element.112, bf16[512,768]{1,0:T(8,128)(2,1)} %get-tuple-element.54, bf16[768,3074]{1,0:T(8,128)(2,1)} %all-gather.2.cloned.1.call-done), kind=kOutput, calls=%fused_computation.25 | convolution fusion | flops 1220540928 | bytes 11016192 | tf_op jit(solution)/shard_map/dot_general | solution.py:224
  186.7 6.0 %collective-permute-done.19 = bf16[512,768]{1,0:T(8,128)(2,1)S(1)} collective-permute-done((bf16[512,768]{1,0:T(8,128)(2,1)}, bf16[512,768]{1,0:T(8,128)(2,1)S(1)}, u32[]{:S(2)}, u32[]{:S(2)}) %collective-permute-start.19) | collective-permute-done | bytes 786464 | tf_op jit(solution)/shard_map/ppermute | solution.py:16
  192.8 3.9 %convert_reduce_fusion = (f32[1536]{0:T(1024)S(1)}, bf16[512,1536]{1,0:T(8,128)(2,1)S(1)}) fusion(f32[512,1536]{1,0:T(8,128)S(1)} %copy-done.63, f32[512,1536]{1,0:T(8,128)S(1)} %copy-done.64, bf16[512,768]{1,0:T(8,128)(2,1)S(1)} %collective-permute-done.19, bf16[768,3074]{1,0:T(8,128)(2,1)} %all-gather.2.cloned.1.call-done), kind=kOutput, calls=%fused_computation.24 | convolution fusion | flops 1220540928 | bytes 11016192 | tf_op jit(solution)/shard_map/dot_general | solution.py:224
  196.7 4.0 %fusion.48 = bf16[512,768]{1,0:T(8,128)(2,1)} fusion(bf16[512,1536]{1,0:T(8,128)(2,1)S(1)} %get-tuple-element.120, bf16[768,3074]{1,0:T(8,128)(2,1)} %all-gather.2.cloned.1.call-done), kind=kOutput, calls=%fused_computation.108 | convolution fusion | flops 1208352768 | bytes 4718592 | tf_op jit(solution)/shard_map/dot_general | solution.py:169
  202.4 4.1 %add_convert_fusion.1 = bf16[768,1536]{1,0:T(8,128)(2,1)} fusion(f32[768,1536]{1,0:T(8,128)S(1)} %fusion.104, bf16[512,768]{1,0:T(8,128)(2,1)} %collective-permute-done.16, bf16[512,1536]{1,0:T(8,128)(2,1)S(1)} %get-tuple-element.120), kind=kOutput, calls=%fused_computation.18 | convolution fusion | flops 1210318848 | bytes 9437184 | tf_op jit(solution)/shard_map/dot_general | solution.py:163
  210.1 5.4 %pad_maximum_fusion.1 = bf16[768,3074]{1,0:T(8,128)(2,1)} fusion(bf16[768,2]{1,0:T(8,128)(2,1)S(1)} %add.340, bf16[768,1536]{1,0:T(8,128)(2,1)} %add_convert_fusion, bf16[768,1536]{1,0:T(8,128)(2,1)} %add_convert_fusion.1), kind=kLoop, calls=%fused_computation.13 | loop fusion | flops 14164992 | bytes 9443328 | tf_op jit(solution)/shard_map/concatenate | solution.py:381
  217.0 3.9 %convert_add_fusion.3 = f32[512,768]{1,0:T(8,128)S(1)} fusion(bf16[512,768]{1,0:T(8,128)(2,1)} %collective-permute-done.20, bf16[512,1536]{1,0:T(8,128)(2,1)} %copy-done.32, bf16[768,3074]{1,0:T(8,128)(2,1)} %all-gather.2.cloned.1.call-done), kind=kOutput, calls=%fused_computation.81 | convolution fusion | flops 1208745984 | bytes 6291456 | tf_op jit(solution)/shard_map/dot_general | solution.py:169
  226.2 9.7 %fusion.54 = bf16[12,64,512]{2,1,0:T(8,128)(2,1)} fusion(bf16[512,12,64]{0,2,1:T(8,128)(2,1)} %bitcast.187, f32[12,512]{1,0:T(8,128)S(1)} %copy-done.47, f32[12,512,512]{1,2,0:T(8,128)} %copy-done.2, pred[512,512]{0,1:T(8,128)(4,1)S(1)} %copy-done.14), kind=kOutput, calls=%fused_computation.110 | convolution fusion | flops 415629312 | bytes 14442496 | tf_op jit(solution)/shard_map/phqk,pqhd->pkhd/dot_general | solution.py:196
  235.9 10.0 %multiply_reduce_fusion = (f32[12,512]{1,0:T(8,128)S(1)}, f32[12,512,512]{1,2,0:T(8,128)}) fusion(f32[12,512]{1,0:T(8,128)S(1)} %copy-done.47, f32[12,512,512]{1,2,0:T(8,128)} %copy-done.2, pred[512,512]{0,1:T(8,128)(4,1)S(1)} %copy-done.14, bf16[512,12,64]{0,2,1:T(8,128)(2,1)S(1)} %bitcast.188, bf16[512,12,64]{0,2,1:T(8,128)(2,1)S(1)} %bitcast.186), kind=kOutput, calls=%fused_computation.1 | convolution fusion | flops 418375680 | bytes 27049984 | tf_op jit(solution)/shard_map/pqhd,pkhd->phqk/dot_general | solution.py:202
  246.0 7.1 %multiply_convert_fusion = bf16[12,512,512]{1,2,0:T(8,128)(2,1)S(1)} fusion(f32[12,512,512]{1,2,0:T(8,128)} %get-tuple-element.116, f32[12,512]{1,0:T(8,128)S(1)} %get-tuple-element.115, f32[12,512]{1,0:T(8,128)S(1)} %copy-done.47, f32[12,512,512]{1,2,0:T(8,128)S(1)} %bitcast.173, pred[512,512]{0,1:T(8,128)(4,1)S(1)} %copy-done.14), kind=kLoop, calls=%fused_computation | loop fusion | flops 18874368 | bytes 31768576 | tf_op jit(solution)/shard_map/convert_element_type | solution.py:206
  282.9 8.8 %concatenate.125 = bf16[32,24,3081]{2,1,0:T(8,128)(2,1)} concatenate(bf16[32,24,2304]{2,1,0:T(8,128)(2,1)S(1)} %bitcast.175, bf16[32,24,3]{2,1,0:T(8,128)(2,1)} %bitcast.199, bf16[32,24,768]{2,1,0:T(8,128)(2,1)} %convolution_convert_fusion.1, bf16[32,24,1]{2,1,0:T(8,128)(2,1)} %stack.65, bf16[32,24,1]{2,1,0:T(8,128)(2,1)} %stack.66, bf16[32,24,1]{2,1,0:T(8,128)(2,1)} %stack.67, ...), dimensions={2} | concatenate | bytes 9464832 | tf_op jit(solution)/shard_map/concatenate | solution.py:429
  300.2 13.2 %collective-permute-done.22 = f32[256,768]{1,0:T(8,128)} collective-permute-done((f32[256,768]{1,0:T(8,128)}, f32[256,768]{1,0:T(8,128)}, u32[]{:S(2)}, u32[]{:S(2)}) %collective-permute-start.22) | collective-permute-done | bytes 786464 | tf_op jit(solution)/shard_map/ppermute | solution.py:16
  318.9 10.6 %collective-permute-done.29 = bf16[2,2,2,24,1033]{4,3,2,1,0:T(8,128)(2,1)S(1)} collective-permute-done((bf16[2,2,2,24,1033]{4,3,2,1,0:T(8,128)(2,1)S(1)}, bf16[2,2,2,24,1033]{4,3,2,1,0:T(8,128)(2,1)S(1)}, u32[]{:S(2)}, u32[]{:S(2)}) %collective-permute-start.29) | collective-permute-done | bytes 396704 | tf_op jit(solution)/shard_map/ppermute | solution.py:79
  335.7 6.7 %collective-permute-done.30 = bf16[2,2,24,1033]{3,2,1,0:T(8,128)(2,1)S(1)} collective-permute-done((bf16[2,2,24,1033]{3,2,1,0:T(8,128)(2,1)S(1)}, bf16[2,2,24,1033]{3,2,1,0:T(8,128)(2,1)S(1)}, u32[]{:S(2)}, u32[]{:S(2)}) %collective-permute-start.30) | collective-permute-done | bytes 198368 | tf_op jit(solution)/shard_map/ppermute | solution.py:79
  (359 shorter events, 164.9 us)
Async XLA Ops:
  7.2 117.7 %all-gather.2.cloned.1.call-start = ((), (), s32[]{:S(2)}) async-start(), calls=%async_computation.1 | async-start | bytes 5222400 | tf_op jit(solution)/shard_map/all_gather | solution.py:291
  9.6 13.2 %collective-permute-start.11 = (bf16[24,1152]{1,0:T(8,128)(2,1)S(1)}, bf16[24,1152]{1,0:T(8,128)(2,1)S(1)}, u32[]{:S(2)}, u32[]{:S(2)}) collective-permute-start(bf16[24,1152]{1,0:T(8,128)(2,1)S(1)} %fusion.79), channel_id=1, source_target_pairs={{0,1},{1,0},{2,3},{3,2},{4,5},{5,4},{6,7},{7,6},{8,9},{9,8},{10,11... | collective-permute-start | bytes 165896 | tf_op jit(solution)/shard_map/ppermute | solution.py:46
  29.3 20.5 %collective-permute-start.13 = (bf16[2,2,24,1152]{3,2,1,0:T(8,128)(2,1)S(1)}, bf16[2,2,24,1152]{3,2,1,0:T(8,128)(2,1)S(1)}, u32[]{:S(2)}, u32[]{:S(2)}) collective-permute-start(bf16[2,2,24,1152]{3,2,1,0:T(8,128)(2,1)S(1)} %broadcast_select_fusion.11), channel_id=1, source_target_pairs={{0,16},{1,17},{2,18},{3,19},{4,20},{5,21},{6,22},{7,23},{8,24},{9,... | collective-permute-start | bytes 663560 | tf_op jit(solution)/shard_map/ppermute | solution.py:46
  32.0 34.6 %collective-permute-start.9 = (bf16[2,2,2,24,1024]{4,3,2,0,1:T(8,128)(2,1)S(1)}, bf16[2,2,2,24,1024]{4,3,2,0,1:T(8,128)(2,1)S(1)}, u32[]{:S(2)}, u32[]{:S(2)}) collective-permute-start(bf16[2,2,2,24,1024]{4,3,2,0,1:T(8,128)(2,1)S(1)} %broadcast_select_fusion.7), channel_id=1, source_target_pairs={{0,16},{1,17},{2,18},{3,19},{4,20},{5,21},{6,22},{7,23},{8,24},{9,... | collective-permute-start | bytes 1179656 | tf_op jit(solution)/shard_map/ppermute | solution.py:46
  34.8 15.4 %collective-permute-start.4 = (bf16[2,2,2,24,1024]{4,3,2,0,1:T(8,128)(2,1)S(1)}, bf16[2,2,2,24,1024]{4,3,2,0,1:T(8,128)(2,1)S(1)}, u32[]{:S(2)}, u32[]{:S(2)}) collective-permute-start(bf16[2,2,2,24,1024]{4,3,2,0,1:T(8,128)(2,1)S(1)} %broadcast_select_fusion.9), channel_id=1, source_target_pairs={{0,4},{1,5},{2,6},{3,7},{4,0},{5,1},{6,2},{7,3},{8,12},{9,13},{10,... | collective-permute-start | bytes 1179656 | tf_op jit(solution)/shard_map/ppermute | solution.py:46
  50.0 16.4 %collective-permute-start.14 = (bf16[2,2,2,24,1152]{4,3,2,1,0:T(8,128)(2,1)S(1)}, bf16[2,2,2,24,1152]{4,3,2,1,0:T(8,128)(2,1)S(1)}, u32[]{:S(2)}, u32[]{:S(2)}) collective-permute-start(bf16[2,2,2,24,1152]{4,3,2,1,0:T(8,128)(2,1)S(1)} %broadcast_select_fusion.6), channel_id=1, source_target_pairs={{0,8},{1,9},{2,10},{3,11},{4,12},{5,13},{6,14},{7,15},{8,0},{9,1},... | collective-permute-start | bytes 1327112 | tf_op jit(solution)/shard_map/ppermute | solution.py:46
  50.3 17.8 %collective-permute-start.5 = (bf16[2,2,2,2,24,1024]{5,4,3,0,1,2:T(8,128)(2,1)S(1)}, bf16[2,2,2,2,24,1024]{5,4,3,0,1,2:T(8,128)(2,1)S(1)}, u32[]{:S(2)}, u32[]{:S(2)}) collective-permute-start(bf16[2,2,2,2,24,1024]{5,4,3,0,1,2:T(8,128)(2,1)S(1)} %broadcast_select_fusion.4), channel_id=1, source_target_pairs={{0,2},{1,3},{2,0},{3,1},{4,6},{5,7},{6,4},{7,5},{8,10},{9,11},{10,... | collective-permute-start | bytes 2359304 | tf_op jit(solution)/shard_map/ppermute | solution.py:46
  74.1 279.1 %reduce-scatter.2.cloned.1.call-start = ((), (), s32[]{:S(2)}) async-start(), calls=%async_computation.2 | async-start | bytes 5222400 | tf_op jit(solution)/shard_map/reduce_scatter | solution.py:382
  77.3 39.2 %collective-permute-start.18 = (bf16[256,768]{1,0:T(8,128)(2,1)}, bf16[256,768]{1,0:T(8,128)(2,1)}, u32[]{:S(2)}, u32[]{:S(2)}) collective-permute-start(bf16[256,768]{1,0:T(8,128)(2,1)} %get-tuple-element.85), channel_id=1, source_target_pairs={{0,1},{1,0},{2,3},{3,2},{4,5},{5,4},{6,7},{7,6},{8,9},{9,8},{10,11... | collective-permute-start | bytes 1179656 | tf_op jit(solution)/shard_map/ppermute | solution.py:16
  116.4 18.1 %collective-permute-start.16 = (bf16[512,768]{1,0:T(8,128)(2,1)S(1)}, bf16[512,768]{1,0:T(8,128)(2,1)}, u32[]{:S(2)}, u32[]{:S(2)}) collective-permute-start(bf16[512,768]{1,0:T(8,128)(2,1)S(1)} %fusion.58), channel_id=1, source_target_pairs={{0,1},{1,0},{2,3},{3,2},{4,5},{5,4},{6,7},{7,6},{8,9},{9,8},{10,11... | collective-permute-start | bytes 2359304 | tf_op jit(solution)/shard_map/ppermute | solution.py:16
  146.9 17.1 %collective-permute-start.17 = (bf16[512,768]{1,0:T(8,128)(2,1)S(1)}, bf16[512,768]{1,0:T(8,128)(2,1)S(1)}, u32[]{:S(2)}, u32[]{:S(2)}) collective-permute-start(bf16[512,768]{1,0:T(8,128)(2,1)S(1)} %fusion.51), channel_id=1, source_target_pairs={{0,1},{1,0},{2,3},{3,2},{4,5},{5,4},{6,7},{7,6},{8,9},{9,8},{10,11... | collective-permute-start | bytes 2359304 | tf_op jit(solution)/shard_map/ppermute | solution.py:16
  176.1 16.6 %collective-permute-start.19 = (bf16[512,768]{1,0:T(8,128)(2,1)}, bf16[512,768]{1,0:T(8,128)(2,1)S(1)}, u32[]{:S(2)}, u32[]{:S(2)}) collective-permute-start(bf16[512,768]{1,0:T(8,128)(2,1)} %get-tuple-element.54), channel_id=1, source_target_pairs={{0,1},{1,0},{2,3},{3,2},{4,5},{5,4},{6,7},{7,6},{8,9},{9,8},{10,11... | collective-permute-start | bytes 2359304 | tf_op jit(solution)/shard_map/ppermute | solution.py:16
  200.7 16.3 %collective-permute-start.20 = (bf16[512,768]{1,0:T(8,128)(2,1)}, bf16[512,768]{1,0:T(8,128)(2,1)}, u32[]{:S(2)}, u32[]{:S(2)}) collective-permute-start(bf16[512,768]{1,0:T(8,128)(2,1)} %fusion.48), channel_id=1, source_target_pairs={{0,1},{1,0},{2,3},{3,2},{4,5},{5,4},{6,7},{7,6},{8,9},{9,8},{10,11... | collective-permute-start | bytes 2359304 | tf_op jit(solution)/shard_map/ppermute | solution.py:16
  265.1 28.6 %collective-permute-start.23 = (bf16[2,2,2,2,24,1024]{5,4,3,2,1,0:T(8,128)(2,1)}, bf16[2,2,2,2,24,1024]{5,4,3,2,1,0:T(8,128)(2,1)}, u32[]{:S(2)}, u32[]{:S(2)}) collective-permute-start(bf16[2,2,2,2,24,1024]{5,4,3,2,1,0:T(8,128)(2,1)} %dynamic-slice_bitcast_fusion.1), channel_id=1, source_target_pairs={{0,2},{1,3},{2,0},{3,1},{4,6},{5,7},{6,4},{7,5},{8,10},{9,11},{10,... | collective-permute-start | bytes 2359304 | tf_op jit(solution)/shard_map/ppermute | solution.py:79
  271.7 23.6 %collective-permute-start.33 = (bf16[2,2,2,2,24,1024]{5,4,3,1,2,0:T(8,128)(2,1)}, bf16[2,2,2,2,24,1024]{5,4,3,1,2,0:T(8,128)(2,1)}, u32[]{:S(2)}, u32[]{:S(2)}) collective-permute-start(bf16[2,2,2,2,24,1024]{5,4,3,1,2,0:T(8,128)(2,1)} %bitcast.171), channel_id=1, source_target_pairs={{0,2},{1,3},{2,0},{3,1},{4,6},{5,7},{6,4},{7,5},{8,10},{9,11},{10,... | collective-permute-start | bytes 2359304 | tf_op jit(solution)/shard_map/ppermute | solution.py:79
  276.7 20.7 %collective-permute-start.21 = (f32[256,768]{1,0:T(8,128)}, f32[256,768]{1,0:T(8,128)}, u32[]{:S(2)}, u32[]{:S(2)}) collective-permute-start(f32[256,768]{1,0:T(8,128)} %get-tuple-element.84), channel_id=1, source_target_pairs={{0,1},{1,0},{2,3},{3,2},{4,5},{5,4},{6,7},{7,6},{8,9},{9,8},{10,11... | collective-permute-start | bytes 2359304 | tf_op jit(solution)/shard_map/ppermute | solution.py:16
  282.7 30.7 %collective-permute-start.22 = (f32[256,768]{1,0:T(8,128)}, f32[256,768]{1,0:T(8,128)}, u32[]{:S(2)}, u32[]{:S(2)}) collective-permute-start(f32[256,768]{1,0:T(8,128)} %get-tuple-element.27), channel_id=1, source_target_pairs={{0,1},{1,0},{2,3},{3,2},{4,5},{5,4},{6,7},{7,6},{8,9},{9,8},{10,11... | collective-permute-start | bytes 2359304 | tf_op jit(solution)/shard_map/ppermute | solution.py:16
  293.6 22.5 %collective-permute-start.28 = (bf16[2,2,2,2,24,1033]{5,4,3,2,1,0:T(8,128)(2,1)S(1)}, bf16[2,2,2,2,24,1033]{5,4,3,2,1,0:T(8,128)(2,1)S(1)}, u32[]{:S(2)}, u32[]{:S(2)}) collective-permute-start(bf16[2,2,2,2,24,1033]{5,4,3,2,1,0:T(8,128)(2,1)S(1)} %dynamic-slice_bitcast_fusion), channel_id=1, source_target_pairs={{0,2},{1,3},{2,0},{3,1},{4,6},{5,7},{6,4},{7,5},{8,10},{9,11},{10,... | collective-permute-start | bytes 2380040 | tf_op jit(solution)/shard_map/ppermute | solution.py:79
  295.2 21.2 %collective-permute-start.24 = (bf16[2,2,2,24,1024]{4,3,2,1,0:T(8,128)(2,1)S(1)}, bf16[2,2,2,24,1024]{4,3,2,1,0:T(8,128)(2,1)S(1)}, u32[]{:S(2)}, u32[]{:S(2)}) collective-permute-start(bf16[2,2,2,24,1024]{4,3,2,1,0:T(8,128)(2,1)S(1)} %fusion.70), channel_id=1, source_target_pairs={{0,4},{1,5},{2,6},{3,7},{4,0},{5,1},{6,2},{7,3},{8,12},{9,13},{10,... | collective-permute-start | bytes 1179656 | tf_op jit(solution)/shard_map/ppermute | solution.py:79
  296.9 21.8 %collective-permute-start.34 = (bf16[2,2,2,24,1024]{4,3,2,0,1:T(8,128)(2,1)S(1)}, bf16[2,2,2,24,1024]{4,3,2,0,1:T(8,128)(2,1)S(1)}, u32[]{:S(2)}, u32[]{:S(2)}) collective-permute-start(bf16[2,2,2,24,1024]{4,3,2,0,1:T(8,128)(2,1)S(1)} %fusion.71), channel_id=1, source_target_pairs={{0,16},{1,17},{2,18},{3,19},{4,20},{5,21},{6,22},{7,23},{8,24},{9,... | collective-permute-start | bytes 1179656 | tf_op jit(solution)/shard_map/ppermute | solution.py:79
  316.4 13.1 %collective-permute-start.29 = (bf16[2,2,2,24,1033]{4,3,2,1,0:T(8,128)(2,1)S(1)}, bf16[2,2,2,24,1033]{4,3,2,1,0:T(8,128)(2,1)S(1)}, u32[]{:S(2)}, u32[]{:S(2)}) collective-permute-start(bf16[2,2,2,24,1033]{4,3,2,1,0:T(8,128)(2,1)S(1)} %fusion.65), channel_id=1, source_target_pairs={{0,8},{1,9},{2,10},{3,11},{4,12},{5,13},{6,14},{7,15},{8,0},{9,1},... | collective-permute-start | bytes 1190024 | tf_op jit(solution)/shard_map/ppermute | solution.py:79
  316.6 16.3 %collective-permute-start.25 = (bf16[2,2,24,1024]{3,2,1,0:T(8,128)(2,1)S(1)}, bf16[2,2,24,1024]{3,2,1,0:T(8,128)(2,1)S(1)}, u32[]{:S(2)}, u32[]{:S(2)}) collective-permute-start(bf16[2,2,24,1024]{3,2,1,0:T(8,128)(2,1)S(1)} %fusion.73), channel_id=1, source_target_pairs={{0,8},{1,9},{2,10},{3,11},{4,12},{5,13},{6,14},{7,15},{8,0},{9,1},... | collective-permute-start | bytes 589832 | tf_op jit(solution)/shard_map/ppermute | solution.py:79
  318.8 14.3 %collective-permute-start.35 = (bf16[2,2,24,1024]{3,2,1,0:T(8,128)(2,1)S(1)}, bf16[2,2,24,1024]{3,2,1,0:T(8,128)(2,1)S(1)}, u32[]{:S(2)}, u32[]{:S(2)}) collective-permute-start(bf16[2,2,24,1024]{3,2,1,0:T(8,128)(2,1)S(1)} %fusion.74), channel_id=1, source_target_pairs={{0,4},{1,5},{2,6},{3,7},{4,0},{5,1},{6,2},{7,3},{8,12},{9,13},{10,... | collective-permute-start | bytes 589832 | tf_op jit(solution)/shard_map/ppermute | solution.py:79
  329.6 12.9 %collective-permute-start.30 = (bf16[2,2,24,1033]{3,2,1,0:T(8,128)(2,1)S(1)}, bf16[2,2,24,1033]{3,2,1,0:T(8,128)(2,1)S(1)}, u32[]{:S(2)}, u32[]{:S(2)}) collective-permute-start(bf16[2,2,24,1033]{3,2,1,0:T(8,128)(2,1)S(1)} %fusion.72), channel_id=1, source_target_pairs={{0,16},{1,17},{2,18},{3,19},{4,20},{5,21},{6,22},{7,23},{8,24},{9,... | collective-permute-start | bytes 595016 | tf_op jit(solution)/shard_map/ppermute | solution.py:79
  (86 other events, 637.9 us)
Sparse Core Ops, SparseCore 0:
  74.3 50.6 all-gather.1
  215.6 72.6 reduce-scatter.1

commit v5 on v4

--- a/solution.py
+++ b/solution.py
@@ -100,15 +100,6 @@
     return jnp.concatenate(pieces, axis=-1)
 
 
-def narrow_gather(rows):
-    n = lax.axis_size("narrow")
-    if n != 2:
-        return lax.all_gather(rows, "narrow", axis=0, tiled=True)
-    other = swapped(rows, "narrow", 0)
-    first = lax.axis_index("narrow") == 0
-    return jnp.where(first, jnp.concatenate([rows, other]), jnp.concatenate([other, rows]))
-
-
 def narrow_scatter_sum(part):
     n = lax.axis_size("narrow")
     if n != 2:
@@ -226,7 +217,7 @@
     return grad_inner, contract_cols(grad_inner, inner_cols)
 
 
-def local(
+def local_body(
     layer_in,
     doc_ids,
     query_weight,
@@ -472,8 +463,12 @@
 
 
 def solution(mesh):
+    return shard_solution(mesh)
+
+
+def shard_solution(mesh):
     return jax.shard_map(
-        local,
+        local_body,
         mesh=mesh,
         in_specs=(
             P(("wide", "narrow"), None),

time: 370 us -> 370 us (level)
  no operation moved by 1% of the time
where the time goes in v5:
time: 370 us; the launch traced here: 365 us
  waiting for transfers between devices  109 us (29%)
  matrix products  92.3 us (25%)
  other arithmetic  55.9 us (15%)
  local copies, waits for them, and re-layouts  55.6 us (15%)
  starting transfers between devices  36 us (10%)
  between operations  15.7 us (4%)
    ppermute x8, waiting for transfers between devices, swapped(): lax.ppermute(shard, axis, [(i, i ^ 1 << bit) for i in range(lax.axis_size...  42.4 us
    ppermute x15, waiting for transfers between devices, doubling_gather(): other = lax.ppermute(cur, ALL, [(i, i ^ 1 << b) for i in range(total)])  36.3 us
    ppermute x15, waiting for transfers between devices, halving_scatter(): lax.ppermute(theirs.astype(jnp.bfloat16), ALL, [(i, i ^ 1 << b) for i in...  25.5 us
    dot_general x2, matrix products, ffn_forward(): jnp.dot(rows, inner_cols, preferred_element_type=jnp.float32) + inner_offset  21 us
    ppermute x15, starting transfers between devices, doubling_gather(): other = lax.ppermute(cur, ALL, [(i, i ^ 1 << b) for i in range(total)])  18.2 us
    dot_general x6, matrix products, contract_rows(): lax.dot_general(left_op, right_op, (((0,), (0,)), ((), ())), preferred_el...  15.3 us
    dot_general x6, matrix products, contract_cols(): lax.dot_general(left_op, right_op, (((1,), (1,)), ((), ())), preferred_el...  14 us
    dot_general x1, matrix products, attend_back(): jnp.einsum('pqhd,pkhd->phqk', grad_mixed, value_low, preferred_element_ty...  10 us
  transfers between devices with their start and end apart: 40, of which 21 were waited for; matrix products, arithmetic and copies ran while one was open for 43% of the time, Pallas kernels for 0%

profile of v5, /device:TPU:0, one launch (start us, length us, event | category | flops | bytes accessed | tf_op | source)
XLA Modules:
  0.0 365.0 jit_solution(16459898749583696382)
XLA Ops:
  36.0 13.8 %collective-permute-done.13 = bf16[2,2,24,1152]{3,2,1,0:T(8,128)(2,1)S(1)} collective-permute-done((bf16[2,2,24,1152]{3,2,1,0:T(8,128)(2,1)S(1)}, bf16[2,2,24,1152]{3,2,1,0:T(8,128)(2,1)S(1)}, u32[]{:S(2)}, u32[]{:S(2)}) %collective-permute-start.13) | collective-permute-done | bytes 221216 | tf_op jit(solution)/shard_map/ppermute | solution.py:46
  50.4 16.0 %collective-permute-done.14 = bf16[2,2,2,24,1152]{4,3,2,1,0:T(8,128)(2,1)S(1)} collective-permute-done((bf16[2,2,2,24,1152]{4,3,2,1,0:T(8,128)(2,1)S(1)}, bf16[2,2,2,24,1152]{4,3,2,1,0:T(8,128)(2,1)S(1)}, u32[]{:S(2)}, u32[]{:S(2)}) %collective-permute-start.14) | collective-permute-done | bytes 442400 | tf_op jit(solution)/shard_map/ppermute | solution.py:46
  80.9 6.6 %collective-permute-done = bf16[256,768]{1,0:T(8,128)(2,1)S(1)} collective-permute-done((bf16[256,768]{1,0:T(8,128)(2,1)}, bf16[256,768]{1,0:T(8,128)(2,1)S(1)}, u32[]{:S(2)}, u32[]{:S(2)}) %collective-permute-start) | collective-permute-done | bytes 393248 | tf_op jit(solution)/shard_map/ppermute | solution.py:16
  110.7 4.0 %fusion.57 = bf16[12,64,512]{2,1,0:T(8,128)(2,1)S(1)} fusion(bf16[512,12,64]{0,2,1:T(8,128)(2,1)S(1)} %bitcast.185, f32[12,512]{1,0:T(8,128)S(1)} %fusion, f32[12,512]{1,0:T(8,128)S(1)} %get-tuple-element.107, f32[12,512,512]{1,2,0:T(8,128)S(1)} %get-tuple-element.108, pred[512,512]{0,1:T(8,128)(4,1)S(1)} %copy-done.13), kind=kOutput, calls=%fused_computation.111 | convolution fusion | flops 418775040 | bytes 14467072 | tf_op jit(solution)/shard_map/phqk,pkhd->pqhd/dot_general | solution.py:179
  119.8 5.2 %all-gather.2.cloned.1.call-done = bf16[768,3074]{1,0:T(8,128)(2,1)} async-done(((bf16[48,3074]{1,0:T(8,128)(2,1)}), bf16[768,3074]{1,0:T(8,128)(2,1)}) %all-gather.2.cloned.1.call-update) | async-done | bytes 4721680 | tf_op jit(solution)/shard_map/all_gather | solution.py:282
  126.1 8.4 %collective-permute-done.16 = bf16[512,768]{1,0:T(8,128)(2,1)} collective-permute-done((bf16[512,768]{1,0:T(8,128)(2,1)S(1)}, bf16[512,768]{1,0:T(8,128)(2,1)}, u32[]{:S(2)}, u32[]{:S(2)}) %collective-permute-start.16) | collective-permute-done | bytes 786464 | tf_op jit(solution)/shard_map/ppermute | solution.py:16
  134.5 10.9 %multiply_convert_fusion.1 = (bf16[512,1536]{1,0:T(8,128)(2,1)S(1)}, f32[512,1536]{1,0:T(8,128)}, f32[512,1536]{1,0:T(8,128)}) fusion(f32[1536]{0:T(1024)S(1)} %reshape.633, bf16[512,768]{1,0:T(8,128)(2,1)} %collective-permute-done.16, bf16[768,3074]{1,0:T(8,128)(2,1)} %all-gather.2.cloned.1.call-done), kind=kOutput, calls=%fused_computation.28 | convolution fusion | flops 1259864064 | bytes 11016192 | tf_op jit(solution)/shard_map/dot_general | solution.py:208
  147.6 10.1 %multiply_convert_fusion.2 = (bf16[512,1536]{1,0:T(8,128)(2,1)S(1)}, f32[512,1536]{1,0:T(8,128)}, f32[512,1536]{1,0:T(8,128)}) fusion(f32[1536]{0:T(1024)S(1)} %reshape.633, bf16[512,768]{1,0:T(8,128)(2,1)S(1)} %fusion.58, bf16[768,3074]{1,0:T(8,128)(2,1)S(1)} %copy-done.60), kind=kOutput, calls=%fused_computation.41 | convolution fusion | flops 1259864064 | bytes 11018240 | tf_op jit(solution)/shard_map/dot_general | solution.py:208
  157.7 6.3 %collective-permute-done.17 = bf16[512,768]{1,0:T(8,128)(2,1)S(1)} collective-permute-done((bf16[512,768]{1,0:T(8,128)(2,1)S(1)}, bf16[512,768]{1,0:T(8,128)(2,1)S(1)}, u32[]{:S(2)}, u32[]{:S(2)}) %collective-permute-start.17) | collective-permute-done | bytes 786464 | tf_op jit(solution)/shard_map/ppermute | solution.py:16
  170.4 3.5 fusion.96
  177.4 6.1 %convert_reduce_fusion.1 = (f32[1536]{0:T(1024)S(1)}, bf16[512,1536]{1,0:T(8,128)(2,1)S(1)}) fusion(f32[512,1536]{1,0:T(8,128)} %get-tuple-element.63, f32[512,1536]{1,0:T(8,128)} %get-tuple-element.112, bf16[512,768]{1,0:T(8,128)(2,1)} %get-tuple-element.54, bf16[768,3074]{1,0:T(8,128)(2,1)} %all-gather.2.cloned.1.call-done), kind=kOutput, calls=%fused_computation.25 | convolution fusion | flops 1220540928 | bytes 11016192 | tf_op jit(solution)/shard_map/dot_general | solution.py:215
  186.7 6.0 %collective-permute-done.19 = bf16[512,768]{1,0:T(8,128)(2,1)S(1)} collective-permute-done((bf16[512,768]{1,0:T(8,128)(2,1)}, bf16[512,768]{1,0:T(8,128)(2,1)S(1)}, u32[]{:S(2)}, u32[]{:S(2)}) %collective-permute-start.19) | collective-permute-done | bytes 786464 | tf_op jit(solution)/shard_map/ppermute | solution.py:16
  192.8 3.9 %convert_reduce_fusion = (f32[1536]{0:T(1024)S(1)}, bf16[512,1536]{1,0:T(8,128)(2,1)S(1)}) fusion(f32[512,1536]{1,0:T(8,128)S(1)} %copy-done.63, f32[512,1536]{1,0:T(8,128)S(1)} %copy-done.64, bf16[512,768]{1,0:T(8,128)(2,1)S(1)} %collective-permute-done.19, bf16[768,3074]{1,0:T(8,128)(2,1)} %all-gather.2.cloned.1.call-done), kind=kOutput, calls=%fused_computation.24 | convolution fusion | flops 1220540928 | bytes 11016192 | tf_op jit(solution)/shard_map/dot_general | solution.py:215
  196.7 4.0 %fusion.48 = bf16[512,768]{1,0:T(8,128)(2,1)} fusion(bf16[512,1536]{1,0:T(8,128)(2,1)S(1)} %get-tuple-element.120, bf16[768,3074]{1,0:T(8,128)(2,1)} %all-gather.2.cloned.1.call-done), kind=kOutput, calls=%fused_computation.108 | convolution fusion | flops 1208352768 | bytes 4718592 | tf_op jit(solution)/shard_map/dot_general | solution.py:160
  202.4 4.1 %add_convert_fusion.1 = bf16[768,1536]{1,0:T(8,128)(2,1)} fusion(f32[768,1536]{1,0:T(8,128)S(1)} %fusion.104, bf16[512,768]{1,0:T(8,128)(2,1)} %collective-permute-done.16, bf16[512,1536]{1,0:T(8,128)(2,1)S(1)} %get-tuple-element.120), kind=kOutput, calls=%fused_computation.18 | convolution fusion | flops 1210318848 | bytes 9437184 | tf_op jit(solution)/shard_map/dot_general | solution.py:154
  210.1 5.4 %pad_maximum_fusion.1 = bf16[768,3074]{1,0:T(8,128)(2,1)} fusion(bf16[768,2]{1,0:T(8,128)(2,1)S(1)} %add.340, bf16[768,1536]{1,0:T(8,128)(2,1)} %add_convert_fusion, bf16[768,1536]{1,0:T(8,128)(2,1)} %add_convert_fusion.1), kind=kLoop, calls=%fused_computation.13 | loop fusion | flops 14164992 | bytes 9443328 | tf_op jit(solution)/shard_map/concatenate | solution.py:372
  217.0 3.9 %convert_add_fusion.3 = f32[512,768]{1,0:T(8,128)S(1)} fusion(bf16[512,768]{1,0:T(8,128)(2,1)} %collective-permute-done.20, bf16[512,1536]{1,0:T(8,128)(2,1)} %copy-done.32, bf16[768,3074]{1,0:T(8,128)(2,1)} %all-gather.2.cloned.1.call-done), kind=kOutput, calls=%fused_computation.81 | convolution fusion | flops 1208745984 | bytes 6291456 | tf_op jit(solution)/shard_map/dot_general | solution.py:160
  226.2 9.7 %fusion.54 = bf16[12,64,512]{2,1,0:T(8,128)(2,1)} fusion(bf16[512,12,64]{0,2,1:T(8,128)(2,1)} %bitcast.187, f32[12,512]{1,0:T(8,128)S(1)} %copy-done.47, f32[12,512,512]{1,2,0:T(8,128)} %copy-done.2, pred[512,512]{0,1:T(8,128)(4,1)S(1)} %copy-done.14), kind=kOutput, calls=%fused_computation.110 | convolution fusion | flops 415629312 | bytes 14442496 | tf_op jit(solution)/shard_map/phqk,pqhd->pkhd/dot_general | solution.py:187
  235.9 10.0 %multiply_reduce_fusion = (f32[12,512]{1,0:T(8,128)S(1)}, f32[12,512,512]{1,2,0:T(8,128)}) fusion(f32[12,512]{1,0:T(8,128)S(1)} %copy-done.47, f32[12,512,512]{1,2,0:T(8,128)} %copy-done.2, pred[512,512]{0,1:T(8,128)(4,1)S(1)} %copy-done.14, bf16[512,12,64]{0,2,1:T(8,128)(2,1)S(1)} %bitcast.188, bf16[512,12,64]{0,2,1:T(8,128)(2,1)S(1)} %bitcast.186), kind=kOutput, calls=%fused_computation.1 | convolution fusion | flops 418375680 | bytes 27049984 | tf_op jit(solution)/shard_map/pqhd,pkhd->phqk/dot_general | solution.py:193
  246.0 7.1 %multiply_convert_fusion = bf16[12,512,512]{1,2,0:T(8,128)(2,1)S(1)} fusion(f32[12,512,512]{1,2,0:T(8,128)} %get-tuple-element.116, f32[12,512]{1,0:T(8,128)S(1)} %get-tuple-element.115, f32[12,512]{1,0:T(8,128)S(1)} %copy-done.47, f32[12,512,512]{1,2,0:T(8,128)S(1)} %bitcast.173, pred[512,512]{0,1:T(8,128)(4,1)S(1)} %copy-done.14), kind=kLoop, calls=%fused_computation | loop fusion | flops 18874368 | bytes 31768576 | tf_op jit(solution)/shard_map/convert_element_type | solution.py:197
  282.9 8.8 %concatenate.125 = bf16[32,24,3081]{2,1,0:T(8,128)(2,1)} concatenate(bf16[32,24,2304]{2,1,0:T(8,128)(2,1)S(1)} %bitcast.175, bf16[32,24,3]{2,1,0:T(8,128)(2,1)} %bitcast.199, bf16[32,24,768]{2,1,0:T(8,128)(2,1)} %convolution_convert_fusion.1, bf16[32,24,1]{2,1,0:T(8,128)(2,1)} %stack.65, bf16[32,24,1]{2,1,0:T(8,128)(2,1)} %stack.66, bf16[32,24,1]{2,1,0:T(8,128)(2,1)} %stack.67, ...), dimensions={2} | concatenate | bytes 9464832 | tf_op jit(solution)/shard_map/concatenate | solution.py:420
  300.2 13.2 %collective-permute-done.22 = f32[256,768]{1,0:T(8,128)} collective-permute-done((f32[256,768]{1,0:T(8,128)}, f32[256,768]{1,0:T(8,128)}, u32[]{:S(2)}, u32[]{:S(2)}) %collective-permute-start.22) | collective-permute-done | bytes 786464 | tf_op jit(solution)/shard_map/ppermute | solution.py:16
  318.9 10.6 %collective-permute-done.29 = bf16[2,2,2,24,1033]{4,3,2,1,0:T(8,128)(2,1)S(1)} collective-permute-done((bf16[2,2,2,24,1033]{4,3,2,1,0:T(8,128)(2,1)S(1)}, bf16[2,2,2,24,1033]{4,3,2,1,0:T(8,128)(2,1)S(1)}, u32[]{:S(2)}, u32[]{:S(2)}) %collective-permute-start.29) | collective-permute-done | bytes 396704 | tf_op jit(solution)/shard_map/ppermute | solution.py:79
  335.7 6.7 %collective-permute-done.30 = bf16[2,2,24,1033]{3,2,1,0:T(8,128)(2,1)S(1)} collective-permute-done((bf16[2,2,24,1033]{3,2,1,0:T(8,128)(2,1)S(1)}, bf16[2,2,24,1033]{3,2,1,0:T(8,128)(2,1)S(1)}, u32[]{:S(2)}, u32[]{:S(2)}) %collective-permute-start.30) | collective-permute-done | bytes 198368 | tf_op jit(solution)/shard_map/ppermute | solution.py:79
  (359 shorter events, 164.9 us)
Async XLA Ops:
  7.2 117.7 %all-gather.2.cloned.1.call-start = ((), (), s32[]{:S(2)}) async-start(), calls=%async_computation.1 | async-start | bytes 5222400 | tf_op jit(solution)/shard_map/all_gather | solution.py:282
  9.6 13.2 %collective-permute-start.11 = (bf16[24,1152]{1,0:T(8,128)(2,1)S(1)}, bf16[24,1152]{1,0:T(8,128)(2,1)S(1)}, u32[]{:S(2)}, u32[]{:S(2)}) collective-permute-start(bf16[24,1152]{1,0:T(8,128)(2,1)S(1)} %fusion.79), channel_id=1, source_target_pairs={{0,1},{1,0},{2,3},{3,2},{4,5},{5,4},{6,7},{7,6},{8,9},{9,8},{10,11... | collective-permute-start | bytes 165896 | tf_op jit(solution)/shard_map/ppermute | solution.py:46
  29.3 20.5 %collective-permute-start.13 = (bf16[2,2,24,1152]{3,2,1,0:T(8,128)(2,1)S(1)}, bf16[2,2,24,1152]{3,2,1,0:T(8,128)(2,1)S(1)}, u32[]{:S(2)}, u32[]{:S(2)}) collective-permute-start(bf16[2,2,24,1152]{3,2,1,0:T(8,128)(2,1)S(1)} %broadcast_select_fusion.11), channel_id=1, source_target_pairs={{0,16},{1,17},{2,18},{3,19},{4,20},{5,21},{6,22},{7,23},{8,24},{9,... | collective-permute-start | bytes 663560 | tf_op jit(solution)/shard_map/ppermute | solution.py:46
  32.0 34.6 %collective-permute-start.9 = (bf16[2,2,2,24,1024]{4,3,2,0,1:T(8,128)(2,1)S(1)}, bf16[2,2,2,24,1024]{4,3,2,0,1:T(8,128)(2,1)S(1)}, u32[]{:S(2)}, u32[]{:S(2)}) collective-permute-start(bf16[2,2,2,24,1024]{4,3,2,0,1:T(8,128)(2,1)S(1)} %broadcast_select_fusion.7), channel_id=1, source_target_pairs={{0,16},{1,17},{2,18},{3,19},{4,20},{5,21},{6,22},{7,23},{8,24},{9,... | collective-permute-start | bytes 1179656 | tf_op jit(solution)/shard_map/ppermute | solution.py:46
  34.8 15.4 %collective-permute-start.4 = (bf16[2,2,2,24,1024]{4,3,2,0,1:T(8,128)(2,1)S(1)}, bf16[2,2,2,24,1024]{4,3,2,0,1:T(8,128)(2,1)S(1)}, u32[]{:S(2)}, u32[]{:S(2)}) collective-permute-start(bf16[2,2,2,24,1024]{4,3,2,0,1:T(8,128)(2,1)S(1)} %broadcast_select_fusion.9), channel_id=1, source_target_pairs={{0,4},{1,5},{2,6},{3,7},{4,0},{5,1},{6,2},{7,3},{8,12},{9,13},{10,... | collective-permute-start | bytes 1179656 | tf_op jit(solution)/shard_map/ppermute | solution.py:46
  50.0 16.4 %collective-permute-start.14 = (bf16[2,2,2,24,1152]{4,3,2,1,0:T(8,128)(2,1)S(1)}, bf16[2,2,2,24,1152]{4,3,2,1,0:T(8,128)(2,1)S(1)}, u32[]{:S(2)}, u32[]{:S(2)}) collective-permute-start(bf16[2,2,2,24,1152]{4,3,2,1,0:T(8,128)(2,1)S(1)} %broadcast_select_fusion.6), channel_id=1, source_target_pairs={{0,8},{1,9},{2,10},{3,11},{4,12},{5,13},{6,14},{7,15},{8,0},{9,1},... | collective-permute-start | bytes 1327112 | tf_op jit(solution)/shard_map/ppermute | solution.py:46
  50.3 17.8 %collective-permute-start.5 = (bf16[2,2,2,2,24,1024]{5,4,3,0,1,2:T(8,128)(2,1)S(1)}, bf16[2,2,2,2,24,1024]{5,4,3,0,1,2:T(8,128)(2,1)S(1)}, u32[]{:S(2)}, u32[]{:S(2)}) collective-permute-start(bf16[2,2,2,2,24,1024]{5,4,3,0,1,2:T(8,128)(2,1)S(1)} %broadcast_select_fusion.4), channel_id=1, source_target_pairs={{0,2},{1,3},{2,0},{3,1},{4,6},{5,7},{6,4},{7,5},{8,10},{9,11},{10,... | collective-permute-start | bytes 2359304 | tf_op jit(solution)/shard_map/ppermute | solution.py:46
  74.1 279.1 %reduce-scatter.2.cloned.1.call-start = ((), (), s32[]{:S(2)}) async-start(), calls=%async_computation.2 | async-start | bytes 5222400 | tf_op jit(solution)/shard_map/reduce_scatter | solution.py:373
  77.3 39.2 %collective-permute-start.18 = (bf16[256,768]{1,0:T(8,128)(2,1)}, bf16[256,768]{1,0:T(8,128)(2,1)}, u32[]{:S(2)}, u32[]{:S(2)}) collective-permute-start(bf16[256,768]{1,0:T(8,128)(2,1)} %get-tuple-element.85), channel_id=1, source_target_pairs={{0,1},{1,0},{2,3},{3,2},{4,5},{5,4},{6,7},{7,6},{8,9},{9,8},{10,11... | collective-permute-start | bytes 1179656 | tf_op jit(solution)/shard_map/ppermute | solution.py:16
  116.4 18.1 %collective-permute-start.16 = (bf16[512,768]{1,0:T(8,128)(2,1)S(1)}, bf16[512,768]{1,0:T(8,128)(2,1)}, u32[]{:S(2)}, u32[]{:S(2)}) collective-permute-start(bf16[512,768]{1,0:T(8,128)(2,1)S(1)} %fusion.58), channel_id=1, source_target_pairs={{0,1},{1,0},{2,3},{3,2},{4,5},{5,4},{6,7},{7,6},{8,9},{9,8},{10,11... | collective-permute-start | bytes 2359304 | tf_op jit(solution)/shard_map/ppermute | solution.py:16
  146.9 17.1 %collective-permute-start.17 = (bf16[512,768]{1,0:T(8,128)(2,1)S(1)}, bf16[512,768]{1,0:T(8,128)(2,1)S(1)}, u32[]{:S(2)}, u32[]{:S(2)}) collective-permute-start(bf16[512,768]{1,0:T(8,128)(2,1)S(1)} %fusion.51), channel_id=1, source_target_pairs={{0,1},{1,0},{2,3},{3,2},{4,5},{5,4},{6,7},{7,6},{8,9},{9,8},{10,11... | collective-permute-start | bytes 2359304 | tf_op jit(solution)/shard_map/ppermute | solution.py:16
  176.1 16.6 %collective-permute-start.19 = (bf16[512,768]{1,0:T(8,128)(2,1)}, bf16[512,768]{1,0:T(8,128)(2,1)S(1)}, u32[]{:S(2)}, u32[]{:S(2)}) collective-permute-start(bf16[512,768]{1,0:T(8,128)(2,1)} %get-tuple-element.54), channel_id=1, source_target_pairs={{0,1},{1,0},{2,3},{3,2},{4,5},{5,4},{6,7},{7,6},{8,9},{9,8},{10,11... | collective-permute-start | bytes 2359304 | tf_op jit(solution)/shard_map/ppermute | solution.py:16
  200.7 16.3 %collective-permute-start.20 = (bf16[512,768]{1,0:T(8,128)(2,1)}, bf16[512,768]{1,0:T(8,128)(2,1)}, u32[]{:S(2)}, u32[]{:S(2)}) collective-permute-start(bf16[512,768]{1,0:T(8,128)(2,1)} %fusion.48), channel_id=1, source_target_pairs={{0,1},{1,0},{2,3},{3,2},{4,5},{5,4},{6,7},{7,6},{8,9},{9,8},{10,11... | collective-permute-start | bytes 2359304 | tf_op jit(solution)/shard_map/ppermute | solution.py:16
  265.1 28.6 %collective-permute-start.23 = (bf16[2,2,2,2,24,1024]{5,4,3,2,1,0:T(8,128)(2,1)}, bf16[2,2,2,2,24,1024]{5,4,3,2,1,0:T(8,128)(2,1)}, u32[]{:S(2)}, u32[]{:S(2)}) collective-permute-start(bf16[2,2,2,2,24,1024]{5,4,3,2,1,0:T(8,128)(2,1)} %dynamic-slice_bitcast_fusion.1), channel_id=1, source_target_pairs={{0,2},{1,3},{2,0},{3,1},{4,6},{5,7},{6,4},{7,5},{8,10},{9,11},{10,... | collective-permute-start | bytes 2359304 | tf_op jit(solution)/shard_map/ppermute | solution.py:79
  271.7 23.6 %collective-permute-start.33 = (bf16[2,2,2,2,24,1024]{5,4,3,1,2,0:T(8,128)(2,1)}, bf16[2,2,2,2,24,1024]{5,4,3,1,2,0:T(8,128)(2,1)}, u32[]{:S(2)}, u32[]{:S(2)}) collective-permute-start(bf16[2,2,2,2,24,1024]{5,4,3,1,2,0:T(8,128)(2,1)} %bitcast.171), channel_id=1, source_target_pairs={{0,2},{1,3},{2,0},{3,1},{4,6},{5,7},{6,4},{7,5},{8,10},{9,11},{10,... | collective-permute-start | bytes 2359304 | tf_op jit(solution)/shard_map/ppermute | solution.py:79
  276.7 20.7 %collective-permute-start.21 = (f32[256,768]{1,0:T(8,128)}, f32[256,768]{1,0:T(8,128)}, u32[]{:S(2)}, u32[]{:S(2)}) collective-permute-start(f32[256,768]{1,0:T(8,128)} %get-tuple-element.84), channel_id=1, source_target_pairs={{0,1},{1,0},{2,3},{3,2},{4,5},{5,4},{6,7},{7,6},{8,9},{9,8},{10,11... | collective-permute-start | bytes 2359304 | tf_op jit(solution)/shard_map/ppermute | solution.py:16
  282.7 30.7 %collective-permute-start.22 = (f32[256,768]{1,0:T(8,128)}, f32[256,768]{1,0:T(8,128)}, u32[]{:S(2)}, u32[]{:S(2)}) collective-permute-start(f32[256,768]{1,0:T(8,128)} %get-tuple-element.27), channel_id=1, source_target_pairs={{0,1},{1,0},{2,3},{3,2},{4,5},{5,4},{6,7},{7,6},{8,9},{9,8},{10,11... | collective-permute-start | bytes 2359304 | tf_op jit(solution)/shard_map/ppermute | solution.py:16
  293.6 22.5 %collective-permute-start.28 = (bf16[2,2,2,2,24,1033]{5,4,3,2,1,0:T(8,128)(2,1)S(1)}, bf16[2,2,2,2,24,1033]{5,4,3,2,1,0:T(8,128)(2,1)S(1)}, u32[]{:S(2)}, u32[]{:S(2)}) collective-permute-start(bf16[2,2,2,2,24,1033]{5,4,3,2,1,0:T(8,128)(2,1)S(1)} %dynamic-slice_bitcast_fusion), channel_id=1, source_target_pairs={{0,2},{1,3},{2,0},{3,1},{4,6},{5,7},{6,4},{7,5},{8,10},{9,11},{10,... | collective-permute-start | bytes 2380040 | tf_op jit(solution)/shard_map/ppermute | solution.py:79
  295.2 21.2 %collective-permute-start.24 = (bf16[2,2,2,24,1024]{4,3,2,1,0:T(8,128)(2,1)S(1)}, bf16[2,2,2,24,1024]{4,3,2,1,0:T(8,128)(2,1)S(1)}, u32[]{:S(2)}, u32[]{:S(2)}) collective-permute-start(bf16[2,2,2,24,1024]{4,3,2,1,0:T(8,128)(2,1)S(1)} %fusion.70), channel_id=1, source_target_pairs={{0,4},{1,5},{2,6},{3,7},{4,0},{5,1},{6,2},{7,3},{8,12},{9,13},{10,... | collective-permute-start | bytes 1179656 | tf_op jit(solution)/shard_map/ppermute | solution.py:79
  296.9 21.8 %collective-permute-start.34 = (bf16[2,2,2,24,1024]{4,3,2,0,1:T(8,128)(2,1)S(1)}, bf16[2,2,2,24,1024]{4,3,2,0,1:T(8,128)(2,1)S(1)}, u32[]{:S(2)}, u32[]{:S(2)}) collective-permute-start(bf16[2,2,2,24,1024]{4,3,2,0,1:T(8,128)(2,1)S(1)} %fusion.71), channel_id=1, source_target_pairs={{0,16},{1,17},{2,18},{3,19},{4,20},{5,21},{6,22},{7,23},{8,24},{9,... | collective-permute-start | bytes 1179656 | tf_op jit(solution)/shard_map/ppermute | solution.py:79
  316.4 13.1 %collective-permute-start.29 = (bf16[2,2,2,24,1033]{4,3,2,1,0:T(8,128)(2,1)S(1)}, bf16[2,2,2,24,1033]{4,3,2,1,0:T(8,128)(2,1)S(1)}, u32[]{:S(2)}, u32[]{:S(2)}) collective-permute-start(bf16[2,2,2,24,1033]{4,3,2,1,0:T(8,128)(2,1)S(1)} %fusion.65), channel_id=1, source_target_pairs={{0,8},{1,9},{2,10},{3,11},{4,12},{5,13},{6,14},{7,15},{8,0},{9,1},... | collective-permute-start | bytes 1190024 | tf_op jit(solution)/shard_map/ppermute | solution.py:79
  316.6 16.3 %collective-permute-start.25 = (bf16[2,2,24,1024]{3,2,1,0:T(8,128)(2,1)S(1)}, bf16[2,2,24,1024]{3,2,1,0:T(8,128)(2,1)S(1)}, u32[]{:S(2)}, u32[]{:S(2)}) collective-permute-start(bf16[2,2,24,1024]{3,2,1,0:T(8,128)(2,1)S(1)} %fusion.73), channel_id=1, source_target_pairs={{0,8},{1,9},{2,10},{3,11},{4,12},{5,13},{6,14},{7,15},{8,0},{9,1},... | collective-permute-start | bytes 589832 | tf_op jit(solution)/shard_map/ppermute | solution.py:79
  318.8 14.3 %collective-permute-start.35 = (bf16[2,2,24,1024]{3,2,1,0:T(8,128)(2,1)S(1)}, bf16[2,2,24,1024]{3,2,1,0:T(8,128)(2,1)S(1)}, u32[]{:S(2)}, u32[]{:S(2)}) collective-permute-start(bf16[2,2,24,1024]{3,2,1,0:T(8,128)(2,1)S(1)} %fusion.74), channel_id=1, source_target_pairs={{0,4},{1,5},{2,6},{3,7},{4,0},{5,1},{6,2},{7,3},{8,12},{9,13},{10,... | collective-permute-start | bytes 589832 | tf_op jit(solution)/shard_map/ppermute | solution.py:79
  329.6 12.9 %collective-permute-start.30 = (bf16[2,2,24,1033]{3,2,1,0:T(8,128)(2,1)S(1)}, bf16[2,2,24,1033]{3,2,1,0:T(8,128)(2,1)S(1)}, u32[]{:S(2)}, u32[]{:S(2)}) collective-permute-start(bf16[2,2,24,1033]{3,2,1,0:T(8,128)(2,1)S(1)} %fusion.72), channel_id=1, source_target_pairs={{0,16},{1,17},{2,18},{3,19},{4,20},{5,21},{6,22},{7,23},{8,24},{9,... | collective-permute-start | bytes 595016 | tf_op jit(solution)/shard_map/ppermute | solution.py:79
  (86 other events, 637.9 us)
Sparse Core Ops, SparseCore 0:
  74.3 50.6 all-gather.1
  215.6 72.6 reduce-scatter.1

commit v6 on v4

--- a/solution.py
+++ b/solution.py
@@ -323,7 +323,8 @@
         )
 
     pack_in = to_pack(layer_in)
-    pack_cot = to_pack(cotangent)
+    late_cot, pack_in = lax.optimization_barrier((cotangent, pack_in))
+    pack_cot = to_pack(late_cot)
 
     def heads_of(values):
         return values.reshape(1, rows_dev, HEADS, HEAD_DIM)

time: 370 us -> 375 us (1.014)
  waiting for transfers between devices: 109 us -> 113 us
    ppermute x8, waiting for transfers between devices: 42.4 us -> 51.1 us  [swapped(): lax.ppermute(shard, axis, [(i, i ^ 1 << bit) for i in range(lax.axis_size...]
  transfers between devices with their start and end apart: 40 -> 40, of which waited for: 21 -> 19; matrix products, arithmetic and copies ran while one was open for 43% -> 43% of each run, Pallas kernels for 0% -> 0%
where the time goes in v6:
time: 375 us; the launch traced here: 370 us
  waiting for transfers between devices  113 us (30%)
  matrix products  92.2 us (25%)
  local copies, waits for them, and re-layouts  55.9 us (15%)
  other arithmetic  55.9 us (15%)
  starting transfers between devices  36.5 us (10%)
  between operations  15.6 us (4%)
    ppermute x8, waiting for transfers between devices, swapped(): lax.ppermute(shard, axis, [(i, i ^ 1 << bit) for i in range(lax.axis_size...  51.1 us
    ppermute x15, waiting for transfers between devices, doubling_gather(): other = lax.ppermute(cur, ALL, [(i, i ^ 1 << b) for i in range(total)])  36.3 us
    ppermute x15, waiting for transfers between devices, halving_scatter(): lax.ppermute(theirs.astype(jnp.bfloat16), ALL, [(i, i ^ 1 << b) for i in...  24.1 us
    dot_general x2, matrix products, ffn_forward(): jnp.dot(rows, inner_cols, preferred_element_type=jnp.float32) + inner_offset  21 us
    ppermute x15, starting transfers between devices, doubling_gather(): other = lax.ppermute(cur, ALL, [(i, i ^ 1 << b) for i in range(total)])  18.2 us
    dot_general x6, matrix products, contract_rows(): lax.dot_general(left_op, right_op, (((0,), (0,)), ((), ())), preferred_el...  15.4 us
    dot_general x6, matrix products, contract_cols(): lax.dot_general(left_op, right_op, (((1,), (1,)), ((), ())), preferred_el...  14 us
    ppermute x15, starting transfers between devices, halving_scatter(): lax.ppermute(theirs.astype(jnp.bfloat16), ALL, [(i, i ^ 1 << b) for i in...  11.2 us
  transfers between devices with their start and end apart: 40, of which 19 were waited for; matrix products, arithmetic and copies ran while one was open for 43% of the time, Pallas kernels for 0%

profile of v6, /device:TPU:0, one launch (start us, length us, event | category | flops | bytes accessed | tf_op | source)
XLA Modules:
  0.0 369.5 jit_solution(8523602153402280175)
XLA Ops:
  36.0 13.8 %collective-permute-done.13 = bf16[2,2,24,1152]{3,2,1,0:T(8,128)(2,1)S(1)} collective-permute-done((bf16[2,2,24,1152]{3,2,1,0:T(8,128)(2,1)S(1)}, bf16[2,2,24,1152]{3,2,1,0:T(8,128)(2,1)S(1)}, u32[]{:S(2)}, u32[]{:S(2)}) %collective-permute-start.13) | collective-permute-done | bytes 221216 | tf_op jit(solution)/shard_map/ppermute | solution.py:46
  50.4 16.0 %collective-permute-done.14 = bf16[2,2,2,24,1152]{4,3,2,1,0:T(8,128)(2,1)S(1)} collective-permute-done((bf16[2,2,2,24,1152]{4,3,2,1,0:T(8,128)(2,1)S(1)}, bf16[2,2,2,24,1152]{4,3,2,1,0:T(8,128)(2,1)S(1)}, u32[]{:S(2)}, u32[]{:S(2)}) %collective-permute-start.14) | collective-permute-done | bytes 442400 | tf_op jit(solution)/shard_map/ppermute | solution.py:46
  76.8 9.8 %collective-permute-done = bf16[256,768]{1,0:T(8,128)(2,1)S(1)} collective-permute-done((bf16[256,768]{1,0:T(8,128)(2,1)}, bf16[256,768]{1,0:T(8,128)(2,1)S(1)}, u32[]{:S(2)}, u32[]{:S(2)}) %collective-permute-start) | collective-permute-done | bytes 393248 | tf_op jit(solution)/shard_map/ppermute | solution.py:16
  112.6 4.0 %fusion.57 = bf16[12,64,512]{2,1,0:T(8,128)(2,1)S(1)} fusion(bf16[512,12,64]{0,2,1:T(8,128)(2,1)S(1)} %bitcast.185, f32[12,512]{1,0:T(8,128)S(1)} %fusion, f32[12,512]{1,0:T(8,128)S(1)} %get-tuple-element.111, f32[12,512,512]{1,2,0:T(8,128)S(1)} %get-tuple-element.112, pred[512,512]{0,1:T(8,128)(4,1)S(1)} %copy-done.13), kind=kOutput, calls=%fused_computation.111 | convolution fusion | flops 418775040 | bytes 14467072 | tf_op jit(solution)/shard_map/phqk,pkhd->pqhd/dot_general | solution.py:188
  126.1 11.2 %collective-permute-done.16 = bf16[512,768]{1,0:T(8,128)(2,1)} collective-permute-done((bf16[512,768]{1,0:T(8,128)(2,1)S(1)}, bf16[512,768]{1,0:T(8,128)(2,1)}, u32[]{:S(2)}, u32[]{:S(2)}) %collective-permute-start.16) | collective-permute-done | bytes 786464 | tf_op jit(solution)/shard_map/ppermute | solution.py:16
  137.3 10.9 %multiply_convert_fusion.1 = (bf16[512,1536]{1,0:T(8,128)(2,1)S(1)}, f32[512,1536]{1,0:T(8,128)}, f32[512,1536]{1,0:T(8,128)}) fusion(f32[1536]{0:T(1024)S(1)} %reshape.633, bf16[512,768]{1,0:T(8,128)(2,1)} %collective-permute-done.16, bf16[768,3074]{1,0:T(8,128)(2,1)} %all-gather.2.cloned.1.call-done), kind=kOutput, calls=%fused_computation.28 | convolution fusion | flops 1259864064 | bytes 11016192 | tf_op jit(solution)/shard_map/dot_general | solution.py:217
  151.1 10.1 %multiply_convert_fusion.2 = (bf16[512,1536]{1,0:T(8,128)(2,1)S(1)}, f32[512,1536]{1,0:T(8,128)}, f32[512,1536]{1,0:T(8,128)}) fusion(f32[1536]{0:T(1024)S(1)} %reshape.633, bf16[512,768]{1,0:T(8,128)(2,1)S(1)} %fusion.58, bf16[768,3074]{1,0:T(8,128)(2,1)S(1)} %copy-done.60), kind=kOutput, calls=%fused_computation.41 | convolution fusion | flops 1259864064 | bytes 11018240 | tf_op jit(solution)/shard_map/dot_general | solution.py:217
  161.2 6.6 %collective-permute-done.17 = bf16[512,768]{1,0:T(8,128)(2,1)S(1)} collective-permute-done((bf16[512,768]{1,0:T(8,128)(2,1)S(1)}, bf16[512,768]{1,0:T(8,128)(2,1)S(1)}, u32[]{:S(2)}, u32[]{:S(2)}) %collective-permute-start.17) | collective-permute-done | bytes 786464 | tf_op jit(solution)/shard_map/ppermute | solution.py:16
  174.2 3.5 fusion.96
  180.7 6.1 %convert_reduce_fusion.1 = (f32[1536]{0:T(1024)S(1)}, bf16[512,1536]{1,0:T(8,128)(2,1)S(1)}) fusion(f32[512,1536]{1,0:T(8,128)} %get-tuple-element.67, f32[512,1536]{1,0:T(8,128)} %get-tuple-element.116, bf16[512,768]{1,0:T(8,128)(2,1)} %get-tuple-element.58, bf16[768,3074]{1,0:T(8,128)(2,1)} %all-gather.2.cloned.1.call-done), kind=kOutput, calls=%fused_computation.25 | convolution fusion | flops 1220540928 | bytes 11016192 | tf_op jit(solution)/shard_map/dot_general | solution.py:224
  190.0 7.2 %collective-permute-done.19 = bf16[512,768]{1,0:T(8,128)(2,1)S(1)} collective-permute-done((bf16[512,768]{1,0:T(8,128)(2,1)}, bf16[512,768]{1,0:T(8,128)(2,1)S(1)}, u32[]{:S(2)}, u32[]{:S(2)}) %collective-permute-start.19) | collective-permute-done | bytes 786464 | tf_op jit(solution)/shard_map/ppermute | solution.py:16
  197.2 3.9 %convert_reduce_fusion = (f32[1536]{0:T(1024)S(1)}, bf16[512,1536]{1,0:T(8,128)(2,1)S(1)}) fusion(f32[512,1536]{1,0:T(8,128)S(1)} %copy-done.63, f32[512,1536]{1,0:T(8,128)S(1)} %copy-done.64, bf16[512,768]{1,0:T(8,128)(2,1)S(1)} %collective-permute-done.19, bf16[768,3074]{1,0:T(8,128)(2,1)} %all-gather.2.cloned.1.call-done), kind=kOutput, calls=%fused_computation.24 | convolution fusion | flops 1220540928 | bytes 11016192 | tf_op jit(solution)/shard_map/dot_general | solution.py:224
  201.2 4.0 %fusion.48 = bf16[512,768]{1,0:T(8,128)(2,1)} fusion(bf16[512,1536]{1,0:T(8,128)(2,1)S(1)} %get-tuple-element.124, bf16[768,3074]{1,0:T(8,128)(2,1)} %all-gather.2.cloned.1.call-done), kind=kOutput, calls=%fused_computation.108 | convolution fusion | flops 1208352768 | bytes 4718592 | tf_op jit(solution)/shard_map/dot_general | solution.py:169
  205.6 4.1 %add_convert_fusion.1 = bf16[768,1536]{1,0:T(8,128)(2,1)} fusion(f32[768,1536]{1,0:T(8,128)S(1)} %fusion.104, bf16[512,768]{1,0:T(8,128)(2,1)} %collective-permute-done.16, bf16[512,1536]{1,0:T(8,128)(2,1)S(1)} %get-tuple-element.124), kind=kOutput, calls=%fused_computation.18 | convolution fusion | flops 1210318848 | bytes 9437184 | tf_op jit(solution)/shard_map/dot_general | solution.py:163
  213.3 5.4 %pad_maximum_fusion.1 = bf16[768,3074]{1,0:T(8,128)(2,1)} fusion(bf16[768,2]{1,0:T(8,128)(2,1)S(1)} %add.340, bf16[768,1536]{1,0:T(8,128)(2,1)} %add_convert_fusion, bf16[768,1536]{1,0:T(8,128)(2,1)} %add_convert_fusion.1), kind=kLoop, calls=%fused_computation.13 | loop fusion | flops 14164992 | bytes 9443328 | tf_op jit(solution)/shard_map/concatenate | solution.py:382
  221.8 4.0 %convert_add_fusion.3 = f32[512,768]{1,0:T(8,128)S(1)} fusion(bf16[512,768]{1,0:T(8,128)(2,1)} %collective-permute-done.20, bf16[512,1536]{1,0:T(8,128)(2,1)} %copy-done.32, bf16[768,3074]{1,0:T(8,128)(2,1)} %all-gather.2.cloned.1.call-done), kind=kOutput, calls=%fused_computation.81 | convolution fusion | flops 1208745984 | bytes 6291456 | tf_op jit(solution)/shard_map/dot_general | solution.py:169
  231.0 9.6 %fusion.54 = bf16[12,64,512]{2,1,0:T(8,128)(2,1)} fusion(bf16[512,12,64]{0,2,1:T(8,128)(2,1)} %bitcast.187, f32[12,512]{1,0:T(8,128)S(1)} %copy-done.47, f32[12,512,512]{1,2,0:T(8,128)} %copy-done.2, pred[512,512]{0,1:T(8,128)(4,1)S(1)} %copy-done.14), kind=kOutput, calls=%fused_computation.110 | convolution fusion | flops 415629312 | bytes 14442496 | tf_op jit(solution)/shard_map/phqk,pqhd->pkhd/dot_general | solution.py:196
  240.6 10.1 %multiply_reduce_fusion = (f32[12,512]{1,0:T(8,128)S(1)}, f32[12,512,512]{1,2,0:T(8,128)}) fusion(f32[12,512]{1,0:T(8,128)S(1)} %copy-done.47, f32[12,512,512]{1,2,0:T(8,128)} %copy-done.2, pred[512,512]{0,1:T(8,128)(4,1)S(1)} %copy-done.14, bf16[512,12,64]{0,2,1:T(8,128)(2,1)S(1)} %bitcast.188, bf16[512,12,64]{0,2,1:T(8,128)(2,1)S(1)} %bitcast.186), kind=kOutput, calls=%fused_computation.1 | convolution fusion | flops 418375680 | bytes 27049984 | tf_op jit(solution)/shard_map/pqhd,pkhd->phqk/dot_general | solution.py:202
  250.7 7.1 %multiply_convert_fusion = bf16[12,512,512]{1,2,0:T(8,128)(2,1)S(1)} fusion(f32[12,512,512]{1,2,0:T(8,128)} %get-tuple-element.120, f32[12,512]{1,0:T(8,128)S(1)} %get-tuple-element.119, f32[12,512]{1,0:T(8,128)S(1)} %copy-done.47, f32[12,512,512]{1,2,0:T(8,128)S(1)} %bitcast.173, pred[512,512]{0,1:T(8,128)(4,1)S(1)} %copy-done.14), kind=kLoop, calls=%fused_computation | loop fusion | flops 18874368 | bytes 31768576 | tf_op jit(solution)/shard_map/convert_element_type | solution.py:206
  277.0 3.2 convolution_convert_fusion.1
  287.7 8.8 %concatenate.125 = bf16[32,24,3081]{2,1,0:T(8,128)(2,1)} concatenate(bf16[32,24,2304]{2,1,0:T(8,128)(2,1)S(1)} %bitcast.175, bf16[32,24,3]{2,1,0:T(8,128)(2,1)} %bitcast.199, bf16[32,24,768]{2,1,0:T(8,128)(2,1)} %convolution_convert_fusion.1, bf16[32,24,1]{2,1,0:T(8,128)(2,1)} %stack.65, bf16[32,24,1]{2,1,0:T(8,128)(2,1)} %stack.66, bf16[32,24,1]{2,1,0:T(8,128)(2,1)} %stack.67, ...), dimensions={2} | concatenate | bytes 9464832 | tf_op jit(solution)/shard_map/concatenate | solution.py:430
  305.0 13.1 %collective-permute-done.22 = f32[256,768]{1,0:T(8,128)} collective-permute-done((f32[256,768]{1,0:T(8,128)}, f32[256,768]{1,0:T(8,128)}, u32[]{:S(2)}, u32[]{:S(2)}) %collective-permute-start.22) | collective-permute-done | bytes 786464 | tf_op jit(solution)/shard_map/ppermute | solution.py:16
  324.6 9.6 %collective-permute-done.29 = bf16[2,2,2,24,1033]{4,3,2,1,0:T(8,128)(2,1)S(1)} collective-permute-done((bf16[2,2,2,24,1033]{4,3,2,1,0:T(8,128)(2,1)S(1)}, bf16[2,2,2,24,1033]{4,3,2,1,0:T(8,128)(2,1)S(1)}, u32[]{:S(2)}, u32[]{:S(2)}) %collective-permute-start.29) | collective-permute-done | bytes 396704 | tf_op jit(solution)/shard_map/ppermute | solution.py:79
  340.1 7.0 %collective-permute-done.30 = bf16[2,2,24,1033]{3,2,1,0:T(8,128)(2,1)S(1)} collective-permute-done((bf16[2,2,24,1033]{3,2,1,0:T(8,128)(2,1)S(1)}, bf16[2,2,24,1033]{3,2,1,0:T(8,128)(2,1)S(1)}, u32[]{:S(2)}, u32[]{:S(2)}) %collective-permute-start.30) | collective-permute-done | bytes 198368 | tf_op jit(solution)/shard_map/ppermute | solution.py:79
  (359 shorter events, 164.6 us)
Async XLA Ops:
  7.2 117.7 %all-gather.2.cloned.1.call-start = ((), (), s32[]{:S(2)}) async-start(), calls=%async_computation.1 | async-start | bytes 5222400 | tf_op jit(solution)/shard_map/all_gather | solution.py:291
  9.6 13.2 %collective-permute-start.11 = (bf16[24,1152]{1,0:T(8,128)(2,1)S(1)}, bf16[24,1152]{1,0:T(8,128)(2,1)S(1)}, u32[]{:S(2)}, u32[]{:S(2)}) collective-permute-start(bf16[24,1152]{1,0:T(8,128)(2,1)S(1)} %fusion.79), channel_id=1, source_target_pairs={{0,1},{1,0},{2,3},{3,2},{4,5},{5,4},{6,7},{7,6},{8,9},{9,8},{10,11... | collective-permute-start | bytes 165896 | tf_op jit(solution)/shard_map/ppermute | solution.py:46
  29.3 20.5 %collective-permute-start.13 = (bf16[2,2,24,1152]{3,2,1,0:T(8,128)(2,1)S(1)}, bf16[2,2,24,1152]{3,2,1,0:T(8,128)(2,1)S(1)}, u32[]{:S(2)}, u32[]{:S(2)}) collective-permute-start(bf16[2,2,24,1152]{3,2,1,0:T(8,128)(2,1)S(1)} %broadcast_select_fusion.11), channel_id=1, source_target_pairs={{0,16},{1,17},{2,18},{3,19},{4,20},{5,21},{6,22},{7,23},{8,24},{9,... | collective-permute-start | bytes 663560 | tf_op jit(solution)/shard_map/ppermute | solution.py:46
  32.0 34.6 %collective-permute-start.9 = (bf16[2,2,2,24,1024]{4,3,2,0,1:T(8,128)(2,1)S(1)}, bf16[2,2,2,24,1024]{4,3,2,0,1:T(8,128)(2,1)S(1)}, u32[]{:S(2)}, u32[]{:S(2)}) collective-permute-start(bf16[2,2,2,24,1024]{4,3,2,0,1:T(8,128)(2,1)S(1)} %broadcast_select_fusion.7), channel_id=1, source_target_pairs={{0,16},{1,17},{2,18},{3,19},{4,20},{5,21},{6,22},{7,23},{8,24},{9,... | collective-permute-start | bytes 1179656 | tf_op jit(solution)/shard_map/ppermute | solution.py:46
  34.8 15.4 %collective-permute-start.4 = (bf16[2,2,2,24,1024]{4,3,2,0,1:T(8,128)(2,1)S(1)}, bf16[2,2,2,24,1024]{4,3,2,0,1:T(8,128)(2,1)S(1)}, u32[]{:S(2)}, u32[]{:S(2)}) collective-permute-start(bf16[2,2,2,24,1024]{4,3,2,0,1:T(8,128)(2,1)S(1)} %broadcast_select_fusion.9), channel_id=1, source_target_pairs={{0,4},{1,5},{2,6},{3,7},{4,0},{5,1},{6,2},{7,3},{8,12},{9,13},{10,... | collective-permute-start | bytes 1179656 | tf_op jit(solution)/shard_map/ppermute | solution.py:46
  50.0 16.4 %collective-permute-start.14 = (bf16[2,2,2,24,1152]{4,3,2,1,0:T(8,128)(2,1)S(1)}, bf16[2,2,2,24,1152]{4,3,2,1,0:T(8,128)(2,1)S(1)}, u32[]{:S(2)}, u32[]{:S(2)}) collective-permute-start(bf16[2,2,2,24,1152]{4,3,2,1,0:T(8,128)(2,1)S(1)} %broadcast_select_fusion.6), channel_id=1, source_target_pairs={{0,8},{1,9},{2,10},{3,11},{4,12},{5,13},{6,14},{7,15},{8,0},{9,1},... | collective-permute-start | bytes 1327112 | tf_op jit(solution)/shard_map/ppermute | solution.py:46
  50.3 17.8 %collective-permute-start.5 = (bf16[2,2,2,2,24,1024]{5,4,3,0,1,2:T(8,128)(2,1)S(1)}, bf16[2,2,2,2,24,1024]{5,4,3,0,1,2:T(8,128)(2,1)S(1)}, u32[]{:S(2)}, u32[]{:S(2)}) collective-permute-start(bf16[2,2,2,2,24,1024]{5,4,3,0,1,2:T(8,128)(2,1)S(1)} %broadcast_select_fusion.4), channel_id=1, source_target_pairs={{0,2},{1,3},{2,0},{3,1},{4,6},{5,7},{6,4},{7,5},{8,10},{9,11},{10,... | collective-permute-start | bytes 2359304 | tf_op jit(solution)/shard_map/ppermute | solution.py:46
  74.1 283.7 %reduce-scatter.2.cloned.1.call-start = ((), (), s32[]{:S(2)}) async-start(), calls=%async_computation.2 | async-start | bytes 5222400 | tf_op jit(solution)/shard_map/reduce_scatter | solution.py:383
  89.4 30.8 %collective-permute-start.18 = (bf16[256,768]{1,0:T(8,128)(2,1)}, bf16[256,768]{1,0:T(8,128)(2,1)}, u32[]{:S(2)}, u32[]{:S(2)}) collective-permute-start(bf16[256,768]{1,0:T(8,128)(2,1)} %get-tuple-element.89), channel_id=1, source_target_pairs={{0,1},{1,0},{2,3},{3,2},{4,5},{5,4},{6,7},{7,6},{8,9},{9,8},{10,11... | collective-permute-start | bytes 1179656 | tf_op jit(solution)/shard_map/ppermute | solution.py:16
  118.3 19.0 %collective-permute-start.16 = (bf16[512,768]{1,0:T(8,128)(2,1)S(1)}, bf16[512,768]{1,0:T(8,128)(2,1)}, u32[]{:S(2)}, u32[]{:S(2)}) collective-permute-start(bf16[512,768]{1,0:T(8,128)(2,1)S(1)} %fusion.58), channel_id=1, source_target_pairs={{0,1},{1,0},{2,3},{3,2},{4,5},{5,4},{6,7},{7,6},{8,9},{9,8},{10,11... | collective-permute-start | bytes 2359304 | tf_op jit(solution)/shard_map/ppermute | solution.py:16
  149.7 18.1 %collective-permute-start.17 = (bf16[512,768]{1,0:T(8,128)(2,1)S(1)}, bf16[512,768]{1,0:T(8,128)(2,1)S(1)}, u32[]{:S(2)}, u32[]{:S(2)}) collective-permute-start(bf16[512,768]{1,0:T(8,128)(2,1)S(1)} %fusion.51), channel_id=1, source_target_pairs={{0,1},{1,0},{2,3},{3,2},{4,5},{5,4},{6,7},{7,6},{8,9},{9,8},{10,11... | collective-permute-start | bytes 2359304 | tf_op jit(solution)/shard_map/ppermute | solution.py:16
  179.9 17.3 %collective-permute-start.19 = (bf16[512,768]{1,0:T(8,128)(2,1)}, bf16[512,768]{1,0:T(8,128)(2,1)S(1)}, u32[]{:S(2)}, u32[]{:S(2)}) collective-permute-start(bf16[512,768]{1,0:T(8,128)(2,1)} %get-tuple-element.58), channel_id=1, source_target_pairs={{0,1},{1,0},{2,3},{3,2},{4,5},{5,4},{6,7},{7,6},{8,9},{9,8},{10,11... | collective-permute-start | bytes 2359304 | tf_op jit(solution)/shard_map/ppermute | solution.py:16
  205.2 16.6 %collective-permute-start.20 = (bf16[512,768]{1,0:T(8,128)(2,1)}, bf16[512,768]{1,0:T(8,128)(2,1)}, u32[]{:S(2)}, u32[]{:S(2)}) collective-permute-start(bf16[512,768]{1,0:T(8,128)(2,1)} %fusion.48), channel_id=1, source_target_pairs={{0,1},{1,0},{2,3},{3,2},{4,5},{5,4},{6,7},{7,6},{8,9},{9,8},{10,11... | collective-permute-start | bytes 2359304 | tf_op jit(solution)/shard_map/ppermute | solution.py:16
  269.9 28.6 %collective-permute-start.23 = (bf16[2,2,2,2,24,1024]{5,4,3,2,1,0:T(8,128)(2,1)}, bf16[2,2,2,2,24,1024]{5,4,3,2,1,0:T(8,128)(2,1)}, u32[]{:S(2)}, u32[]{:S(2)}) collective-permute-start(bf16[2,2,2,2,24,1024]{5,4,3,2,1,0:T(8,128)(2,1)} %dynamic-slice_bitcast_fusion.1), channel_id=1, source_target_pairs={{0,2},{1,3},{2,0},{3,1},{4,6},{5,7},{6,4},{7,5},{8,10},{9,11},{10,... | collective-permute-start | bytes 2359304 | tf_op jit(solution)/shard_map/ppermute | solution.py:79
  276.5 24.0 %collective-permute-start.33 = (bf16[2,2,2,2,24,1024]{5,4,3,1,2,0:T(8,128)(2,1)}, bf16[2,2,2,2,24,1024]{5,4,3,1,2,0:T(8,128)(2,1)}, u32[]{:S(2)}, u32[]{:S(2)}) collective-permute-start(bf16[2,2,2,2,24,1024]{5,4,3,1,2,0:T(8,128)(2,1)} %bitcast.171), channel_id=1, source_target_pairs={{0,2},{1,3},{2,0},{3,1},{4,6},{5,7},{6,4},{7,5},{8,10},{9,11},{10,... | collective-permute-start | bytes 2359304 | tf_op jit(solution)/shard_map/ppermute | solution.py:79
  281.5 20.7 %collective-permute-start.21 = (f32[256,768]{1,0:T(8,128)}, f32[256,768]{1,0:T(8,128)}, u32[]{:S(2)}, u32[]{:S(2)}) collective-permute-start(f32[256,768]{1,0:T(8,128)} %get-tuple-element.88), channel_id=1, source_target_pairs={{0,1},{1,0},{2,3},{3,2},{4,5},{5,4},{6,7},{7,6},{8,9},{9,8},{10,11... | collective-permute-start | bytes 2359304 | tf_op jit(solution)/shard_map/ppermute | solution.py:16
  285.7 32.4 %collective-permute-start.22 = (f32[256,768]{1,0:T(8,128)}, f32[256,768]{1,0:T(8,128)}, u32[]{:S(2)}, u32[]{:S(2)}) collective-permute-start(f32[256,768]{1,0:T(8,128)} %get-tuple-element.31), channel_id=1, source_target_pairs={{0,1},{1,0},{2,3},{3,2},{4,5},{5,4},{6,7},{7,6},{8,9},{9,8},{10,11... | collective-permute-start | bytes 2359304 | tf_op jit(solution)/shard_map/ppermute | solution.py:16
  298.4 22.4 %collective-permute-start.28 = (bf16[2,2,2,2,24,1033]{5,4,3,2,1,0:T(8,128)(2,1)S(1)}, bf16[2,2,2,2,24,1033]{5,4,3,2,1,0:T(8,128)(2,1)S(1)}, u32[]{:S(2)}, u32[]{:S(2)}) collective-permute-start(bf16[2,2,2,2,24,1033]{5,4,3,2,1,0:T(8,128)(2,1)S(1)} %dynamic-slice_bitcast_fusion), channel_id=1, source_target_pairs={{0,2},{1,3},{2,0},{3,1},{4,6},{5,7},{6,4},{7,5},{8,10},{9,11},{10,... | collective-permute-start | bytes 2380040 | tf_op jit(solution)/shard_map/ppermute | solution.py:79
  300.1 22.4 %collective-permute-start.24 = (bf16[2,2,2,24,1024]{4,3,2,1,0:T(8,128)(2,1)S(1)}, bf16[2,2,2,24,1024]{4,3,2,1,0:T(8,128)(2,1)S(1)}, u32[]{:S(2)}, u32[]{:S(2)}) collective-permute-start(bf16[2,2,2,24,1024]{4,3,2,1,0:T(8,128)(2,1)S(1)} %fusion.70), channel_id=1, source_target_pairs={{0,4},{1,5},{2,6},{3,7},{4,0},{5,1},{6,2},{7,3},{8,12},{9,13},{10,... | collective-permute-start | bytes 1179656 | tf_op jit(solution)/shard_map/ppermute | solution.py:79
  302.1 21.3 %collective-permute-start.34 = (bf16[2,2,2,24,1024]{4,3,2,0,1:T(8,128)(2,1)S(1)}, bf16[2,2,2,24,1024]{4,3,2,0,1:T(8,128)(2,1)S(1)}, u32[]{:S(2)}, u32[]{:S(2)}) collective-permute-start(bf16[2,2,2,24,1024]{4,3,2,0,1:T(8,128)(2,1)S(1)} %fusion.71), channel_id=1, source_target_pairs={{0,16},{1,17},{2,18},{3,19},{4,20},{5,21},{6,22},{7,23},{8,24},{9,... | collective-permute-start | bytes 1179656 | tf_op jit(solution)/shard_map/ppermute | solution.py:79
  321.1 13.1 %collective-permute-start.29 = (bf16[2,2,2,24,1033]{4,3,2,1,0:T(8,128)(2,1)S(1)}, bf16[2,2,2,24,1033]{4,3,2,1,0:T(8,128)(2,1)S(1)}, u32[]{:S(2)}, u32[]{:S(2)}) collective-permute-start(bf16[2,2,2,24,1033]{4,3,2,1,0:T(8,128)(2,1)S(1)} %fusion.65), channel_id=1, source_target_pairs={{0,8},{1,9},{2,10},{3,11},{4,12},{5,13},{6,14},{7,15},{8,0},{9,1},... | collective-permute-start | bytes 1190024 | tf_op jit(solution)/shard_map/ppermute | solution.py:79
  322.6 14.9 %collective-permute-start.25 = (bf16[2,2,24,1024]{3,2,1,0:T(8,128)(2,1)S(1)}, bf16[2,2,24,1024]{3,2,1,0:T(8,128)(2,1)S(1)}, u32[]{:S(2)}, u32[]{:S(2)}) collective-permute-start(bf16[2,2,24,1024]{3,2,1,0:T(8,128)(2,1)S(1)} %fusion.73), channel_id=1, source_target_pairs={{0,8},{1,9},{2,10},{3,11},{4,12},{5,13},{6,14},{7,15},{8,0},{9,1},... | collective-permute-start | bytes 589832 | tf_op jit(solution)/shard_map/ppermute | solution.py:79
  323.5 14.1 %collective-permute-start.35 = (bf16[2,2,24,1024]{3,2,1,0:T(8,128)(2,1)S(1)}, bf16[2,2,24,1024]{3,2,1,0:T(8,128)(2,1)S(1)}, u32[]{:S(2)}, u32[]{:S(2)}) collective-permute-start(bf16[2,2,24,1024]{3,2,1,0:T(8,128)(2,1)S(1)} %fusion.74), channel_id=1, source_target_pairs={{0,4},{1,5},{2,6},{3,7},{4,0},{5,1},{6,2},{7,3},{8,12},{9,13},{10,... | collective-permute-start | bytes 589832 | tf_op jit(solution)/shard_map/ppermute | solution.py:79
  334.3 12.7 %collective-permute-start.30 = (bf16[2,2,24,1033]{3,2,1,0:T(8,128)(2,1)S(1)}, bf16[2,2,24,1033]{3,2,1,0:T(8,128)(2,1)S(1)}, u32[]{:S(2)}, u32[]{:S(2)}) collective-permute-start(bf16[2,2,24,1033]{3,2,1,0:T(8,128)(2,1)S(1)} %fusion.72), channel_id=1, source_target_pairs={{0,16},{1,17},{2,18},{3,19},{4,20},{5,21},{6,22},{7,23},{8,24},{9,... | collective-permute-start | bytes 595016 | tf_op jit(solution)/shard_map/ppermute | solution.py:79
  (86 other events, 656.6 us)
Sparse Core Ops, SparseCore 0:
  74.3 50.6 all-gather.1
  218.8 73.3 reduce-scatter.1

commit v7 on v4

--- a/solution.py
+++ b/solution.py
@@ -98,6 +98,18 @@
         for (a, b), order in zip(splits, orders)
     ]
     return jnp.concatenate(pieces, axis=-1)
+
+
+def scatter_sum_parts(part_list):
+    total = lax.axis_size("wide") * lax.axis_size("narrow")
+    narrow_n = lax.axis_size("narrow")
+    if not (is_pow2(total) and is_pow2(narrow_n)):
+        return jnp.concatenate([scatter_sum_all(x, 1) for x in part_list], axis=-1)
+    orders = part_orders(total, narrow_n, len(part_list))
+    return jnp.concatenate(
+        [halving_scatter(x, list(reversed(o)), total) for x, o in zip(part_list, orders)],
+        axis=-1,
+    )
 
 
 def narrow_gather(rows):
@@ -426,15 +438,22 @@
     )
     qkv_wsum = contract_rows(pack_in, grad_qkv)
     qkv_bsum = jnp.sum(grad_qkv.astype(jnp.float32), axis=0).reshape(3, D)
-    late = jnp.concatenate(
+    wsum_parts = qkv_wsum.reshape(total, share, 3 * D).astype(jnp.bfloat16)
+    cut = 3 * D * 4 // 9 // 128 * 128
+    late_mine = scatter_sum_parts(
         [
-            qkv_wsum.reshape(total, share, 3 * D).astype(jnp.bfloat16),
-            qkv_bsum.T.reshape(total, share, 3).astype(jnp.bfloat16),
-            early.astype(jnp.bfloat16),
-        ],
-        axis=2,
-    )
-    late_mine = scatter_sum_all(late)
+            wsum_parts[..., :cut],
+            wsum_parts[..., cut : 2 * cut],
+            jnp.concatenate(
+                [
+                    wsum_parts[..., 2 * cut :],
+                    qkv_bsum.T.reshape(total, share, 3).astype(jnp.bfloat16),
+                    early.astype(jnp.bfloat16),
+                ],
+                axis=2,
+            ),
+        ]
+    )
     early_mine = late_mine[:, 3 * D + 3 :]
     query_wgrad = late_mine[:, :D]
     key_wgrad = late_mine[:, D : 2 * D]

time: 370 us -> 367 us (level)
  waiting for transfers between devices: 109 us -> 119 us
  local copies, waits for them, and re-layouts: 55.6 us -> 47.8 us
    ppermute x8, waiting for transfers between devices: 42.4 us -> 51.2 us  [swapped(): lax.ppermute(shard, axis, [(i, i ^ 1 << bit) for i in range(lax.axis_size...]
    concatenate x1, local copies, waits for them, and re-layouts: 8.84 us -> 4.59 us  [local(): jnp.concatenate([wsum_parts[..., 2 * cut:], qkv_bsum.T.reshape(total, sha...]
  transfers between devices with their start and end apart: 40 -> 40, of which waited for: 21 -> 19; matrix products, arithmetic and copies ran while one was open for 43% -> 40% of each run, Pallas kernels for 0% -> 0%
where the time goes in v7:
time: 367 us; the launch traced here: 362 us
  waiting for transfers between devices  119 us (32%)
  matrix products  90.9 us (25%)
  other arithmetic  53.9 us (15%)
  local copies, waits for them, and re-layouts  47.8 us (13%)
  starting transfers between devices  35.4 us (10%)
  between operations  15.8 us (4%)
    ppermute x8, waiting for transfers between devices, swapped(): lax.ppermute(shard, axis, [(i, i ^ 1 << bit) for i in range(lax.axis_size...  51.2 us
    ppermute x15, waiting for transfers between devices, doubling_gather(): other = lax.ppermute(cur, ALL, [(i, i ^ 1 << b) for i in range(total)])  36.3 us
    ppermute x15, waiting for transfers between devices, halving_scatter(): lax.ppermute(theirs.astype(jnp.bfloat16), ALL, [(i, i ^ 1 << b) for i in...  26 us
    dot_general x2, matrix products, ffn_forward(): jnp.dot(rows, inner_cols, preferred_element_type=jnp.float32) + inner_offset  21 us
    ppermute x15, starting transfers between devices, doubling_gather(): other = lax.ppermute(cur, ALL, [(i, i ^ 1 << b) for i in range(total)])  18.2 us
    dot_general x6, matrix products, contract_cols(): lax.dot_general(left_op, right_op, (((1,), (1,)), ((), ())), preferred_el...  14 us
    dot_general x6, matrix products, contract_rows(): lax.dot_general(left_op, right_op, (((0,), (0,)), ((), ())), preferred_el...  13.9 us
    dot_general x2, matrix products, ffn_backward(): grad_act = jnp.dot(grads, outer_cols, preferred_element_type=jnp.float32)  10 us
  transfers between devices with their start and end apart: 40, of which 19 were waited for; matrix products, arithmetic and copies ran while one was open for 40% of the time, Pallas kernels for 0%

profile of v7, /device:TPU:0, one launch (start us, length us, event | category | flops | bytes accessed | tf_op | source)
XLA Modules:
  0.0 362.4 jit_solution(434644807900255123)
XLA Ops:
  36.0 13.8 %collective-permute-done.13 = bf16[2,2,24,1152]{3,2,1,0:T(8,128)(2,1)S(1)} collective-permute-done((bf16[2,2,24,1152]{3,2,1,0:T(8,128)(2,1)S(1)}, bf16[2,2,24,1152]{3,2,1,0:T(8,128)(2,1)S(1)}, u32[]{:S(2)}, u32[]{:S(2)}) %collective-permute-start.13) | collective-permute-done | bytes 221216 | tf_op jit(solution)/shard_map/ppermute | solution.py:46
  50.4 16.0 %collective-permute-done.14 = bf16[2,2,2,24,1152]{4,3,2,1,0:T(8,128)(2,1)S(1)} collective-permute-done((bf16[2,2,2,24,1152]{4,3,2,1,0:T(8,128)(2,1)S(1)}, bf16[2,2,2,24,1152]{4,3,2,1,0:T(8,128)(2,1)S(1)}, u32[]{:S(2)}, u32[]{:S(2)}) %collective-permute-start.14) | collective-permute-done | bytes 442400 | tf_op jit(solution)/shard_map/ppermute | solution.py:46
  81.0 6.6 %collective-permute-done = bf16[256,768]{1,0:T(8,128)(2,1)S(1)} collective-permute-done((bf16[256,768]{1,0:T(8,128)(2,1)}, bf16[256,768]{1,0:T(8,128)(2,1)S(1)}, u32[]{:S(2)}, u32[]{:S(2)}) %collective-permute-start) | collective-permute-done | bytes 393248 | tf_op jit(solution)/shard_map/ppermute | solution.py:16
  110.8 4.0 %fusion.57 = bf16[12,64,512]{2,1,0:T(8,128)(2,1)S(1)} fusion(bf16[512,12,64]{0,2,1:T(8,128)(2,1)S(1)} %bitcast.189, f32[12,512]{1,0:T(8,128)S(1)} %fusion, f32[12,512]{1,0:T(8,128)S(1)} %get-tuple-element.111, f32[12,512,512]{1,2,0:T(8,128)S(1)} %get-tuple-element.112, pred[512,512]{0,1:T(8,128)(4,1)S(1)} %copy-done.10), kind=kOutput, calls=%fused_computation.111 | convolution fusion | flops 418775040 | bytes 14467072 | tf_op jit(solution)/shard_map/phqk,pkhd->pqhd/dot_general | solution.py:200
  119.9 5.1 %all-gather.2.cloned.1.call-done = bf16[768,3074]{1,0:T(8,128)(2,1)} async-done(((bf16[48,3074]{1,0:T(8,128)(2,1)}), bf16[768,3074]{1,0:T(8,128)(2,1)}) %all-gather.2.cloned.1.call-update) | async-done | bytes 4721680 | tf_op jit(solution)/shard_map/all_gather | solution.py:303
  126.1 8.5 %collective-permute-done.16 = bf16[512,768]{1,0:T(8,128)(2,1)} collective-permute-done((bf16[512,768]{1,0:T(8,128)(2,1)S(1)}, bf16[512,768]{1,0:T(8,128)(2,1)}, u32[]{:S(2)}, u32[]{:S(2)}) %collective-permute-start.16) | collective-permute-done | bytes 786464 | tf_op jit(solution)/shard_map/ppermute | solution.py:16
  134.6 11.0 %multiply_convert_fusion.1 = (bf16[512,1536]{1,0:T(8,128)(2,1)S(1)}, f32[512,1536]{1,0:T(8,128)}, f32[512,1536]{1,0:T(8,128)}) fusion(f32[1536]{0:T(1024)S(1)} %reshape.633, bf16[512,768]{1,0:T(8,128)(2,1)} %collective-permute-done.16, bf16[768,3074]{1,0:T(8,128)(2,1)} %all-gather.2.cloned.1.call-done), kind=kOutput, calls=%fused_computation.28 | convolution fusion | flops 1259864064 | bytes 11016192 | tf_op jit(solution)/shard_map/dot_general | solution.py:229
  147.8 10.0 %multiply_convert_fusion.2 = (bf16[512,1536]{1,0:T(8,128)(2,1)S(1)}, f32[512,1536]{1,0:T(8,128)}, f32[512,1536]{1,0:T(8,128)}) fusion(f32[1536]{0:T(1024)S(1)} %reshape.633, bf16[512,768]{1,0:T(8,128)(2,1)S(1)} %fusion.58, bf16[768,3074]{1,0:T(8,128)(2,1)S(1)} %copy-done.58), kind=kOutput, calls=%fused_computation.41 | convolution fusion | flops 1259864064 | bytes 11018240 | tf_op jit(solution)/shard_map/dot_general | solution.py:229
  157.8 6.4 %collective-permute-done.17 = bf16[512,768]{1,0:T(8,128)(2,1)S(1)} collective-permute-done((bf16[512,768]{1,0:T(8,128)(2,1)S(1)}, bf16[512,768]{1,0:T(8,128)(2,1)S(1)}, u32[]{:S(2)}, u32[]{:S(2)}) %collective-permute-start.17) | collective-permute-done | bytes 786464 | tf_op jit(solution)/shard_map/ppermute | solution.py:16
  177.6 6.1 %convert_reduce_fusion.1 = (f32[1536]{0:T(1024)S(1)}, bf16[512,1536]{1,0:T(8,128)(2,1)S(1)}) fusion(f32[512,1536]{1,0:T(8,128)} %get-tuple-element.63, f32[512,1536]{1,0:T(8,128)} %get-tuple-element.116, bf16[512,768]{1,0:T(8,128)(2,1)} %get-tuple-element.54, bf16[768,3074]{1,0:T(8,128)(2,1)} %all-gather.2.cloned.1.call-done), kind=kOutput, calls=%fused_computation.25 | convolution fusion | flops 1220540928 | bytes 11016192 | tf_op jit(solution)/shard_map/dot_general | solution.py:236
  186.9 6.0 %collective-permute-done.19 = bf16[512,768]{1,0:T(8,128)(2,1)S(1)} collective-permute-done((bf16[512,768]{1,0:T(8,128)(2,1)}, bf16[512,768]{1,0:T(8,128)(2,1)S(1)}, u32[]{:S(2)}, u32[]{:S(2)}) %collective-permute-start.19) | collective-permute-done | bytes 786464 | tf_op jit(solution)/shard_map/ppermute | solution.py:16
  196.9 4.0 %fusion.48 = bf16[512,768]{1,0:T(8,128)(2,1)} fusion(bf16[512,1536]{1,0:T(8,128)(2,1)S(1)} %get-tuple-element.124, bf16[768,3074]{1,0:T(8,128)(2,1)} %all-gather.2.cloned.1.call-done), kind=kOutput, calls=%fused_computation.108 | convolution fusion | flops 1208352768 | bytes 4718592 | tf_op jit(solution)/shard_map/dot_general | solution.py:181
  202.6 4.0 %add_convert_fusion.1 = bf16[768,1536]{1,0:T(8,128)(2,1)} fusion(f32[768,1536]{1,0:T(8,128)S(1)} %fusion.104, bf16[512,768]{1,0:T(8,128)(2,1)} %collective-permute-done.16, bf16[512,1536]{1,0:T(8,128)(2,1)S(1)} %get-tuple-element.124), kind=kOutput, calls=%fused_computation.18 | convolution fusion | flops 1210318848 | bytes 9437184 | tf_op jit(solution)/shard_map/dot_general | solution.py:175
  210.2 5.4 %pad_maximum_fusion.1 = bf16[768,3074]{1,0:T(8,128)(2,1)} fusion(bf16[768,2]{1,0:T(8,128)(2,1)S(1)} %add.340, bf16[768,1536]{1,0:T(8,128)(2,1)} %add_convert_fusion, bf16[768,1536]{1,0:T(8,128)(2,1)} %add_convert_fusion.1), kind=kLoop, calls=%fused_computation.13 | loop fusion | flops 14164992 | bytes 9443328 | tf_op jit(solution)/shard_map/concatenate | solution.py:393
  217.2 4.0 %convert_add_fusion.3 = f32[512,768]{1,0:T(8,128)S(1)} fusion(bf16[512,768]{1,0:T(8,128)(2,1)} %collective-permute-done.20, bf16[512,1536]{1,0:T(8,128)(2,1)} %copy-done.29, bf16[768,3074]{1,0:T(8,128)(2,1)} %all-gather.2.cloned.1.call-done), kind=kOutput, calls=%fused_computation.81 | convolution fusion | flops 1208745984 | bytes 6291456 | tf_op jit(solution)/shard_map/dot_general | solution.py:181
  226.4 9.8 %fusion.54 = bf16[12,64,512]{2,1,0:T(8,128)(2,1)} fusion(bf16[512,12,64]{0,2,1:T(8,128)(2,1)} %bitcast.191, f32[12,512]{1,0:T(8,128)S(1)} %copy-done.45, f32[12,512,512]{1,2,0:T(8,128)} %copy-done.2, pred[512,512]{0,1:T(8,128)(4,1)S(1)} %copy-done.11), kind=kOutput, calls=%fused_computation.110 | convolution fusion | flops 415629312 | bytes 14442496 | tf_op jit(solution)/shard_map/phqk,pqhd->pkhd/dot_general | solution.py:208
  236.1 10.0 %multiply_reduce_fusion = (f32[12,512]{1,0:T(8,128)S(1)}, f32[12,512,512]{1,2,0:T(8,128)}) fusion(f32[12,512]{1,0:T(8,128)S(1)} %copy-done.45, f32[12,512,512]{1,2,0:T(8,128)} %copy-done.2, pred[512,512]{0,1:T(8,128)(4,1)S(1)} %copy-done.11, bf16[512,12,64]{0,2,1:T(8,128)(2,1)S(1)} %bitcast.192, bf16[512,12,64]{0,2,1:T(8,128)(2,1)S(1)} %bitcast.190), kind=kOutput, calls=%fused_computation.1 | convolution fusion | flops 418375680 | bytes 27049984 | tf_op jit(solution)/shard_map/pqhd,pkhd->phqk/dot_general | solution.py:214
  246.2 7.2 %multiply_convert_fusion = bf16[12,512,512]{1,2,0:T(8,128)(2,1)S(1)} fusion(f32[12,512,512]{1,2,0:T(8,128)} %get-tuple-element.120, f32[12,512]{1,0:T(8,128)S(1)} %get-tuple-element.119, f32[12,512]{1,0:T(8,128)S(1)} %copy-done.45, f32[12,512,512]{1,2,0:T(8,128)S(1)} %bitcast.179, pred[512,512]{0,1:T(8,128)(4,1)S(1)} %copy-done.11), kind=kLoop, calls=%fused_computation | loop fusion | flops 18874368 | bytes 31768576 | tf_op jit(solution)/shard_map/convert_element_type | solution.py:218
  276.9 4.6 %concatenate.125 = bf16[32,24,1033]{2,1,0:T(8,128)(2,1)S(1)} concatenate(bf16[32,24,256]{2,1,0:T(8,128)(2,1)S(1)} %slice.236, bf16[32,24,3]{2,1,0:T(8,128)(2,1)S(1)} %bitcast.201, bf16[32,24,768]{2,1,0:T(8,128)(2,1)} %convolution_convert_fusion.1, bf16[32,24,1]{2,1,0:T(8,128)(2,1)} %stack.65, bf16[32,24,1]{2,1,0:T(8,128)(2,1)} %stack.66, bf16[32,24,1]{2,1,0:T(8,128)(2,1)} %stack.67, ...), dimensions={2} | concatenate | bytes 3173376 | tf_op jit(solution)/shard_map/concatenate | solution.py:447
  285.9 9.1 %collective-permute-done.21 = f32[256,768]{1,0:T(8,128)} collective-permute-done((f32[256,768]{1,0:T(8,128)}, f32[256,768]{1,0:T(8,128)}, u32[]{:S(2)}, u32[]{:S(2)}) %collective-permute-start.21) | collective-permute-done | bytes 786464 | tf_op jit(solution)/shard_map/ppermute | solution.py:16
  297.7 13.1 %collective-permute-done.22 = f32[256,768]{1,0:T(8,128)} collective-permute-done((f32[256,768]{1,0:T(8,128)}, f32[256,768]{1,0:T(8,128)}, u32[]{:S(2)}, u32[]{:S(2)}) %collective-permute-start.22) | collective-permute-done | bytes 786464 | tf_op jit(solution)/shard_map/ppermute | solution.py:16
  316.4 10.6 %collective-permute-done.29 = bf16[2,2,2,24,1033]{4,3,2,1,0:T(8,128)(2,1)S(1)} collective-permute-done((bf16[2,2,2,24,1033]{4,3,2,1,0:T(8,128)(2,1)S(1)}, bf16[2,2,2,24,1033]{4,3,2,1,0:T(8,128)(2,1)S(1)}, u32[]{:S(2)}, u32[]{:S(2)}) %collective-permute-start.29) | collective-permute-done | bytes 396704 | tf_op jit(solution)/shard_map/ppermute | solution.py:79
  328.7 4.1 %collective-permute-done.25 = bf16[2,2,24,1024]{3,2,1,0:T(8,128)(2,1)S(1)} collective-permute-done((bf16[2,2,24,1024]{3,2,1,0:T(8,128)(2,1)S(1)}, bf16[2,2,24,1024]{3,2,1,0:T(8,128)(2,1)S(1)}, u32[]{:S(2)}, u32[]{:S(2)}) %collective-permute-start.25) | collective-permute-done | bytes 196640 | tf_op jit(solution)/shard_map/ppermute | solution.py:79
  333.0 6.9 %collective-permute-done.30 = bf16[2,2,24,1033]{3,2,1,0:T(8,128)(2,1)S(1)} collective-permute-done((bf16[2,2,24,1033]{3,2,1,0:T(8,128)(2,1)S(1)}, bf16[2,2,24,1033]{3,2,1,0:T(8,128)(2,1)S(1)}, u32[]{:S(2)}, u32[]{:S(2)}) %collective-permute-start.30) | collective-permute-done | bytes 198368 | tf_op jit(solution)/shard_map/ppermute | solution.py:79
  (359 shorter events, 160.4 us)
Async XLA Ops:
  7.2 117.7 %all-gather.2.cloned.1.call-start = ((), (), s32[]{:S(2)}) async-start(), calls=%async_computation.1 | async-start | bytes 5222400 | tf_op jit(solution)/shard_map/all_gather | solution.py:303
  9.6 13.2 %collective-permute-start.11 = (bf16[24,1152]{1,0:T(8,128)(2,1)S(1)}, bf16[24,1152]{1,0:T(8,128)(2,1)S(1)}, u32[]{:S(2)}, u32[]{:S(2)}) collective-permute-start(bf16[24,1152]{1,0:T(8,128)(2,1)S(1)} %fusion.79), channel_id=1, source_target_pairs={{0,1},{1,0},{2,3},{3,2},{4,5},{5,4},{6,7},{7,6},{8,9},{9,8},{10,11... | collective-permute-start | bytes 165896 | tf_op jit(solution)/shard_map/ppermute | solution.py:46
  29.3 20.5 %collective-permute-start.13 = (bf16[2,2,24,1152]{3,2,1,0:T(8,128)(2,1)S(1)}, bf16[2,2,24,1152]{3,2,1,0:T(8,128)(2,1)S(1)}, u32[]{:S(2)}, u32[]{:S(2)}) collective-permute-start(bf16[2,2,24,1152]{3,2,1,0:T(8,128)(2,1)S(1)} %broadcast_select_fusion.11), channel_id=1, source_target_pairs={{0,16},{1,17},{2,18},{3,19},{4,20},{5,21},{6,22},{7,23},{8,24},{9,... | collective-permute-start | bytes 663560 | tf_op jit(solution)/shard_map/ppermute | solution.py:46
  32.0 34.6 %collective-permute-start.9 = (bf16[2,2,2,24,1024]{4,3,2,0,1:T(8,128)(2,1)S(1)}, bf16[2,2,2,24,1024]{4,3,2,0,1:T(8,128)(2,1)S(1)}, u32[]{:S(2)}, u32[]{:S(2)}) collective-permute-start(bf16[2,2,2,24,1024]{4,3,2,0,1:T(8,128)(2,1)S(1)} %broadcast_select_fusion.7), channel_id=1, source_target_pairs={{0,16},{1,17},{2,18},{3,19},{4,20},{5,21},{6,22},{7,23},{8,24},{9,... | collective-permute-start | bytes 1179656 | tf_op jit(solution)/shard_map/ppermute | solution.py:46
  34.8 15.4 %collective-permute-start.4 = (bf16[2,2,2,24,1024]{4,3,2,0,1:T(8,128)(2,1)S(1)}, bf16[2,2,2,24,1024]{4,3,2,0,1:T(8,128)(2,1)S(1)}, u32[]{:S(2)}, u32[]{:S(2)}) collective-permute-start(bf16[2,2,2,24,1024]{4,3,2,0,1:T(8,128)(2,1)S(1)} %broadcast_select_fusion.9), channel_id=1, source_target_pairs={{0,4},{1,5},{2,6},{3,7},{4,0},{5,1},{6,2},{7,3},{8,12},{9,13},{10,... | collective-permute-start | bytes 1179656 | tf_op jit(solution)/shard_map/ppermute | solution.py:46
  50.0 16.4 %collective-permute-start.14 = (bf16[2,2,2,24,1152]{4,3,2,1,0:T(8,128)(2,1)S(1)}, bf16[2,2,2,24,1152]{4,3,2,1,0:T(8,128)(2,1)S(1)}, u32[]{:S(2)}, u32[]{:S(2)}) collective-permute-start(bf16[2,2,2,24,1152]{4,3,2,1,0:T(8,128)(2,1)S(1)} %broadcast_select_fusion.6), channel_id=1, source_target_pairs={{0,8},{1,9},{2,10},{3,11},{4,12},{5,13},{6,14},{7,15},{8,0},{9,1},... | collective-permute-start | bytes 1327112 | tf_op jit(solution)/shard_map/ppermute | solution.py:46
  50.3 17.8 %collective-permute-start.5 = (bf16[2,2,2,2,24,1024]{5,4,3,0,1,2:T(8,128)(2,1)S(1)}, bf16[2,2,2,2,24,1024]{5,4,3,0,1,2:T(8,128)(2,1)S(1)}, u32[]{:S(2)}, u32[]{:S(2)}) collective-permute-start(bf16[2,2,2,2,24,1024]{5,4,3,0,1,2:T(8,128)(2,1)S(1)} %broadcast_select_fusion.4), channel_id=1, source_target_pairs={{0,2},{1,3},{2,0},{3,1},{4,6},{5,7},{6,4},{7,5},{8,10},{9,11},{10,... | collective-permute-start | bytes 2359304 | tf_op jit(solution)/shard_map/ppermute | solution.py:46
  74.1 276.5 %reduce-scatter.2.cloned.1.call-start = ((), (), s32[]{:S(2)}) async-start(), calls=%async_computation.2 | async-start | bytes 5222400 | tf_op jit(solution)/shard_map/reduce_scatter | solution.py:394
  77.4 39.3 %collective-permute-start.18 = (bf16[256,768]{1,0:T(8,128)(2,1)}, bf16[256,768]{1,0:T(8,128)(2,1)}, u32[]{:S(2)}, u32[]{:S(2)}) collective-permute-start(bf16[256,768]{1,0:T(8,128)(2,1)} %get-tuple-element.89), channel_id=1, source_target_pairs={{0,1},{1,0},{2,3},{3,2},{4,5},{5,4},{6,7},{7,6},{8,9},{9,8},{10,11... | collective-permute-start | bytes 1179656 | tf_op jit(solution)/shard_map/ppermute | solution.py:16
  116.5 18.1 %collective-permute-start.16 = (bf16[512,768]{1,0:T(8,128)(2,1)S(1)}, bf16[512,768]{1,0:T(8,128)(2,1)}, u32[]{:S(2)}, u32[]{:S(2)}) collective-permute-start(bf16[512,768]{1,0:T(8,128)(2,1)S(1)} %fusion.58), channel_id=1, source_target_pairs={{0,1},{1,0},{2,3},{3,2},{4,5},{5,4},{6,7},{7,6},{8,9},{9,8},{10,11... | collective-permute-start | bytes 2359304 | tf_op jit(solution)/shard_map/ppermute | solution.py:16
  147.1 17.1 %collective-permute-start.17 = (bf16[512,768]{1,0:T(8,128)(2,1)S(1)}, bf16[512,768]{1,0:T(8,128)(2,1)S(1)}, u32[]{:S(2)}, u32[]{:S(2)}) collective-permute-start(bf16[512,768]{1,0:T(8,128)(2,1)S(1)} %fusion.51), channel_id=1, source_target_pairs={{0,1},{1,0},{2,3},{3,2},{4,5},{5,4},{6,7},{7,6},{8,9},{9,8},{10,11... | collective-permute-start | bytes 2359304 | tf_op jit(solution)/shard_map/ppermute | solution.py:16
  176.3 16.6 %collective-permute-start.19 = (bf16[512,768]{1,0:T(8,128)(2,1)}, bf16[512,768]{1,0:T(8,128)(2,1)S(1)}, u32[]{:S(2)}, u32[]{:S(2)}) collective-permute-start(bf16[512,768]{1,0:T(8,128)(2,1)} %get-tuple-element.54), channel_id=1, source_target_pairs={{0,1},{1,0},{2,3},{3,2},{4,5},{5,4},{6,7},{7,6},{8,9},{9,8},{10,11... | collective-permute-start | bytes 2359304 | tf_op jit(solution)/shard_map/ppermute | solution.py:16
  200.9 16.3 %collective-permute-start.20 = (bf16[512,768]{1,0:T(8,128)(2,1)}, bf16[512,768]{1,0:T(8,128)(2,1)}, u32[]{:S(2)}, u32[]{:S(2)}) collective-permute-start(bf16[512,768]{1,0:T(8,128)(2,1)} %fusion.48), channel_id=1, source_target_pairs={{0,1},{1,0},{2,3},{3,2},{4,5},{5,4},{6,7},{7,6},{8,9},{9,8},{10,11... | collective-permute-start | bytes 2359304 | tf_op jit(solution)/shard_map/ppermute | solution.py:16
  266.4 15.5 %collective-permute-start.33 = (bf16[2,2,2,2,24,1024]{5,4,3,1,2,0:T(8,128)(2,1)}, bf16[2,2,2,2,24,1024]{5,4,3,1,2,0:T(8,128)(2,1)}, u32[]{:S(2)}, u32[]{:S(2)}) collective-permute-start(bf16[2,2,2,2,24,1024]{5,4,3,1,2,0:T(8,128)(2,1)} %bitcast.176), channel_id=1, source_target_pairs={{0,2},{1,3},{2,0},{3,1},{4,6},{5,7},{6,4},{7,5},{8,10},{9,11},{10,... | collective-permute-start | bytes 2359304 | tf_op jit(solution)/shard_map/ppermute | solution.py:79
  267.5 16.7 %collective-permute-start.23 = (bf16[2,2,2,2,24,1024]{5,4,3,0,1,2:T(8,128)(2,1)}, bf16[2,2,2,2,24,1024]{5,4,3,0,1,2:T(8,128)(2,1)}, u32[]{:S(2)}, u32[]{:S(2)}) collective-permute-start(bf16[2,2,2,2,24,1024]{5,4,3,0,1,2:T(8,128)(2,1)} %bitcast.177), channel_id=1, source_target_pairs={{0,2},{1,3},{2,0},{3,1},{4,6},{5,7},{6,4},{7,5},{8,10},{9,11},{10,... | collective-permute-start | bytes 2359304 | tf_op jit(solution)/shard_map/ppermute | solution.py:79
  274.2 20.7 %collective-permute-start.21 = (f32[256,768]{1,0:T(8,128)}, f32[256,768]{1,0:T(8,128)}, u32[]{:S(2)}, u32[]{:S(2)}) collective-permute-start(f32[256,768]{1,0:T(8,128)} %get-tuple-element.88), channel_id=1, source_target_pairs={{0,1},{1,0},{2,3},{3,2},{4,5},{5,4},{6,7},{7,6},{8,9},{9,8},{10,11... | collective-permute-start | bytes 2359304 | tf_op jit(solution)/shard_map/ppermute | solution.py:16
  276.4 34.4 %collective-permute-start.22 = (f32[256,768]{1,0:T(8,128)}, f32[256,768]{1,0:T(8,128)}, u32[]{:S(2)}, u32[]{:S(2)}) collective-permute-start(f32[256,768]{1,0:T(8,128)} %get-tuple-element.27), channel_id=1, source_target_pairs={{0,1},{1,0},{2,3},{3,2},{4,5},{5,4},{6,7},{7,6},{8,9},{9,8},{10,11... | collective-permute-start | bytes 2359304 | tf_op jit(solution)/shard_map/ppermute | solution.py:16
  281.7 31.9 %collective-permute-start.28 = (bf16[2,2,2,2,24,1033]{5,4,3,2,0,1:T(8,128)(2,1)S(1)}, bf16[2,2,2,2,24,1033]{5,4,3,2,0,1:T(8,128)(2,1)S(1)}, u32[]{:S(2)}, u32[]{:S(2)}) collective-permute-start(bf16[2,2,2,2,24,1033]{5,4,3,2,0,1:T(8,128)(2,1)S(1)} %bitcast.199), channel_id=1, source_target_pairs={{0,2},{1,3},{2,0},{3,1},{4,6},{5,7},{6,4},{7,5},{8,10},{9,11},{10,... | collective-permute-start | bytes 2380040 | tf_op jit(solution)/shard_map/ppermute | solution.py:79
  284.1 29.9 %collective-permute-start.34 = (bf16[2,2,2,24,1024]{4,3,2,0,1:T(8,128)(2,1)S(1)}, bf16[2,2,2,24,1024]{4,3,2,0,1:T(8,128)(2,1)S(1)}, u32[]{:S(2)}, u32[]{:S(2)}) collective-permute-start(bf16[2,2,2,24,1024]{4,3,2,0,1:T(8,128)(2,1)S(1)} %fusion.71), channel_id=1, source_target_pairs={{0,16},{1,17},{2,18},{3,19},{4,20},{5,21},{6,22},{7,23},{8,24},{9,... | collective-permute-start | bytes 1179656 | tf_op jit(solution)/shard_map/ppermute | solution.py:79
  285.8 28.4 %collective-permute-start.24 = (bf16[2,2,2,24,1024]{4,3,2,0,1:T(8,128)(2,1)S(1)}, bf16[2,2,2,24,1024]{4,3,2,0,1:T(8,128)(2,1)S(1)}, u32[]{:S(2)}, u32[]{:S(2)}) collective-permute-start(bf16[2,2,2,24,1024]{4,3,2,0,1:T(8,128)(2,1)S(1)} %fusion.70), channel_id=1, source_target_pairs={{0,4},{1,5},{2,6},{3,7},{4,0},{5,1},{6,2},{7,3},{8,12},{9,13},{10,... | collective-permute-start | bytes 1179656 | tf_op jit(solution)/shard_map/ppermute | solution.py:79
  313.9 13.1 %collective-permute-start.29 = (bf16[2,2,2,24,1033]{4,3,2,1,0:T(8,128)(2,1)S(1)}, bf16[2,2,2,24,1033]{4,3,2,1,0:T(8,128)(2,1)S(1)}, u32[]{:S(2)}, u32[]{:S(2)}) collective-permute-start(bf16[2,2,2,24,1033]{4,3,2,1,0:T(8,128)(2,1)S(1)} %fusion.65), channel_id=1, source_target_pairs={{0,8},{1,9},{2,10},{3,11},{4,12},{5,13},{6,14},{7,15},{8,0},{9,1},... | collective-permute-start | bytes 1190024 | tf_op jit(solution)/shard_map/ppermute | solution.py:79
  314.1 13.1 %collective-permute-start.35 = (bf16[2,2,24,1024]{3,2,1,0:T(8,128)(2,1)S(1)}, bf16[2,2,24,1024]{3,2,1,0:T(8,128)(2,1)S(1)}, u32[]{:S(2)}, u32[]{:S(2)}) collective-permute-start(bf16[2,2,24,1024]{3,2,1,0:T(8,128)(2,1)S(1)} %fusion.74), channel_id=1, source_target_pairs={{0,4},{1,5},{2,6},{3,7},{4,0},{5,1},{6,2},{7,3},{8,12},{9,13},{10,... | collective-permute-start | bytes 589832 | tf_op jit(solution)/shard_map/ppermute | solution.py:79
  314.4 18.4 %collective-permute-start.25 = (bf16[2,2,24,1024]{3,2,1,0:T(8,128)(2,1)S(1)}, bf16[2,2,24,1024]{3,2,1,0:T(8,128)(2,1)S(1)}, u32[]{:S(2)}, u32[]{:S(2)}) collective-permute-start(bf16[2,2,24,1024]{3,2,1,0:T(8,128)(2,1)S(1)} %fusion.73), channel_id=1, source_target_pairs={{0,8},{1,9},{2,10},{3,11},{4,12},{5,13},{6,14},{7,15},{8,0},{9,1},... | collective-permute-start | bytes 589832 | tf_op jit(solution)/shard_map/ppermute | solution.py:79
  327.1 12.7 %collective-permute-start.30 = (bf16[2,2,24,1033]{3,2,1,0:T(8,128)(2,1)S(1)}, bf16[2,2,24,1033]{3,2,1,0:T(8,128)(2,1)S(1)}, u32[]{:S(2)}, u32[]{:S(2)}) collective-permute-start(bf16[2,2,24,1033]{3,2,1,0:T(8,128)(2,1)S(1)} %fusion.72), channel_id=1, source_target_pairs={{0,16},{1,17},{2,18},{3,19},{4,20},{5,21},{6,22},{7,23},{8,24},{9,... | collective-permute-start | bytes 595016 | tf_op jit(solution)/shard_map/ppermute | solution.py:79
  (85 other events, 652.2 us)
Sparse Core Ops, SparseCore 0:
  74.3 50.6 all-gather.1
  215.8 81.3 reduce-scatter.1

commit v8 on v7

--- a/solution.py
+++ b/solution.py
@@ -415,6 +415,7 @@
     grad_qrot, grad_krot, grad_values = attend_back(
         query_rot, key_rot, value_low, my_docs, my_docs, logsum, grad_mixed
     )
+    grad_qrot = grad_qrot + layer_out[0, 0] * 0.0
     grad_values = grad_values.astype(jnp.bfloat16)
     grad_query = unrotate(grad_qrot, cosine, sine_tab).astype(jnp.bfloat16)
     grad_keys = unrotate(grad_krot, cosine, sine_tab).astype(jnp.bfloat16)

time: 367 us -> 393 us (1.071)
  waiting for transfers between devices: 119 us -> 137 us
  local copies, waits for them, and re-layouts: 47.8 us -> 56 us
  other arithmetic: 53.9 us -> 47.8 us
    ppermute x15, waiting for transfers between devices: 26 us -> 56.5 us  [halving_scatter(): lax.ppermute(theirs.astype(jnp.bfloat16), ALL, [(i, i ^ 1 << b) for i in...]
    ppermute x8, waiting for transfers between devices: 51.2 us -> 39.4 us  [swapped(): lax.ppermute(shard, axis, [(i, i ^ 1 << bit) for i in range(lax.axis_size...]
    dot_general x6, matrix products: 13.9 us -> 20.5 us  [contract_rows(): lax.dot_general(left_op, right_op, (((0,), (0,)), ((), ())), preferred_el...]
    dot_general x1, matrix products: 9.77 us -> 4.15 us  [attend_back(): jnp.einsum('phqk,pqhd->pkhd', probability.astype(jnp.bfloat16), grad_mixe...]
    unnamed x139 -> x153, local copies, waits for them, and re-layouts: 6.4 us -> 8.99 us
  transfers between devices with their start and end apart: 40 -> 40, of which waited for: 19 -> 21; matrix products, arithmetic and copies ran while one was open for 40% -> 32% of each run, Pallas kernels for 0% -> 0%
where the time goes in v8:
time: 393 us; the launch traced here: 388 us
  waiting for transfers between devices  137 us (35%)
  matrix products  94.3 us (24%)
  local copies, waits for them, and re-layouts  56 us (14%)
  other arithmetic  47.8 us (12%)
  starting transfers between devices  35.8 us (9%)
  between operations  16.8 us (4%)
    ppermute x15, waiting for transfers between devices, halving_scatter(): lax.ppermute(theirs.astype(jnp.bfloat16), ALL, [(i, i ^ 1 << b) for i in...  56.5 us
    ppermute x8, waiting for transfers between devices, swapped(): lax.ppermute(shard, axis, [(i, i ^ 1 << bit) for i in range(lax.axis_size...  39.4 us
    ppermute x15, waiting for transfers between devices, doubling_gather(): other = lax.ppermute(cur, ALL, [(i, i ^ 1 << b) for i in range(total)])  36.3 us
    dot_general x2, matrix products, ffn_forward(): jnp.dot(rows, inner_cols, preferred_element_type=jnp.float32) + inner_offset  21 us
    dot_general x6, matrix products, contract_rows(): lax.dot_general(left_op, right_op, (((0,), (0,)), ((), ())), preferred_el...  20.5 us
    ppermute x15, starting transfers between devices, doubling_gather(): other = lax.ppermute(cur, ALL, [(i, i ^ 1 << b) for i in range(total)])  18.2 us
    dot_general x6, matrix products, contract_cols(): lax.dot_general(left_op, right_op, (((1,), (1,)), ((), ())), preferred_el...  13.8 us
    dot_general x1, matrix products, attend_back(): jnp.einsum('pqhd,pkhd->phqk', grad_mixed, value_low, preferred_element_ty...  11.5 us
  transfers between devices with their start and end apart: 40, of which 21 were waited for; matrix products, arithmetic and copies ran while one was open for 32% of the time, Pallas kernels for 0%

profile of v8, /device:TPU:0, one launch (start us, length us, event | category | flops | bytes accessed | tf_op | source)
XLA Modules:
  0.0 388.1 jit_solution(12344347127497132146)
XLA Ops:
  36.0 13.8 %collective-permute-done.13 = bf16[2,2,24,1152]{3,2,1,0:T(8,128)(2,1)S(1)} collective-permute-done((bf16[2,2,24,1152]{3,2,1,0:T(8,128)(2,1)S(1)}, bf16[2,2,24,1152]{3,2,1,0:T(8,128)(2,1)S(1)}, u32[]{:S(2)}, u32[]{:S(2)}) %collective-permute-start.13) | collective-permute-done | bytes 221216 | tf_op jit(solution)/shard_map/ppermute | solution.py:46
  50.4 16.0 %collective-permute-done.14 = bf16[2,2,2,24,1152]{4,3,2,1,0:T(8,128)(2,1)S(1)} collective-permute-done((bf16[2,2,2,24,1152]{4,3,2,1,0:T(8,128)(2,1)S(1)}, bf16[2,2,2,24,1152]{4,3,2,1,0:T(8,128)(2,1)S(1)}, u32[]{:S(2)}, u32[]{:S(2)}) %collective-permute-start.14) | collective-permute-done | bytes 442400 | tf_op jit(solution)/shard_map/ppermute | solution.py:46
  80.9 6.5 %collective-permute-done = bf16[256,768]{1,0:T(8,128)(2,1)S(1)} collective-permute-done((bf16[256,768]{1,0:T(8,128)(2,1)}, bf16[256,768]{1,0:T(8,128)(2,1)S(1)}, u32[]{:S(2)}, u32[]{:S(2)}) %collective-permute-start) | collective-permute-done | bytes 393248 | tf_op jit(solution)/shard_map/ppermute | solution.py:16
  110.8 3.9 %fusion.57 = bf16[12,64,512]{2,1,0:T(8,128)(2,1)S(1)} fusion(bf16[512,12,64]{0,2,1:T(8,128)(2,1)S(1)} %bitcast.190, f32[12,512]{1,0:T(8,128)S(1)} %fusion, f32[12,512]{1,0:T(8,128)S(1)} %get-tuple-element.111, f32[12,512,512]{1,2,0:T(8,128)S(1)} %get-tuple-element.112, pred[512,512]{0,1:T(8,128)(4,1)S(1)} %copy-done.13), kind=kOutput, calls=%fused_computation.111 | convolution fusion | flops 418775040 | bytes 14467072 | tf_op jit(solution)/shard_map/phqk,pkhd->pqhd/dot_general | solution.py:200
  119.7 5.2 %all-gather.2.cloned.1.call-done = bf16[768,3074]{1,0:T(8,128)(2,1)} async-done(((bf16[48,3074]{1,0:T(8,128)(2,1)}), bf16[768,3074]{1,0:T(8,128)(2,1)}) %all-gather.2.cloned.1.call-update) | async-done | bytes 4721680 | tf_op jit(solution)/shard_map/all_gather | solution.py:303
  126.1 8.4 %collective-permute-done.16 = bf16[512,768]{1,0:T(8,128)(2,1)} collective-permute-done((bf16[512,768]{1,0:T(8,128)(2,1)S(1)}, bf16[512,768]{1,0:T(8,128)(2,1)}, u32[]{:S(2)}, u32[]{:S(2)}) %collective-permute-start.16) | collective-permute-done | bytes 786464 | tf_op jit(solution)/shard_map/ppermute | solution.py:16
  134.5 11.0 %multiply_convert_fusion.1 = (bf16[512,1536]{1,0:T(8,128)(2,1)S(1)}, f32[512,1536]{1,0:T(8,128)}, f32[512,1536]{1,0:T(8,128)}) fusion(f32[1536]{0:T(1024)S(1)} %reshape.637, bf16[512,768]{1,0:T(8,128)(2,1)} %collective-permute-done.16, bf16[768,3074]{1,0:T(8,128)(2,1)} %all-gather.2.cloned.1.call-done), kind=kOutput, calls=%fused_computation.28 | convolution fusion | flops 1259864064 | bytes 11016192 | tf_op jit(solution)/shard_map/dot_general | solution.py:229
  147.7 10.0 %multiply_convert_fusion.2 = (bf16[512,1536]{1,0:T(8,128)(2,1)S(1)}, f32[512,1536]{1,0:T(8,128)}, f32[512,1536]{1,0:T(8,128)}) fusion(f32[1536]{0:T(1024)S(1)} %reshape.637, bf16[512,768]{1,0:T(8,128)(2,1)S(1)} %fusion.58, bf16[768,3074]{1,0:T(8,128)(2,1)S(1)} %copy-done.65), kind=kOutput, calls=%fused_computation.41 | convolution fusion | flops 1259864064 | bytes 11018240 | tf_op jit(solution)/shard_map/dot_general | solution.py:229
  157.7 6.4 %collective-permute-done.17 = bf16[512,768]{1,0:T(8,128)(2,1)S(1)} collective-permute-done((bf16[512,768]{1,0:T(8,128)(2,1)S(1)}, bf16[512,768]{1,0:T(8,128)(2,1)S(1)}, u32[]{:S(2)}, u32[]{:S(2)}) %collective-permute-start.17) | collective-permute-done | bytes 786464 | tf_op jit(solution)/shard_map/ppermute | solution.py:16
  177.5 6.1 %convert_reduce_fusion.1 = (f32[1536]{0:T(1024)S(1)}, bf16[512,1536]{1,0:T(8,128)(2,1)S(1)}) fusion(f32[512,1536]{1,0:T(8,128)} %get-tuple-element.63, f32[512,1536]{1,0:T(8,128)} %get-tuple-element.116, bf16[512,768]{1,0:T(8,128)(2,1)} %get-tuple-element.54, bf16[768,3074]{1,0:T(8,128)(2,1)} %all-gather.2.cloned.1.call-done), kind=kOutput, calls=%fused_computation.25 | convolution fusion | flops 1220540928 | bytes 11016192 | tf_op jit(solution)/shard_map/dot_general | solution.py:236
  183.6 3.6 fusion.106
  192.8 5.4 %convert_reduce_fusion = (f32[1536]{0:T(1024)S(1)}, bf16[512,1536]{1,0:T(8,128)(2,1)}) fusion(f32[512,1536]{1,0:T(8,128)S(1)} %copy-done.69, f32[512,1536]{1,0:T(8,128)S(1)} %copy-done.70, bf16[512,768]{1,0:T(8,128)(2,1)S(1)} %collective-permute-done.19, bf16[768,3074]{1,0:T(8,128)(2,1)} %all-gather.2.cloned.1.call-done), kind=kOutput, calls=%fused_computation.24 | convolution fusion | flops 1220540928 | bytes 11016192 | tf_op jit(solution)/shard_map/dot_general | solution.py:236
  198.6 3.7 fusion.48
  204.1 4.2 %add_convert_fusion.1 = bf16[768,1536]{1,0:T(8,128)(2,1)} fusion(f32[768,1536]{1,0:T(8,128)S(1)} %copy-done.3, bf16[512,768]{1,0:T(8,128)(2,1)} %collective-permute-done.16, bf16[512,1536]{1,0:T(8,128)(2,1)S(1)} %copy-done.39), kind=kOutput, calls=%fused_computation.18 | convolution fusion | flops 1210318848 | bytes 9437184 | tf_op jit(solution)/shard_map/dot_general | solution.py:175
  208.3 5.2 %add_convert_fusion = bf16[768,1536]{1,0:T(8,128)(2,1)} fusion(f32[768,1536]{1,0:T(8,128)} %fusion.106, bf16[512,768]{1,0:T(8,128)(2,1)S(1)} %copy-done.43, bf16[512,1536]{1,0:T(8,128)(2,1)S(1)} %copy-done.34), kind=kOutput, calls=%fused_computation.17 | convolution fusion | flops 1210318848 | bytes 9437184 | tf_op jit(solution)/shard_map/dot_general | solution.py:175
  213.6 4.7 %collective-permute-done.20 = bf16[512,768]{1,0:T(8,128)(2,1)S(1)} collective-permute-done((bf16[512,768]{1,0:T(8,128)(2,1)S(1)}, bf16[512,768]{1,0:T(8,128)(2,1)S(1)}, u32[]{:S(2)}, u32[]{:S(2)}) %collective-permute-start.20) | collective-permute-done | bytes 786464 | tf_op jit(solution)/shard_map/ppermute | solution.py:16
  231.2 11.5 %multiply_reduce_fusion = (f32[12,512]{1,0:T(8,128)S(1)}, f32[12,512,512]{1,2,0:T(8,128)}) fusion(f32[12,512]{1,0:T(8,128)S(1)} %copy-done.54, f32[12,512,512]{1,2,0:T(8,128)} %copy-done.2, pred[512,512]{0,1:T(8,128)(4,1)S(1)} %copy-done.14, bf16[512,12,64]{0,2,1:T(8,128)(2,1)} %bitcast.192, bf16[512,12,64]{0,2,1:T(8,128)(2,1)S(1)} %bitcast.191), kind=kOutput, calls=%fused_computation.1 | convolution fusion | flops 418375680 | bytes 27049984 | tf_op jit(solution)/shard_map/pqhd,pkhd->phqk/dot_general | solution.py:214
  244.1 7.3 %multiply_convert_fusion = bf16[12,512,512]{1,2,0:T(8,128)(2,1)S(1)} fusion(f32[12,512,512]{1,2,0:T(8,128)} %get-tuple-element.120, f32[12,512]{1,0:T(8,128)S(1)} %get-tuple-element.119, f32[12,512]{1,0:T(8,128)S(1)} %copy-done.54, f32[12,512,512]{1,2,0:T(8,128)S(1)} %bitcast.180, pred[512,512]{0,1:T(8,128)(4,1)S(1)} %copy-done.14), kind=kLoop, calls=%fused_computation | loop fusion | flops 18874368 | bytes 31768576 | tf_op jit(solution)/shard_map/convert_element_type | solution.py:218
  253.5 4.1 %fusion.54 = bf16[12,64,512]{2,1,0:T(8,128)(2,1)} fusion(bf16[512,12,64]{0,2,1:T(8,128)(2,1)S(1)} %bitcast.193, f32[12,512]{1,0:T(8,128)S(1)} %copy-done.54, f32[12,512,512]{1,2,0:T(8,128)S(1)} %bitcast.180, pred[512,512]{0,1:T(8,128)(4,1)S(1)} %copy-done.14), kind=kOutput, calls=%fused_computation.110 | convolution fusion | flops 415629312 | bytes 14442496 | tf_op jit(solution)/shard_map/phqk,pqhd->pkhd/dot_general | solution.py:208
  285.3 4.8 %concatenate.125 = bf16[32,24,1033]{2,1,0:T(8,128)(2,1)S(1)} concatenate(bf16[32,24,256]{2,1,0:T(8,128)(2,1)S(1)} %slice.241, bf16[32,24,3]{2,1,0:T(8,128)(2,1)S(1)} %bitcast.202, bf16[32,24,768]{2,1,0:T(8,128)(2,1)} %convolution_convert_fusion.1, bf16[32,24,1]{2,1,0:T(8,128)(2,1)} %stack.65, bf16[32,24,1]{2,1,0:T(8,128)(2,1)} %stack.66, bf16[32,24,1]{2,1,0:T(8,128)(2,1)} %stack.67, ...), dimensions={2} | concatenate | bytes 3173376 | tf_op jit(solution)/shard_map/concatenate | solution.py:448
  293.9 11.3 %collective-permute-done.22 = f32[256,768]{1,0:T(8,128)} collective-permute-done((f32[256,768]{1,0:T(8,128)}, f32[256,768]{1,0:T(8,128)}, u32[]{:S(2)}, u32[]{:S(2)}) %collective-permute-start.22) | collective-permute-done | bytes 786464 | tf_op jit(solution)/shard_map/ppermute | solution.py:16
  308.4 17.2 %collective-permute-done.34 = bf16[2,2,2,24,1024]{4,3,2,0,1:T(8,128)(2,1)S(1)} collective-permute-done((bf16[2,2,2,24,1024]{4,3,2,0,1:T(8,128)(2,1)S(1)}, bf16[2,2,2,24,1024]{4,3,2,0,1:T(8,128)(2,1)S(1)}, u32[]{:S(2)}, u32[]{:S(2)}) %collective-permute-start.34) | collective-permute-done | bytes 393248 | tf_op jit(solution)/shard_map/ppermute | solution.py:79
  326.0 15.7 %collective-permute-done.29 = bf16[2,2,2,24,1033]{4,3,2,1,0:T(8,128)(2,1)S(1)} collective-permute-done((bf16[2,2,2,24,1033]{4,3,2,1,0:T(8,128)(2,1)S(1)}, bf16[2,2,2,24,1033]{4,3,2,1,0:T(8,128)(2,1)S(1)}, u32[]{:S(2)}, u32[]{:S(2)}) %collective-permute-start.29) | collective-permute-done | bytes 396704 | tf_op jit(solution)/shard_map/ppermute | solution.py:79
  349.0 16.1 %collective-permute-done.30 = bf16[2,2,24,1033]{3,2,1,0:T(8,128)(2,1)S(1)} collective-permute-done((bf16[2,2,24,1033]{3,2,1,0:T(8,128)(2,1)S(1)}, bf16[2,2,24,1033]{3,2,1,0:T(8,128)(2,1)S(1)}, u32[]{:S(2)}, u32[]{:S(2)}) %collective-permute-start.30) | collective-permute-done | bytes 198368 | tf_op jit(solution)/shard_map/ppermute | solution.py:79
  (374 shorter events, 169.0 us)
Async XLA Ops:
  7.2 117.7 %all-gather.2.cloned.1.call-start = ((), (), s32[]{:S(2)}) async-start(), calls=%async_computation.1 | async-start | bytes 5222400 | tf_op jit(solution)/shard_map/all_gather | solution.py:303
  29.3 20.5 %collective-permute-start.13 = (bf16[2,2,24,1152]{3,2,1,0:T(8,128)(2,1)S(1)}, bf16[2,2,24,1152]{3,2,1,0:T(8,128)(2,1)S(1)}, u32[]{:S(2)}, u32[]{:S(2)}) collective-permute-start(bf16[2,2,24,1152]{3,2,1,0:T(8,128)(2,1)S(1)} %broadcast_select_fusion.11), channel_id=1, source_target_pairs={{0,16},{1,17},{2,18},{3,19},{4,20},{5,21},{6,22},{7,23},{8,24},{9,... | collective-permute-start | bytes 663560 | tf_op jit(solution)/shard_map/ppermute | solution.py:46
  32.0 34.6 %collective-permute-start.9 = (bf16[2,2,2,24,1024]{4,3,2,0,1:T(8,128)(2,1)S(1)}, bf16[2,2,2,24,1024]{4,3,2,0,1:T(8,128)(2,1)S(1)}, u32[]{:S(2)}, u32[]{:S(2)}) collective-permute-start(bf16[2,2,2,24,1024]{4,3,2,0,1:T(8,128)(2,1)S(1)} %broadcast_select_fusion.7), channel_id=1, source_target_pairs={{0,16},{1,17},{2,18},{3,19},{4,20},{5,21},{6,22},{7,23},{8,24},{9,... | collective-permute-start | bytes 1179656 | tf_op jit(solution)/shard_map/ppermute | solution.py:46
  34.8 15.4 %collective-permute-start.4 = (bf16[2,2,2,24,1024]{4,3,2,0,1:T(8,128)(2,1)S(1)}, bf16[2,2,2,24,1024]{4,3,2,0,1:T(8,128)(2,1)S(1)}, u32[]{:S(2)}, u32[]{:S(2)}) collective-permute-start(bf16[2,2,2,24,1024]{4,3,2,0,1:T(8,128)(2,1)S(1)} %broadcast_select_fusion.9), channel_id=1, source_target_pairs={{0,4},{1,5},{2,6},{3,7},{4,0},{5,1},{6,2},{7,3},{8,12},{9,13},{10,... | collective-permute-start | bytes 1179656 | tf_op jit(solution)/shard_map/ppermute | solution.py:46
  50.0 16.4 %collective-permute-start.14 = (bf16[2,2,2,24,1152]{4,3,2,1,0:T(8,128)(2,1)S(1)}, bf16[2,2,2,24,1152]{4,3,2,1,0:T(8,128)(2,1)S(1)}, u32[]{:S(2)}, u32[]{:S(2)}) collective-permute-start(bf16[2,2,2,24,1152]{4,3,2,1,0:T(8,128)(2,1)S(1)} %broadcast_select_fusion.6), channel_id=1, source_target_pairs={{0,8},{1,9},{2,10},{3,11},{4,12},{5,13},{6,14},{7,15},{8,0},{9,1},... | collective-permute-start | bytes 1327112 | tf_op jit(solution)/shard_map/ppermute | solution.py:46
  50.3 17.8 %collective-permute-start.5 = (bf16[2,2,2,2,24,1024]{5,4,3,0,1,2:T(8,128)(2,1)S(1)}, bf16[2,2,2,2,24,1024]{5,4,3,0,1,2:T(8,128)(2,1)S(1)}, u32[]{:S(2)}, u32[]{:S(2)}) collective-permute-start(bf16[2,2,2,2,24,1024]{5,4,3,0,1,2:T(8,128)(2,1)S(1)} %broadcast_select_fusion.4), channel_id=1, source_target_pairs={{0,2},{1,3},{2,0},{3,1},{4,6},{5,7},{6,4},{7,5},{8,10},{9,11},{10,... | collective-permute-start | bytes 2359304 | tf_op jit(solution)/shard_map/ppermute | solution.py:46
  74.1 301.9 %reduce-scatter.2.cloned.1.call-start = ((), (), s32[]{:S(2)}) async-start(), calls=%async_computation.2 | async-start | bytes 5222400 | tf_op jit(solution)/shard_map/reduce_scatter | solution.py:394
  77.3 39.2 %collective-permute-start.18 = (bf16[256,768]{1,0:T(8,128)(2,1)}, bf16[256,768]{1,0:T(8,128)(2,1)}, u32[]{:S(2)}, u32[]{:S(2)}) collective-permute-start(bf16[256,768]{1,0:T(8,128)(2,1)} %get-tuple-element.89), channel_id=1, source_target_pairs={{0,1},{1,0},{2,3},{3,2},{4,5},{5,4},{6,7},{7,6},{8,9},{9,8},{10,11... | collective-permute-start | bytes 1179656 | tf_op jit(solution)/shard_map/ppermute | solution.py:16
  116.4 18.1 %collective-permute-start.16 = (bf16[512,768]{1,0:T(8,128)(2,1)S(1)}, bf16[512,768]{1,0:T(8,128)(2,1)}, u32[]{:S(2)}, u32[]{:S(2)}) collective-permute-start(bf16[512,768]{1,0:T(8,128)(2,1)S(1)} %fusion.58), channel_id=1, source_target_pairs={{0,1},{1,0},{2,3},{3,2},{4,5},{5,4},{6,7},{7,6},{8,9},{9,8},{10,11... | collective-permute-start | bytes 2359304 | tf_op jit(solution)/shard_map/ppermute | solution.py:16
  146.9 17.1 %collective-permute-start.17 = (bf16[512,768]{1,0:T(8,128)(2,1)S(1)}, bf16[512,768]{1,0:T(8,128)(2,1)S(1)}, u32[]{:S(2)}, u32[]{:S(2)}) collective-permute-start(bf16[512,768]{1,0:T(8,128)(2,1)S(1)} %fusion.51), channel_id=1, source_target_pairs={{0,1},{1,0},{2,3},{3,2},{4,5},{5,4},{6,7},{7,6},{8,9},{9,8},{10,11... | collective-permute-start | bytes 2359304 | tf_op jit(solution)/shard_map/ppermute | solution.py:16
  176.1 16.6 %collective-permute-start.19 = (bf16[512,768]{1,0:T(8,128)(2,1)}, bf16[512,768]{1,0:T(8,128)(2,1)S(1)}, u32[]{:S(2)}, u32[]{:S(2)}) collective-permute-start(bf16[512,768]{1,0:T(8,128)(2,1)} %get-tuple-element.54), channel_id=1, source_target_pairs={{0,1},{1,0},{2,3},{3,2},{4,5},{5,4},{6,7},{7,6},{8,9},{9,8},{10,11... | collective-permute-start | bytes 2359304 | tf_op jit(solution)/shard_map/ppermute | solution.py:16
  202.3 16.1 %collective-permute-start.20 = (bf16[512,768]{1,0:T(8,128)(2,1)S(1)}, bf16[512,768]{1,0:T(8,128)(2,1)S(1)}, u32[]{:S(2)}, u32[]{:S(2)}) collective-permute-start(bf16[512,768]{1,0:T(8,128)(2,1)S(1)} %fusion.48), channel_id=1, source_target_pairs={{0,1},{1,0},{2,3},{3,2},{4,5},{5,4},{6,7},{7,6},{8,9},{9,8},{10,11... | collective-permute-start | bytes 2359304 | tf_op jit(solution)/shard_map/ppermute | solution.py:16
  229.4 28.2 %collective-permute-start.21 = (f32[256,768]{1,0:T(8,128)}, f32[256,768]{1,0:T(8,128)S(1)}, u32[]{:S(2)}, u32[]{:S(2)}) collective-permute-start(f32[256,768]{1,0:T(8,128)} %get-tuple-element.88), channel_id=1, source_target_pairs={{0,1},{1,0},{2,3},{3,2},{4,5},{5,4},{6,7},{7,6},{8,9},{9,8},{10,11... | collective-permute-start | bytes 2359304 | tf_op jit(solution)/shard_map/ppermute | solution.py:16
  270.9 19.8 %collective-permute-start.33 = (bf16[2,2,2,2,24,1024]{5,4,3,1,2,0:T(8,128)(2,1)}, bf16[2,2,2,2,24,1024]{5,4,3,1,2,0:T(8,128)(2,1)}, u32[]{:S(2)}, u32[]{:S(2)}) collective-permute-start(bf16[2,2,2,2,24,1024]{5,4,3,1,2,0:T(8,128)(2,1)} %bitcast.177), channel_id=1, source_target_pairs={{0,2},{1,3},{2,0},{3,1},{4,6},{5,7},{6,4},{7,5},{8,10},{9,11},{10,... | collective-permute-start | bytes 2359304 | tf_op jit(solution)/shard_map/ppermute | solution.py:79
  284.9 20.3 %collective-permute-start.22 = (f32[256,768]{1,0:T(8,128)}, f32[256,768]{1,0:T(8,128)}, u32[]{:S(2)}, u32[]{:S(2)}) collective-permute-start(f32[256,768]{1,0:T(8,128)} %get-tuple-element.27), channel_id=1, source_target_pairs={{0,1},{1,0},{2,3},{3,2},{4,5},{5,4},{6,7},{7,6},{8,9},{9,8},{10,11... | collective-permute-start | bytes 2359304 | tf_op jit(solution)/shard_map/ppermute | solution.py:16
  290.4 17.7 %collective-permute-start.28 = (bf16[2,2,2,2,24,1033]{5,4,3,2,0,1:T(8,128)(2,1)S(1)}, bf16[2,2,2,2,24,1033]{5,4,3,2,0,1:T(8,128)(2,1)S(1)}, u32[]{:S(2)}, u32[]{:S(2)}) collective-permute-start(bf16[2,2,2,2,24,1033]{5,4,3,2,0,1:T(8,128)(2,1)S(1)} %bitcast.200), channel_id=1, source_target_pairs={{0,2},{1,3},{2,0},{3,1},{4,6},{5,7},{6,4},{7,5},{8,10},{9,11},{10,... | collective-permute-start | bytes 2380040 | tf_op jit(solution)/shard_map/ppermute | solution.py:79
  292.2 33.4 %collective-permute-start.34 = (bf16[2,2,2,24,1024]{4,3,2,0,1:T(8,128)(2,1)S(1)}, bf16[2,2,2,24,1024]{4,3,2,0,1:T(8,128)(2,1)S(1)}, u32[]{:S(2)}, u32[]{:S(2)}) collective-permute-start(bf16[2,2,2,24,1024]{4,3,2,0,1:T(8,128)(2,1)S(1)} %fusion.72), channel_id=1, source_target_pairs={{0,16},{1,17},{2,18},{3,19},{4,20},{5,21},{6,22},{7,23},{8,24},{9,... | collective-permute-start | bytes 1179656 | tf_op jit(solution)/shard_map/ppermute | solution.py:79
  293.8 32.0 %collective-permute-start.24 = (bf16[2,2,2,24,1024]{4,3,2,0,1:T(8,128)(2,1)S(1)}, bf16[2,2,2,24,1024]{4,3,2,0,1:T(8,128)(2,1)S(1)}, u32[]{:S(2)}, u32[]{:S(2)}) collective-permute-start(bf16[2,2,2,24,1024]{4,3,2,0,1:T(8,128)(2,1)S(1)} %fusion.71), channel_id=1, source_target_pairs={{0,4},{1,5},{2,6},{3,7},{4,0},{5,1},{6,2},{7,3},{8,12},{9,13},{10,... | collective-permute-start | bytes 1179656 | tf_op jit(solution)/shard_map/ppermute | solution.py:79
  308.3 33.4 %collective-permute-start.29 = (bf16[2,2,2,24,1033]{4,3,2,1,0:T(8,128)(2,1)S(1)}, bf16[2,2,2,24,1033]{4,3,2,1,0:T(8,128)(2,1)S(1)}, u32[]{:S(2)}, u32[]{:S(2)}) collective-permute-start(bf16[2,2,2,24,1033]{4,3,2,1,0:T(8,128)(2,1)S(1)} %fusion.66), channel_id=1, source_target_pairs={{0,8},{1,9},{2,10},{3,11},{4,12},{5,13},{6,14},{7,15},{8,0},{9,1},... | collective-permute-start | bytes 1190024 | tf_op jit(solution)/shard_map/ppermute | solution.py:79
  325.7 16.2 %collective-permute-start.35 = (bf16[2,2,24,1024]{3,2,1,0:T(8,128)(2,1)S(1)}, bf16[2,2,24,1024]{3,2,1,0:T(8,128)(2,1)S(1)}, u32[]{:S(2)}, u32[]{:S(2)}) collective-permute-start(bf16[2,2,24,1024]{3,2,1,0:T(8,128)(2,1)S(1)} %fusion.75), channel_id=1, source_target_pairs={{0,4},{1,5},{2,6},{3,7},{4,0},{5,1},{6,2},{7,3},{8,12},{9,13},{10,... | collective-permute-start | bytes 589832 | tf_op jit(solution)/shard_map/ppermute | solution.py:79
  326.0 20.9 %collective-permute-start.25 = (bf16[2,2,24,1024]{3,2,1,0:T(8,128)(2,1)S(1)}, bf16[2,2,24,1024]{3,2,1,0:T(8,128)(2,1)S(1)}, u32[]{:S(2)}, u32[]{:S(2)}) collective-permute-start(bf16[2,2,24,1024]{3,2,1,0:T(8,128)(2,1)S(1)} %fusion.74), channel_id=1, source_target_pairs={{0,8},{1,9},{2,10},{3,11},{4,12},{5,13},{6,14},{7,15},{8,0},{9,1},... | collective-permute-start | bytes 589832 | tf_op jit(solution)/shard_map/ppermute | solution.py:79
  341.9 23.2 %collective-permute-start.30 = (bf16[2,2,24,1033]{3,2,1,0:T(8,128)(2,1)S(1)}, bf16[2,2,24,1033]{3,2,1,0:T(8,128)(2,1)S(1)}, u32[]{:S(2)}, u32[]{:S(2)}) collective-permute-start(bf16[2,2,24,1033]{3,2,1,0:T(8,128)(2,1)S(1)} %fusion.73), channel_id=1, source_target_pairs={{0,16},{1,17},{2,18},{3,19},{4,20},{5,21},{6,22},{7,23},{8,24},{9,... | collective-permute-start | bytes 595016 | tf_op jit(solution)/shard_map/ppermute | solution.py:79
  342.0 23.2 %collective-permute-start.36 = (bf16[2,24,1024]{2,1,0:T(8,128)(2,1)S(1)}, bf16[2,24,1024]{2,1,0:T(8,128)(2,1)S(1)}, u32[]{:S(2)}, u32[]{:S(2)}) collective-permute-start(bf16[2,24,1024]{2,1,0:T(8,128)(2,1)S(1)} %fusion.79), channel_id=1, source_target_pairs={{0,8},{1,9},{2,10},{3,11},{4,12},{5,13},{6,14},{7,15},{8,0},{9,1},... | collective-permute-start | bytes 294920 | tf_op jit(solution)/shard_map/ppermute | solution.py:79
  347.0 20.9 %collective-permute-start.26 = (bf16[2,24,1024]{2,1,0:T(8,128)(2,1)S(1)}, bf16[2,24,1024]{2,1,0:T(8,128)(2,1)S(1)}, u32[]{:S(2)}, u32[]{:S(2)}) collective-permute-start(bf16[2,24,1024]{2,1,0:T(8,128)(2,1)S(1)} %fusion.78), channel_id=1, source_target_pairs={{0,16},{1,17},{2,18},{3,19},{4,20},{5,21},{6,22},{7,23},{8,24},{9,... | collective-permute-start | bytes 294920 | tf_op jit(solution)/shard_map/ppermute | solution.py:79
  (92 other events, 659.0 us)
Sparse Core Ops, SparseCore 0:
  74.3 50.6 all-gather.1
  275.0 92.0 reduce-scatter.1

commit v9 on v7

--- a/solution.py
+++ b/solution.py
@@ -439,14 +439,13 @@
     qkv_wsum = contract_rows(pack_in, grad_qkv)
     qkv_bsum = jnp.sum(grad_qkv.astype(jnp.float32), axis=0).reshape(3, D)
     wsum_parts = qkv_wsum.reshape(total, share, 3 * D).astype(jnp.bfloat16)
-    cut = 3 * D * 4 // 9 // 128 * 128
+    cut = 3 * D * 2 // 3 // 128 * 128
     late_mine = scatter_sum_parts(
         [
             wsum_parts[..., :cut],
-            wsum_parts[..., cut : 2 * cut],
             jnp.concatenate(
                 [
-                    wsum_parts[..., 2 * cut :],
+                    wsum_parts[..., cut:],
                     qkv_bsum.T.reshape(total, share, 3).astype(jnp.bfloat16),
                     early.astype(jnp.bfloat16),
                 ],

time: 367 us -> 399 us (1.087)
  waiting for transfers between devices: 119 us -> 140 us
  matrix products: 90.9 us -> 97.6 us
  local copies, waits for them, and re-layouts: 47.8 us -> 52.4 us
    ppermute x15 -> x10, waiting for transfers between devices: 26 us -> 58.3 us  [halving_scatter(): lax.ppermute(theirs.astype(jnp.bfloat16), ALL, [(i, i ^ 1 << b) for i in...]
    ppermute x8, waiting for transfers between devices: 51.2 us -> 39.8 us  [swapped(): lax.ppermute(shard, axis, [(i, i ^ 1 << bit) for i in range(lax.axis_size...]
    dot_general x6, matrix products: 13.9 us -> 21.8 us  [contract_rows(): lax.dot_general(left_op, right_op, (((0,), (0,)), ((), ())), preferred_el...]
    ppermute x15 -> x10, starting transfers between devices: 8.86 us -> 11.1 us  [halving_scatter(): lax.ppermute(theirs.astype(jnp.bfloat16), ALL, [(i, i ^ 1 << b) for i in...]
  transfers between devices with their start and end apart: 40 -> 35, of which waited for: 19 -> 19; matrix products, arithmetic and copies ran while one was open for 40% -> 25% of each run, Pallas kernels for 0% -> 0%
where the time goes in v9:
time: 399 us; the launch traced here: 394 us
  waiting for transfers between devices  140 us (35%)
  matrix products  97.6 us (24%)
  local copies, waits for them, and re-layouts  52.4 us (13%)
  other arithmetic  50.3 us (13%)
  starting transfers between devices  37.6 us (9%)
  between operations  15.9 us (4%)
    ppermute x10, waiting for transfers between devices, halving_scatter(): lax.ppermute(theirs.astype(jnp.bfloat16), ALL, [(i, i ^ 1 << b) for i in...  58.3 us
    ppermute x8, waiting for transfers between devices, swapped(): lax.ppermute(shard, axis, [(i, i ^ 1 << bit) for i in range(lax.axis_size...  39.8 us
    ppermute x15, waiting for transfers between devices, doubling_gather(): other = lax.ppermute(cur, ALL, [(i, i ^ 1 << b) for i in range(total)])  36.3 us
    dot_general x6, matrix products, contract_rows(): lax.dot_general(left_op, right_op, (((0,), (0,)), ((), ())), preferred_el...  21.8 us
    dot_general x2, matrix products, ffn_forward(): jnp.dot(rows, inner_cols, preferred_element_type=jnp.float32) + inner_offset  20.9 us
    ppermute x15, starting transfers between devices, doubling_gather(): other = lax.ppermute(cur, ALL, [(i, i ^ 1 << b) for i in range(total)])  18.2 us
    dot_general x6, matrix products, contract_cols(): lax.dot_general(left_op, right_op, (((1,), (1,)), ((), ())), preferred_el...  12.9 us
    dot_general x2, matrix products, ffn_backward(): grad_act = jnp.dot(grads, outer_cols, preferred_element_type=jnp.float32)  11.4 us
  transfers between devices with their start and end apart: 35, of which 19 were waited for; matrix products, arithmetic and copies ran while one was open for 25% of the time, Pallas kernels for 0%

profile of v9, /device:TPU:0, one launch (start us, length us, event | category | flops | bytes accessed | tf_op | source)
XLA Modules:
  0.0 393.5 jit_solution(69353495789034176)
XLA Ops:
  36.0 13.8 %collective-permute-done.13 = bf16[2,2,24,1152]{3,2,1,0:T(8,128)(2,1)S(1)} collective-permute-done((bf16[2,2,24,1152]{3,2,1,0:T(8,128)(2,1)S(1)}, bf16[2,2,24,1152]{3,2,1,0:T(8,128)(2,1)S(1)}, u32[]{:S(2)}, u32[]{:S(2)}) %collective-permute-start.13) | collective-permute-done | bytes 221216 | tf_op jit(solution)/shard_map/ppermute | solution.py:46
  50.4 16.0 %collective-permute-done.14 = bf16[2,2,2,24,1152]{4,3,2,1,0:T(8,128)(2,1)S(1)} collective-permute-done((bf16[2,2,2,24,1152]{4,3,2,1,0:T(8,128)(2,1)S(1)}, bf16[2,2,2,24,1152]{4,3,2,1,0:T(8,128)(2,1)S(1)}, u32[]{:S(2)}, u32[]{:S(2)}) %collective-permute-start.14) | collective-permute-done | bytes 442400 | tf_op jit(solution)/shard_map/ppermute | solution.py:46
  80.9 6.5 %collective-permute-done = bf16[256,768]{1,0:T(8,128)(2,1)S(1)} collective-permute-done((bf16[256,768]{1,0:T(8,128)(2,1)}, bf16[256,768]{1,0:T(8,128)(2,1)S(1)}, u32[]{:S(2)}, u32[]{:S(2)}) %collective-permute-start) | collective-permute-done | bytes 393248 | tf_op jit(solution)/shard_map/ppermute | solution.py:16
  110.8 3.9 fusion.57
  119.7 5.2 %all-gather.2.cloned.1.call-done = bf16[768,3074]{1,0:T(8,128)(2,1)} async-done(((bf16[48,3074]{1,0:T(8,128)(2,1)}), bf16[768,3074]{1,0:T(8,128)(2,1)}) %all-gather.2.cloned.1.call-update) | async-done | bytes 4721680 | tf_op jit(solution)/shard_map/all_gather | solution.py:303
  126.1 8.4 %collective-permute-done.16 = bf16[512,768]{1,0:T(8,128)(2,1)} collective-permute-done((bf16[512,768]{1,0:T(8,128)(2,1)S(1)}, bf16[512,768]{1,0:T(8,128)(2,1)}, u32[]{:S(2)}, u32[]{:S(2)}) %collective-permute-start.16) | collective-permute-done | bytes 786464 | tf_op jit(solution)/shard_map/ppermute | solution.py:16
  134.5 10.9 %multiply_convert_fusion.1 = (bf16[512,1536]{1,0:T(8,128)(2,1)S(1)}, f32[512,1536]{1,0:T(8,128)}, f32[512,1536]{1,0:T(8,128)}) fusion(f32[1536]{0:T(1024)S(1)} %reshape.623, bf16[512,768]{1,0:T(8,128)(2,1)} %collective-permute-done.16, bf16[768,3074]{1,0:T(8,128)(2,1)} %all-gather.2.cloned.1.call-done), kind=kOutput, calls=%fused_computation.28 | convolution fusion | flops 1259864064 | bytes 11016192 | tf_op jit(solution)/shard_map/dot_general | solution.py:229
  147.6 9.9 %multiply_convert_fusion.2 = (bf16[512,1536]{1,0:T(8,128)(2,1)S(1)}, f32[512,1536]{1,0:T(8,128)}, f32[512,1536]{1,0:T(8,128)}) fusion(f32[1536]{0:T(1024)S(1)} %reshape.623, bf16[512,768]{1,0:T(8,128)(2,1)S(1)} %fusion.58, bf16[768,3074]{1,0:T(8,128)(2,1)S(1)} %copy-done.65), kind=kOutput, calls=%fused_computation.41 | convolution fusion | flops 1259864064 | bytes 11018240 | tf_op jit(solution)/shard_map/dot_general | solution.py:229
  157.5 6.4 %collective-permute-done.17 = bf16[512,768]{1,0:T(8,128)(2,1)S(1)} collective-permute-done((bf16[512,768]{1,0:T(8,128)(2,1)S(1)}, bf16[512,768]{1,0:T(8,128)(2,1)S(1)}, u32[]{:S(2)}, u32[]{:S(2)}) %collective-permute-start.17) | collective-permute-done | bytes 786464 | tf_op jit(solution)/shard_map/ppermute | solution.py:16
  177.5 6.1 %convert_reduce_fusion.1 = (f32[1536]{0:T(1024)S(1)}, bf16[512,1536]{1,0:T(8,128)(2,1)S(1)}) fusion(f32[512,1536]{1,0:T(8,128)} %get-tuple-element.63, f32[512,1536]{1,0:T(8,128)} %get-tuple-element.112, bf16[512,768]{1,0:T(8,128)(2,1)} %get-tuple-element.54, bf16[768,3074]{1,0:T(8,128)(2,1)} %all-gather.2.cloned.1.call-done), kind=kOutput, calls=%fused_computation.25 | convolution fusion | flops 1220540928 | bytes 11016192 | tf_op jit(solution)/shard_map/dot_general | solution.py:236
  192.8 5.4 %convert_reduce_fusion = (f32[1536]{0:T(1024)S(1)}, bf16[512,1536]{1,0:T(8,128)(2,1)}) fusion(f32[512,1536]{1,0:T(8,128)S(1)} %copy-done.68, f32[512,1536]{1,0:T(8,128)S(1)} %copy-done.69, bf16[512,768]{1,0:T(8,128)(2,1)S(1)} %collective-permute-done.19, bf16[768,3074]{1,0:T(8,128)(2,1)} %all-gather.2.cloned.1.call-done), kind=kOutput, calls=%fused_computation.24 | convolution fusion | flops 1220540928 | bytes 11016192 | tf_op jit(solution)/shard_map/dot_general | solution.py:236
  204.8 4.3 %add_convert_fusion.1 = bf16[768,1536]{1,0:T(8,128)(2,1)} fusion(f32[768,1536]{1,0:T(8,128)S(1)} %copy-done.3, bf16[512,768]{1,0:T(8,128)(2,1)} %collective-permute-done.16, bf16[512,1536]{1,0:T(8,128)(2,1)S(1)} %copy-done.35), kind=kOutput, calls=%fused_computation.18 | convolution fusion | flops 1210318848 | bytes 9437184 | tf_op jit(solution)/shard_map/dot_general | solution.py:175
  209.1 5.3 %add_convert_fusion = bf16[768,1536]{1,0:T(8,128)(2,1)} fusion(f32[768,1536]{1,0:T(8,128)} %fusion.101, bf16[512,768]{1,0:T(8,128)(2,1)S(1)} %copy-done.43, bf16[512,1536]{1,0:T(8,128)(2,1)S(1)} %copy-done.30), kind=kOutput, calls=%fused_computation.17 | convolution fusion | flops 1210318848 | bytes 9437184 | tf_op jit(solution)/shard_map/dot_general | solution.py:175
  214.3 4.7 %collective-permute-done.20 = bf16[512,768]{1,0:T(8,128)(2,1)S(1)} collective-permute-done((bf16[512,768]{1,0:T(8,128)(2,1)S(1)}, bf16[512,768]{1,0:T(8,128)(2,1)S(1)}, u32[]{:S(2)}, u32[]{:S(2)}) %collective-permute-start.20) | collective-permute-done | bytes 786464 | tf_op jit(solution)/shard_map/ppermute | solution.py:16
  226.9 9.0 %fusion.54 = bf16[12,64,512]{2,1,0:T(8,128)(2,1)} fusion(bf16[512,12,64]{0,2,1:T(8,128)(2,1)} %bitcast.165, f32[12,512]{1,0:T(8,128)S(1)} %copy-done.54, f32[12,512,512]{1,2,0:T(8,128)} %copy-done.2, pred[512,512]{0,1:T(8,128)(4,1)S(1)} %copy-done.17), kind=kOutput, calls=%fused_computation.109 | convolution fusion | flops 415629312 | bytes 14442496 | tf_op jit(solution)/shard_map/phqk,pqhd->pkhd/dot_general | solution.py:208
  235.9 9.6 %multiply_reduce_fusion = (f32[12,512]{1,0:T(8,128)S(1)}, f32[12,512,512]{1,2,0:T(8,128)}) fusion(f32[12,512]{1,0:T(8,128)S(1)} %copy-done.54, f32[12,512,512]{1,2,0:T(8,128)} %copy-done.2, pred[512,512]{0,1:T(8,128)(4,1)S(1)} %copy-done.17, bf16[512,12,64]{0,2,1:T(8,128)(2,1)S(1)} %bitcast.166, bf16[512,12,64]{0,2,1:T(8,128)(2,1)S(1)} %bitcast.164), kind=kOutput, calls=%fused_computation.1 | convolution fusion | flops 418375680 | bytes 27049984 | tf_op jit(solution)/shard_map/pqhd,pkhd->phqk/dot_general | solution.py:214
  245.5 7.1 %multiply_convert_fusion = bf16[12,512,512]{1,2,0:T(8,128)(2,1)S(1)} fusion(f32[12,512,512]{1,2,0:T(8,128)} %get-tuple-element.116, f32[12,512]{1,0:T(8,128)S(1)} %get-tuple-element.115, f32[12,512]{1,0:T(8,128)S(1)} %copy-done.54, f32[12,512,512]{1,2,0:T(8,128)S(1)} %bitcast.154, pred[512,512]{0,1:T(8,128)(4,1)S(1)} %copy-done.17), kind=kLoop, calls=%fused_computation | loop fusion | flops 18874368 | bytes 31768576 | tf_op jit(solution)/shard_map/convert_element_type | solution.py:218
  279.5 4.5 %concatenate.118 = bf16[32,24,1545]{2,1,0:T(8,128)(2,1)S(1)} concatenate(bf16[32,24,768]{2,1,0:T(8,128)(2,1)} %slice.230, bf16[32,24,3]{2,1,0:T(8,128)(2,1)} %bitcast.174, bf16[32,24,768]{2,1,0:T(8,128)(2,1)} %convolution_convert_fusion.1, bf16[32,24,1]{2,1,0:T(8,128)(2,1)} %stack.65, bf16[32,24,1]{2,1,0:T(8,128)(2,1)} %stack.66, bf16[32,24,1]{2,1,0:T(8,128)(2,1)} %stack.67, ...), dimensions={2} | concatenate | bytes 4746240 | tf_op jit(solution)/shard_map/concatenate | solution.py:446
  295.7 8.8 %collective-permute-done.22 = f32[256,768]{1,0:T(8,128)} collective-permute-done((f32[256,768]{1,0:T(8,128)}, f32[256,768]{1,0:T(8,128)}, u32[]{:S(2)}, u32[]{:S(2)}) %collective-permute-start.22) | collective-permute-done | bytes 786464 | tf_op jit(solution)/shard_map/ppermute | solution.py:16
  311.0 12.8 %collective-permute-done.24 = bf16[2,2,2,24,1536]{4,3,2,0,1:T(8,128)(2,1)S(1)} collective-permute-done((bf16[2,2,2,24,1536]{4,3,2,0,1:T(8,128)(2,1)S(1)}, bf16[2,2,2,24,1536]{4,3,2,0,1:T(8,128)(2,1)S(1)}, u32[]{:S(2)}, u32[]{:S(2)}) %collective-permute-start.24) | collective-permute-done | bytes 589856 | tf_op jit(solution)/shard_map/ppermute | solution.py:79
  324.1 30.1 %collective-permute-done.29 = bf16[2,2,2,24,1545]{4,3,2,0,1:T(8,128)(2,1)S(1)} collective-permute-done((bf16[2,2,2,24,1545]{4,3,2,0,1:T(8,128)(2,1)S(1)}, bf16[2,2,2,24,1545]{4,3,2,0,1:T(8,128)(2,1)S(1)}, u32[]{:S(2)}, u32[]{:S(2)}) %collective-permute-start.29) | collective-permute-done | bytes 593312 | tf_op jit(solution)/shard_map/ppermute | solution.py:79
  356.3 9.2 %collective-permute-done.30 = bf16[2,2,24,1545]{3,2,1,0:T(8,128)(2,1)S(1)} collective-permute-done((bf16[2,2,24,1545]{3,2,1,0:T(8,128)(2,1)S(1)}, bf16[2,2,24,1545]{3,2,1,0:T(8,128)(2,1)S(1)}, u32[]{:S(2)}, u32[]{:S(2)}) %collective-permute-start.30) | collective-permute-done | bytes 296672 | tf_op jit(solution)/shard_map/ppermute | solution.py:79
  365.8 4.1 %collective-permute-start.27 = (bf16[24,1536]{1,0:T(8,128)(2,1)S(1)}, bf16[24,1536]{1,0:T(8,128)(2,1)S(1)}, u32[]{:S(2)}, u32[]{:S(2)}) collective-permute-start(bf16[24,1536]{1,0:T(8,128)(2,1)S(1)} %fusion.77), channel_id=1, source_target_pairs={{0,1},{1,0},{2,3},{3,2},{4,5},{5,4},{6,7},{7,6},{8,9},{9,8},{10,11... | collective-permute-start | bytes 221192 | tf_op jit(solution)/shard_map/ppermute | solution.py:79
  369.9 4.4 %collective-permute-done.31 = bf16[2,24,1545]{2,1,0:T(8,128)(2,1)S(1)} collective-permute-done((bf16[2,24,1545]{2,1,0:T(8,128)(2,1)S(1)}, bf16[2,24,1545]{2,1,0:T(8,128)(2,1)S(1)}, u32[]{:S(2)}, u32[]{:S(2)}) %collective-permute-start.31) | collective-permute-done | bytes 148352 | tf_op jit(solution)/shard_map/ppermute | solution.py:79
  (351 shorter events, 171.2 us)
Async XLA Ops:
  7.2 117.7 %all-gather.2.cloned.1.call-start = ((), (), s32[]{:S(2)}) async-start(), calls=%async_computation.1 | async-start | bytes 5222400 | tf_op jit(solution)/shard_map/all_gather | solution.py:303
  9.6 13.2 %collective-permute-start.11 = (bf16[24,1152]{1,0:T(8,128)(2,1)S(1)}, bf16[24,1152]{1,0:T(8,128)(2,1)S(1)}, u32[]{:S(2)}, u32[]{:S(2)}) collective-permute-start(bf16[24,1152]{1,0:T(8,128)(2,1)S(1)} %fusion.78), channel_id=1, source_target_pairs={{0,1},{1,0},{2,3},{3,2},{4,5},{5,4},{6,7},{7,6},{8,9},{9,8},{10,11... | collective-permute-start | bytes 165896 | tf_op jit(solution)/shard_map/ppermute | solution.py:46
  29.3 20.5 %collective-permute-start.13 = (bf16[2,2,24,1152]{3,2,1,0:T(8,128)(2,1)S(1)}, bf16[2,2,24,1152]{3,2,1,0:T(8,128)(2,1)S(1)}, u32[]{:S(2)}, u32[]{:S(2)}) collective-permute-start(bf16[2,2,24,1152]{3,2,1,0:T(8,128)(2,1)S(1)} %broadcast_select_fusion.11), channel_id=1, source_target_pairs={{0,16},{1,17},{2,18},{3,19},{4,20},{5,21},{6,22},{7,23},{8,24},{9,... | collective-permute-start | bytes 663560 | tf_op jit(solution)/shard_map/ppermute | solution.py:46
  32.0 34.6 %collective-permute-start.9 = (bf16[2,2,2,24,1024]{4,3,2,0,1:T(8,128)(2,1)S(1)}, bf16[2,2,2,24,1024]{4,3,2,0,1:T(8,128)(2,1)S(1)}, u32[]{:S(2)}, u32[]{:S(2)}) collective-permute-start(bf16[2,2,2,24,1024]{4,3,2,0,1:T(8,128)(2,1)S(1)} %broadcast_select_fusion.7), channel_id=1, source_target_pairs={{0,16},{1,17},{2,18},{3,19},{4,20},{5,21},{6,22},{7,23},{8,24},{9,... | collective-permute-start | bytes 1179656 | tf_op jit(solution)/shard_map/ppermute | solution.py:46
  34.8 15.4 %collective-permute-start.4 = (bf16[2,2,2,24,1024]{4,3,2,0,1:T(8,128)(2,1)S(1)}, bf16[2,2,2,24,1024]{4,3,2,0,1:T(8,128)(2,1)S(1)}, u32[]{:S(2)}, u32[]{:S(2)}) collective-permute-start(bf16[2,2,2,24,1024]{4,3,2,0,1:T(8,128)(2,1)S(1)} %broadcast_select_fusion.9), channel_id=1, source_target_pairs={{0,4},{1,5},{2,6},{3,7},{4,0},{5,1},{6,2},{7,3},{8,12},{9,13},{10,... | collective-permute-start | bytes 1179656 | tf_op jit(solution)/shard_map/ppermute | solution.py:46
  50.0 16.4 %collective-permute-start.14 = (bf16[2,2,2,24,1152]{4,3,2,1,0:T(8,128)(2,1)S(1)}, bf16[2,2,2,24,1152]{4,3,2,1,0:T(8,128)(2,1)S(1)}, u32[]{:S(2)}, u32[]{:S(2)}) collective-permute-start(bf16[2,2,2,24,1152]{4,3,2,1,0:T(8,128)(2,1)S(1)} %broadcast_select_fusion.6), channel_id=1, source_target_pairs={{0,8},{1,9},{2,10},{3,11},{4,12},{5,13},{6,14},{7,15},{8,0},{9,1},... | collective-permute-start | bytes 1327112 | tf_op jit(solution)/shard_map/ppermute | solution.py:46
  50.3 17.8 %collective-permute-start.5 = (bf16[2,2,2,2,24,1024]{5,4,3,0,1,2:T(8,128)(2,1)S(1)}, bf16[2,2,2,2,24,1024]{5,4,3,0,1,2:T(8,128)(2,1)S(1)}, u32[]{:S(2)}, u32[]{:S(2)}) collective-permute-start(bf16[2,2,2,2,24,1024]{5,4,3,0,1,2:T(8,128)(2,1)S(1)} %broadcast_select_fusion.4), channel_id=1, source_target_pairs={{0,2},{1,3},{2,0},{3,1},{4,6},{5,7},{6,4},{7,5},{8,10},{9,11},{10,... | collective-permute-start | bytes 2359304 | tf_op jit(solution)/shard_map/ppermute | solution.py:46
  74.1 307.3 %reduce-scatter.2.cloned.1.call-start = ((), (), s32[]{:S(2)}) async-start(), calls=%async_computation.2 | async-start | bytes 5222400 | tf_op jit(solution)/shard_map/reduce_scatter | solution.py:394
  75.2 12.2 %collective-permute-start = (bf16[256,768]{1,0:T(8,128)(2,1)}, bf16[256,768]{1,0:T(8,128)(2,1)S(1)}, u32[]{:S(2)}, u32[]{:S(2)}) collective-permute-start(bf16[256,768]{1,0:T(8,128)(2,1)} %get-tuple-element.88), channel_id=1, source_target_pairs={{0,1},{1,0},{2,3},{3,2},{4,5},{5,4},{6,7},{7,6},{8,9},{9,8},{10,11... | collective-permute-start | bytes 1179656 | tf_op jit(solution)/shard_map/ppermute | solution.py:16
  77.3 39.2 %collective-permute-start.18 = (bf16[256,768]{1,0:T(8,128)(2,1)}, bf16[256,768]{1,0:T(8,128)(2,1)}, u32[]{:S(2)}, u32[]{:S(2)}) collective-permute-start(bf16[256,768]{1,0:T(8,128)(2,1)} %get-tuple-element.85), channel_id=1, source_target_pairs={{0,1},{1,0},{2,3},{3,2},{4,5},{5,4},{6,7},{7,6},{8,9},{9,8},{10,11... | collective-permute-start | bytes 1179656 | tf_op jit(solution)/shard_map/ppermute | solution.py:16
  116.4 18.1 %collective-permute-start.16 = (bf16[512,768]{1,0:T(8,128)(2,1)S(1)}, bf16[512,768]{1,0:T(8,128)(2,1)}, u32[]{:S(2)}, u32[]{:S(2)}) collective-permute-start(bf16[512,768]{1,0:T(8,128)(2,1)S(1)} %fusion.58), channel_id=1, source_target_pairs={{0,1},{1,0},{2,3},{3,2},{4,5},{5,4},{6,7},{7,6},{8,9},{9,8},{10,11... | collective-permute-start | bytes 2359304 | tf_op jit(solution)/shard_map/ppermute | solution.py:16
  146.9 17.1 %collective-permute-start.17 = (bf16[512,768]{1,0:T(8,128)(2,1)S(1)}, bf16[512,768]{1,0:T(8,128)(2,1)S(1)}, u32[]{:S(2)}, u32[]{:S(2)}) collective-permute-start(bf16[512,768]{1,0:T(8,128)(2,1)S(1)} %fusion.51), channel_id=1, source_target_pairs={{0,1},{1,0},{2,3},{3,2},{4,5},{5,4},{6,7},{7,6},{8,9},{9,8},{10,11... | collective-permute-start | bytes 2359304 | tf_op jit(solution)/shard_map/ppermute | solution.py:16
  176.1 16.7 %collective-permute-start.19 = (bf16[512,768]{1,0:T(8,128)(2,1)}, bf16[512,768]{1,0:T(8,128)(2,1)S(1)}, u32[]{:S(2)}, u32[]{:S(2)}) collective-permute-start(bf16[512,768]{1,0:T(8,128)(2,1)} %get-tuple-element.54), channel_id=1, source_target_pairs={{0,1},{1,0},{2,3},{3,2},{4,5},{5,4},{6,7},{7,6},{8,9},{9,8},{10,11... | collective-permute-start | bytes 2359304 | tf_op jit(solution)/shard_map/ppermute | solution.py:16
  203.0 16.1 %collective-permute-start.20 = (bf16[512,768]{1,0:T(8,128)(2,1)S(1)}, bf16[512,768]{1,0:T(8,128)(2,1)S(1)}, u32[]{:S(2)}, u32[]{:S(2)}) collective-permute-start(bf16[512,768]{1,0:T(8,128)(2,1)S(1)} %fusion.48), channel_id=1, source_target_pairs={{0,1},{1,0},{2,3},{3,2},{4,5},{5,4},{6,7},{7,6},{8,9},{9,8},{10,11... | collective-permute-start | bytes 2359304 | tf_op jit(solution)/shard_map/ppermute | solution.py:16
  272.2 20.7 %collective-permute-start.21 = (f32[256,768]{1,0:T(8,128)}, f32[256,768]{1,0:T(8,128)}, u32[]{:S(2)}, u32[]{:S(2)}) collective-permute-start(f32[256,768]{1,0:T(8,128)} %get-tuple-element.84), channel_id=1, source_target_pairs={{0,1},{1,0},{2,3},{3,2},{4,5},{5,4},{6,7},{7,6},{8,9},{9,8},{10,11... | collective-permute-start | bytes 2359304 | tf_op jit(solution)/shard_map/ppermute | solution.py:16
  276.8 27.7 %collective-permute-start.22 = (f32[256,768]{1,0:T(8,128)}, f32[256,768]{1,0:T(8,128)}, u32[]{:S(2)}, u32[]{:S(2)}) collective-permute-start(f32[256,768]{1,0:T(8,128)} %get-tuple-element.27), channel_id=1, source_target_pairs={{0,1},{1,0},{2,3},{3,2},{4,5},{5,4},{6,7},{7,6},{8,9},{9,8},{10,11... | collective-permute-start | bytes 2359304 | tf_op jit(solution)/shard_map/ppermute | solution.py:16
  279.5 27.8 %collective-permute-start.23 = (bf16[2,2,2,2,24,1536]{5,4,3,0,1,2:T(8,128)(2,1)}, bf16[2,2,2,2,24,1536]{5,4,3,0,1,2:T(8,128)(2,1)}, u32[]{:S(2)}, u32[]{:S(2)}) collective-permute-start(bf16[2,2,2,2,24,1536]{5,4,3,0,1,2:T(8,128)(2,1)} %bitcast.152), channel_id=1, source_target_pairs={{0,2},{1,3},{2,0},{3,1},{4,6},{5,7},{6,4},{7,5},{8,10},{9,11},{10,... | collective-permute-start | bytes 3538952 | tf_op jit(solution)/shard_map/ppermute | solution.py:79
  286.5 22.8 %collective-permute-start.28 = (bf16[2,2,2,2,24,1545]{5,4,3,1,2,0:T(8,128)(2,1)}, bf16[2,2,2,2,24,1545]{5,4,3,1,2,0:T(8,128)(2,1)S(1)}, u32[]{:S(2)}, u32[]{:S(2)}) collective-permute-start(bf16[2,2,2,2,24,1545]{5,4,3,1,2,0:T(8,128)(2,1)} %bitcast.151), channel_id=1, source_target_pairs={{0,2},{1,3},{2,0},{3,1},{4,6},{5,7},{6,4},{7,5},{8,10},{9,11},{10,... | collective-permute-start | bytes 3559688 | tf_op jit(solution)/shard_map/ppermute | solution.py:79
  309.2 14.7 %collective-permute-start.24 = (bf16[2,2,2,24,1536]{4,3,2,0,1:T(8,128)(2,1)S(1)}, bf16[2,2,2,24,1536]{4,3,2,0,1:T(8,128)(2,1)S(1)}, u32[]{:S(2)}, u32[]{:S(2)}) collective-permute-start(bf16[2,2,2,24,1536]{4,3,2,0,1:T(8,128)(2,1)S(1)} %fusion.65), channel_id=1, source_target_pairs={{0,4},{1,5},{2,6},{3,7},{4,0},{5,1},{6,2},{7,3},{8,12},{9,13},{10,... | collective-permute-start | bytes 1769480 | tf_op jit(solution)/shard_map/ppermute | solution.py:79
  309.6 44.6 %collective-permute-start.29 = (bf16[2,2,2,24,1545]{4,3,2,0,1:T(8,128)(2,1)S(1)}, bf16[2,2,2,24,1545]{4,3,2,0,1:T(8,128)(2,1)S(1)}, u32[]{:S(2)}, u32[]{:S(2)}) collective-permute-start(bf16[2,2,2,24,1545]{4,3,2,0,1:T(8,128)(2,1)S(1)} %fusion.64), channel_id=1, source_target_pairs={{0,16},{1,17},{2,18},{3,19},{4,20},{5,21},{6,22},{7,23},{8,24},{9,... | collective-permute-start | bytes 1779848 | tf_op jit(solution)/shard_map/ppermute | solution.py:79
  324.0 32.1 %collective-permute-start.25 = (bf16[2,2,24,1536]{3,2,1,0:T(8,128)(2,1)S(1)}, bf16[2,2,24,1536]{3,2,1,0:T(8,128)(2,1)S(1)}, u32[]{:S(2)}, u32[]{:S(2)}) collective-permute-start(bf16[2,2,24,1536]{3,2,1,0:T(8,128)(2,1)S(1)} %fusion.72), channel_id=1, source_target_pairs={{0,8},{1,9},{2,10},{3,11},{4,12},{5,13},{6,14},{7,15},{8,0},{9,1},... | collective-permute-start | bytes 884744 | tf_op jit(solution)/shard_map/ppermute | solution.py:79
  354.4 11.1 %collective-permute-start.30 = (bf16[2,2,24,1545]{3,2,1,0:T(8,128)(2,1)S(1)}, bf16[2,2,24,1545]{3,2,1,0:T(8,128)(2,1)S(1)}, u32[]{:S(2)}, u32[]{:S(2)}) collective-permute-start(bf16[2,2,24,1545]{3,2,1,0:T(8,128)(2,1)S(1)} %fusion.71), channel_id=1, source_target_pairs={{0,4},{1,5},{2,6},{3,7},{4,0},{5,1},{6,2},{7,3},{8,12},{9,13},{10,... | collective-permute-start | bytes 889928 | tf_op jit(solution)/shard_map/ppermute | solution.py:79
  356.2 9.5 %collective-permute-start.26 = (bf16[2,24,1536]{2,1,0:T(8,128)(2,1)S(1)}, bf16[2,24,1536]{2,1,0:T(8,128)(2,1)S(1)}, u32[]{:S(2)}, u32[]{:S(2)}) collective-permute-start(bf16[2,24,1536]{2,1,0:T(8,128)(2,1)S(1)} %fusion.74), channel_id=1, source_target_pairs={{0,16},{1,17},{2,18},{3,19},{4,20},{5,21},{6,22},{7,23},{8,24},{9,... | collective-permute-start | bytes 442376 | tf_op jit(solution)/shard_map/ppermute | solution.py:79
  365.8 11.7 %collective-permute-start.27 = (bf16[24,1536]{1,0:T(8,128)(2,1)S(1)}, bf16[24,1536]{1,0:T(8,128)(2,1)S(1)}, u32[]{:S(2)}, u32[]{:S(2)}) collective-permute-start(bf16[24,1536]{1,0:T(8,128)(2,1)S(1)} %fusion.77), channel_id=1, source_target_pairs={{0,1},{1,0},{2,3},{3,2},{4,5},{5,4},{6,7},{7,6},{8,9},{9,8},{10,11... | collective-permute-start | bytes 221192 | tf_op jit(solution)/shard_map/ppermute | solution.py:79
  (86 other events, 626.4 us)
Sparse Core Ops, SparseCore 0:
  74.3 50.6 all-gather.1
  290.1 88.6 reduce-scatter.1

commit v10 on v9

--- a/solution.py
+++ b/solution.py
@@ -1,3 +1,5 @@
+import itertools
+
 import jax
 import jax.numpy as jnp
 from jax import lax
@@ -21,11 +23,10 @@
     core_bit = narrow_n.bit_length() - 1
     narrow_bits = list(range(core_bit))
     wide_bits = [b for b in reversed(range(core_bit + 1, bits))]
-    orders = []
-    for p in range(parts):
-        k = p % max(1, len(wide_bits))
-        orders.append(narrow_bits + wide_bits[k:] + wide_bits[:k] + [core_bit])
-    return orders
+    rotations = [wide_bits[k:] + wide_bits[:k] for k in range(max(1, len(wide_bits)))]
+    others = [list(p) for p in itertools.permutations(wide_bits) if list(p) not in rotations]
+    choices = rotations + others
+    return [narrow_bits + choices[p % len(choices)] + [core_bit] for p in range(parts)]
 
 
 def is_pow2(n):
@@ -439,13 +440,13 @@
     qkv_wsum = contract_rows(pack_in, grad_qkv)
     qkv_bsum = jnp.sum(grad_qkv.astype(jnp.float32), axis=0).reshape(3, D)
     wsum_parts = qkv_wsum.reshape(total, share, 3 * D).astype(jnp.bfloat16)
-    cut = 3 * D * 2 // 3 // 128 * 128
     late_mine = scatter_sum_parts(
         [
-            wsum_parts[..., :cut],
+            wsum_parts[..., :D],
+            wsum_parts[..., D : 2 * D],
+            wsum_parts[..., 2 * D :],
             jnp.concatenate(
                 [
-                    wsum_parts[..., cut:],
                     qkv_bsum.T.reshape(total, share, 3).astype(jnp.bfloat16),
                     early.astype(jnp.bfloat16),
                 ],

time: 399 us -> 351 us (0.88)
  waiting for transfers between devices: 140 us -> 89.3 us
  starting transfers between devices: 37.6 us -> 43.9 us
  matrix products: 97.6 us -> 93.4 us
  other arithmetic: 50.3 us -> 54.4 us
    ppermute x10 -> x20, waiting for transfers between devices: 58.3 us -> 8.64 us  [halving_scatter(): lax.ppermute(theirs.astype(jnp.bfloat16), ALL, [(i, i ^ 1 << b) for i in...]
    dot_general x6, matrix products: 21.8 us -> 15.3 us  [contract_rows(): lax.dot_general(left_op, right_op, (((0,), (0,)), ((), ())), preferred_el...]
    ppermute x10 -> x20, starting transfers between devices: 11.1 us -> 17.4 us  [halving_scatter(): lax.ppermute(theirs.astype(jnp.bfloat16), ALL, [(i, i ^ 1 << b) for i in...]
    dynamic_slice x4 -> x0, local copies, waits for them, and re-layouts: 4.84 us -> none  [the longest x2 2.59 us: halving_scatter(): mine = lax.dynamic_index_in_dim(cur, bit, axis=a, keepdims=False)]
  transfers between devices with their start and end apart: 35 -> 45, of which waited for: 19 -> 18; matrix products, arithmetic and copies ran while one was open for 25% -> 43% of each run, Pallas kernels for 0% -> 0%
where the time goes in v10:
time: 351 us; the launch traced here: 346 us
  matrix products  93.4 us (27%)
  waiting for transfers between devices  89.3 us (25%)
  other arithmetic  54.4 us (15%)
  local copies, waits for them, and re-layouts  49.2 us (14%)
  starting transfers between devices  43.9 us (13%)
  between operations  15.8 us (5%)
    ppermute x8, waiting for transfers between devices, swapped(): lax.ppermute(shard, axis, [(i, i ^ 1 << bit) for i in range(lax.axis_size...  39.3 us
    ppermute x15, waiting for transfers between devices, doubling_gather(): other = lax.ppermute(cur, ALL, [(i, i ^ 1 << b) for i in range(total)])  36.3 us
    dot_general x2, matrix products, ffn_forward(): jnp.dot(rows, inner_cols, preferred_element_type=jnp.float32) + inner_offset  21 us
    ppermute x15, starting transfers between devices, doubling_gather(): other = lax.ppermute(cur, ALL, [(i, i ^ 1 << b) for i in range(total)])  18.2 us
    ppermute x20, starting transfers between devices, halving_scatter(): lax.ppermute(theirs.astype(jnp.bfloat16), ALL, [(i, i ^ 1 << b) for i in...  17.4 us
    dot_general x6, matrix products, contract_rows(): lax.dot_general(left_op, right_op, (((0,), (0,)), ((), ())), preferred_el...  15.3 us
    dot_general x6, matrix products, contract_cols(): lax.dot_general(left_op, right_op, (((1,), (1,)), ((), ())), preferred_el...  15.2 us
    dot_general x2, matrix products, ffn_backward(): grad_act = jnp.dot(grads, outer_cols, preferred_element_type=jnp.float32)  10 us
  transfers between devices with their start and end apart: 45, of which 18 were waited for; matrix products, arithmetic and copies ran while one was open for 43% of the time, Pallas kernels for 0%

profile of v10, /device:TPU:0, one launch (start us, length us, event | category | flops | bytes accessed | tf_op | source)
XLA Modules:
  0.0 346.0 jit_solution(12718361822150734126)
XLA Ops:
  36.0 13.8 %collective-permute-done.13 = bf16[2,2,24,1152]{3,2,1,0:T(8,128)(2,1)S(1)} collective-permute-done((bf16[2,2,24,1152]{3,2,1,0:T(8,128)(2,1)S(1)}, bf16[2,2,24,1152]{3,2,1,0:T(8,128)(2,1)S(1)}, u32[]{:S(2)}, u32[]{:S(2)}) %collective-permute-start.13) | collective-permute-done | bytes 221216 | tf_op jit(solution)/shard_map/ppermute | solution.py:47
  50.4 16.0 %collective-permute-done.14 = bf16[2,2,2,24,1152]{4,3,2,1,0:T(8,128)(2,1)S(1)} collective-permute-done((bf16[2,2,2,24,1152]{4,3,2,1,0:T(8,128)(2,1)S(1)}, bf16[2,2,2,24,1152]{4,3,2,1,0:T(8,128)(2,1)S(1)}, u32[]{:S(2)}, u32[]{:S(2)}) %collective-permute-start.14) | collective-permute-done | bytes 442400 | tf_op jit(solution)/shard_map/ppermute | solution.py:47
  81.0 6.5 %collective-permute-done = bf16[256,768]{1,0:T(8,128)(2,1)S(1)} collective-permute-done((bf16[256,768]{1,0:T(8,128)(2,1)}, bf16[256,768]{1,0:T(8,128)(2,1)S(1)}, u32[]{:S(2)}, u32[]{:S(2)}) %collective-permute-start) | collective-permute-done | bytes 393248 | tf_op jit(solution)/shard_map/ppermute | solution.py:18
  110.8 4.0 %fusion.57 = bf16[12,64,512]{2,1,0:T(8,128)(2,1)S(1)} fusion(bf16[512,12,64]{0,2,1:T(8,128)(2,1)S(1)} %bitcast.205, f32[12,512]{1,0:T(8,128)S(1)} %fusion, f32[12,512]{1,0:T(8,128)S(1)} %get-tuple-element.102, f32[12,512,512]{1,2,0:T(8,128)S(1)} %get-tuple-element.103, pred[512,512]{0,1:T(8,128)(4,1)S(1)} %copy-done.13), kind=kOutput, calls=%fused_computation.108 | convolution fusion | flops 418775040 | bytes 14467072 | tf_op jit(solution)/shard_map/phqk,pkhd->pqhd/dot_general | solution.py:201
  120.0 5.0 %all-gather.2.cloned.1.call-done = bf16[768,3074]{1,0:T(8,128)(2,1)} async-done(((bf16[48,3074]{1,0:T(8,128)(2,1)}), bf16[768,3074]{1,0:T(8,128)(2,1)}) %all-gather.2.cloned.1.call-update) | async-done | bytes 4721680 | tf_op jit(solution)/shard_map/all_gather | solution.py:304
  126.1 8.5 %collective-permute-done.16 = bf16[512,768]{1,0:T(8,128)(2,1)} collective-permute-done((bf16[512,768]{1,0:T(8,128)(2,1)S(1)}, bf16[512,768]{1,0:T(8,128)(2,1)}, u32[]{:S(2)}, u32[]{:S(2)}) %collective-permute-start.16) | collective-permute-done | bytes 786464 | tf_op jit(solution)/shard_map/ppermute | solution.py:18
  134.6 11.0 %multiply_convert_fusion.1 = (bf16[512,1536]{1,0:T(8,128)(2,1)S(1)}, f32[512,1536]{1,0:T(8,128)}, f32[512,1536]{1,0:T(8,128)}) fusion(f32[1536]{0:T(1024)S(1)} %reshape.659, bf16[512,768]{1,0:T(8,128)(2,1)} %collective-permute-done.16, bf16[768,3074]{1,0:T(8,128)(2,1)} %all-gather.2.cloned.1.call-done), kind=kOutput, calls=%fused_computation.28 | convolution fusion | flops 1259864064 | bytes 11016192 | tf_op jit(solution)/shard_map/dot_general | solution.py:230
  147.9 10.0 %multiply_convert_fusion.2 = (bf16[512,1536]{1,0:T(8,128)(2,1)S(1)}, f32[512,1536]{1,0:T(8,128)}, f32[512,1536]{1,0:T(8,128)}) fusion(f32[1536]{0:T(1024)S(1)} %reshape.659, bf16[512,768]{1,0:T(8,128)(2,1)S(1)} %fusion.58, bf16[768,3074]{1,0:T(8,128)(2,1)S(1)} %copy-done.64), kind=kOutput, calls=%fused_computation.41 | convolution fusion | flops 1259864064 | bytes 11018240 | tf_op jit(solution)/shard_map/dot_general | solution.py:230
  157.8 6.4 %collective-permute-done.17 = bf16[512,768]{1,0:T(8,128)(2,1)S(1)} collective-permute-done((bf16[512,768]{1,0:T(8,128)(2,1)S(1)}, bf16[512,768]{1,0:T(8,128)(2,1)S(1)}, u32[]{:S(2)}, u32[]{:S(2)}) %collective-permute-start.17) | collective-permute-done | bytes 786464 | tf_op jit(solution)/shard_map/ppermute | solution.py:18
  170.7 3.5 %fusion.100 = (f32[512]{0:T(512)S(1)}, f32[512,768]{1,0:T(8,128)S(1)}, f32[512,768]{1,0:T(8,128)}) fusion(f32[512]{0:T(512)} %multiply_multiply_fusion.11, f32[512,768]{1,0:T(8,128)} %copy-done.3, f32[512]{0:T(512)} %copy-done.56, f32[512]{0:T(512)} %copy-done.59, f32[768]{0:T(1024)S(1)} %get-tuple-element.35, bf16[256,768]{1,0:T(8,128)(2,1)S(1)} %copy-done.7, ...), kind=kLoop, calls=%fused_computation.277 | loop fusion | flops 7863808 | bytes 5519361 | tf_op jit(solution)/shard_map/transpose(jvp())/reduce_sum | solution.py:139
  177.8 6.1 %convert_reduce_fusion.1 = (f32[1536]{0:T(1024)S(1)}, bf16[512,1536]{1,0:T(8,128)(2,1)S(1)}) fusion(f32[512,1536]{1,0:T(8,128)} %get-tuple-element.63, f32[512,1536]{1,0:T(8,128)} %get-tuple-element.107, bf16[512,768]{1,0:T(8,128)(2,1)} %get-tuple-element.54, bf16[768,3074]{1,0:T(8,128)(2,1)} %all-gather.2.cloned.1.call-done), kind=kOutput, calls=%fused_computation.25 | convolution fusion | flops 1220540928 | bytes 11016192 | tf_op jit(solution)/shard_map/dot_general | solution.py:237
  187.0 6.1 %collective-permute-done.19 = bf16[512,768]{1,0:T(8,128)(2,1)S(1)} collective-permute-done((bf16[512,768]{1,0:T(8,128)(2,1)}, bf16[512,768]{1,0:T(8,128)(2,1)S(1)}, u32[]{:S(2)}, u32[]{:S(2)}) %collective-permute-start.19) | collective-permute-done | bytes 786464 | tf_op jit(solution)/shard_map/ppermute | solution.py:18
  193.1 3.9 %convert_reduce_fusion = (f32[1536]{0:T(1024)S(1)}, bf16[512,1536]{1,0:T(8,128)(2,1)S(1)}) fusion(f32[512,1536]{1,0:T(8,128)S(1)} %copy-done.67, f32[512,1536]{1,0:T(8,128)S(1)} %copy-done.68, bf16[512,768]{1,0:T(8,128)(2,1)S(1)} %collective-permute-done.19, bf16[768,3074]{1,0:T(8,128)(2,1)} %all-gather.2.cloned.1.call-done), kind=kOutput, calls=%fused_computation.24 | convolution fusion | flops 1220540928 | bytes 11016192 | tf_op jit(solution)/shard_map/dot_general | solution.py:237
  197.0 4.0 %fusion.48 = bf16[512,768]{1,0:T(8,128)(2,1)} fusion(bf16[512,1536]{1,0:T(8,128)(2,1)S(1)} %get-tuple-element.115, bf16[768,3074]{1,0:T(8,128)(2,1)} %all-gather.2.cloned.1.call-done), kind=kOutput, calls=%fused_computation.105 | convolution fusion | flops 1208352768 | bytes 4718592 | tf_op jit(solution)/shard_map/dot_general | solution.py:182
  202.8 4.1 %add_convert_fusion.1 = bf16[768,1536]{1,0:T(8,128)(2,1)} fusion(f32[768,1536]{1,0:T(8,128)S(1)} %fusion.107, bf16[512,768]{1,0:T(8,128)(2,1)} %collective-permute-done.16, bf16[512,1536]{1,0:T(8,128)(2,1)S(1)} %get-tuple-element.115), kind=kOutput, calls=%fused_computation.18 | convolution fusion | flops 1210318848 | bytes 9437184 | tf_op jit(solution)/shard_map/dot_general | solution.py:176
  210.4 5.4 %pad_maximum_fusion.1 = bf16[768,3074]{1,0:T(8,128)(2,1)} fusion(bf16[768,2]{1,0:T(8,128)(2,1)S(1)} %add.373, bf16[768,1536]{1,0:T(8,128)(2,1)} %add_convert_fusion, bf16[768,1536]{1,0:T(8,128)(2,1)} %add_convert_fusion.1), kind=kLoop, calls=%fused_computation.13 | loop fusion | flops 14164992 | bytes 9443328 | tf_op jit(solution)/shard_map/concatenate | solution.py:394
  217.3 3.9 %convert_add_fusion = f32[512,768]{1,0:T(8,128)S(1)} fusion(bf16[512,768]{1,0:T(8,128)(2,1)} %collective-permute-done.20, bf16[512,1536]{1,0:T(8,128)(2,1)} %copy-done.31, bf16[768,3074]{1,0:T(8,128)(2,1)} %all-gather.2.cloned.1.call-done), kind=kOutput, calls=%fused_computation.78 | convolution fusion | flops 1208745984 | bytes 6291456 | tf_op jit(solution)/shard_map/dot_general | solution.py:182
  226.5 9.8 %fusion.54 = bf16[12,64,512]{2,1,0:T(8,128)(2,1)} fusion(bf16[512,12,64]{0,2,1:T(8,128)(2,1)} %bitcast.207, f32[12,512]{1,0:T(8,128)S(1)} %copy-done.51, f32[12,512,512]{1,2,0:T(8,128)} %copy-done.2, pred[512,512]{0,1:T(8,128)(4,1)S(1)} %copy-done.14), kind=kOutput, calls=%fused_computation.107 | convolution fusion | flops 415629312 | bytes 14442496 | tf_op jit(solution)/shard_map/phqk,pqhd->pkhd/dot_general | solution.py:209
  236.3 10.0 %multiply_reduce_fusion = (f32[12,512]{1,0:T(8,128)S(1)}, f32[12,512,512]{1,2,0:T(8,128)}) fusion(f32[12,512]{1,0:T(8,128)S(1)} %copy-done.51, f32[12,512,512]{1,2,0:T(8,128)} %copy-done.2, pred[512,512]{0,1:T(8,128)(4,1)S(1)} %copy-done.14, bf16[512,12,64]{0,2,1:T(8,128)(2,1)S(1)} %bitcast.208, bf16[512,12,64]{0,2,1:T(8,128)(2,1)S(1)} %bitcast.206), kind=kOutput, calls=%fused_computation.1 | convolution fusion | flops 418375680 | bytes 27049984 | tf_op jit(solution)/shard_map/pqhd,pkhd->phqk/dot_general | solution.py:215
  246.3 7.2 %multiply_convert_fusion = bf16[12,512,512]{1,2,0:T(8,128)(2,1)S(1)} fusion(f32[12,512,512]{1,2,0:T(8,128)} %get-tuple-element.111, f32[12,512]{1,0:T(8,128)S(1)} %get-tuple-element.110, f32[12,512]{1,0:T(8,128)S(1)} %copy-done.51, f32[12,512,512]{1,2,0:T(8,128)S(1)} %bitcast.193, pred[512,512]{0,1:T(8,128)(4,1)S(1)} %copy-done.14), kind=kLoop, calls=%fused_computation | loop fusion | flops 18874368 | bytes 31768576 | tf_op jit(solution)/shard_map/convert_element_type | solution.py:219
  258.4 3.2 add_add_fusion.4
  282.0 3.3 concatenate.121
  295.3 10.3 %collective-permute-done.22 = f32[256,768]{1,0:T(8,128)S(1)} collective-permute-done((f32[256,768]{1,0:T(8,128)}, f32[256,768]{1,0:T(8,128)S(1)}, u32[]{:S(2)}, u32[]{:S(2)}) %collective-permute-start.22) | collective-permute-done | bytes 786464 | tf_op jit(solution)/shard_map/ppermute | solution.py:18
  308.9 6.7 %collective-permute-done.29 = bf16[2,2,2,24,777]{4,3,2,1,0:T(8,128)(2,1)S(1)} collective-permute-done((bf16[2,2,2,24,777]{4,3,2,1,0:T(8,128)(2,1)S(1)}, bf16[2,2,2,24,777]{4,3,2,1,0:T(8,128)(2,1)S(1)}, u32[]{:S(2)}, u32[]{:S(2)}) %collective-permute-start.29) | collective-permute-done | bytes 298400 | tf_op jit(solution)/shard_map/ppermute | solution.py:80
  (385 shorter events, 161.3 us)
Async XLA Ops:
  7.2 117.7 %all-gather.2.cloned.1.call-start = ((), (), s32[]{:S(2)}) async-start(), calls=%async_computation.1 | async-start | bytes 5222400 | tf_op jit(solution)/shard_map/all_gather | solution.py:304
  9.6 13.2 %collective-permute-start.11 = (bf16[24,1152]{1,0:T(8,128)(2,1)S(1)}, bf16[24,1152]{1,0:T(8,128)(2,1)S(1)}, u32[]{:S(2)}, u32[]{:S(2)}) collective-permute-start(bf16[24,1152]{1,0:T(8,128)(2,1)S(1)} %fusion.82), channel_id=1, source_target_pairs={{0,1},{1,0},{2,3},{3,2},{4,5},{5,4},{6,7},{7,6},{8,9},{9,8},{10,11... | collective-permute-start | bytes 165896 | tf_op jit(solution)/shard_map/ppermute | solution.py:47
  29.3 20.5 %collective-permute-start.13 = (bf16[2,2,24,1152]{3,2,1,0:T(8,128)(2,1)S(1)}, bf16[2,2,24,1152]{3,2,1,0:T(8,128)(2,1)S(1)}, u32[]{:S(2)}, u32[]{:S(2)}) collective-permute-start(bf16[2,2,24,1152]{3,2,1,0:T(8,128)(2,1)S(1)} %broadcast_select_fusion.11), channel_id=1, source_target_pairs={{0,16},{1,17},{2,18},{3,19},{4,20},{5,21},{6,22},{7,23},{8,24},{9,... | collective-permute-start | bytes 663560 | tf_op jit(solution)/shard_map/ppermute | solution.py:47
  32.0 34.6 %collective-permute-start.9 = (bf16[2,2,2,24,1024]{4,3,2,0,1:T(8,128)(2,1)S(1)}, bf16[2,2,2,24,1024]{4,3,2,0,1:T(8,128)(2,1)S(1)}, u32[]{:S(2)}, u32[]{:S(2)}) collective-permute-start(bf16[2,2,2,24,1024]{4,3,2,0,1:T(8,128)(2,1)S(1)} %broadcast_select_fusion.7), channel_id=1, source_target_pairs={{0,16},{1,17},{2,18},{3,19},{4,20},{5,21},{6,22},{7,23},{8,24},{9,... | collective-permute-start | bytes 1179656 | tf_op jit(solution)/shard_map/ppermute | solution.py:47
  34.8 15.4 %collective-permute-start.4 = (bf16[2,2,2,24,1024]{4,3,2,0,1:T(8,128)(2,1)S(1)}, bf16[2,2,2,24,1024]{4,3,2,0,1:T(8,128)(2,1)S(1)}, u32[]{:S(2)}, u32[]{:S(2)}) collective-permute-start(bf16[2,2,2,24,1024]{4,3,2,0,1:T(8,128)(2,1)S(1)} %broadcast_select_fusion.9), channel_id=1, source_target_pairs={{0,4},{1,5},{2,6},{3,7},{4,0},{5,1},{6,2},{7,3},{8,12},{9,13},{10,... | collective-permute-start | bytes 1179656 | tf_op jit(solution)/shard_map/ppermute | solution.py:47
  50.0 16.4 %collective-permute-start.14 = (bf16[2,2,2,24,1152]{4,3,2,1,0:T(8,128)(2,1)S(1)}, bf16[2,2,2,24,1152]{4,3,2,1,0:T(8,128)(2,1)S(1)}, u32[]{:S(2)}, u32[]{:S(2)}) collective-permute-start(bf16[2,2,2,24,1152]{4,3,2,1,0:T(8,128)(2,1)S(1)} %broadcast_select_fusion.6), channel_id=1, source_target_pairs={{0,8},{1,9},{2,10},{3,11},{4,12},{5,13},{6,14},{7,15},{8,0},{9,1},... | collective-permute-start | bytes 1327112 | tf_op jit(solution)/shard_map/ppermute | solution.py:47
  50.3 17.8 %collective-permute-start.5 = (bf16[2,2,2,2,24,1024]{5,4,3,0,1,2:T(8,128)(2,1)S(1)}, bf16[2,2,2,2,24,1024]{5,4,3,0,1,2:T(8,128)(2,1)S(1)}, u32[]{:S(2)}, u32[]{:S(2)}) collective-permute-start(bf16[2,2,2,2,24,1024]{5,4,3,0,1,2:T(8,128)(2,1)S(1)} %broadcast_select_fusion.4), channel_id=1, source_target_pairs={{0,2},{1,3},{2,0},{3,1},{4,6},{5,7},{6,4},{7,5},{8,10},{9,11},{10,... | collective-permute-start | bytes 2359304 | tf_op jit(solution)/shard_map/ppermute | solution.py:47
  74.2 260.0 %reduce-scatter.2.cloned.1.call-start = ((), (), s32[]{:S(2)}) async-start(), calls=%async_computation.2 | async-start | bytes 5222400 | tf_op jit(solution)/shard_map/reduce_scatter | solution.py:395
  75.3 12.2 %collective-permute-start = (bf16[256,768]{1,0:T(8,128)(2,1)}, bf16[256,768]{1,0:T(8,128)(2,1)S(1)}, u32[]{:S(2)}, u32[]{:S(2)}) collective-permute-start(bf16[256,768]{1,0:T(8,128)(2,1)} %get-tuple-element.87), channel_id=1, source_target_pairs={{0,1},{1,0},{2,3},{3,2},{4,5},{5,4},{6,7},{7,6},{8,9},{9,8},{10,11... | collective-permute-start | bytes 1179656 | tf_op jit(solution)/shard_map/ppermute | solution.py:18
  77.4 39.3 %collective-permute-start.18 = (bf16[256,768]{1,0:T(8,128)(2,1)}, bf16[256,768]{1,0:T(8,128)(2,1)}, u32[]{:S(2)}, u32[]{:S(2)}) collective-permute-start(bf16[256,768]{1,0:T(8,128)(2,1)} %get-tuple-element.84), channel_id=1, source_target_pairs={{0,1},{1,0},{2,3},{3,2},{4,5},{5,4},{6,7},{7,6},{8,9},{9,8},{10,11... | collective-permute-start | bytes 1179656 | tf_op jit(solution)/shard_map/ppermute | solution.py:18
  116.6 18.1 %collective-permute-start.16 = (bf16[512,768]{1,0:T(8,128)(2,1)S(1)}, bf16[512,768]{1,0:T(8,128)(2,1)}, u32[]{:S(2)}, u32[]{:S(2)}) collective-permute-start(bf16[512,768]{1,0:T(8,128)(2,1)S(1)} %fusion.58), channel_id=1, source_target_pairs={{0,1},{1,0},{2,3},{3,2},{4,5},{5,4},{6,7},{7,6},{8,9},{9,8},{10,11... | collective-permute-start | bytes 2359304 | tf_op jit(solution)/shard_map/ppermute | solution.py:18
  147.1 17.1 %collective-permute-start.17 = (bf16[512,768]{1,0:T(8,128)(2,1)S(1)}, bf16[512,768]{1,0:T(8,128)(2,1)S(1)}, u32[]{:S(2)}, u32[]{:S(2)}) collective-permute-start(bf16[512,768]{1,0:T(8,128)(2,1)S(1)} %fusion.51), channel_id=1, source_target_pairs={{0,1},{1,0},{2,3},{3,2},{4,5},{5,4},{6,7},{7,6},{8,9},{9,8},{10,11... | collective-permute-start | bytes 2359304 | tf_op jit(solution)/shard_map/ppermute | solution.py:18
  176.4 16.7 %collective-permute-start.19 = (bf16[512,768]{1,0:T(8,128)(2,1)}, bf16[512,768]{1,0:T(8,128)(2,1)S(1)}, u32[]{:S(2)}, u32[]{:S(2)}) collective-permute-start(bf16[512,768]{1,0:T(8,128)(2,1)} %get-tuple-element.54), channel_id=1, source_target_pairs={{0,1},{1,0},{2,3},{3,2},{4,5},{5,4},{6,7},{7,6},{8,9},{9,8},{10,11... | collective-permute-start | bytes 2359304 | tf_op jit(solution)/shard_map/ppermute | solution.py:18
  201.0 16.3 %collective-permute-start.20 = (bf16[512,768]{1,0:T(8,128)(2,1)}, bf16[512,768]{1,0:T(8,128)(2,1)}, u32[]{:S(2)}, u32[]{:S(2)}) collective-permute-start(bf16[512,768]{1,0:T(8,128)(2,1)} %fusion.48), channel_id=1, source_target_pairs={{0,1},{1,0},{2,3},{3,2},{4,5},{5,4},{6,7},{7,6},{8,9},{9,8},{10,11... | collective-permute-start | bytes 2359304 | tf_op jit(solution)/shard_map/ppermute | solution.py:18
  265.3 26.6 %collective-permute-start.21 = (f32[256,768]{1,0:T(8,128)}, f32[256,768]{1,0:T(8,128)}, u32[]{:S(2)}, u32[]{:S(2)}) collective-permute-start(f32[256,768]{1,0:T(8,128)} %get-tuple-element.83), channel_id=1, source_target_pairs={{0,1},{1,0},{2,3},{3,2},{4,5},{5,4},{6,7},{7,6},{8,9},{9,8},{10,11... | collective-permute-start | bytes 2359304 | tf_op jit(solution)/shard_map/ppermute | solution.py:18
  272.9 12.8 %collective-permute-start.23 = (bf16[2,2,2,2,24,768]{5,4,3,2,1,0:T(8,128)(2,1)}, bf16[2,2,2,2,24,768]{5,4,3,2,1,0:T(8,128)(2,1)}, u32[]{:S(2)}, u32[]{:S(2)}) collective-permute-start(bf16[2,2,2,2,24,768]{5,4,3,2,1,0:T(8,128)(2,1)} %dynamic-slice_bitcast_fusion.3), channel_id=1, source_target_pairs={{0,2},{1,3},{2,0},{3,1},{4,6},{5,7},{6,4},{7,5},{8,10},{9,11},{10,... | collective-permute-start | bytes 1769480 | tf_op jit(solution)/shard_map/ppermute | solution.py:80
  285.7 19.9 %collective-permute-start.22 = (f32[256,768]{1,0:T(8,128)}, f32[256,768]{1,0:T(8,128)S(1)}, u32[]{:S(2)}, u32[]{:S(2)}) collective-permute-start(f32[256,768]{1,0:T(8,128)} %get-tuple-element.27), channel_id=1, source_target_pairs={{0,1},{1,0},{2,3},{3,2},{4,5},{5,4},{6,7},{7,6},{8,9},{9,8},{10,11... | collective-permute-start | bytes 2359304 | tf_op jit(solution)/shard_map/ppermute | solution.py:18
  287.5 19.4 %collective-permute-start.24 = (bf16[2,2,2,24,768]{4,3,2,1,0:T(8,128)(2,1)S(1)}, bf16[2,2,2,24,768]{4,3,2,1,0:T(8,128)(2,1)S(1)}, u32[]{:S(2)}, u32[]{:S(2)}) collective-permute-start(bf16[2,2,2,24,768]{4,3,2,1,0:T(8,128)(2,1)S(1)} %fusion.70), channel_id=1, source_target_pairs={{0,4},{1,5},{2,6},{3,7},{4,0},{5,1},{6,2},{7,3},{8,12},{9,13},{10,... | collective-permute-start | bytes 884744 | tf_op jit(solution)/shard_map/ppermute | solution.py:80
  288.9 18.2 %collective-permute-start.39 = (bf16[2,2,2,24,768]{4,3,2,1,0:T(8,128)(2,1)S(1)}, bf16[2,2,2,24,768]{4,3,2,1,0:T(8,128)(2,1)S(1)}, u32[]{:S(2)}, u32[]{:S(2)}) collective-permute-start(bf16[2,2,2,24,768]{4,3,2,1,0:T(8,128)(2,1)S(1)} %fusion.72), channel_id=1, source_target_pairs={{0,8},{1,9},{2,10},{3,11},{4,12},{5,13},{6,14},{7,15},{8,0},{9,1},... | collective-permute-start | bytes 884744 | tf_op jit(solution)/shard_map/ppermute | solution.py:80
  290.3 17.1 %collective-permute-start.34 = (bf16[2,2,2,24,768]{4,3,2,1,0:T(8,128)(2,1)S(1)}, bf16[2,2,2,24,768]{4,3,2,1,0:T(8,128)(2,1)S(1)}, u32[]{:S(2)}, u32[]{:S(2)}) collective-permute-start(bf16[2,2,2,24,768]{4,3,2,1,0:T(8,128)(2,1)S(1)} %fusion.71), channel_id=1, source_target_pairs={{0,16},{1,17},{2,18},{3,19},{4,20},{5,21},{6,22},{7,23},{8,24},{9,... | collective-permute-start | bytes 884744 | tf_op jit(solution)/shard_map/ppermute | solution.py:80
  292.0 23.7 %collective-permute-start.29 = (bf16[2,2,2,24,777]{4,3,2,1,0:T(8,128)(2,1)S(1)}, bf16[2,2,2,24,777]{4,3,2,1,0:T(8,128)(2,1)S(1)}, u32[]{:S(2)}, u32[]{:S(2)}) collective-permute-start(bf16[2,2,2,24,777]{4,3,2,1,0:T(8,128)(2,1)S(1)} %fusion.69), channel_id=1, source_target_pairs={{0,8},{1,9},{2,10},{3,11},{4,12},{5,13},{6,14},{7,15},{8,0},{9,1},... | collective-permute-start | bytes 895112 | tf_op jit(solution)/shard_map/ppermute | solution.py:80
  307.0 10.9 %collective-permute-start.25 = (bf16[2,2,24,768]{3,2,1,0:T(8,128)(2,1)S(1)}, bf16[2,2,24,768]{3,2,1,0:T(8,128)(2,1)S(1)}, u32[]{:S(2)}, u32[]{:S(2)}) collective-permute-start(bf16[2,2,24,768]{3,2,1,0:T(8,128)(2,1)S(1)} %fusion.74), channel_id=1, source_target_pairs={{0,8},{1,9},{2,10},{3,11},{4,12},{5,13},{6,14},{7,15},{8,0},{9,1},... | collective-permute-start | bytes 442376 | tf_op jit(solution)/shard_map/ppermute | solution.py:80
  307.2 10.9 %collective-permute-start.40 = (bf16[2,2,24,768]{3,2,1,0:T(8,128)(2,1)S(1)}, bf16[2,2,24,768]{3,2,1,0:T(8,128)(2,1)S(1)}, u32[]{:S(2)}, u32[]{:S(2)}) collective-permute-start(bf16[2,2,24,768]{3,2,1,0:T(8,128)(2,1)S(1)} %fusion.76), channel_id=1, source_target_pairs={{0,16},{1,17},{2,18},{3,19},{4,20},{5,21},{6,22},{7,23},{8,24},{9,... | collective-permute-start | bytes 442376 | tf_op jit(solution)/shard_map/ppermute | solution.py:80
  307.5 12.4 %collective-permute-start.35 = (bf16[2,2,24,768]{3,2,1,0:T(8,128)(2,1)S(1)}, bf16[2,2,24,768]{3,2,1,0:T(8,128)(2,1)S(1)}, u32[]{:S(2)}, u32[]{:S(2)}) collective-permute-start(bf16[2,2,24,768]{3,2,1,0:T(8,128)(2,1)S(1)} %fusion.75), channel_id=1, source_target_pairs={{0,4},{1,5},{2,6},{3,7},{4,0},{5,1},{6,2},{7,3},{8,12},{9,13},{10,... | collective-permute-start | bytes 442376 | tf_op jit(solution)/shard_map/ppermute | solution.py:80
  (95 other events, 687.4 us)
Sparse Core Ops, SparseCore 0:
  74.3 50.6 all-gather.1
  215.9 72.9 reduce-scatter.1

commit v11 on v10

--- a/solution.py
+++ b/solution.py
@@ -440,20 +440,23 @@
     qkv_wsum = contract_rows(pack_in, grad_qkv)
     qkv_bsum = jnp.sum(grad_qkv.astype(jnp.float32), axis=0).reshape(3, D)
     wsum_parts = qkv_wsum.reshape(total, share, 3 * D).astype(jnp.bfloat16)
-    late_mine = scatter_sum_parts(
-        [
-            wsum_parts[..., :D],
-            wsum_parts[..., D : 2 * D],
-            wsum_parts[..., 2 * D :],
-            jnp.concatenate(
-                [
-                    qkv_bsum.T.reshape(total, share, 3).astype(jnp.bfloat16),
-                    early.astype(jnp.bfloat16),
-                ],
-                axis=2,
-            ),
+    segments = [
+        wsum_parts,
+        qkv_bsum.T.reshape(total, share, 3).astype(jnp.bfloat16),
+        early.astype(jnp.bfloat16),
+    ]
+    starts = [0]
+    for seg in segments:
+        starts.append(starts[-1] + seg.shape[-1])
+    chunks = []
+    for a, c in column_splits(starts[-1], 6):
+        bits_of = [
+            seg[..., max(a, lo) - lo : min(c, hi) - lo]
+            for seg, lo, hi in zip(segments, starts[:-1], starts[1:])
+            if min(c, hi) > max(a, lo)
         ]
-    )
+        chunks.append(bits_of[0] if len(bits_of) == 1 else jnp.concatenate(bits_of, axis=2))
+    late_mine = scatter_sum_parts(chunks)
     early_mine = late_mine[:, 3 * D + 3 :]
     query_wgrad = late_mine[:, :D]
     key_wgrad = late_mine[:, D : 2 * D]

time: 351 us -> 370 us (1.054)
  waiting for transfers between devices: 89.3 us -> 107 us
    ppermute x20 -> x30, waiting for transfers between devices: 8.64 us -> 36.8 us  [halving_scatter(): lax.ppermute(theirs.astype(jnp.bfloat16), ALL, [(i, i ^ 1 << b) for i in...]
    ppermute x8, waiting for transfers between devices: 39.3 us -> 28.8 us  [swapped(): lax.ppermute(shard, axis, [(i, i ^ 1 << bit) for i in range(lax.axis_size...]
    slice x2 -> x5, local copies, waits for them, and re-layouts: 0.95 us -> 5.76 us  [the longest x4 5.03 us: local(): seg[..., max(a, lo) - lo:min(c, hi) - lo]]
    add x20 -> x30, other arithmetic: 6.33 us -> 2.25 us  [halving_scatter(): cur = mine.astype(jnp.float32) + got.astype(jnp.float32)]
    ppermute x20 -> x30, starting transfers between devices: 17.4 us -> 20.7 us  [halving_scatter(): lax.ppermute(theirs.astype(jnp.bfloat16), ALL, [(i, i ^ 1 << b) for i in...]
  transfers between devices with their start and end apart: 45 -> 55, of which waited for: 18 -> 32; matrix products, arithmetic and copies ran while one was open for 43% -> 40% of each run, Pallas kernels for 0% -> 0%
where the time goes in v11:
time: 370 us; the launch traced here: 365 us
  waiting for transfers between devices  107 us (29%)
  matrix products  91 us (25%)
  other arithmetic  52.4 us (14%)
  local copies, waits for them, and re-layouts  51.1 us (14%)
  starting transfers between devices  47.2 us (13%)
  between operations  16 us (4%)
    ppermute x30, waiting for transfers between devices, halving_scatter(): lax.ppermute(theirs.astype(jnp.bfloat16), ALL, [(i, i ^ 1 << b) for i in...  36.8 us
    ppermute x15, waiting for transfers between devices, doubling_gather(): other = lax.ppermute(cur, ALL, [(i, i ^ 1 << b) for i in range(total)])  36.3 us
    ppermute x8, waiting for transfers between devices, swapped(): lax.ppermute(shard, axis, [(i, i ^ 1 << bit) for i in range(lax.axis_size...  28.8 us
    dot_general x2, matrix products, ffn_forward(): jnp.dot(rows, inner_cols, preferred_element_type=jnp.float32) + inner_offset  21.1 us
    ppermute x30, starting transfers between devices, halving_scatter(): lax.ppermute(theirs.astype(jnp.bfloat16), ALL, [(i, i ^ 1 << b) for i in...  20.7 us
    ppermute x15, starting transfers between devices, doubling_gather(): other = lax.ppermute(cur, ALL, [(i, i ^ 1 << b) for i in range(total)])  18.2 us
    dot_general x6, matrix products, contract_rows(): lax.dot_general(left_op, right_op, (((0,), (0,)), ((), ())), preferred_el...  14.3 us
    dot_general x6, matrix products, contract_cols(): lax.dot_general(left_op, right_op, (((1,), (1,)), ((), ())), preferred_el...  14 us
  transfers between devices with their start and end apart: 55, of which 32 were waited for; matrix products, arithmetic and copies ran while one was open for 40% of the time, Pallas kernels for 0%

profile of v11, /device:TPU:0, one launch (start us, length us, event | category | flops | bytes accessed | tf_op | source)
XLA Modules:
  0.0 364.8 jit_solution(7306867349461768494)
XLA Ops:
  36.0 13.8 %collective-permute-done.13 = bf16[2,2,24,1152]{3,2,1,0:T(8,128)(2,1)S(1)} collective-permute-done((bf16[2,2,24,1152]{3,2,1,0:T(8,128)(2,1)S(1)}, bf16[2,2,24,1152]{3,2,1,0:T(8,128)(2,1)S(1)}, u32[]{:S(2)}, u32[]{:S(2)}) %collective-permute-start.13) | collective-permute-done | bytes 221216 | tf_op jit(solution)/shard_map/ppermute | solution.py:47
  50.4 16.0 %collective-permute-done.14 = bf16[2,2,2,24,1152]{4,3,2,1,0:T(8,128)(2,1)S(1)} collective-permute-done((bf16[2,2,2,24,1152]{4,3,2,1,0:T(8,128)(2,1)S(1)}, bf16[2,2,2,24,1152]{4,3,2,1,0:T(8,128)(2,1)S(1)}, u32[]{:S(2)}, u32[]{:S(2)}) %collective-permute-start.14) | collective-permute-done | bytes 442400 | tf_op jit(solution)/shard_map/ppermute | solution.py:47
  81.0 6.5 %collective-permute-done = bf16[256,768]{1,0:T(8,128)(2,1)S(1)} collective-permute-done((bf16[256,768]{1,0:T(8,128)(2,1)}, bf16[256,768]{1,0:T(8,128)(2,1)S(1)}, u32[]{:S(2)}, u32[]{:S(2)}) %collective-permute-start) | collective-permute-done | bytes 393248 | tf_op jit(solution)/shard_map/ppermute | solution.py:18
  110.8 4.0 %fusion.57 = bf16[12,64,512]{2,1,0:T(8,128)(2,1)S(1)} fusion(bf16[512,12,64]{0,2,1:T(8,128)(2,1)S(1)} %bitcast.256, f32[12,512]{1,0:T(8,128)S(1)} %fusion, f32[12,512]{1,0:T(8,128)S(1)} %get-tuple-element.113, f32[12,512,512]{1,2,0:T(8,128)S(1)} %get-tuple-element.114, pred[512,512]{0,1:T(8,128)(4,1)S(1)} %copy-done.10), kind=kOutput, calls=%fused_computation.108 | convolution fusion | flops 418775040 | bytes 14467072 | tf_op jit(solution)/shard_map/phqk,pkhd->pqhd/dot_general | solution.py:201
  119.9 5.0 %all-gather.2.cloned.1.call-done = bf16[768,3074]{1,0:T(8,128)(2,1)} async-done(((bf16[48,3074]{1,0:T(8,128)(2,1)}), bf16[768,3074]{1,0:T(8,128)(2,1)}) %all-gather.2.cloned.1.call-update) | async-done | bytes 4721680 | tf_op jit(solution)/shard_map/all_gather | solution.py:304
  126.1 8.5 %collective-permute-done.16 = bf16[512,768]{1,0:T(8,128)(2,1)} collective-permute-done((bf16[512,768]{1,0:T(8,128)(2,1)S(1)}, bf16[512,768]{1,0:T(8,128)(2,1)}, u32[]{:S(2)}, u32[]{:S(2)}) %collective-permute-start.16) | collective-permute-done | bytes 786464 | tf_op jit(solution)/shard_map/ppermute | solution.py:18
  134.6 11.0 %multiply_convert_fusion.1 = (bf16[512,1536]{1,0:T(8,128)(2,1)S(1)}, f32[512,1536]{1,0:T(8,128)}, f32[512,1536]{1,0:T(8,128)}) fusion(f32[1536]{0:T(1024)S(1)} %reshape.663, bf16[512,768]{1,0:T(8,128)(2,1)} %collective-permute-done.16, bf16[768,3074]{1,0:T(8,128)(2,1)} %all-gather.2.cloned.1.call-done), kind=kOutput, calls=%fused_computation.28 | convolution fusion | flops 1259864064 | bytes 11016192 | tf_op jit(solution)/shard_map/dot_general | solution.py:230
  147.8 10.1 %multiply_convert_fusion.2 = (bf16[512,1536]{1,0:T(8,128)(2,1)S(1)}, f32[512,1536]{1,0:T(8,128)}, f32[512,1536]{1,0:T(8,128)}) fusion(f32[1536]{0:T(1024)S(1)} %reshape.663, bf16[512,768]{1,0:T(8,128)(2,1)S(1)} %fusion.58, bf16[768,3074]{1,0:T(8,128)(2,1)S(1)} %copy-done.59), kind=kOutput, calls=%fused_computation.41 | convolution fusion | flops 1259864064 | bytes 11018240 | tf_op jit(solution)/shard_map/dot_general | solution.py:230
  157.9 6.2 %collective-permute-done.17 = bf16[512,768]{1,0:T(8,128)(2,1)S(1)} collective-permute-done((bf16[512,768]{1,0:T(8,128)(2,1)S(1)}, bf16[512,768]{1,0:T(8,128)(2,1)S(1)}, u32[]{:S(2)}, u32[]{:S(2)}) %collective-permute-start.17) | collective-permute-done | bytes 786464 | tf_op jit(solution)/shard_map/ppermute | solution.py:18
  170.6 3.5 fusion.108
  177.6 6.1 %convert_reduce_fusion.1 = (f32[1536]{0:T(1024)S(1)}, bf16[512,1536]{1,0:T(8,128)(2,1)S(1)}) fusion(f32[512,1536]{1,0:T(8,128)} %get-tuple-element.63, f32[512,1536]{1,0:T(8,128)} %get-tuple-element.118, bf16[512,768]{1,0:T(8,128)(2,1)} %get-tuple-element.54, bf16[768,3074]{1,0:T(8,128)(2,1)} %all-gather.2.cloned.1.call-done), kind=kOutput, calls=%fused_computation.25 | convolution fusion | flops 1220540928 | bytes 11016192 | tf_op jit(solution)/shard_map/dot_general | solution.py:237
  186.9 6.1 %collective-permute-done.19 = bf16[512,768]{1,0:T(8,128)(2,1)S(1)} collective-permute-done((bf16[512,768]{1,0:T(8,128)(2,1)}, bf16[512,768]{1,0:T(8,128)(2,1)S(1)}, u32[]{:S(2)}, u32[]{:S(2)}) %collective-permute-start.19) | collective-permute-done | bytes 786464 | tf_op jit(solution)/shard_map/ppermute | solution.py:18
  192.9 3.9 %convert_reduce_fusion = (f32[1536]{0:T(1024)S(1)}, bf16[512,1536]{1,0:T(8,128)(2,1)S(1)}) fusion(f32[512,1536]{1,0:T(8,128)S(1)} %copy-done.62, f32[512,1536]{1,0:T(8,128)S(1)} %copy-done.63, bf16[512,768]{1,0:T(8,128)(2,1)S(1)} %collective-permute-done.19, bf16[768,3074]{1,0:T(8,128)(2,1)} %all-gather.2.cloned.1.call-done), kind=kOutput, calls=%fused_computation.24 | convolution fusion | flops 1220540928 | bytes 11016192 | tf_op jit(solution)/shard_map/dot_general | solution.py:237
  196.9 4.0 %fusion.48 = bf16[512,768]{1,0:T(8,128)(2,1)} fusion(bf16[512,1536]{1,0:T(8,128)(2,1)S(1)} %get-tuple-element.126, bf16[768,3074]{1,0:T(8,128)(2,1)} %all-gather.2.cloned.1.call-done), kind=kOutput, calls=%fused_computation.105 | convolution fusion | flops 1208352768 | bytes 4718592 | tf_op jit(solution)/shard_map/dot_general | solution.py:182
  202.6 4.1 %add_convert_fusion.1 = bf16[768,1536]{1,0:T(8,128)(2,1)} fusion(f32[768,1536]{1,0:T(8,128)S(1)} %fusion.115, bf16[512,768]{1,0:T(8,128)(2,1)} %collective-permute-done.16, bf16[512,1536]{1,0:T(8,128)(2,1)S(1)} %get-tuple-element.126), kind=kOutput, calls=%fused_computation.18 | convolution fusion | flops 1210318848 | bytes 9437184 | tf_op jit(solution)/shard_map/dot_general | solution.py:176
  210.2 5.4 %pad_maximum_fusion.1 = bf16[768,3074]{1,0:T(8,128)(2,1)} fusion(bf16[768,2]{1,0:T(8,128)(2,1)S(1)} %add.435, bf16[768,1536]{1,0:T(8,128)(2,1)} %add_convert_fusion, bf16[768,1536]{1,0:T(8,128)(2,1)} %add_convert_fusion.1), kind=kLoop, calls=%fused_computation.13 | loop fusion | flops 14164992 | bytes 9443328 | tf_op jit(solution)/shard_map/concatenate | solution.py:394
  217.2 3.9 %convert_add_fusion = f32[512,768]{1,0:T(8,128)S(1)} fusion(bf16[512,768]{1,0:T(8,128)(2,1)} %collective-permute-done.20, bf16[512,1536]{1,0:T(8,128)(2,1)} %copy-done.32, bf16[768,3074]{1,0:T(8,128)(2,1)} %all-gather.2.cloned.1.call-done), kind=kOutput, calls=%fused_computation.78 | convolution fusion | flops 1208745984 | bytes 6291456 | tf_op jit(solution)/shard_map/dot_general | solution.py:182
  225.9 9.9 %fusion.54 = bf16[12,64,512]{2,1,0:T(8,128)(2,1)} fusion(bf16[512,12,64]{0,2,1:T(8,128)(2,1)} %bitcast.258, f32[12,512]{1,0:T(8,128)S(1)} %copy-done.48, f32[12,512,512]{1,2,0:T(8,128)} %copy-done.2, pred[512,512]{0,1:T(8,128)(4,1)S(1)} %copy-done.11), kind=kOutput, calls=%fused_computation.107 | convolution fusion | flops 415629312 | bytes 14442496 | tf_op jit(solution)/shard_map/phqk,pqhd->pkhd/dot_general | solution.py:209
  235.8 9.6 %multiply_reduce_fusion = (f32[12,512]{1,0:T(8,128)S(1)}, f32[12,512,512]{1,2,0:T(8,128)}) fusion(f32[12,512]{1,0:T(8,128)S(1)} %copy-done.48, f32[12,512,512]{1,2,0:T(8,128)} %copy-done.2, pred[512,512]{0,1:T(8,128)(4,1)S(1)} %copy-done.11, bf16[512,12,64]{0,2,1:T(8,128)(2,1)S(1)} %bitcast.259, bf16[512,12,64]{0,2,1:T(8,128)(2,1)S(1)} %bitcast.257), kind=kOutput, calls=%fused_computation.1 | convolution fusion | flops 418375680 | bytes 27049984 | tf_op jit(solution)/shard_map/pqhd,pkhd->phqk/dot_general | solution.py:215
  245.4 7.2 %multiply_convert_fusion = bf16[12,512,512]{1,2,0:T(8,128)(2,1)S(1)} fusion(f32[12,512,512]{1,2,0:T(8,128)} %get-tuple-element.122, f32[12,512]{1,0:T(8,128)S(1)} %get-tuple-element.121, f32[12,512]{1,0:T(8,128)S(1)} %copy-done.48, f32[12,512,512]{1,2,0:T(8,128)S(1)} %bitcast.247, pred[512,512]{0,1:T(8,128)(4,1)S(1)} %copy-done.11), kind=kLoop, calls=%fused_computation | loop fusion | flops 18874368 | bytes 31768576 | tf_op jit(solution)/shard_map/convert_element_type | solution.py:219
  273.5 3.8 %concatenate.136 = bf16[32,24,774]{2,1,0:T(8,128)(2,1)} concatenate(bf16[32,24,768]{2,1,0:T(8,128)(2,1)S(1)} %convolution_convert_fusion.1, bf16[32,24,1]{2,1,0:T(8,128)(2,1)} %stack.65, bf16[32,24,1]{2,1,0:T(8,128)(2,1)} %stack.66, bf16[32,24,1]{2,1,0:T(8,128)(2,1)} %stack.67, bf16[32,24,1]{2,1,0:T(8,128)(2,1)} %stack.68, bf16[32,24,1]{2,1,0:T(8,128)(2,1)} %stack.69, ...), dimensions={2} | concatenate | bytes 2377728 | tf_op jit(solution)/shard_map/concatenate | solution.py:411
  292.2 7.0 %collective-permute-done.29 = bf16[2,2,2,24,512]{4,3,2,0,1:T(8,128)(2,1)S(1)} collective-permute-done((bf16[2,2,2,24,512]{4,3,2,0,1:T(8,128)(2,1)S(1)}, bf16[2,2,2,24,512]{4,3,2,0,1:T(8,128)(2,1)S(1)}, u32[]{:S(2)}, u32[]{:S(2)}) %collective-permute-start.29) | collective-permute-done | bytes 196640 | tf_op jit(solution)/shard_map/ppermute | solution.py:80
  302.4 9.9 %collective-permute-done.39 = bf16[2,2,2,24,512]{4,3,2,1,0:T(8,128)(2,1)S(1)} collective-permute-done((bf16[2,2,2,24,512]{4,3,2,1,0:T(8,128)(2,1)S(1)}, bf16[2,2,2,24,512]{4,3,2,1,0:T(8,128)(2,1)S(1)}, u32[]{:S(2)}, u32[]{:S(2)}) %collective-permute-start.39) | collective-permute-done | bytes 196640 | tf_op jit(solution)/shard_map/ppermute | solution.py:80
  318.9 5.4 %collective-permute-done.35 = bf16[2,2,24,512]{3,2,1,0:T(8,128)(2,1)S(1)} collective-permute-done((bf16[2,2,24,512]{3,2,1,0:T(8,128)(2,1)S(1)}, bf16[2,2,24,512]{3,2,1,0:T(8,128)(2,1)S(1)}, u32[]{:S(2)}, u32[]{:S(2)}) %collective-permute-start.35) | collective-permute-done | bytes 98336 | tf_op jit(solution)/shard_map/ppermute | solution.py:80
  (424 shorter events, 177.7 us)
Async XLA Ops:
  7.2 117.7 %all-gather.2.cloned.1.call-start = ((), (), s32[]{:S(2)}) async-start(), calls=%async_computation.1 | async-start | bytes 5222400 | tf_op jit(solution)/shard_map/all_gather | solution.py:304
  9.6 13.2 %collective-permute-start.11 = (bf16[24,1152]{1,0:T(8,128)(2,1)S(1)}, bf16[24,1152]{1,0:T(8,128)(2,1)S(1)}, u32[]{:S(2)}, u32[]{:S(2)}) collective-permute-start(bf16[24,1152]{1,0:T(8,128)(2,1)S(1)} %fusion.83), channel_id=1, source_target_pairs={{0,1},{1,0},{2,3},{3,2},{4,5},{5,4},{6,7},{7,6},{8,9},{9,8},{10,11... | collective-permute-start | bytes 165896 | tf_op jit(solution)/shard_map/ppermute | solution.py:47
  18.6 8.9 %collective-permute-start.2 = (bf16[2,24,1024]{2,1,0:T(8,128)(2,1)S(1)}, bf16[2,24,1024]{2,1,0:T(8,128)(2,1)S(1)}, u32[]{:S(2)}, u32[]{:S(2)}) collective-permute-start(bf16[2,24,1024]{2,1,0:T(8,128)(2,1)S(1)} %get-tuple-element.109), channel_id=1, source_target_pairs={{0,16},{1,17},{2,18},{3,19},{4,20},{5,21},{6,22},{7,23},{8,24},{9,... | collective-permute-start | bytes 294920 | tf_op jit(solution)/shard_map/ppermute | solution.py:47
  29.3 20.5 %collective-permute-start.13 = (bf16[2,2,24,1152]{3,2,1,0:T(8,128)(2,1)S(1)}, bf16[2,2,24,1152]{3,2,1,0:T(8,128)(2,1)S(1)}, u32[]{:S(2)}, u32[]{:S(2)}) collective-permute-start(bf16[2,2,24,1152]{3,2,1,0:T(8,128)(2,1)S(1)} %broadcast_select_fusion.11), channel_id=1, source_target_pairs={{0,16},{1,17},{2,18},{3,19},{4,20},{5,21},{6,22},{7,23},{8,24},{9,... | collective-permute-start | bytes 663560 | tf_op jit(solution)/shard_map/ppermute | solution.py:47
  32.0 34.6 %collective-permute-start.9 = (bf16[2,2,2,24,1024]{4,3,2,0,1:T(8,128)(2,1)S(1)}, bf16[2,2,2,24,1024]{4,3,2,0,1:T(8,128)(2,1)S(1)}, u32[]{:S(2)}, u32[]{:S(2)}) collective-permute-start(bf16[2,2,2,24,1024]{4,3,2,0,1:T(8,128)(2,1)S(1)} %broadcast_select_fusion.7), channel_id=1, source_target_pairs={{0,16},{1,17},{2,18},{3,19},{4,20},{5,21},{6,22},{7,23},{8,24},{9,... | collective-permute-start | bytes 1179656 | tf_op jit(solution)/shard_map/ppermute | solution.py:47
  34.8 15.4 %collective-permute-start.4 = (bf16[2,2,2,24,1024]{4,3,2,0,1:T(8,128)(2,1)S(1)}, bf16[2,2,2,24,1024]{4,3,2,0,1:T(8,128)(2,1)S(1)}, u32[]{:S(2)}, u32[]{:S(2)}) collective-permute-start(bf16[2,2,2,24,1024]{4,3,2,0,1:T(8,128)(2,1)S(1)} %broadcast_select_fusion.9), channel_id=1, source_target_pairs={{0,4},{1,5},{2,6},{3,7},{4,0},{5,1},{6,2},{7,3},{8,12},{9,13},{10,... | collective-permute-start | bytes 1179656 | tf_op jit(solution)/shard_map/ppermute | solution.py:47
  50.0 16.4 %collective-permute-start.14 = (bf16[2,2,2,24,1152]{4,3,2,1,0:T(8,128)(2,1)S(1)}, bf16[2,2,2,24,1152]{4,3,2,1,0:T(8,128)(2,1)S(1)}, u32[]{:S(2)}, u32[]{:S(2)}) collective-permute-start(bf16[2,2,2,24,1152]{4,3,2,1,0:T(8,128)(2,1)S(1)} %broadcast_select_fusion.6), channel_id=1, source_target_pairs={{0,8},{1,9},{2,10},{3,11},{4,12},{5,13},{6,14},{7,15},{8,0},{9,1},... | collective-permute-start | bytes 1327112 | tf_op jit(solution)/shard_map/ppermute | solution.py:47
  50.3 17.8 %collective-permute-start.5 = (bf16[2,2,2,2,24,1024]{5,4,3,0,1,2:T(8,128)(2,1)S(1)}, bf16[2,2,2,2,24,1024]{5,4,3,0,1,2:T(8,128)(2,1)S(1)}, u32[]{:S(2)}, u32[]{:S(2)}) collective-permute-start(bf16[2,2,2,2,24,1024]{5,4,3,0,1,2:T(8,128)(2,1)S(1)} %broadcast_select_fusion.4), channel_id=1, source_target_pairs={{0,2},{1,3},{2,0},{3,1},{4,6},{5,7},{6,4},{7,5},{8,10},{9,11},{10,... | collective-permute-start | bytes 2359304 | tf_op jit(solution)/shard_map/ppermute | solution.py:47
  74.1 278.9 %reduce-scatter.2.cloned.1.call-start = ((), (), s32[]{:S(2)}) async-start(), calls=%async_computation.2 | async-start | bytes 5222400 | tf_op jit(solution)/shard_map/reduce_scatter | solution.py:395
  75.3 12.2 %collective-permute-start = (bf16[256,768]{1,0:T(8,128)(2,1)}, bf16[256,768]{1,0:T(8,128)(2,1)S(1)}, u32[]{:S(2)}, u32[]{:S(2)}) collective-permute-start(bf16[256,768]{1,0:T(8,128)(2,1)} %get-tuple-element.94), channel_id=1, source_target_pairs={{0,1},{1,0},{2,3},{3,2},{4,5},{5,4},{6,7},{7,6},{8,9},{9,8},{10,11... | collective-permute-start | bytes 1179656 | tf_op jit(solution)/shard_map/ppermute | solution.py:18
  77.4 39.3 %collective-permute-start.18 = (bf16[256,768]{1,0:T(8,128)(2,1)}, bf16[256,768]{1,0:T(8,128)(2,1)}, u32[]{:S(2)}, u32[]{:S(2)}) collective-permute-start(bf16[256,768]{1,0:T(8,128)(2,1)} %get-tuple-element.91), channel_id=1, source_target_pairs={{0,1},{1,0},{2,3},{3,2},{4,5},{5,4},{6,7},{7,6},{8,9},{9,8},{10,11... | collective-permute-start | bytes 1179656 | tf_op jit(solution)/shard_map/ppermute | solution.py:18
  116.6 18.1 %collective-permute-start.16 = (bf16[512,768]{1,0:T(8,128)(2,1)S(1)}, bf16[512,768]{1,0:T(8,128)(2,1)}, u32[]{:S(2)}, u32[]{:S(2)}) collective-permute-start(bf16[512,768]{1,0:T(8,128)(2,1)S(1)} %fusion.58), channel_id=1, source_target_pairs={{0,1},{1,0},{2,3},{3,2},{4,5},{5,4},{6,7},{7,6},{8,9},{9,8},{10,11... | collective-permute-start | bytes 2359304 | tf_op jit(solution)/shard_map/ppermute | solution.py:18
  147.1 17.1 %collective-permute-start.17 = (bf16[512,768]{1,0:T(8,128)(2,1)S(1)}, bf16[512,768]{1,0:T(8,128)(2,1)S(1)}, u32[]{:S(2)}, u32[]{:S(2)}) collective-permute-start(bf16[512,768]{1,0:T(8,128)(2,1)S(1)} %fusion.51), channel_id=1, source_target_pairs={{0,1},{1,0},{2,3},{3,2},{4,5},{5,4},{6,7},{7,6},{8,9},{9,8},{10,11... | collective-permute-start | bytes 2359304 | tf_op jit(solution)/shard_map/ppermute | solution.py:18
  176.3 16.6 %collective-permute-start.19 = (bf16[512,768]{1,0:T(8,128)(2,1)}, bf16[512,768]{1,0:T(8,128)(2,1)S(1)}, u32[]{:S(2)}, u32[]{:S(2)}) collective-permute-start(bf16[512,768]{1,0:T(8,128)(2,1)} %get-tuple-element.54), channel_id=1, source_target_pairs={{0,1},{1,0},{2,3},{3,2},{4,5},{5,4},{6,7},{7,6},{8,9},{9,8},{10,11... | collective-permute-start | bytes 2359304 | tf_op jit(solution)/shard_map/ppermute | solution.py:18
  200.9 16.3 %collective-permute-start.20 = (bf16[512,768]{1,0:T(8,128)(2,1)}, bf16[512,768]{1,0:T(8,128)(2,1)}, u32[]{:S(2)}, u32[]{:S(2)}) collective-permute-start(bf16[512,768]{1,0:T(8,128)(2,1)} %fusion.48), channel_id=1, source_target_pairs={{0,1},{1,0},{2,3},{3,2},{4,5},{5,4},{6,7},{7,6},{8,9},{9,8},{10,11... | collective-permute-start | bytes 2359304 | tf_op jit(solution)/shard_map/ppermute | solution.py:18
  279.8 9.1 %collective-permute-start.48 = (bf16[2,2,2,2,24,521]{5,4,3,2,1,0:T(8,128)(2,1)}, bf16[2,2,2,2,24,521]{5,4,3,2,1,0:T(8,128)(2,1)}, u32[]{:S(2)}, u32[]{:S(2)}) collective-permute-start(bf16[2,2,2,2,24,521]{5,4,3,2,1,0:T(8,128)(2,1)} %dynamic-slice_bitcast_fusion), channel_id=1, source_target_pairs={{0,2},{1,3},{2,0},{3,1},{4,6},{5,7},{6,4},{7,5},{8,10},{9,11},{10,... | collective-permute-start | bytes 1200392 | tf_op jit(solution)/shard_map/ppermute | solution.py:80
  279.8 69.3 %collective-permute-start.21 = (f32[256,768]{1,0:T(8,128)}, f32[256,768]{1,0:T(8,128)}, u32[]{:S(2)}, u32[]{:S(2)}) collective-permute-start(f32[256,768]{1,0:T(8,128)} %get-tuple-element.84), channel_id=1, source_target_pairs={{0,1},{1,0},{2,3},{3,2},{4,5},{5,4},{6,7},{7,6},{8,9},{9,8},{10,11... | collective-permute-start | bytes 2359304 | tf_op jit(solution)/shard_map/ppermute | solution.py:18
  287.6 64.2 %collective-permute-start.22 = (f32[256,768]{1,0:T(8,128)S(1)}, f32[256,768]{1,0:T(8,128)S(1)}, u32[]{:S(2)}, u32[]{:S(2)}) collective-permute-start(f32[256,768]{1,0:T(8,128)S(1)} %copy-done.42), channel_id=1, source_target_pairs={{0,1},{1,0},{2,3},{3,2},{4,5},{5,4},{6,7},{7,6},{8,9},{9,8},{10,11... | collective-permute-start | bytes 2359304 | tf_op jit(solution)/shard_map/ppermute | solution.py:18
  288.2 11.0 %collective-permute-start.29 = (bf16[2,2,2,24,512]{4,3,2,0,1:T(8,128)(2,1)S(1)}, bf16[2,2,2,24,512]{4,3,2,0,1:T(8,128)(2,1)S(1)}, u32[]{:S(2)}, u32[]{:S(2)}) collective-permute-start(bf16[2,2,2,24,512]{4,3,2,0,1:T(8,128)(2,1)S(1)} %fusion.71), channel_id=1, source_target_pairs={{0,16},{1,17},{2,18},{3,19},{4,20},{5,21},{6,22},{7,23},{8,24},{9,... | collective-permute-start | bytes 589832 | tf_op jit(solution)/shard_map/ppermute | solution.py:80
  288.8 10.5 %collective-permute-start.34 = (bf16[2,2,2,24,512]{4,3,2,1,0:T(8,128)(2,1)S(1)}, bf16[2,2,2,24,512]{4,3,2,1,0:T(8,128)(2,1)S(1)}, u32[]{:S(2)}, u32[]{:S(2)}) collective-permute-start(bf16[2,2,2,24,512]{4,3,2,1,0:T(8,128)(2,1)S(1)} %fusion.72), channel_id=1, source_target_pairs={{0,4},{1,5},{2,6},{3,7},{4,0},{5,1},{6,2},{7,3},{8,12},{9,13},{10,... | collective-permute-start | bytes 589832 | tf_op jit(solution)/shard_map/ppermute | solution.py:80
  288.9 12.5 %collective-permute-start.24 = (bf16[2,2,2,24,512]{4,3,2,1,0:T(8,128)(2,1)S(1)}, bf16[2,2,2,24,512]{4,3,2,1,0:T(8,128)(2,1)S(1)}, u32[]{:S(2)}, u32[]{:S(2)}) collective-permute-start(bf16[2,2,2,24,512]{4,3,2,1,0:T(8,128)(2,1)S(1)} %fusion.70), channel_id=1, source_target_pairs={{0,4},{1,5},{2,6},{3,7},{4,0},{5,1},{6,2},{7,3},{8,12},{9,13},{10,... | collective-permute-start | bytes 589832 | tf_op jit(solution)/shard_map/ppermute | solution.py:80
  299.2 13.0 %collective-permute-start.39 = (bf16[2,2,2,24,512]{4,3,2,1,0:T(8,128)(2,1)S(1)}, bf16[2,2,2,24,512]{4,3,2,1,0:T(8,128)(2,1)S(1)}, u32[]{:S(2)}, u32[]{:S(2)}) collective-permute-start(bf16[2,2,2,24,512]{4,3,2,1,0:T(8,128)(2,1)S(1)} %fusion.73), channel_id=1, source_target_pairs={{0,8},{1,9},{2,10},{3,11},{4,12},{5,13},{6,14},{7,15},{8,0},{9,1},... | collective-permute-start | bytes 589832 | tf_op jit(solution)/shard_map/ppermute | solution.py:80
  299.3 16.2 %collective-permute-start.44 = (bf16[2,2,2,24,512]{4,3,2,0,1:T(8,128)(2,1)S(1)}, bf16[2,2,2,24,512]{4,3,2,0,1:T(8,128)(2,1)S(1)}, u32[]{:S(2)}, u32[]{:S(2)}) collective-permute-start(bf16[2,2,2,24,512]{4,3,2,0,1:T(8,128)(2,1)S(1)} %fusion.74), channel_id=1, source_target_pairs={{0,8},{1,9},{2,10},{3,11},{4,12},{5,13},{6,14},{7,15},{8,0},{9,1},... | collective-permute-start | bytes 589832 | tf_op jit(solution)/shard_map/ppermute | solution.py:80
  301.5 14.2 %collective-permute-start.49 = (bf16[2,2,2,24,521]{4,3,2,1,0:T(8,128)(2,1)S(1)}, bf16[2,2,2,24,521]{4,3,2,1,0:T(8,128)(2,1)S(1)}, u32[]{:S(2)}, u32[]{:S(2)}) collective-permute-start(bf16[2,2,2,24,521]{4,3,2,1,0:T(8,128)(2,1)S(1)} %fusion.69), channel_id=1, source_target_pairs={{0,16},{1,17},{2,18},{3,19},{4,20},{5,21},{6,22},{7,23},{8,24},{9,... | collective-permute-start | bytes 600200 | tf_op jit(solution)/shard_map/ppermute | solution.py:80
  (100 other events, 696.7 us)
Sparse Core Ops, SparseCore 0:
  74.3 50.6 all-gather.1
  215.8 72.9 reduce-scatter.1

commit v12 on v10

--- a/solution.py
+++ b/solution.py
@@ -437,14 +437,15 @@
         jnp.concatenate([keep_grad, got_grad]),
         jnp.concatenate([got_grad, keep_grad]),
     )
-    qkv_wsum = contract_rows(pack_in, grad_qkv)
     qkv_bsum = jnp.sum(grad_qkv.astype(jnp.float32), axis=0).reshape(3, D)
-    wsum_parts = qkv_wsum.reshape(total, share, 3 * D).astype(jnp.bfloat16)
     late_mine = scatter_sum_parts(
         [
-            wsum_parts[..., :D],
-            wsum_parts[..., D : 2 * D],
-            wsum_parts[..., 2 * D :],
+            *[
+                contract_rows(pack_in, grad_qkv[:, k * D : (k + 1) * D])
+                .reshape(total, share, D)
+                .astype(jnp.bfloat16)
+                for k in range(3)
+            ],
             jnp.concatenate(
                 [
                     qkv_bsum.T.reshape(total, share, 3).astype(jnp.bfloat16),

time: 351 us -> 351 us (level)
    dynamic_slice x0 -> x6, local copies, waits for them, and re-layouts: none -> 4.9 us  [the longest x3 2.84 us: halving_scatter(): theirs = lax.dynamic_index_in_dim(cur, 1 - bit, axis=a, keepdims=False)]
    unnamed x149 -> x147, local copies, waits for them, and re-layouts: 7.15 us -> 5.83 us
    dot_general x6 -> x8, matrix products: 15.3 us -> 15.6 us  [contract_rows(): lax.dot_general(left_op, right_op, (((0,), (0,)), ((), ())), preferred_el...]
where the time goes in v12:
time: 351 us; the launch traced here: 346 us
  matrix products  92.6 us (26%)
  waiting for transfers between devices  92.4 us (26%)
  other arithmetic  53.7 us (15%)
  local copies, waits for them, and re-layouts  50 us (14%)
  starting transfers between devices  41.1 us (12%)
  between operations  15.9 us (5%)
    ppermute x8, waiting for transfers between devices, swapped(): lax.ppermute(shard, axis, [(i, i ^ 1 << bit) for i in range(lax.axis_size...  40 us
    ppermute x15, waiting for transfers between devices, doubling_gather(): other = lax.ppermute(cur, ALL, [(i, i ^ 1 << b) for i in range(total)])  36.3 us
    dot_general x2, matrix products, ffn_forward(): jnp.dot(rows, inner_cols, preferred_element_type=jnp.float32) + inner_offset  21 us
    ppermute x15, starting transfers between devices, doubling_gather(): other = lax.ppermute(cur, ALL, [(i, i ^ 1 << b) for i in range(total)])  18.2 us
    dot_general x8, matrix products, contract_rows(): lax.dot_general(left_op, right_op, (((0,), (0,)), ((), ())), preferred_el...  15.6 us
    ppermute x20, starting transfers between devices, halving_scatter(): lax.ppermute(theirs.astype(jnp.bfloat16), ALL, [(i, i ^ 1 << b) for i in...  14.6 us
    dot_general x6, matrix products, contract_cols(): lax.dot_general(left_op, right_op, (((1,), (1,)), ((), ())), preferred_el...  14 us
    ppermute x20, waiting for transfers between devices, halving_scatter(): lax.ppermute(theirs.astype(jnp.bfloat16), ALL, [(i, i ^ 1 << b) for i in...  11.1 us
  transfers between devices with their start and end apart: 45, of which 18 were waited for; matrix products, arithmetic and copies ran while one was open for 43% of the time, Pallas kernels for 0%

profile of v12, /device:TPU:0, one launch (start us, length us, event | category | flops | bytes accessed | tf_op | source)
XLA Modules:
  0.0 345.6 jit_solution(12748299241943762666)
XLA Ops:
  36.0 13.8 %collective-permute-done.13 = bf16[2,2,24,1152]{3,2,1,0:T(8,128)(2,1)S(1)} collective-permute-done((bf16[2,2,24,1152]{3,2,1,0:T(8,128)(2,1)S(1)}, bf16[2,2,24,1152]{3,2,1,0:T(8,128)(2,1)S(1)}, u32[]{:S(2)}, u32[]{:S(2)}) %collective-permute-start.13) | collective-permute-done | bytes 221216 | tf_op jit(solution)/shard_map/ppermute | solution.py:47
  50.4 16.0 %collective-permute-done.14 = bf16[2,2,2,24,1152]{4,3,2,1,0:T(8,128)(2,1)S(1)} collective-permute-done((bf16[2,2,2,24,1152]{4,3,2,1,0:T(8,128)(2,1)S(1)}, bf16[2,2,2,24,1152]{4,3,2,1,0:T(8,128)(2,1)S(1)}, u32[]{:S(2)}, u32[]{:S(2)}) %collective-permute-start.14) | collective-permute-done | bytes 442400 | tf_op jit(solution)/shard_map/ppermute | solution.py:47
  81.0 6.5 %collective-permute-done = bf16[256,768]{1,0:T(8,128)(2,1)S(1)} collective-permute-done((bf16[256,768]{1,0:T(8,128)(2,1)}, bf16[256,768]{1,0:T(8,128)(2,1)S(1)}, u32[]{:S(2)}, u32[]{:S(2)}) %collective-permute-start) | collective-permute-done | bytes 393248 | tf_op jit(solution)/shard_map/ppermute | solution.py:18
  110.8 4.0 %fusion.57 = bf16[12,64,512]{2,1,0:T(8,128)(2,1)S(1)} fusion(bf16[512,12,64]{0,2,1:T(8,128)(2,1)S(1)} %bitcast.207, f32[12,512]{1,0:T(8,128)S(1)} %fusion, f32[12,512]{1,0:T(8,128)S(1)} %get-tuple-element.105, f32[12,512,512]{1,2,0:T(8,128)S(1)} %get-tuple-element.106, pred[512,512]{0,1:T(8,128)(4,1)S(1)} %copy-done.11), kind=kOutput, calls=%fused_computation.110 | convolution fusion | flops 418775040 | bytes 14467072 | tf_op jit(solution)/shard_map/phqk,pkhd->pqhd/dot_general | solution.py:201
  119.9 5.0 %all-gather.2.cloned.1.call-done = bf16[768,3074]{1,0:T(8,128)(2,1)} async-done(((bf16[48,3074]{1,0:T(8,128)(2,1)}), bf16[768,3074]{1,0:T(8,128)(2,1)}) %all-gather.2.cloned.1.call-update) | async-done | bytes 4721680 | tf_op jit(solution)/shard_map/all_gather | solution.py:304
  126.1 8.5 %collective-permute-done.16 = bf16[512,768]{1,0:T(8,128)(2,1)} collective-permute-done((bf16[512,768]{1,0:T(8,128)(2,1)S(1)}, bf16[512,768]{1,0:T(8,128)(2,1)}, u32[]{:S(2)}, u32[]{:S(2)}) %collective-permute-start.16) | collective-permute-done | bytes 786464 | tf_op jit(solution)/shard_map/ppermute | solution.py:18
  134.6 10.9 %multiply_convert_fusion.1 = (bf16[512,1536]{1,0:T(8,128)(2,1)S(1)}, f32[512,1536]{1,0:T(8,128)}, f32[512,1536]{1,0:T(8,128)}) fusion(f32[1536]{0:T(1024)S(1)} %reshape.657, bf16[512,768]{1,0:T(8,128)(2,1)} %collective-permute-done.16, bf16[768,3074]{1,0:T(8,128)(2,1)} %all-gather.2.cloned.1.call-done), kind=kOutput, calls=%fused_computation.27 | convolution fusion | flops 1259864064 | bytes 11016192 | tf_op jit(solution)/shard_map/dot_general | solution.py:230
  147.8 10.0 %multiply_convert_fusion.2 = (bf16[512,1536]{1,0:T(8,128)(2,1)S(1)}, f32[512,1536]{1,0:T(8,128)}, f32[512,1536]{1,0:T(8,128)}) fusion(f32[1536]{0:T(1024)S(1)} %reshape.657, bf16[512,768]{1,0:T(8,128)(2,1)S(1)} %fusion.58, bf16[768,3074]{1,0:T(8,128)(2,1)S(1)} %copy-done.62), kind=kOutput, calls=%fused_computation.40 | convolution fusion | flops 1259864064 | bytes 11018240 | tf_op jit(solution)/shard_map/dot_general | solution.py:230
  157.8 6.3 %collective-permute-done.17 = bf16[512,768]{1,0:T(8,128)(2,1)S(1)} collective-permute-done((bf16[512,768]{1,0:T(8,128)(2,1)S(1)}, bf16[512,768]{1,0:T(8,128)(2,1)S(1)}, u32[]{:S(2)}, u32[]{:S(2)}) %collective-permute-start.17) | collective-permute-done | bytes 786464 | tf_op jit(solution)/shard_map/ppermute | solution.py:18
  170.6 3.5 %fusion.103 = (f32[512]{0:T(512)S(1)}, f32[512,768]{1,0:T(8,128)S(1)}, f32[512,768]{1,0:T(8,128)}) fusion(f32[512]{0:T(512)} %multiply_multiply_fusion.11, f32[512,768]{1,0:T(8,128)} %copy-done.3, f32[512]{0:T(512)} %copy-done.54, f32[512]{0:T(512)} %copy-done.57, f32[768]{0:T(1024)S(1)} %get-tuple-element.35, bf16[256,768]{1,0:T(8,128)(2,1)S(1)} %copy-done.7, ...), kind=kLoop, calls=%fused_computation.291 | loop fusion | flops 7863808 | bytes 5519361 | tf_op jit(solution)/shard_map/transpose(jvp())/reduce_sum | solution.py:139
  177.6 6.1 %convert_reduce_fusion.1 = (f32[1536]{0:T(1024)S(1)}, bf16[512,1536]{1,0:T(8,128)(2,1)S(1)}) fusion(f32[512,1536]{1,0:T(8,128)} %get-tuple-element.63, f32[512,1536]{1,0:T(8,128)} %get-tuple-element.110, bf16[512,768]{1,0:T(8,128)(2,1)} %get-tuple-element.54, bf16[768,3074]{1,0:T(8,128)(2,1)} %all-gather.2.cloned.1.call-done), kind=kOutput, calls=%fused_computation.24 | convolution fusion | flops 1220540928 | bytes 11016192 | tf_op jit(solution)/shard_map/dot_general | solution.py:237
  186.9 6.1 %collective-permute-done.19 = bf16[512,768]{1,0:T(8,128)(2,1)S(1)} collective-permute-done((bf16[512,768]{1,0:T(8,128)(2,1)}, bf16[512,768]{1,0:T(8,128)(2,1)S(1)}, u32[]{:S(2)}, u32[]{:S(2)}) %collective-permute-start.19) | collective-permute-done | bytes 786464 | tf_op jit(solution)/shard_map/ppermute | solution.py:18
  192.9 4.0 %convert_reduce_fusion = (f32[1536]{0:T(1024)S(1)}, bf16[512,1536]{1,0:T(8,128)(2,1)S(1)}) fusion(f32[512,1536]{1,0:T(8,128)S(1)} %copy-done.66, f32[512,1536]{1,0:T(8,128)S(1)} %copy-done.67, bf16[512,768]{1,0:T(8,128)(2,1)S(1)} %collective-permute-done.19, bf16[768,3074]{1,0:T(8,128)(2,1)} %all-gather.2.cloned.1.call-done), kind=kOutput, calls=%fused_computation.23 | convolution fusion | flops 1220540928 | bytes 11016192 | tf_op jit(solution)/shard_map/dot_general | solution.py:237
  196.9 4.0 %fusion.48 = bf16[512,768]{1,0:T(8,128)(2,1)} fusion(bf16[512,1536]{1,0:T(8,128)(2,1)S(1)} %get-tuple-element.118, bf16[768,3074]{1,0:T(8,128)(2,1)} %all-gather.2.cloned.1.call-done), kind=kOutput, calls=%fused_computation.107 | convolution fusion | flops 1208352768 | bytes 4718592 | tf_op jit(solution)/shard_map/dot_general | solution.py:182
  202.6 4.1 %add_convert_fusion.1 = bf16[768,1536]{1,0:T(8,128)(2,1)} fusion(f32[768,1536]{1,0:T(8,128)S(1)} %fusion.109, bf16[512,768]{1,0:T(8,128)(2,1)} %collective-permute-done.16, bf16[512,1536]{1,0:T(8,128)(2,1)S(1)} %get-tuple-element.118), kind=kOutput, calls=%fused_computation.17 | convolution fusion | flops 1210318848 | bytes 9437184 | tf_op jit(solution)/shard_map/dot_general | solution.py:176
  206.7 3.2 add_convert_fusion
  210.2 5.4 %pad_maximum_fusion.1 = bf16[768,3074]{1,0:T(8,128)(2,1)} fusion(bf16[768,2]{1,0:T(8,128)(2,1)S(1)} %add.373, bf16[768,1536]{1,0:T(8,128)(2,1)} %add_convert_fusion, bf16[768,1536]{1,0:T(8,128)(2,1)} %add_convert_fusion.1), kind=kLoop, calls=%fused_computation.12 | loop fusion | flops 14164992 | bytes 9443328 | tf_op jit(solution)/shard_map/concatenate | solution.py:394
  217.2 3.9 %convert_add_fusion = f32[512,768]{1,0:T(8,128)S(1)} fusion(bf16[512,768]{1,0:T(8,128)(2,1)} %collective-permute-done.20, bf16[512,1536]{1,0:T(8,128)(2,1)} %copy-done.30, bf16[768,3074]{1,0:T(8,128)(2,1)} %all-gather.2.cloned.1.call-done), kind=kOutput, calls=%fused_computation.77 | convolution fusion | flops 1208745984 | bytes 6291456 | tf_op jit(solution)/shard_map/dot_general | solution.py:182
  226.4 9.8 %fusion.54 = bf16[12,64,512]{2,1,0:T(8,128)(2,1)} fusion(bf16[512,12,64]{0,2,1:T(8,128)(2,1)} %bitcast.209, f32[12,512]{1,0:T(8,128)S(1)} %copy-done.49, f32[12,512,512]{1,2,0:T(8,128)} %copy-done.2, pred[512,512]{0,1:T(8,128)(4,1)S(1)} %copy-done.12), kind=kOutput, calls=%fused_computation.109 | convolution fusion | flops 415629312 | bytes 14442496 | tf_op jit(solution)/shard_map/phqk,pqhd->pkhd/dot_general | solution.py:209
  236.2 10.0 %multiply_reduce_fusion = (f32[12,512]{1,0:T(8,128)S(1)}, f32[12,512,512]{1,2,0:T(8,128)}) fusion(f32[12,512]{1,0:T(8,128)S(1)} %copy-done.49, f32[12,512,512]{1,2,0:T(8,128)} %copy-done.2, pred[512,512]{0,1:T(8,128)(4,1)S(1)} %copy-done.12, bf16[512,12,64]{0,2,1:T(8,128)(2,1)S(1)} %bitcast.210, bf16[512,12,64]{0,2,1:T(8,128)(2,1)S(1)} %bitcast.208), kind=kOutput, calls=%fused_computation.1 | convolution fusion | flops 418375680 | bytes 27049984 | tf_op jit(solution)/shard_map/pqhd,pkhd->phqk/dot_general | solution.py:215
  246.2 7.2 %multiply_convert_fusion = bf16[12,512,512]{1,2,0:T(8,128)(2,1)S(1)} fusion(f32[12,512,512]{1,2,0:T(8,128)} %get-tuple-element.114, f32[12,512]{1,0:T(8,128)S(1)} %get-tuple-element.113, f32[12,512]{1,0:T(8,128)S(1)} %copy-done.49, f32[12,512,512]{1,2,0:T(8,128)S(1)} %bitcast.202, pred[512,512]{0,1:T(8,128)(4,1)S(1)} %copy-done.12), kind=kLoop, calls=%fused_computation | loop fusion | flops 18874368 | bytes 31768576 | tf_op jit(solution)/shard_map/convert_element_type | solution.py:219
  279.1 4.3 %concatenate.121 = bf16[2,2,2,2,2,24,777]{6,5,4,3,2,1,0:T(8,128)(2,1)} concatenate(bf16[2,2,2,2,2,24,3]{6,5,4,3,2,1,0:T(8,128)(2,1)} %bitcast.224, bf16[2,2,2,2,2,24,768]{6,5,4,3,2,1,0:T(8,128)(2,1)} %convolution_convert_fusion.2, bf16[2,2,2,2,2,24,1]{6,5,4,3,2,1,0:T(8,128)(2,1)} %stack.65, bf16[2,2,2,2,2,24,1]{6,5,4,3,2,1,0:T(8,128)(2,1)} %stack.66, ...), dimensions={6} | concatenate | bytes 2386944 | tf_op jit(solution)/shard_map/concatenate | solution.py:449
  294.7 11.0 %collective-permute-done.22 = f32[256,768]{1,0:T(8,128)S(1)} collective-permute-done((f32[256,768]{1,0:T(8,128)S(1)}, f32[256,768]{1,0:T(8,128)S(1)}, u32[]{:S(2)}, u32[]{:S(2)}) %collective-permute-start.22) | collective-permute-done | bytes 786464 | tf_op jit(solution)/shard_map/ppermute | solution.py:18
  308.1 3.6 %collective-permute-done.29 = bf16[2,2,2,24,777]{4,3,2,1,0:T(8,128)(2,1)S(1)} collective-permute-done((bf16[2,2,2,24,777]{4,3,2,1,0:T(8,128)(2,1)S(1)}, bf16[2,2,2,24,777]{4,3,2,1,0:T(8,128)(2,1)S(1)}, u32[]{:S(2)}, u32[]{:S(2)}) %collective-permute-start.29) | collective-permute-done | bytes 298400 | tf_op jit(solution)/shard_map/ppermute | solution.py:80
  (387 shorter events, 162.4 us)
Async XLA Ops:
  7.2 117.7 %all-gather.2.cloned.1.call-start = ((), (), s32[]{:S(2)}) async-start(), calls=%async_computation.1 | async-start | bytes 5222400 | tf_op jit(solution)/shard_map/all_gather | solution.py:304
  9.6 13.2 %collective-permute-start.11 = (bf16[24,1152]{1,0:T(8,128)(2,1)S(1)}, bf16[24,1152]{1,0:T(8,128)(2,1)S(1)}, u32[]{:S(2)}, u32[]{:S(2)}) collective-permute-start(bf16[24,1152]{1,0:T(8,128)(2,1)S(1)} %fusion.85), channel_id=1, source_target_pairs={{0,1},{1,0},{2,3},{3,2},{4,5},{5,4},{6,7},{7,6},{8,9},{9,8},{10,11... | collective-permute-start | bytes 165896 | tf_op jit(solution)/shard_map/ppermute | solution.py:47
  29.3 20.5 %collective-permute-start.13 = (bf16[2,2,24,1152]{3,2,1,0:T(8,128)(2,1)S(1)}, bf16[2,2,24,1152]{3,2,1,0:T(8,128)(2,1)S(1)}, u32[]{:S(2)}, u32[]{:S(2)}) collective-permute-start(bf16[2,2,24,1152]{3,2,1,0:T(8,128)(2,1)S(1)} %broadcast_select_fusion.11), channel_id=1, source_target_pairs={{0,16},{1,17},{2,18},{3,19},{4,20},{5,21},{6,22},{7,23},{8,24},{9,... | collective-permute-start | bytes 663560 | tf_op jit(solution)/shard_map/ppermute | solution.py:47
  32.0 34.6 %collective-permute-start.9 = (bf16[2,2,2,24,1024]{4,3,2,0,1:T(8,128)(2,1)S(1)}, bf16[2,2,2,24,1024]{4,3,2,0,1:T(8,128)(2,1)S(1)}, u32[]{:S(2)}, u32[]{:S(2)}) collective-permute-start(bf16[2,2,2,24,1024]{4,3,2,0,1:T(8,128)(2,1)S(1)} %broadcast_select_fusion.7), channel_id=1, source_target_pairs={{0,16},{1,17},{2,18},{3,19},{4,20},{5,21},{6,22},{7,23},{8,24},{9,... | collective-permute-start | bytes 1179656 | tf_op jit(solution)/shard_map/ppermute | solution.py:47
  34.8 15.4 %collective-permute-start.4 = (bf16[2,2,2,24,1024]{4,3,2,0,1:T(8,128)(2,1)S(1)}, bf16[2,2,2,24,1024]{4,3,2,0,1:T(8,128)(2,1)S(1)}, u32[]{:S(2)}, u32[]{:S(2)}) collective-permute-start(bf16[2,2,2,24,1024]{4,3,2,0,1:T(8,128)(2,1)S(1)} %broadcast_select_fusion.9), channel_id=1, source_target_pairs={{0,4},{1,5},{2,6},{3,7},{4,0},{5,1},{6,2},{7,3},{8,12},{9,13},{10,... | collective-permute-start | bytes 1179656 | tf_op jit(solution)/shard_map/ppermute | solution.py:47
  50.0 16.4 %collective-permute-start.14 = (bf16[2,2,2,24,1152]{4,3,2,1,0:T(8,128)(2,1)S(1)}, bf16[2,2,2,24,1152]{4,3,2,1,0:T(8,128)(2,1)S(1)}, u32[]{:S(2)}, u32[]{:S(2)}) collective-permute-start(bf16[2,2,2,24,1152]{4,3,2,1,0:T(8,128)(2,1)S(1)} %broadcast_select_fusion.6), channel_id=1, source_target_pairs={{0,8},{1,9},{2,10},{3,11},{4,12},{5,13},{6,14},{7,15},{8,0},{9,1},... | collective-permute-start | bytes 1327112 | tf_op jit(solution)/shard_map/ppermute | solution.py:47
  50.3 17.8 %collective-permute-start.5 = (bf16[2,2,2,2,24,1024]{5,4,3,0,1,2:T(8,128)(2,1)S(1)}, bf16[2,2,2,2,24,1024]{5,4,3,0,1,2:T(8,128)(2,1)S(1)}, u32[]{:S(2)}, u32[]{:S(2)}) collective-permute-start(bf16[2,2,2,2,24,1024]{5,4,3,0,1,2:T(8,128)(2,1)S(1)} %broadcast_select_fusion.4), channel_id=1, source_target_pairs={{0,2},{1,3},{2,0},{3,1},{4,6},{5,7},{6,4},{7,5},{8,10},{9,11},{10,... | collective-permute-start | bytes 2359304 | tf_op jit(solution)/shard_map/ppermute | solution.py:47
  74.1 259.7 %reduce-scatter.2.cloned.1.call-start = ((), (), s32[]{:S(2)}) async-start(), calls=%async_computation.2 | async-start | bytes 5222400 | tf_op jit(solution)/shard_map/reduce_scatter | solution.py:395
  75.3 12.2 %collective-permute-start = (bf16[256,768]{1,0:T(8,128)(2,1)}, bf16[256,768]{1,0:T(8,128)(2,1)S(1)}, u32[]{:S(2)}, u32[]{:S(2)}) collective-permute-start(bf16[256,768]{1,0:T(8,128)(2,1)} %get-tuple-element.90), channel_id=1, source_target_pairs={{0,1},{1,0},{2,3},{3,2},{4,5},{5,4},{6,7},{7,6},{8,9},{9,8},{10,11... | collective-permute-start | bytes 1179656 | tf_op jit(solution)/shard_map/ppermute | solution.py:18
  77.4 39.3 %collective-permute-start.18 = (bf16[256,768]{1,0:T(8,128)(2,1)}, bf16[256,768]{1,0:T(8,128)(2,1)}, u32[]{:S(2)}, u32[]{:S(2)}) collective-permute-start(bf16[256,768]{1,0:T(8,128)(2,1)} %get-tuple-element.87), channel_id=1, source_target_pairs={{0,1},{1,0},{2,3},{3,2},{4,5},{5,4},{6,7},{7,6},{8,9},{9,8},{10,11... | collective-permute-start | bytes 1179656 | tf_op jit(solution)/shard_map/ppermute | solution.py:18
  116.5 18.1 %collective-permute-start.16 = (bf16[512,768]{1,0:T(8,128)(2,1)S(1)}, bf16[512,768]{1,0:T(8,128)(2,1)}, u32[]{:S(2)}, u32[]{:S(2)}) collective-permute-start(bf16[512,768]{1,0:T(8,128)(2,1)S(1)} %fusion.58), channel_id=1, source_target_pairs={{0,1},{1,0},{2,3},{3,2},{4,5},{5,4},{6,7},{7,6},{8,9},{9,8},{10,11... | collective-permute-start | bytes 2359304 | tf_op jit(solution)/shard_map/ppermute | solution.py:18
  147.0 17.1 %collective-permute-start.17 = (bf16[512,768]{1,0:T(8,128)(2,1)S(1)}, bf16[512,768]{1,0:T(8,128)(2,1)S(1)}, u32[]{:S(2)}, u32[]{:S(2)}) collective-permute-start(bf16[512,768]{1,0:T(8,128)(2,1)S(1)} %fusion.51), channel_id=1, source_target_pairs={{0,1},{1,0},{2,3},{3,2},{4,5},{5,4},{6,7},{7,6},{8,9},{9,8},{10,11... | collective-permute-start | bytes 2359304 | tf_op jit(solution)/shard_map/ppermute | solution.py:18
  176.3 16.6 %collective-permute-start.19 = (bf16[512,768]{1,0:T(8,128)(2,1)}, bf16[512,768]{1,0:T(8,128)(2,1)S(1)}, u32[]{:S(2)}, u32[]{:S(2)}) collective-permute-start(bf16[512,768]{1,0:T(8,128)(2,1)} %get-tuple-element.54), channel_id=1, source_target_pairs={{0,1},{1,0},{2,3},{3,2},{4,5},{5,4},{6,7},{7,6},{8,9},{9,8},{10,11... | collective-permute-start | bytes 2359304 | tf_op jit(solution)/shard_map/ppermute | solution.py:18
  200.9 16.3 %collective-permute-start.20 = (bf16[512,768]{1,0:T(8,128)(2,1)}, bf16[512,768]{1,0:T(8,128)(2,1)}, u32[]{:S(2)}, u32[]{:S(2)}) collective-permute-start(bf16[512,768]{1,0:T(8,128)(2,1)} %fusion.48), channel_id=1, source_target_pairs={{0,1},{1,0},{2,3},{3,2},{4,5},{5,4},{6,7},{7,6},{8,9},{9,8},{10,11... | collective-permute-start | bytes 2359304 | tf_op jit(solution)/shard_map/ppermute | solution.py:18
  266.4 24.5 %collective-permute-start.21 = (f32[256,768]{1,0:T(8,128)}, f32[256,768]{1,0:T(8,128)}, u32[]{:S(2)}, u32[]{:S(2)}) collective-permute-start(f32[256,768]{1,0:T(8,128)} %get-tuple-element.80), channel_id=1, source_target_pairs={{0,1},{1,0},{2,3},{3,2},{4,5},{5,4},{6,7},{7,6},{8,9},{9,8},{10,11... | collective-permute-start | bytes 2359304 | tf_op jit(solution)/shard_map/ppermute | solution.py:18
  269.9 16.3 %collective-permute-start.38 = (bf16[2,2,2,2,24,768]{5,4,3,2,0,1:T(8,128)(2,1)}, bf16[2,2,2,2,24,768]{5,4,3,2,0,1:T(8,128)(2,1)}, u32[]{:S(2)}, u32[]{:S(2)}) collective-permute-start(bf16[2,2,2,2,24,768]{5,4,3,2,0,1:T(8,128)(2,1)} %bitcast.198), channel_id=1, source_target_pairs={{0,2},{1,3},{2,0},{3,1},{4,6},{5,7},{6,4},{7,5},{8,10},{9,11},{10,... | collective-permute-start | bytes 1769480 | tf_op jit(solution)/shard_map/ppermute | solution.py:80
  285.8 19.9 %collective-permute-start.22 = (f32[256,768]{1,0:T(8,128)S(1)}, f32[256,768]{1,0:T(8,128)S(1)}, u32[]{:S(2)}, u32[]{:S(2)}) collective-permute-start(f32[256,768]{1,0:T(8,128)S(1)} %copy-done.40), channel_id=1, source_target_pairs={{0,1},{1,0},{2,3},{3,2},{4,5},{5,4},{6,7},{7,6},{8,9},{9,8},{10,11... | collective-permute-start | bytes 2359304 | tf_op jit(solution)/shard_map/ppermute | solution.py:18
  287.9 19.0 %collective-permute-start.39 = (bf16[2,2,2,24,768]{4,3,2,1,0:T(8,128)(2,1)S(1)}, bf16[2,2,2,24,768]{4,3,2,1,0:T(8,128)(2,1)S(1)}, u32[]{:S(2)}, u32[]{:S(2)}) collective-permute-start(bf16[2,2,2,24,768]{4,3,2,1,0:T(8,128)(2,1)S(1)} %fusion.75), channel_id=1, source_target_pairs={{0,8},{1,9},{2,10},{3,11},{4,12},{5,13},{6,14},{7,15},{8,0},{9,1},... | collective-permute-start | bytes 884744 | tf_op jit(solution)/shard_map/ppermute | solution.py:80
  289.3 17.8 %collective-permute-start.24 = (bf16[2,2,2,24,768]{4,3,2,0,1:T(8,128)(2,1)S(1)}, bf16[2,2,2,24,768]{4,3,2,0,1:T(8,128)(2,1)S(1)}, u32[]{:S(2)}, u32[]{:S(2)}) collective-permute-start(bf16[2,2,2,24,768]{4,3,2,0,1:T(8,128)(2,1)S(1)} %fusion.73), channel_id=1, source_target_pairs={{0,4},{1,5},{2,6},{3,7},{4,0},{5,1},{6,2},{7,3},{8,12},{9,13},{10,... | collective-permute-start | bytes 884744 | tf_op jit(solution)/shard_map/ppermute | solution.py:80
  289.6 17.7 %collective-permute-start.34 = (bf16[2,2,2,24,768]{4,3,2,0,1:T(8,128)(2,1)S(1)}, bf16[2,2,2,24,768]{4,3,2,0,1:T(8,128)(2,1)S(1)}, u32[]{:S(2)}, u32[]{:S(2)}) collective-permute-start(bf16[2,2,2,24,768]{4,3,2,0,1:T(8,128)(2,1)S(1)} %fusion.74), channel_id=1, source_target_pairs={{0,16},{1,17},{2,18},{3,19},{4,20},{5,21},{6,22},{7,23},{8,24},{9,... | collective-permute-start | bytes 884744 | tf_op jit(solution)/shard_map/ppermute | solution.py:80
  290.9 20.7 %collective-permute-start.29 = (bf16[2,2,2,24,777]{4,3,2,1,0:T(8,128)(2,1)S(1)}, bf16[2,2,2,24,777]{4,3,2,1,0:T(8,128)(2,1)S(1)}, u32[]{:S(2)}, u32[]{:S(2)}) collective-permute-start(bf16[2,2,2,24,777]{4,3,2,1,0:T(8,128)(2,1)S(1)} %fusion.72), channel_id=1, source_target_pairs={{0,8},{1,9},{2,10},{3,11},{4,12},{5,13},{6,14},{7,15},{8,0},{9,1},... | collective-permute-start | bytes 895112 | tf_op jit(solution)/shard_map/ppermute | solution.py:80
  307.2 9.8 %collective-permute-start.25 = (bf16[2,2,24,768]{3,2,1,0:T(8,128)(2,1)S(1)}, bf16[2,2,24,768]{3,2,1,0:T(8,128)(2,1)S(1)}, u32[]{:S(2)}, u32[]{:S(2)}) collective-permute-start(bf16[2,2,24,768]{3,2,1,0:T(8,128)(2,1)S(1)} %fusion.77), channel_id=1, source_target_pairs={{0,8},{1,9},{2,10},{3,11},{4,12},{5,13},{6,14},{7,15},{8,0},{9,1},... | collective-permute-start | bytes 442376 | tf_op jit(solution)/shard_map/ppermute | solution.py:80
  307.4 9.8 %collective-permute-start.35 = (bf16[2,2,24,768]{3,2,1,0:T(8,128)(2,1)S(1)}, bf16[2,2,24,768]{3,2,1,0:T(8,128)(2,1)S(1)}, u32[]{:S(2)}, u32[]{:S(2)}) collective-permute-start(bf16[2,2,24,768]{3,2,1,0:T(8,128)(2,1)S(1)} %fusion.78), channel_id=1, source_target_pairs={{0,4},{1,5},{2,6},{3,7},{4,0},{5,1},{6,2},{7,3},{8,12},{9,13},{10,... | collective-permute-start | bytes 442376 | tf_op jit(solution)/shard_map/ppermute | solution.py:80
  317.3 10.3 %collective-permute-start.36 = (bf16[2,24,768]{2,1,0:T(8,128)(2,1)S(1)}, bf16[2,24,768]{2,1,0:T(8,128)(2,1)S(1)}, u32[]{:S(2)}, u32[]{:S(2)}) collective-permute-start(bf16[2,24,768]{2,1,0:T(8,128)(2,1)S(1)} %fusion.83), channel_id=1, source_target_pairs={{0,8},{1,9},{2,10},{3,11},{4,12},{5,13},{6,14},{7,15},{8,0},{9,1},... | collective-permute-start | bytes 221192 | tf_op jit(solution)/shard_map/ppermute | solution.py:80
  (94 other events, 670.9 us)
Sparse Core Ops, SparseCore 0:
  74.3 50.6 all-gather.1
  215.8 72.8 reduce-scatter.1
